TPU v7x, 32 devices: a whole 2x2x4 slice. The times are simulated.
32 devices in a mesh: ctx: 8 (over y, x, core), fsdp: 4 (over z).
Axes of the slice: x: 2, y: 2, z: 4, core: 2. Of those that a mesh axis runs over, the one named last changes fastest.
Arguments:
- block_input: bfloat16 [4, 2048, 1536], P('fsdp', 'ctx'), may hold values from -6 to 6
- block_table: int32 [4, 16], P('fsdp'), may hold values from 0 to 15, as said below
- output_grad: bfloat16 [4, 2048, 1536], P('fsdp', 'ctx'), may hold values from -6 to 6
- attention_gain: bfloat16 [1536], P('fsdp'), may hold values from 0.099609375 to 1.8984375
- query_weight: bfloat16 [1536, 1536], P('fsdp'), may hold values from -5 to 5
- key_weight: bfloat16 [1536, 768], P('fsdp'), may hold values from -1 to 1
- value_projection: bfloat16 [1536, 768], P('fsdp'), may hold values from -0.15625 to 0.15625
- output_weight: bfloat16 [1536, 1536], P('fsdp'), may hold values from -2.5 to 2.5
- feedforward_gain: bfloat16 [1536], P('fsdp'), may hold values from 0.099609375 to 1.8984375
- gate_weight: bfloat16 [1536, 4096], P('fsdp'), may hold values from -0.15625 to 0.15625
- up_weight: bfloat16 [1536, 4096], P('fsdp'), may hold values from -0.15625 to 0.15625
- down_weight: bfloat16 [4096, 1536], P('fsdp'), may hold values from -0.09375 to 0.09375
Outputs:
- layer_output: bfloat16 [4, 2048, 1536], P('fsdp', 'ctx')
- input_grad: float32 [4, 2048, 1536], P('fsdp', 'ctx')
- attention_gain_grad: float32 [1536], P('fsdp')
- query_weight_grad: float32 [1536, 1536], P('fsdp')
- key_weight_grad: float32 [1536, 768], P('fsdp')
- value_weight_grad: float32 [1536, 768], P('fsdp')
- output_weight_grad: float32 [1536, 1536], P('fsdp')
- feedforward_gain_grad: float32 [1536], P('fsdp')
- gate_weight_grad: float32 [1536, 4096], P('fsdp')
- up_weight_grad: float32 [1536, 4096], P('fsdp')
- down_weight_grad: float32 [4096, 1536], P('fsdp')
Inputs may be any that keep to these rules, and one draw needn't show every extreme that they name: `block_table`: in every sequence, the two storage slots 2 c and 2 c + 1 hold the blocks p and 15 - p for some p, in either order, and every block stands in exactly one slot.
All inputs are finite; a program needn't handle non-finite values.
Results may differ from a plain program's by a relative error of at most 0.024.
Values may be sent and summed in bfloat16 or wider, within the bound.
A program may use at most 384 MiB of HBM per device.

v0:
```python
import math

import jax
import jax.numpy as jnp
from jax import lax
from jax.sharding import PartitionSpec as P

QUERY_HEADS = 16
KEY_VALUE_HEADS = 8
HEAD_SIZE = 96


norm_epsilon = 1e-05
rotary_base = 100000.0
score_with_mask = -1e30


def rope_tables(positions):
    half_width = HEAD_SIZE // 2
    steps_index = jnp.arange(half_width, dtype=jnp.float32)
    inverse = jnp.exp(steps_index * jnp.float32(-2.0 * math.log(rotary_base) / HEAD_SIZE))
    angles = positions.astype(jnp.float32)[:, None] * inverse[None, :]
    return (jnp.cos(angles), jnp.sin(angles))


def rotate(value_rows, cosine, sine_values, direction):
    count_of_rows = value_rows.shape[0]
    head_count = value_rows.shape[1] // HEAD_SIZE
    half_width = HEAD_SIZE // 2
    shaped = value_rows.reshape(count_of_rows, head_count, HEAD_SIZE)
    first_half = shaped[:, :, :half_width]
    second_half = shaped[:, :, half_width:]
    cos_part = cosine[:, None, :]
    sin_part = sine_values[:, None, :] * direction
    turned = jnp.concatenate(
        [
            first_half * cos_part - second_half * sin_part,
            second_half * cos_part + first_half * sin_part,
        ],
        axis=2,
    )
    return turned.reshape(count_of_rows, head_count * HEAD_SIZE)


def norm_scale(value_rows):
    return lax.rsqrt(jnp.mean(value_rows * value_rows, axis=-1, keepdims=True) + norm_epsilon)


def product(matrix, operand):
    return jnp.dot(matrix, operand, preferred_element_type=jnp.float32)


def cross_rows(matrix, operand):
    return lax.dot_general(
        matrix, operand, (((0,), (0,)), ((), ())), preferred_element_type=jnp.float32
    )


def back_product(matrix, operand):
    return lax.dot_general(
        matrix, operand, (((1,), (1,)), ((), ())), preferred_element_type=jnp.float32
    )


def block_scores(query_rank_four, block_of_keys, query_positions, key_positions):
    keys_rank_three = block_of_keys.reshape(block_of_keys.shape[0], KEY_VALUE_HEADS, HEAD_SIZE)
    scores = jnp.einsum(
        "rgjd,kgd->gjrk", query_rank_four, keys_rank_three, preferred_element_type=jnp.float32
    ) * HEAD_SIZE ** (-0.5)
    allowed = (key_positions[None, :] <= query_positions[:, None])[None, None]
    return (jnp.where(allowed, scores, score_with_mask), allowed)


def local(
    block_input,
    block_table,
    output_grad,
    attention_gain,
    query_weight,
    key_weight,
    value_projection,
    output_weight,
    feedforward_gain,
    gate_weight,
    up_weight,
    down_weight,
):
    query_group_width = QUERY_HEADS // KEY_VALUE_HEADS
    score_scale = HEAD_SIZE ** (-0.5)
    inputs = block_input[0].astype(jnp.float32)
    count_of_rows = inputs.shape[0]
    block_rows = count_of_rows // 2
    ctx_index = lax.axis_index("ctx")
    table_row = block_table[0]
    offsets = jnp.arange(block_rows, dtype=jnp.int32)
    query_blocks = lax.dynamic_slice_in_dim(table_row, 2 * ctx_index, 2)
    query_positions = (query_blocks[:, None] * block_rows + offsets[None, :]).reshape(count_of_rows)
    key_positions = (table_row[:, None] * block_rows + offsets[None, :]).reshape(-1)
    cosine, sine_values = rope_tables(query_positions)
    gain_one, query_full, key_full, value_full, out_full = (
        lax.all_gather(attention_gain, "fsdp", axis=0, tiled=True),
        lax.all_gather(query_weight, "fsdp", axis=0, tiled=True),
        lax.all_gather(key_weight, "fsdp", axis=0, tiled=True),
        lax.all_gather(value_projection, "fsdp", axis=0, tiled=True),
        lax.all_gather(output_weight, "fsdp", axis=0, tiled=True),
    )
    scale_one = norm_scale(inputs)
    normed_one = inputs * scale_one
    gained_one = (normed_one * gain_one.astype(jnp.float32)).astype(jnp.bfloat16)
    query_rows = rotate(product(gained_one, query_full), cosine, sine_values, 1.0).astype(
        jnp.bfloat16
    )
    keys_local = rotate(product(gained_one, key_full), cosine, sine_values, 1.0).astype(
        jnp.bfloat16
    )
    values_local = product(gained_one, value_full).astype(jnp.bfloat16)
    keys_all, values_all = (
        lax.all_gather(keys_local, "ctx", axis=0, tiled=True),
        lax.all_gather(values_local, "ctx", axis=0, tiled=True),
    )
    key_total_count = keys_all.shape[0]
    key_block_pass = 1024
    block_count = key_total_count // key_block_pass
    query_rank_four = query_rows.reshape(
        count_of_rows, KEY_VALUE_HEADS, query_group_width, HEAD_SIZE
    )
    key_places = key_positions.reshape(block_count, key_block_pass)

    def split_keys(array_in):
        return array_in.reshape(block_count, key_block_pass, array_in.shape[-1])

    def statistics_step(state_now, block_data):
        running_max, running_sum = state_now
        block_of_keys, key_place = block_data
        masked, allowed = block_scores(query_rank_four, block_of_keys, query_positions, key_place)
        new_max = jnp.maximum(running_max, jnp.max(masked, axis=-1))
        block_sum = jnp.sum(jnp.where(allowed, jnp.exp(masked - new_max[..., None]), 0.0), axis=-1)
        return ((new_max, running_sum * jnp.exp(running_max - new_max) + block_sum), None)

    initial_maximum = jnp.full(
        (KEY_VALUE_HEADS, query_group_width, count_of_rows), score_with_mask, jnp.float32
    )
    initial_sum = jnp.zeros((KEY_VALUE_HEADS, query_group_width, count_of_rows), jnp.float32)
    (final_max, final_sum), unused = lax.scan(
        statistics_step, (initial_maximum, initial_sum), (split_keys(keys_all), key_places)
    )
    log_total = final_max + jnp.log(final_sum)

    def output_step(state_now, block_data):
        block_of_keys, block_of_values, key_place = block_data
        masked, allowed = block_scores(query_rank_four, block_of_keys, query_positions, key_place)
        weights_half = jnp.where(allowed, jnp.exp(masked - log_total[..., None]), 0.0).astype(
            jnp.bfloat16
        )
        values_rank_three = block_of_values.reshape(key_block_pass, KEY_VALUE_HEADS, HEAD_SIZE)
        return (
            state_now
            + jnp.einsum(
                "gjrk,kgd->rgjd",
                weights_half,
                values_rank_three,
                preferred_element_type=jnp.float32,
            ),
            None,
        )

    initial_output = jnp.zeros(
        (count_of_rows, KEY_VALUE_HEADS, query_group_width, HEAD_SIZE), jnp.float32
    )
    summed_out, unused = lax.scan(
        output_step, initial_output, (split_keys(keys_all), split_keys(values_all), key_places)
    )
    attended_rows = summed_out.reshape(count_of_rows, QUERY_HEADS * HEAD_SIZE).astype(jnp.bfloat16)
    residual = inputs + product(attended_rows, out_full)
    scale_two = norm_scale(residual)
    normed_two = residual * scale_two
    gain_two, gate_full, up_full, down_full = (
        lax.all_gather(feedforward_gain, "fsdp", axis=0, tiled=True),
        lax.all_gather(gate_weight, "fsdp", axis=0, tiled=True),
        lax.all_gather(up_weight, "fsdp", axis=0, tiled=True),
        lax.all_gather(down_weight, "fsdp", axis=0, tiled=True),
    )
    gained_two = (normed_two * gain_two.astype(jnp.float32)).astype(jnp.bfloat16)
    gate_values = product(gained_two, gate_full)
    up_values = product(gained_two, up_full)
    sigmoid_gate = jax.nn.sigmoid(gate_values)
    activated = gate_values * sigmoid_gate
    hidden_act = (activated * up_values).astype(jnp.bfloat16)
    layer_output = (residual + product(hidden_act, down_full)).astype(jnp.bfloat16)
    gain_two_again, gate_back, up_back, down_back = (
        lax.all_gather(feedforward_gain, "fsdp", axis=0, tiled=True),
        lax.all_gather(gate_weight, "fsdp", axis=0, tiled=True),
        lax.all_gather(up_weight, "fsdp", axis=0, tiled=True),
        lax.all_gather(down_weight, "fsdp", axis=0, tiled=True),
    )
    grad_rows = output_grad[0]
    grad_hidden = back_product(grad_rows, down_back)
    down_term = cross_rows(hidden_act, grad_rows)
    grad_gate = (
        grad_hidden * up_values * sigmoid_gate * (1.0 + gate_values * (1.0 - sigmoid_gate))
    ).astype(jnp.bfloat16)
    grad_up = (grad_hidden * activated).astype(jnp.bfloat16)
    gate_term = cross_rows(gained_two, grad_gate)
    up_term = cross_rows(gained_two, grad_up)
    grad_normed_two = back_product(grad_gate, gate_back) + back_product(grad_up, up_back)
    feedforward_term = jnp.sum(grad_normed_two * normed_two, axis=0)
    grad_scaled_two = grad_normed_two * gain_two_again.astype(jnp.float32)
    grad_residual = grad_rows.astype(jnp.float32) + scale_two * (
        grad_scaled_two
        - normed_two * jnp.mean(grad_scaled_two * normed_two, axis=-1, keepdims=True)
    )
    gain_one_again, query_back, key_back, value_back, out_back = (
        lax.all_gather(attention_gain, "fsdp", axis=0, tiled=True),
        lax.all_gather(query_weight, "fsdp", axis=0, tiled=True),
        lax.all_gather(key_weight, "fsdp", axis=0, tiled=True),
        lax.all_gather(value_projection, "fsdp", axis=0, tiled=True),
        lax.all_gather(output_weight, "fsdp", axis=0, tiled=True),
    )
    grad_attn = grad_residual.astype(jnp.bfloat16)
    output_term = cross_rows(attended_rows, grad_attn)
    attended_gradient = back_product(grad_attn, out_back).astype(jnp.bfloat16)
    gradient_rank_four = attended_gradient.reshape(
        count_of_rows, KEY_VALUE_HEADS, query_group_width, HEAD_SIZE
    )
    attended_rank_four = attended_rows.reshape(
        count_of_rows, KEY_VALUE_HEADS, query_group_width, HEAD_SIZE
    )
    row_delta = jnp.transpose(
        jnp.sum(
            gradient_rank_four.astype(jnp.float32) * attended_rank_four.astype(jnp.float32), axis=-1
        ),
        (1, 2, 0),
    )
    keys_again, values_again = (
        lax.all_gather(keys_local, "ctx", axis=0, tiled=True),
        lax.all_gather(values_local, "ctx", axis=0, tiled=True),
    )

    def back_step(state_now, block_data):
        block_of_keys, block_of_values, key_place = block_data
        masked, allowed = block_scores(query_rank_four, block_of_keys, query_positions, key_place)
        weights_half = jnp.where(allowed, jnp.exp(masked - log_total[..., None]), 0.0).astype(
            jnp.bfloat16
        )
        values_rank_three = block_of_values.reshape(key_block_pass, KEY_VALUE_HEADS, HEAD_SIZE)
        keys_rank_three = block_of_keys.reshape(key_block_pass, KEY_VALUE_HEADS, HEAD_SIZE)
        grad_weights = jnp.einsum(
            "rgjd,kgd->gjrk",
            gradient_rank_four,
            values_rank_three,
            preferred_element_type=jnp.float32,
        )
        grad_scores = (
            weights_half.astype(jnp.float32) * (grad_weights - row_delta[..., None]) * score_scale
        ).astype(jnp.bfloat16)
        state_now = state_now + jnp.einsum(
            "gjrk,kgd->rgjd", grad_scores, keys_rank_three, preferred_element_type=jnp.float32
        )
        key_gradient = jnp.einsum(
            "gjrk,rgjd->kgd", grad_scores, query_rank_four, preferred_element_type=jnp.float32
        )
        value_gradient = jnp.einsum(
            "gjrk,rgjd->kgd", weights_half, gradient_rank_four, preferred_element_type=jnp.float32
        )
        return (
            state_now,
            (
                key_gradient.reshape(key_block_pass, KEY_VALUE_HEADS * HEAD_SIZE).astype(
                    jnp.bfloat16
                ),
                value_gradient.reshape(key_block_pass, KEY_VALUE_HEADS * HEAD_SIZE).astype(
                    jnp.bfloat16
                ),
            ),
        )

    first_query_index = jnp.zeros(
        (count_of_rows, KEY_VALUE_HEADS, query_group_width, HEAD_SIZE), jnp.float32
    )
    query_sum, (key_gradients, value_gradients) = lax.scan(
        back_step, first_query_index, (split_keys(keys_again), split_keys(values_again), key_places)
    )
    key_gradients = key_gradients.reshape(key_total_count, KEY_VALUE_HEADS * HEAD_SIZE)
    value_gradients = value_gradients.reshape(key_total_count, KEY_VALUE_HEADS * HEAD_SIZE)
    key_sums, value_sums = (
        lax.psum_scatter(key_gradients, "ctx", scatter_dimension=0, tiled=True).astype(jnp.float32),
        lax.psum_scatter(value_gradients, "ctx", scatter_dimension=0, tiled=True).astype(
            jnp.float32
        ),
    )
    query_gradients = rotate(
        query_sum.reshape(count_of_rows, QUERY_HEADS * HEAD_SIZE), cosine, sine_values, -1.0
    ).astype(jnp.bfloat16)
    grad_keys = rotate(key_sums, cosine, sine_values, -1.0).astype(jnp.bfloat16)
    grad_values = value_sums.astype(jnp.bfloat16)
    query_term = cross_rows(gained_one, query_gradients)
    key_term = cross_rows(gained_one, grad_keys)
    value_term = cross_rows(gained_one, grad_values)
    grad_normed_one = (
        back_product(query_gradients, query_back)
        + back_product(grad_keys, key_back)
        + back_product(grad_values, value_back)
    )
    attention_term = jnp.sum(grad_normed_one * normed_one, axis=0)
    grad_scaled_one = grad_normed_one * gain_one_again.astype(jnp.float32)
    input_grad = grad_residual + scale_one * (
        grad_scaled_one
        - normed_one * jnp.mean(grad_scaled_one * normed_one, axis=-1, keepdims=True)
    )
    shares = (
        lax.psum_scatter(
            attention_term.astype(jnp.bfloat16), "fsdp", scatter_dimension=0, tiled=True
        ).astype(jnp.float32),
        lax.psum_scatter(
            query_term.astype(jnp.bfloat16), "fsdp", scatter_dimension=0, tiled=True
        ).astype(jnp.float32),
        lax.psum_scatter(
            key_term.astype(jnp.bfloat16), "fsdp", scatter_dimension=0, tiled=True
        ).astype(jnp.float32),
        lax.psum_scatter(
            value_term.astype(jnp.bfloat16), "fsdp", scatter_dimension=0, tiled=True
        ).astype(jnp.float32),
        lax.psum_scatter(
            output_term.astype(jnp.bfloat16), "fsdp", scatter_dimension=0, tiled=True
        ).astype(jnp.float32),
        lax.psum_scatter(
            feedforward_term.astype(jnp.bfloat16), "fsdp", scatter_dimension=0, tiled=True
        ).astype(jnp.float32),
        lax.psum_scatter(
            gate_term.astype(jnp.bfloat16), "fsdp", scatter_dimension=0, tiled=True
        ).astype(jnp.float32),
        lax.psum_scatter(
            up_term.astype(jnp.bfloat16), "fsdp", scatter_dimension=0, tiled=True
        ).astype(jnp.float32),
        lax.psum_scatter(
            down_term.astype(jnp.bfloat16), "fsdp", scatter_dimension=0, tiled=True
        ).astype(jnp.float32),
    )
    totals = (
        lax.psum(shares[0].astype(jnp.bfloat16), "ctx").astype(jnp.float32),
        lax.psum(shares[1].astype(jnp.bfloat16), "ctx").astype(jnp.float32),
        lax.psum(shares[2].astype(jnp.bfloat16), "ctx").astype(jnp.float32),
        lax.psum(shares[3].astype(jnp.bfloat16), "ctx").astype(jnp.float32),
        lax.psum(shares[4].astype(jnp.bfloat16), "ctx").astype(jnp.float32),
        lax.psum(shares[5].astype(jnp.bfloat16), "ctx").astype(jnp.float32),
        lax.psum(shares[6].astype(jnp.bfloat16), "ctx").astype(jnp.float32),
        lax.psum(shares[7].astype(jnp.bfloat16), "ctx").astype(jnp.float32),
        lax.psum(shares[8].astype(jnp.bfloat16), "ctx").astype(jnp.float32),
    )
    return (
        layer_output[None],
        input_grad[None],
        totals[0],
        totals[1],
        totals[2],
        totals[3],
        totals[4],
        totals[5],
        totals[6],
        totals[7],
        totals[8],
    )


def solution(mesh):
    return jax.shard_map(
        local,
        mesh=mesh,
        in_specs=(
            P("fsdp", "ctx", None),
            P("fsdp", None),
            P("fsdp", "ctx", None),
            P("fsdp"),
            P("fsdp", None),
            P("fsdp", None),
            P("fsdp", None),
            P("fsdp", None),
            P("fsdp"),
            P("fsdp", None),
            P("fsdp", None),
            P("fsdp", None),
        ),
        out_specs=(
            P("fsdp", "ctx", None),
            P("fsdp", "ctx", None),
            P("fsdp"),
            P("fsdp", None),
            P("fsdp", None),
            P("fsdp", None),
            P("fsdp", None),
            P("fsdp"),
            P("fsdp", None),
            P("fsdp", None),
            P("fsdp", None),
        ),
        check_vma=False,
    )
```

profile of v0, /device:TPU:0, one launch (start us, length us, event | category | flops | bytes accessed | tf_op | source)
XLA Modules:
  0.0 2365.5 jit_solution(15789600976923604086)
XLA Ops:
  9.5 13.6 all-gather
  23.4 38.9 %all-gather.12.cloned.1.call-done = bf16[1536,768]{1,0:T(8,128)(2,1)} async-done(((bf16[384,768]{1,0:T(8,128)(2,1)}), bf16[1536,768]{1,0:T(8,128)(2,1)}) %all-gather.12.cloned.1.call-update) | async-done | bytes 2359312 | tf_op jit(solution)/shard_map/all_gather | solution.py:104
  66.7 46.0 %all-gather.16.cloned.1.call-done = bf16[1536,768]{1,0:T(8,128)(2,1)} async-done(((bf16[384,768]{1,0:T(8,128)(2,1)}), bf16[1536,768]{1,0:T(8,128)(2,1)}) %all-gather.16.cloned.1.call-update) | async-done | bytes 2359312 | tf_op jit(solution)/shard_map/all_gather | solution.py:103
  120.5 12.5 all-gather.1
  133.2 69.4 %all-gather.20.cloned.1.call-done = bf16[1536,1536]{1,0:T(8,128)(2,1)} async-done(((bf16[384,1536]{1,0:T(8,128)(2,1)}), bf16[1536,1536]{1,0:T(8,128)(2,1)}) %all-gather.20.cloned.1.call-update) | async-done | bytes 4718608 | tf_op jit(solution)/shard_map/all_gather | solution.py:102
  202.6 6.6 copy.56
  214.4 21.0 all-gather.14.cloned.1.call-done
  240.1 29.9 %all-gather.18.cloned.1.call-done = bf16[2048,768]{1,0:T(8,128)(2,1)} async-done(((bf16[256,768]{1,0:T(8,128)(2,1)}), bf16[2048,768]{1,0:T(8,128)(2,1)}) %all-gather.18.cloned.1.call-update) | async-done | bytes 3145744 | tf_op jit(solution)/shard_map/all_gather | solution.py:118
  273.2 34.0 %while.39 = (s32[]{:T(128)}, f32[8,2,256]{2,1,0:T(2,128)S(1)}, f32[8,2,256]{2,1,0:T(2,128)S(1)}, s32[2,1024]{1,0:T(2,128)S(1)}, bf16[2,1024,768]{1,2,0:T(8,128)(...) while((s32[]{:T(128)}, f32[8,2,256]{2,1,0:T(2,128)S(1)}, ...), condition=%wide.region_4.5_spmd.clone, body=%wide.region_1.4_spmd.clone.sunk | while | flops 839143680 | bytes 43219096 | solution.py:144
  274.4 8.0 fusion.133
  282.4 8.0 select_reduce_fusion.2
  291.7 7.4 fusion.133
  299.1 8.1 select_reduce_fusion.2
  307.3 26.3 %while.40 = (s32[]{:T(128)}, f32[256,8,2,96]{0,3,2,1:T(8,128)}, bf16[2,1024,768]{1,2,0:T(8,128)(2,1)}, s32[2,1024]{1,0:T(2,128)S(1)}, bf16[2,1024,768]{1,2,0:T(8...) while((s32[]{:T(128)}, f32[256,8,2,96]{0,3,2,1:T(8,128)}, ...), condition=%wide.region_6.7_spmd.clone, body=%wide.region_5.6_spmd.clone.sunk | while | flops 1632633088 | bytes 13924487 | solution.py:170
  311.0 9.0 bitcast_add_fusion.5
  323.6 9.5 bitcast_add_fusion.5
  336.0 24.9 %all-gather.22.cloned.1.call-done = bf16[1536,1536]{1,0:T(8,128)(2,1)} async-done(((bf16[384,1536]{1,0:T(8,128)(2,1)}), bf16[1536,1536]{1,0:T(8,128)(2,1)}) %all-gather.22.cloned.1.call-update) | async-done | bytes 4718608 | tf_op jit(solution)/shard_map/all_gather | solution.py:105
  367.4 211.7 %all-gather.24.cloned.1.call-done = bf16[1536,4096]{1,0:T(8,128)(2,1)} async-done(((bf16[384,4096]{1,0:T(8,128)(2,1)}), bf16[1536,4096]{1,0:T(8,128)(2,1)}) %all-gather.24.cloned.1.call-update) | async-done | bytes 12582928 | tf_op jit(solution)/shard_map/all_gather | solution.py:179
  579.1 10.4 fusion.60
  589.5 207.5 %all-gather.26.cloned.1.call-done = bf16[1536,4096]{1,0:T(8,128)(2,1)} async-done(((bf16[384,4096]{1,0:T(8,128)(2,1)}), bf16[1536,4096]{1,0:T(8,128)(2,1)}) %all-gather.26.cloned.1.call-update) | async-done | bytes 12582928 | tf_op jit(solution)/shard_map/all_gather | solution.py:180
  797.0 10.4 fusion.61
  807.5 207.5 %all-gather.28.cloned.1.call-done = bf16[4096,1536]{1,0:T(8,128)(2,1)} async-done(((bf16[1024,1536]{1,0:T(8,128)(2,1)}), bf16[4096,1536]{1,0:T(8,128)(2,1)}) %all-gather.28.cloned.1.call-update) | async-done | bytes 12582928 | tf_op jit(solution)/shard_map/all_gather | solution.py:181
  1015.0 11.4 multiply_convert_fusion
  1026.4 7.3 fusion.62
  1033.7 10.8 multiply_reduce_fusion
  1054.2 87.8 %while.41 = (s32[]{:T(128)}, f32[256,8,2,96]{0,3,2,1:T(8,128)}, bf16[2,1024,768]{2,1,0:T(8,128)(2,1)}, bf16[2,1024,768]{2,1,0:T(8,128)(2,1)}, bf16[2,1024,768]{1...) while((s32[]{:T(128)}, f32[256,8,2,96]{0,3,2,1:T(8,128)}, ...), condition=%wide.region_11.12_spmd.clone, body=%wide.region_10.11_spmd.clone.sunk | while | flops 4071096576 | bytes 179353984 | solution.py:280
  1064.3 7.0 fusion.150
  1071.4 6.5 bitcast_add_fusion.6
  1084.3 7.3 bitcast_convert_fusion.5
  1107.9 7.0 fusion.150
  1115.0 7.0 bitcast_add_fusion.6
  1128.4 7.3 bitcast_convert_fusion.5
  1148.1 38.4 %reduce-scatter.10.cloned.1.call-done = bf16[256,768]{1,0:T(8,128)(2,1)} async-done(((bf16[2048,768]{1,0:T(8,128)(2,1)}), bf16[256,768]{1,0:T(8,128)(2,1)}) %reduce-scatter.10.cloned.1.call-update) | async-done | bytes 393232 | tf_op jit(solution)/shard_map/reduce_scatter | solution.py:286
  1190.1 45.7 %reduce-scatter.12.cloned.1.call-done = bf16[256,768]{1,0:T(8,128)(2,1)} async-done(((bf16[2048,768]{1,0:T(8,128)(2,1)}), bf16[256,768]{1,0:T(8,128)(2,1)}) %reduce-scatter.12.cloned.1.call-update) | async-done | bytes 393232 | tf_op jit(solution)/shard_map/reduce_scatter | solution.py:287
  1245.6 7.9 convolution_convert_fusion.2
  1253.6 8.1 convolution_convert_fusion.1
  1262.9 8.1 convolution_convert_fusion
  1271.3 52.6 %reduce-scatter.14.cloned.1.call-done = bf16[384,1536]{1,0:T(8,128)(2,1)} async-done(((bf16[1536,1536]{1,0:T(8,128)(2,1)}), bf16[384,1536]{1,0:T(8,128)(2,1)}) %reduce-scatter.14.cloned.1.call-update) | async-done | bytes 1179664 | tf_op jit(solution)/shard_map/reduce_scatter | solution.py:314
  1323.9 51.1 %reduce-scatter.16.cloned.1.call-done = bf16[384,768]{1,0:T(8,128)(2,1)} async-done(((bf16[1536,768]{1,0:T(8,128)(2,1)}), bf16[384,768]{1,0:T(8,128)(2,1)}) %reduce-scatter.16.cloned.1.call-update) | async-done | bytes 589840 | tf_op jit(solution)/shard_map/reduce_scatter | solution.py:317
  1375.1 49.9 %reduce-scatter.18.cloned.1.call-done = bf16[384,768]{1,0:T(8,128)(2,1)} async-done(((bf16[1536,768]{1,0:T(8,128)(2,1)}), bf16[384,768]{1,0:T(8,128)(2,1)}) %reduce-scatter.18.cloned.1.call-update) | async-done | bytes 589840 | tf_op jit(solution)/shard_map/reduce_scatter | solution.py:320
  1424.9 87.4 %reduce-scatter.20.cloned.1.call-done = bf16[384,1536]{1,0:T(8,128)(2,1)} async-done(((bf16[1536,1536]{1,0:T(8,128)(2,1)}), bf16[384,1536]{1,0:T(8,128)(2,1)}) %reduce-scatter.20.cloned.1.call-update) | async-done | bytes 1179664 | tf_op jit(solution)/shard_map/reduce_scatter | solution.py:323
  1512.3 214.6 %reduce-scatter.22.cloned.1.call-done = bf16[384,4096]{1,0:T(8,128)(2,1)} async-done(((bf16[1536,4096]{1,0:T(8,128)(2,1)}), bf16[384,4096]{1,0:T(8,128)(2,1)}) %reduce-scatter.22.cloned.1.call-update) | async-done | bytes 3145744 | tf_op jit(solution)/shard_map/reduce_scatter | solution.py:329
  1727.0 215.1 %reduce-scatter.24.cloned.1.call-done = bf16[384,4096]{1,0:T(8,128)(2,1)} async-done(((bf16[1536,4096]{1,0:T(8,128)(2,1)}), bf16[384,4096]{1,0:T(8,128)(2,1)}) %reduce-scatter.24.cloned.1.call-update) | async-done | bytes 3145744 | tf_op jit(solution)/shard_map/reduce_scatter | solution.py:332
  1942.1 215.2 %reduce-scatter.26.cloned.1.call-done = bf16[1024,1536]{1,0:T(8,128)(2,1)} async-done(((bf16[4096,1536]{1,0:T(8,128)(2,1)}), bf16[1024,1536]{1,0:T(8,128)(2,1)}) %reduce-scatter.26.cloned.1.call-update) | async-done | bytes 3145744 | tf_op jit(solution)/shard_map/reduce_scatter | solution.py:335
  2163.1 7.6 fusion.26
  2174.6 11.7 all-reduce.4
  2186.4 12.7 all-reduce.2
  2203.2 136.9 %all-reduce.7.cloned.1.call-done = (bf16[384,1536]{1,0:T(8,128)(2,1)}, bf16[384,768]{1,0:T(8,128)(2,1)}, bf16[384,768]{1,0:T(8,128)(2,1)}, bf16[384,1536]{1,0:T(...) async-done(((bf16[384,1536]{1,0:T(8,128)(2,1)}, bf16[384,768]{1,0:T(8,128)(2,1)}, bf16[384,768]{1,0:T(8,128)(2,1)}, ...) | async-done | bytes 12976144 | tf_op jit(solution)/shard_map/psum | solution.py:341
  (253 shorter events, 154.0 us)
Async XLA Ops:
  7.2 16.0 copy-start.9
  7.2 55.1 %all-gather.12.cloned.1.call-start = ((), (), s32[]{:S(2)}) async-start(), calls=%async_computation.9 | async-start | bytes 2949120 | tf_op jit(solution)/shard_map/all_gather | solution.py:104
  7.9 104.7 %all-gather.16.cloned.1.call-start = ((), (), s32[]{:S(2)}) async-start(), calls=%async_computation.11 | async-start | bytes 2949120 | tf_op jit(solution)/shard_map/all_gather | solution.py:103
  8.7 193.9 %all-gather.20.cloned.1.call-start = ((), (), s32[]{:S(2)}) async-start(), calls=%async_computation.13 | async-start | bytes 5898240 | tf_op jit(solution)/shard_map/all_gather | solution.py:102
  9.4 226.1 %all-gather.14.cloned.1.call-start = ((), (), s32[]{:S(2)}) async-start(), calls=%async_computation.10 | async-start | bytes 3538944 | tf_op jit(solution)/shard_map/all_gather | solution.py:119
  23.2 186.0 %copy-start.31 = (f32[1536]{0:T(1024)}, f32[1536]{0:T(1024)S(1)}, u32[]{:S(2)}) copy-start(f32[1536]{0:T(1024)S(1)} %reshape.429) | copy-start | bytes 18436
  23.4 185.8 %copy-start.34 = (f32[256]{0:T(256)}, f32[256]{0:T(256)S(1)}, u32[]{:S(2)}) copy-start(f32[256]{0:T(256)S(1)} %add_rsqrt_fusion.1) | copy-start | bytes 3076
  23.4 42.2 %copy-start.39 = (s32[1,16]{1,0:T(1,128)S(1)}, s32[1,16]{1,0:T(1,128)}, u32[]{:S(2)}) copy-start(s32[1,16]{1,0:T(1,128)} %param.19) | copy-start | bytes 196
  65.6 204.4 %all-gather.18.cloned.1.call-start = ((), (), s32[]{:S(2)}) async-start(), calls=%async_computation.12 | async-start | bytes 3538944 | tf_op jit(solution)/shard_map/all_gather | solution.py:118
  66.7 146.6 %copy-start.25 = (f32[256,48]{0,1:T(8,128)}, f32[256,48]{0,1:T(8,128)S(1)}, u32[]{:S(2)}) copy-start(f32[256,48]{0,1:T(8,128)S(1)} %get-tuple-element.422) | copy-start | bytes 147460
  117.5 243.4 %all-gather.22.cloned.1.call-start = ((), (), s32[]{:S(2)}) async-start(), calls=%async_computation.14 | async-start | bytes 5898240 | tf_op jit(solution)/shard_map/all_gather | solution.py:105
  118.1 461.0 %all-gather.24.cloned.1.call-start = ((), (), s32[]{:S(2)}) async-start(), calls=%async_computation.15 | async-start | bytes 15728640 | tf_op jit(solution)/shard_map/all_gather | solution.py:179
  118.8 678.2 %all-gather.26.cloned.1.call-start = ((), (), s32[]{:S(2)}) async-start(), calls=%async_computation.16 | async-start | bytes 15728640 | tf_op jit(solution)/shard_map/all_gather | solution.py:180
  119.6 895.4 %all-gather.28.cloned.1.call-start = ((), (), s32[]{:S(2)}) async-start(), calls=%async_computation.17 | async-start | bytes 15728640 | tf_op jit(solution)/shard_map/all_gather | solution.py:181
  120.3 1066.1 %reduce-scatter.10.cloned.1.call-start = ((), (), s32[]{:S(2)}) async-start(), calls=%async_computation.18 | async-start | bytes 3538944 | tf_op jit(solution)/shard_map/reduce_scatter | solution.py:286
  1026.4 7.3 copy-start.13
  1026.4 21.4 slice-start
  1033.7 14.1 slice-start.1
  1054.5 6.0 copy-start.2
  1055.7 4.9 copy-start.5
  1060.5 3.8 copy-start
  1060.5 3.8 copy-start.7
  1071.4 6.5 copy-start.1
  1071.4 6.6 copy-start.8
  1098.0 6.1 copy-start.2
  1099.3 4.9 copy-start.5
  1104.1 3.8 copy-start
  1104.1 3.8 copy-start.7
  1115.0 7.0 copy-start.1
  1115.0 7.0 copy-start.8
  1142.0 93.8 %reduce-scatter.12.cloned.1.call-start = ((), (), s32[]{:S(2)}) async-start(), calls=%async_computation.19 | async-start | bytes 3538944 | tf_op jit(solution)/shard_map/reduce_scatter | solution.py:287
  1142.8 181.1 %reduce-scatter.14.cloned.1.call-start = ((), (), s32[]{:S(2)}) async-start(), calls=%async_computation.20 | async-start | bytes 5898240 | tf_op jit(solution)/shard_map/reduce_scatter | solution.py:314
  1147.8 227.3 %reduce-scatter.16.cloned.1.call-start = ((), (), s32[]{:S(2)}) async-start(), calls=%async_computation.21 | async-start | bytes 2949120 | tf_op jit(solution)/shard_map/reduce_scatter | solution.py:317
  1190.1 49.2 %copy-start.11 = (bf16[256,8,2,96]{0,3,2,1:T(8,128)(2,1)S(1)}, bf16[256,8,2,96]{0,3,2,1:T(8,128)(2,1)}, u32[]{:S(2)}) copy-start(bf16[256,8,2,96]{0,3,2,1:T(8,128)(2,1)} %convert_element_type.247) | copy-start | bytes 2359300
  1190.1 234.8 %reduce-scatter.18.cloned.1.call-start = ((), (), s32[]{:S(2)}) async-start(), calls=%async_computation.22 | async-start | bytes 2949120 | tf_op jit(solution)/shard_map/reduce_scatter | solution.py:320
  1239.2 273.1 %reduce-scatter.20.cloned.1.call-start = ((), (), s32[]{:S(2)}) async-start(), calls=%async_computation.23 | async-start | bytes 5898240 | tf_op jit(solution)/shard_map/reduce_scatter | solution.py:323
  1244.3 482.7 %reduce-scatter.22.cloned.1.call-start = ((), (), s32[]{:S(2)}) async-start(), calls=%async_computation.24 | async-start | bytes 15728640 | tf_op jit(solution)/shard_map/reduce_scatter | solution.py:329
  1253.6 688.5 %reduce-scatter.24.cloned.1.call-start = ((), (), s32[]{:S(2)}) async-start(), calls=%async_computation.25 | async-start | bytes 15728640 | tf_op jit(solution)/shard_map/reduce_scatter | solution.py:332
  1261.8 895.5 %reduce-scatter.26.cloned.1.call-start = ((), (), s32[]{:S(2)}) async-start(), calls=%async_computation.26 | async-start | bytes 15728640 | tf_op jit(solution)/shard_map/reduce_scatter | solution.py:335
  1271.0 1069.1 %all-reduce.7.cloned.1.call-start = ((), (), s32[]{:S(2)}) async-start(), calls=%async_computation.27 | async-start | bytes 25952256 | tf_op jit(solution)/shard_map/psum | solution.py:341
  2159.2 3.9 copy-start.14
  2159.2 3.9 copy-start.19
  2163.1 7.6 copy-start.17
  2172.5 27.8 %copy-start.16 = (f32[256,1536]{1,0:T(8,128)S(1)}, f32[256,1536]{1,0:T(8,128)}, u32[]{:S(2)}) copy-start(f32[256,1536]{1,0:T(8,128)} %copy-done.15) | copy-start | bytes 4718596
  2340.1 3.1 copy-start.29
  2340.1 4.2 copy-start.28
  2348.1 3.5 copy-start.22
  2351.6 3.5 copy-start.21
  (22 other events, 32.1 us)
Sparse Core Ops, SparseCore 0:
  9.6 52.6 all-gather.11
  63.9 48.7 all-gather.15
  114.2 88.2 all-gather.19
  204.9 30.5 all-gather.13
  237.8 32.1 all-gather.17
  271.4 89.3 all-gather.21
  362.4 216.6 all-gather.23
  580.6 216.3 all-gather.25
  798.6 216.3 all-gather.27
  1142.1 44.2 reduce-scatter.9
  1189.8 46.0 reduce-scatter.11
  1238.6 85.2 reduce-scatter.13
  1326.8 48.2 reduce-scatter.15
  1377.8 47.0 reduce-scatter.17
  1427.6 84.6 reduce-scatter.19
  1514.5 212.3 reduce-scatter.21
  1729.2 212.8 reduce-scatter.23
  1944.3 212.8 reduce-scatter.25
  2162.2 177.8 all-reduce.6
where the time goes:
time: 2370 us
  waiting for transfers between devices  1970 us (83%)
  matrix products  211 us (9%)
  local copies, waits for them, and re-layouts  66.7 us (3%)
  blocking collectives  50.5 us (2%)
  other arithmetic  50 us (2%)
    reduce_scatter x1, waiting for transfers between devices, local(): lax.psum_scatter(down_term.astype(jnp.bfloat16), 'fsdp', scatter_dimensio...  215 us
    reduce_scatter x1, waiting for transfers between devices, local(): lax.psum_scatter(up_term.astype(jnp.bfloat16), 'fsdp', scatter_dimension=...  215 us
    reduce_scatter x1, waiting for transfers between devices, local(): lax.psum_scatter(gate_term.astype(jnp.bfloat16), 'fsdp', scatter_dimensio...  215 us
    all_gather x1, waiting for transfers between devices, local(): lax.all_gather(gate_weight, 'fsdp', axis=0, tiled=True)  212 us
    all_gather x1, waiting for transfers between devices, local(): lax.all_gather(down_weight, 'fsdp', axis=0, tiled=True)  208 us
    all_gather x1, waiting for transfers between devices, local(): lax.all_gather(up_weight, 'fsdp', axis=0, tiled=True)  208 us
    psum x1, waiting for transfers between devices, local(): lax.psum(shares[1].astype(jnp.bfloat16), 'ctx').astype(jnp.float32)  137 us
    reduce_scatter x1, waiting for transfers between devices, local(): lax.psum_scatter(output_term.astype(jnp.bfloat16), 'fsdp', scatter_dimens...  87.4 us
  transfers between devices with their start and end apart: 19, of which 19 were waited for; matrix products, arithmetic and copies ran while one was open for 7% of the time, Pallas kernels for 0%

commit v1 on v0

--- a/solution.py
+++ b/solution.py
@@ -1,8 +1,11 @@
+import functools
 import math
 
 import jax
 import jax.numpy as jnp
 from jax import lax
+from jax.experimental import pallas as pl
+from jax.experimental.pallas import tpu as pltpu
 from jax.sharding import PartitionSpec as P
 
 QUERY_HEADS = 16
@@ -362,9 +365,458 @@
     )
 
 
+LANES = 128
+HALF = HEAD_SIZE // 2
+GROUP = QUERY_HEADS // KEY_VALUE_HEADS
+score_scale = HEAD_SIZE ** (-0.5)
+
+
+def pad_head(columns):
+    rows, heads = columns.shape[0], columns.shape[1] // HEAD_SIZE
+    halves = columns.reshape(rows, heads, 2, HALF)
+    return jnp.pad(halves, ((0, 0), (0, 0), (0, 0), (0, LANES // 2 - HALF))).reshape(
+        rows, heads * LANES
+    )
+
+
+def unpad_head(columns):
+    rows, heads = columns.shape[0], columns.shape[1] // LANES
+    halves = columns.reshape(rows, heads, 2, LANES // 2)
+    return halves[:, :, :, :HALF].reshape(rows, heads * HEAD_SIZE)
+
+
+def contract(left, right, left_dim, right_dim):
+    return lax.dot_general(
+        left, right, (((left_dim,), (right_dim,)), ((), ())), preferred_element_type=jnp.float32
+    )
+
+
+def turn(value, cosine, sine):
+    heads = value.shape[1] // LANES
+    parts = []
+    for head in range(heads):
+        part = value[:, head * LANES : (head + 1) * LANES]
+        parts.append(part * cosine + pltpu.roll(part, LANES // 2, 1) * sine)
+    return parts[0] if heads == 1 else jnp.concatenate(parts, axis=1)
+
+
+def forward_kernel(block, tile, slot_ref, q_ref, k_ref, v_ref, o_ref, lse_ref, qs, ks, vt, s_ref):
+    rows = q_ref.shape[0]
+    tiles = rows // tile
+    per_tile = tile // block
+    width = GROUP * tile
+
+    def place(index, carry):
+        source = pl.ds(pl.multiple_of(slot_ref[index] * block, block), block)
+        target = pl.ds(pl.multiple_of(index * block, block), block)
+        for head in range(GROUP):
+            at = pl.multiple_of(
+                (index // per_tile) * width + head * tile + (index % per_tile) * block, block
+            )
+            qs[pl.ds(at, block), :] = q_ref[source, head * LANES : (head + 1) * LANES]
+        ks[target, :] = k_ref[source, :]
+        vt[:, target] = v_ref[source, :].T
+        return carry
+
+    lax.fori_loop(0, rows // block, place, 0)
+    key_at = lax.broadcasted_iota(jnp.int32, (tile, width), 0)
+    query_at = lax.rem(lax.broadcasted_iota(jnp.int32, (tile, width), 1), tile)
+    diagonal = key_at <= query_at
+
+    def one_tile(index, carry):
+        queries = qs[pl.ds(pl.multiple_of(index * width, width), width), :]
+
+        def scores_of(step):
+            keys = ks[pl.ds(pl.multiple_of(step * tile, tile), tile), :]
+            return contract(keys, queries, 1, 1) * score_scale
+
+        last = jnp.where(diagonal, scores_of(index), score_with_mask)
+        s_ref[pl.ds(pl.multiple_of(index * tile, tile), tile), :] = last
+        peak = jnp.max(last, axis=0, keepdims=True)
+
+        def first_pass(step, peak):
+            scores = scores_of(step)
+            s_ref[pl.ds(pl.multiple_of(step * tile, tile), tile), :] = scores
+            return jnp.maximum(peak, jnp.max(scores, axis=0, keepdims=True))
+
+        peak = lax.fori_loop(0, index, first_pass, peak)
+
+        def second_pass(step, state):
+            total, out = state
+            at = pl.ds(pl.multiple_of(step * tile, tile), tile)
+            probs = jnp.exp(s_ref[at, :] - peak)
+            total = total + jnp.sum(probs, axis=0, keepdims=True)
+            out = out + contract(vt[:, at], probs.astype(jnp.bfloat16), 1, 0)
+            return (total, out)
+
+        total, out = lax.fori_loop(
+            0,
+            index + 1,
+            second_pass,
+            (jnp.zeros((1, width), jnp.float32), jnp.zeros((LANES, width), jnp.float32)),
+        )
+        lse_ref[pl.ds(index, 1), :] = peak + jnp.log(total)
+        out = (out * (1.0 / total)).T.astype(jnp.bfloat16)
+        for part in range(per_tile):
+            target = pl.ds(pl.multiple_of(slot_ref[index * per_tile + part] * block, block), block)
+            for head in range(GROUP):
+                at = head * tile + part * block
+                o_ref[target, head * LANES : (head + 1) * LANES] = out[at : at + block, :]
+        return carry
+
+    lax.fori_loop(0, tiles, one_tile, 0)
+
+
+def backward_kernel(
+    block,
+    tile,
+    slot_ref,
+    q_ref,
+    k_ref,
+    v_ref,
+    o_ref,
+    g_ref,
+    lse_ref,
+    dq_ref,
+    dk_ref,
+    dv_ref,
+    qs,
+    ks,
+    vs,
+    kt,
+    gs,
+    os,
+    dk,
+    dv,
+):
+    rows = q_ref.shape[0]
+    tiles = rows // tile
+    per_tile = tile // block
+    width = GROUP * tile
+
+    def place(index, carry):
+        source = pl.ds(pl.multiple_of(slot_ref[index] * block, block), block)
+        target = pl.ds(pl.multiple_of(index * block, block), block)
+        for head in range(GROUP):
+            at = pl.multiple_of(
+                (index // per_tile) * width + head * tile + (index % per_tile) * block, block
+            )
+            at = pl.ds(at, block)
+            lanes = slice(head * LANES, (head + 1) * LANES)
+            qs[at, :] = q_ref[source, lanes]
+            gs[at, :] = g_ref[source, lanes]
+            os[at, :] = o_ref[source, lanes]
+        ks[target, :] = k_ref[source, :]
+        vs[target, :] = v_ref[source, :]
+        kt[:, target] = k_ref[source, :].T
+        return carry
+
+    lax.fori_loop(0, rows // block, place, 0)
+    dk[...] = jnp.zeros_like(dk)
+    dv[...] = jnp.zeros_like(dv)
+    key_at = lax.broadcasted_iota(jnp.int32, (tile, width), 0)
+    query_at = lax.rem(lax.broadcasted_iota(jnp.int32, (tile, width), 1), tile)
+    diagonal = key_at <= query_at
+
+    def one_tile(index, carry):
+        here = pl.ds(pl.multiple_of(index * width, width), width)
+        queries = qs[here, :]
+        grads = gs[here, :]
+        products = grads.astype(jnp.float32) * os[here, :].astype(jnp.float32)
+        delta = jnp.sum(products.T, axis=0, keepdims=True)
+        lse = lse_ref[pl.ds(index, 1), :]
+
+        def piece(step, masked):
+            at = pl.ds(pl.multiple_of(step * tile, tile), tile)
+            scores = contract(ks[at, :], queries, 1, 1) * score_scale
+            probs = jnp.exp(scores - lse)
+            if masked:
+                probs = jnp.where(diagonal, probs, 0.0)
+            probs = probs.astype(jnp.bfloat16)
+            dv[at, :] += contract(probs, grads, 1, 0)
+            grad_probs = contract(vs[at, :], grads, 1, 1)
+            grad_scores = (probs.astype(jnp.float32) * (grad_probs - delta) * score_scale).astype(
+                jnp.bfloat16
+            )
+            dk[at, :] += contract(grad_scores, queries, 1, 0)
+            return contract(kt[:, at], grad_scores, 1, 0)
+
+        dq = piece(index, True)
+        dq = lax.fori_loop(0, index, lambda step, total: total + piece(step, False), dq)
+        dq = dq.T
+        for part in range(per_tile):
+            target = pl.ds(pl.multiple_of(slot_ref[index * per_tile + part] * block, block), block)
+            for head in range(GROUP):
+                at = head * tile + part * block
+                dq_ref[target, head * LANES : (head + 1) * LANES] = dq[at : at + block, :]
+        return carry
+
+    lax.fori_loop(0, tiles, one_tile, 0)
+
+    def give(index, carry):
+        target = pl.ds(pl.multiple_of(slot_ref[index] * block, block), block)
+        source = pl.ds(pl.multiple_of(index * block, block), block)
+        dk_ref[target, :] = dk[source, :]
+        dv_ref[target, :] = dv[source, :]
+        return carry
+
+    lax.fori_loop(0, rows // block, give, 0)
+
+
+def in_vmem(count):
+    return [pl.BlockSpec(memory_space=pltpu.VMEM)] * count
+
+
+def attend(slots, q, k, v):
+    rows = q.shape[0]
+    block = rows // slots.shape[0]
+    tile = 2 * block
+    width = GROUP * tile
+    return pl.pallas_call(
+        functools.partial(forward_kernel, block, tile),
+        out_shape=(
+            jax.ShapeDtypeStruct(q.shape, jnp.bfloat16),
+            jax.ShapeDtypeStruct((rows // tile, width), jnp.float32),
+        ),
+        in_specs=[pl.BlockSpec(memory_space=pltpu.SMEM)] + in_vmem(3),
+        out_specs=tuple(in_vmem(2)),
+        scratch_shapes=[
+            pltpu.VMEM((GROUP * rows, LANES), jnp.bfloat16),
+            pltpu.VMEM((rows, LANES), jnp.bfloat16),
+            pltpu.VMEM((LANES, rows), jnp.bfloat16),
+            pltpu.VMEM((rows, width), jnp.float32),
+        ],
+        compiler_params=pltpu.CompilerParams(vmem_limit_bytes=40 << 20),
+        cost_estimate=pl.CostEstimate(
+            flops=4 * GROUP * rows * rows * LANES // 2,
+            bytes_accessed=12 * rows * LANES,
+            transcendentals=GROUP * rows * rows // 2,
+        ),
+        name="attend",
+    )(slots, q, k, v)
+
+
+def attend_back(slots, q, k, v, o, g, lse):
+    rows = q.shape[0]
+    block = rows // slots.shape[0]
+    tile = 2 * block
+    return pl.pallas_call(
+        functools.partial(backward_kernel, block, tile),
+        out_shape=(
+            jax.ShapeDtypeStruct(q.shape, jnp.float32),
+            jax.ShapeDtypeStruct(k.shape, jnp.float32),
+            jax.ShapeDtypeStruct(k.shape, jnp.float32),
+        ),
+        in_specs=[pl.BlockSpec(memory_space=pltpu.SMEM)] + in_vmem(6),
+        out_specs=tuple(in_vmem(3)),
+        scratch_shapes=[
+            pltpu.VMEM((GROUP * rows, LANES), jnp.bfloat16),
+            pltpu.VMEM((rows, LANES), jnp.bfloat16),
+            pltpu.VMEM((rows, LANES), jnp.bfloat16),
+            pltpu.VMEM((LANES, rows), jnp.bfloat16),
+            pltpu.VMEM((GROUP * rows, LANES), jnp.bfloat16),
+            pltpu.VMEM((GROUP * rows, LANES), jnp.bfloat16),
+            pltpu.VMEM((rows, LANES), jnp.float32),
+            pltpu.VMEM((rows, LANES), jnp.float32),
+        ],
+        compiler_params=pltpu.CompilerParams(vmem_limit_bytes=40 << 20),
+        cost_estimate=pl.CostEstimate(
+            flops=10 * GROUP * rows * rows * LANES // 2,
+            bytes_accessed=24 * rows * LANES,
+            transcendentals=GROUP * rows * rows // 2,
+        ),
+        name="attend_back",
+    )(slots, q, k, v, o, g, lse)
+
+
+def head_local(
+    block_input,
+    block_table,
+    output_grad,
+    attention_gain,
+    query_weight,
+    key_weight,
+    value_projection,
+    output_weight,
+    feedforward_gain,
+    gate_weight,
+    up_weight,
+    down_weight,
+):
+    me = lax.axis_index("ctx")
+    plane = lax.axis_size("ctx")
+    line = lax.axis_size("fsdp")
+    rows, model = block_input.shape[1:]
+    shard = model // line
+    hidden = gate_weight.shape[1]
+    unit = hidden // (line * plane)
+    table_row = block_table[0]
+    slot_count = table_row.shape[0]
+    block = rows * plane // slot_count
+    places = jnp.arange(slot_count, dtype=jnp.int32)
+    slots = jnp.sum(jnp.where(table_row[None, :] == places[:, None], places[None, :], 0), axis=1)
+
+    def mine(array, width):
+        return lax.dynamic_slice_in_dim(array, me * width, width, 1)
+
+    def gather(array, name, axis=0):
+        return lax.all_gather(array, name, axis=axis, tiled=True)
+
+    gains = gather(jnp.stack([attention_gain, feedforward_gain]), "fsdp", 1).astype(jnp.float32)
+    query_width = query_weight.shape[1] // plane
+    key_width = key_weight.shape[1] // plane
+    qkv = gather(
+        jnp.concatenate(
+            [
+                mine(query_weight, query_width),
+                mine(key_weight, key_width),
+                mine(value_projection, key_width),
+            ],
+            axis=1,
+        ),
+        "fsdp",
+    )
+    qkv_pad = pad_head(qkv)
+    out_width = model // plane
+    out_part = gather(mine(output_weight, out_width), "fsdp")
+    out_full = gather(out_part, "ctx", 1)
+
+    def hidden_part(array):
+        split = array.reshape(shard, line, plane, unit)
+        return lax.dynamic_index_in_dim(split, me, 2, keepdims=False).reshape(shard, line * unit)
+
+    gate_up = gather(
+        jnp.concatenate([hidden_part(gate_weight), hidden_part(up_weight)], axis=1), "fsdp"
+    )
+    down = gather(lax.dynamic_slice_in_dim(down_weight, me * unit, unit, 0), "fsdp")
+    gate, up = gate_up[:, : line * unit], gate_up[:, line * unit :]
+
+    positions = (
+        table_row[:, None] * block + jnp.arange(block, dtype=jnp.int32)[None, :]
+    ).reshape(-1)
+    cos, sin = rope_tables(positions)
+    blank = jnp.zeros((rows * plane, LANES // 2 - HALF), jnp.float32)
+    cosine = jnp.concatenate([cos, blank, cos, blank], axis=1)
+    sine = jnp.concatenate([-sin, blank, sin, blank], axis=1)
+
+    def swap(value):
+        heads = value.shape[1] // LANES
+        halves = value.reshape(-1, heads, 2, LANES // 2)
+        return halves[:, :, ::-1, :].reshape(value.shape)
+
+    def turned(value, direction):
+        heads = value.shape[1] // LANES
+        return value * jnp.tile(cosine, (1, heads)) + swap(value) * jnp.tile(
+            sine * direction, (1, heads)
+        )
+
+    inputs = block_input[0].astype(jnp.float32)
+    scale_one = norm_scale(inputs)
+    normed_one = inputs * scale_one
+    gained_one = gather((normed_one * gains[0]).astype(jnp.bfloat16), "ctx")
+    raw = product(gained_one, qkv_pad)
+    split_one, split_two = GROUP * LANES, (GROUP + 1) * LANES
+    q = turned(raw[:, :split_one], 1.0).astype(jnp.bfloat16)
+    k = turned(raw[:, split_one:split_two], 1.0).astype(jnp.bfloat16)
+    v = raw[:, split_two:].astype(jnp.bfloat16)
+    o, lse = attend(slots, q, k, v)
+
+    attended = lax.all_to_all(o, "ctx", 0, 1, tiled=True)
+    out_pad = pad_head(out_full.T).T
+    residual = inputs + product(attended, out_pad)
+    scale_two = norm_scale(residual)
+    normed_two = residual * scale_two
+    gained_two = gather((normed_two * gains[1]).astype(jnp.bfloat16), "ctx")
+    grad_all = gather(output_grad[0], "ctx")
+
+    gate_values = product(gained_two, gate)
+    up_values = product(gained_two, up)
+    sigmoid_gate = jax.nn.sigmoid(gate_values)
+    activated = gate_values * sigmoid_gate
+    hidden_act = (activated * up_values).astype(jnp.bfloat16)
+    out_sum = lax.psum_scatter(
+        product(hidden_act, down).astype(jnp.bfloat16), "ctx", scatter_dimension=0, tiled=True
+    )
+    layer_output = (residual + out_sum.astype(jnp.float32)).astype(jnp.bfloat16)
+    grad_hidden = back_product(grad_all, down)
+    down_term = cross_rows(hidden_act, grad_all)
+    grad_gate = (
+        grad_hidden * up_values * sigmoid_gate * (1.0 + gate_values * (1.0 - sigmoid_gate))
+    ).astype(jnp.bfloat16)
+    grad_up = (grad_hidden * activated).astype(jnp.bfloat16)
+    gate_term = cross_rows(gained_two, grad_gate)
+    up_term = cross_rows(gained_two, grad_up)
+    grad_normed_two = lax.psum_scatter(
+        (back_product(grad_gate, gate) + back_product(grad_up, up)).astype(jnp.bfloat16),
+        "ctx",
+        scatter_dimension=0,
+        tiled=True,
+    ).astype(jnp.float32)
+    feedforward_term = jnp.sum(grad_normed_two * normed_two, axis=0)
+    grad_scaled_two = grad_normed_two * gains[1]
+    grad_residual = output_grad[0].astype(jnp.float32) + scale_two * (
+        grad_scaled_two
+        - normed_two * jnp.mean(grad_scaled_two * normed_two, axis=-1, keepdims=True)
+    )
+    grad_attn = grad_residual.astype(jnp.bfloat16)
+    grad_attended = back_product(grad_attn, out_pad).astype(jnp.bfloat16)
+    grad_o = lax.all_to_all(grad_attended, "ctx", 1, 0, tiled=True)
+    attended_all = gather(unpad_head(o), "ctx", 1)
+    grad_attn_mine = lax.all_to_all(grad_attn, "ctx", 1, 0, tiled=True)
+    output_term = cross_rows(attended_all, grad_attn_mine)
+
+    dq, dk, dv = attend_back(slots, q, k, v, o, grad_o, lse)
+    grads = jnp.concatenate([turned(dq, -1.0), turned(dk, -1.0), dv], axis=1).astype(jnp.bfloat16)
+    qkv_term = unpad_head(cross_rows(gained_one, grads))
+    grad_normed_one = lax.psum_scatter(
+        back_product(grads, qkv_pad).astype(jnp.bfloat16), "ctx", scatter_dimension=0, tiled=True
+    ).astype(jnp.float32)
+    attention_term = jnp.sum(grad_normed_one * normed_one, axis=0)
+    grad_scaled_one = grad_normed_one * gains[0]
+    input_grad = grad_residual + scale_one * (
+        grad_scaled_one
+        - normed_one * jnp.mean(grad_scaled_one * normed_one, axis=-1, keepdims=True)
+    )
+
+    def reduce_line(term):
+        return lax.psum_scatter(
+            term.astype(jnp.bfloat16), "fsdp", scatter_dimension=0, tiled=True
+        )
+
+    gate_up_grad = gather(reduce_line(jnp.concatenate([gate_term, up_term], axis=1)), "ctx")
+    down_grad = gather(reduce_line(down_term), "ctx").astype(jnp.float32)
+    gate_up_grad = jnp.transpose(
+        gate_up_grad.reshape(plane, shard, 2, line, unit), (2, 1, 3, 0, 4)
+    ).reshape(2, shard, hidden)
+    attention_grad = gather(
+        reduce_line(jnp.concatenate([qkv_term, output_term], axis=1)), "ctx"
+    ).reshape(plane, shard, -1)
+
+    def columns(first, width):
+        part = attention_grad[:, :, first : first + width]
+        return jnp.transpose(part, (1, 0, 2)).reshape(shard, plane * width).astype(jnp.float32)
+
+    gain_terms = lax.psum(jnp.stack([attention_term, feedforward_term]), ("ctx", "fsdp"))
+    gain_terms = lax.dynamic_slice_in_dim(gain_terms, lax.axis_index("fsdp") * shard, shard, 1)
+    return (
+        layer_output[None],
+        input_grad[None],
+        gain_terms[0],
+        columns(0, query_width),
+        columns(query_width, key_width),
+        columns(query_width + key_width, key_width),
+        columns(query_width + 2 * key_width, out_width),
+        gain_terms[1],
+        gate_up_grad[0].astype(jnp.float32),
+        gate_up_grad[1].astype(jnp.float32),
+        down_grad,
+    )
+
+
 def solution(mesh):
+    plan = head_local if mesh.shape["ctx"] == KEY_VALUE_HEADS else local
     return jax.shard_map(
-        local,
+        plan,
         mesh=mesh,
         in_specs=(
             P("fsdp", "ctx", None),

time: 2370 us -> 928 us (0.39)
  waiting for transfers between devices: 1970 us -> 453 us
  matrix products: 211 us -> 102 us
  local copies, waits for them, and re-layouts: 66.7 us -> 161 us
  Pallas kernels: 0 us -> 48.1 us
  blocking collectives: 50.5 us -> 78 us
    reduce_scatter x9 -> x4, waiting for transfers between devices: 970 us -> 82.3 us  [the longest x1 33.1 us: head_local(): lax.psum_scatter((back_product(grad_gate, gate) + back_product(grad_up, u...]
    all_gather x9 -> x11, waiting for transfers between devices: 857 us -> 298 us  [gather(): return lax.all_gather(array, name, axis=axis, tiled=True)]
    psum x1 -> x0, waiting for transfers between devices: 137 us -> none  [local(): lax.psum(shares[1].astype(jnp.bfloat16), 'ctx').astype(jnp.float32)]
    dot_general x14 -> x0, matrix products: 93.4 us -> none  [the longest x4 25.1 us: block_scores(): jnp.einsum('rgjd,kgd->gjrk', query_rank_four, keys_rank_three, preferred_...]
    unnamed x19, waiting for transfers between devices: 5.51 us -> 54.8 us
    pallas_call x0 -> x2, Pallas kernels: none -> 48.1 us  [the longest x1 27.3 us: attend_back(): pl.pallas_call(functools.partial(backward_kernel, block, tile), out_shape...]
    unnamed x78 -> x118, local copies, waits for them, and re-layouts: 16.9 us -> 56.7 us
    convert_element_type x4 -> x9, local copies, waits for them, and re-layouts: 3.23 us -> 39.7 us  [the longest x2 14.5 us: head_local(): gate_up_grad[0].astype(jnp.float32)]
  transfers between devices with their start and end apart: 19 -> 20, of which waited for: 19 -> 16; matrix products, arithmetic and copies ran while one was open for 7% -> 26% of each run, Pallas kernels for 0% -> 5%
where the time goes in v1:
time: 928 us; the launch traced here: 917 us
  waiting for transfers between devices  453 us (49%)
  local copies, waits for them, and re-layouts  161 us (17%)
  matrix products  102 us (11%)
  blocking collectives  78 us (8%)
  Pallas kernels  48.1 us (5%)
  other arithmetic  47.7 us (5%)
  between operations  14.9 us (2%)
  starting transfers between devices  13.3 us (1%)
    all_gather x11, waiting for transfers between devices, gather(): return lax.all_gather(array, name, axis=axis, tiled=True)  298 us
    unnamed x118, local copies, waits for them, and re-layouts  56.7 us
    unnamed x19, waiting for transfers between devices  54.8 us
    psum x1, blocking collectives, head_local(): lax.psum(jnp.stack([attention_term, feedforward_term]), ('ctx', 'fsdp'))  40.2 us
    all_gather x2, blocking collectives, gather(): return lax.all_gather(array, name, axis=axis, tiled=True)  37.8 us
    dot_general x5, matrix products, cross_rows(): lax.dot_general(matrix, operand, (((0,), (0,)), ((), ())), preferred_elem...  35.3 us
    dot_general x5, matrix products, back_product(): lax.dot_general(matrix, operand, (((1,), (1,)), ((), ())), preferred_elem...  34.6 us
    reduce_scatter x1, waiting for transfers between devices, head_local(): lax.psum_scatter((back_product(grad_gate, gate) + back_product(grad_up, u...  33.1 us
  transfers between devices with their start and end apart: 20, of which 16 were waited for; matrix products, arithmetic and copies ran while one was open for 26% of the time, Pallas kernels for 5%

profile of v1, /device:TPU:0, one launch (start us, length us, event | category | flops | bytes accessed | tf_op | source)
XLA Modules:
  0.0 917.1 jit_solution(8416644193968285024)
XLA Ops:
  13.1 13.6 %all_gather.39 = bf16[2,1536]{1,0:T(2,128)(2,1)S(1)} all-gather(bf16[2,384]{1,0:T(2,128)(2,1)S(1)} %pad_maximum_fusion.12), channel_id=1, replica_groups=mesh['ctx'=8,'fsdp'=4] {'fsdp'}, dimensions={1}, use_global_device_ids=true | all-gather | bytes 7680 | tf_op jit(solution)/shard_map/all_gather | solution.py:663
  32.3 24.2 %all_gather.42 = bf16[1536,192]{0,1:T(8,128)(2,1)} all-gather(bf16[384,192]{0,1:T(8,128)(2,1)S(1)} %copy.202), channel_id=1, replica_groups=mesh['ctx'=8,'fsdp'=4] {'fsdp'}, dimensions={0}, use_global_device_ids=true | all-gather | bytes 737280 | tf_op jit(solution)/shard_map/all_gather | solution.py:663
  56.6 4.6 copy.173
  61.2 4.7 copy.172
  68.2 5.3 multiply_cosine_fusion
  78.6 23.7 %all-gather.13.cloned.1.call-done = bf16[2048,1536]{1,0:T(8,128)(2,1)} async-done(((bf16[256,1536]{1,0:T(8,128)(2,1)}), bf16[2048,1536]{1,0:T(8,128)(2,1)}) %all-gather.13.cloned.1.call-update) | async-done | bytes 6291472 | tf_op jit(solution)/shard_map/all_gather | solution.py:663
  102.3 6.0 fusion.49
  128.9 4.2 add_convert_fusion.3
  138.2 20.8 %attend.1 = (bf16[2048,256]{1,0:T(8,128)(2,1)S(1)}, f32[8,512]{1,0:T(8,128)S(1)}) custom-call(s32[16]{0:T(128)S(1)} %select_reduce_fusion.slot_ref, bf16[2048,256]{1,0:T(8,128)(2,1)S(1)} %fusion.19.q_ref, bf16[2048,128]{1,0:T(8,128)(2,1)S(1)} %get-tuple-element.95.k_ref, bf16[2048,128]{1,0:T(8,128)(2,1)S(1)} %copy-done.11), custom_call_target="tpu_custom_call" | custom-call | flops 2147483648 | bytes 3145728 | tf_op jit(solution)/shard_map/attend/pallas_call | solution.py:575
  162.2 4.2 all-to-all-start
  167.0 6.6 copy.171
  173.7 5.8 pad.9
  181.9 5.2 multiply_reduce_fusion
  191.0 17.2 %all-gather.21.cloned.1.call-done = bf16[1536,1024]{0,1:T(8,128)(2,1)} async-done(((bf16[384,1024]{0,1:T(8,128)(2,1)}), bf16[1536,1024]{0,1:T(8,128)(2,1)}) %all-gather.21.cloned.1.call-update) | async-done | bytes 3145744 | tf_op jit(solution)/shard_map/all_gather | solution.py:663
  208.3 46.4 %all-gather.19.cloned.1.call-done = bf16[2048,1536]{1,0:T(8,128)(2,1)} async-done(((bf16[256,1536]{1,0:T(8,128)(2,1)}), bf16[2048,1536]{1,0:T(8,128)(2,1)}) %all-gather.19.cloned.1.call-update) | async-done | bytes 6291472 | tf_op jit(solution)/shard_map/all_gather | solution.py:663
  254.7 8.8 fusion.39
  263.5 5.0 fusion.35
  268.5 25.2 %all-gather.23.cloned.1.call-done = bf16[512,1536]{1,0:T(8,128)(2,1)} async-done(((bf16[128,1536]{1,0:T(8,128)(2,1)}), bf16[512,1536]{1,0:T(8,128)(2,1)}) %all-gather.23.cloned.1.call-update) | async-done | bytes 1572880 | tf_op jit(solution)/shard_map/all_gather | solution.py:663
  293.7 46.2 %all-gather.33.cloned.1.call-done = bf16[1,2048,1536]{2,1,0:T(8,128)(2,1)} async-done(((bf16[1,256,1536]{2,1,0:T(8,128)(2,1)}), bf16[1,2048,1536]{2,1,0:T(8,128)(2,1)}) %all-gather.33.cloned.1.call-update) | async-done | bytes 6291472 | tf_op jit(solution)/shard_map/all_gather | solution.py:663
  339.9 13.0 %fusion.7 = (bf16[2048,512]{1,0:T(8,128)(2,1)}, bf16[2048,512]{1,0:T(8,128)(2,1)S(1)}, bf16[2048,512]{1,0:T(8,128)(2,1)}) fusion(f32[2048,512]{1,0:T(8,128)} %fusion.39, f32[2048,512]{1,0:T(8,128)} %fusion.35, bf16[512,1536]{1,0:T(8,128)(2,1)} %all-gather.23.cloned.1.call-done, bf16[1,2048,1536]{2,1,0:T(8,128)(2,1)} %all-gather.33.cloned.1.call-done), kind=kOutput, calls=%fused_computation.12 | convolution fusion | flops 3236954112 | bytes 22544384 | tf_op jit(solution)/shard_map/dot_general | solution.py:63
  356.3 7.0 add_convert_fusion
  366.4 8.6 fusion.9
  375.0 7.8 convolution_convert_fusion.2
  382.8 6.2 convolution_convert_fusion.3
  392.2 33.1 %reduce-scatter.13.cloned.1.call-done = bf16[256,1536]{1,0:T(8,128)(2,1)} async-done(((bf16[2048,1536]{1,0:T(8,128)(2,1)}), bf16[256,1536]{1,0:T(8,128)(2,1)}) %reduce-scatter.13.cloned.1.call-update) | async-done | bytes 786448 | tf_op jit(solution)/shard_map/reduce_scatter | solution.py:749
  434.6 4.9 convolution_convert_fusion.5
  440.5 14.7 %all-to-all-done.2 = bf16[256,8,192]{0,2,1:T(8,128)(2,1)S(1)} async-done(((bf16[256,8,192]{0,2,1:T(8,128)(2,1)}), bf16[256,8,192]{0,2,1:T(8,128)(2,1)S(1)}, u32[]{:S(2)}, u32[]{:S(2)}) %all-to-all-start.2) | async-done | bytes 786464 | tf_op jit(solution)/shard_map/all_to_all | solution.py:765
  459.8 32.0 %all-gather.25.cloned.1.call-done = bf16[2048,1536]{0,1:T(8,128)(2,1)} async-done(((bf16[2048,192]{0,1:T(8,128)(2,1)}), bf16[2048,1536]{0,1:T(8,128)(2,1)}) %all-gather.25.cloned.1.call-update) | async-done | bytes 6291472 | tf_op jit(solution)/shard_map/all_gather | solution.py:663
  491.8 6.1 convolution_convert_fusion.6
  503.5 27.3 %attend_back.1 = (f32[2048,256]{1,0:T(8,128)S(1)}, f32[2048,128]{1,0:T(8,128)S(1)}, f32[2048,128]{1,0:T(8,128)S(1)}) custom-call(s32[16]{0:T(128)S(1)} %select_reduce_fusion.slot_ref, bf16[2048,256]{1,0:T(8,128)(2,1)S(1)} %copy-done.8, bf16[2048,128]{1,0:T(8,128)(2,1)S(1)} %copy-done.14, bf16[2048,128]{1,0:T(8,128)(2,1)S(1)} %copy-done.12, ...), custom_call_target="tpu_custom_call" | custom-call | flops 5368709120 | bytes 6291456 | tf_op jit(solution)/shard_map/attend_back/pallas_call | solution.py:603
  554.2 6.6 convolution_convert_fusion.4
  565.5 26.1 %reduce-scatter.21.cloned.1.call-done = bf16[384,1024]{1,0:T(8,128)(2,1)} async-done(((bf16[1536,1024]{1,0:T(8,128)(2,1)}), bf16[384,1024]{1,0:T(8,128)(2,1)}) %reduce-scatter.21.cloned.1.call-update) | async-done | bytes 786448
  594.0 6.3 convolution_convert_fusion
  601.8 6.9 convolution_convert_fusion.1
  608.8 27.1 %reduce-scatter.19.cloned.1.call-done = bf16[384,576]{1,0:T(8,128)(2,1)} async-done(((bf16[1536,576]{1,0:T(8,128)(2,1)}), bf16[384,576]{1,0:T(8,128)(2,1)}) %reduce-scatter.19.cloned.1.call-update) | async-done | bytes 442384
  637.9 31.2 %all-gather.31.cloned.1.call-done = bf16[1024,1536]{1,0:T(8,128)(2,1)} async-done(((bf16[128,1536]{1,0:T(8,128)(2,1)}), bf16[1024,1536]{1,0:T(8,128)(2,1)}) %all-gather.31.cloned.1.call-update) | async-done | bytes 3145744 | tf_op jit(solution)/shard_map/all_gather | solution.py:663
  669.1 5.5 convert_element_type.171
  674.5 43.4 %all-gather.29.cloned.1.call-done = bf16[3072,1024]{0,1:T(8,128)(2,1)} async-done(((bf16[384,1024]{0,1:T(8,128)(2,1)}), bf16[3072,1024]{0,1:T(8,128)(2,1)}) %all-gather.29.cloned.1.call-update) | async-done | bytes 6291472 | tf_op jit(solution)/shard_map/all_gather | solution.py:663
  718.0 4.4 copy.209
  722.4 5.6 slice_convert_fusion
  728.0 7.3 copy.187
  735.3 7.2 reshape.256
  742.5 6.9 copy.188
  749.4 7.3 reshape.257
  756.7 26.3 %reduce-scatter.15.cloned.1.call-done = bf16[256,1536]{1,0:T(8,128)(2,1)} async-done(((bf16[2048,1536]{1,0:T(8,128)(2,1)}), bf16[256,1536]{1,0:T(8,128)(2,1)}) %reduce-scatter.15.cloned.1.call-update) | async-done | bytes 786448 | tf_op jit(solution)/shard_map/reduce_scatter | solution.py:771
  784.8 40.2 %psum.7 = f32[2,1536]{1,0:T(2,128)S(1)} all-reduce(f32[2,1536]{1,0:T(2,128)S(1)} %pad_maximum_fusion.11), channel_id=1, replica_groups=mesh['ctx'=8,'fsdp'=4] {'ctx','fsdp'}, use_global_device_ids=true, to_apply=%region_10.11 | all-reduce | flops 3072 | bytes 24576 | tf_op jit(solution)/shard_map/psum | solution.py:799
  825.7 22.9 %reduce-scatter.11.cloned.1.call-done = bf16[256,1536]{1,0:T(8,128)(2,1)} async-done(((bf16[2048,1536]{1,0:T(8,128)(2,1)}), bf16[256,1536]{1,0:T(8,128)(2,1)}) %reduce-scatter.11.cloned.1.call-update) | async-done | bytes 786448 | tf_op jit(solution)/shard_map/reduce_scatter | solution.py:737
  852.5 32.9 %all-gather.27.cloned.1.call-done = bf16[3072,576]{0,1:T(8,128)(2,1)} async-done(((bf16[384,576]{0,1:T(8,128)(2,1)}), bf16[3072,576]{0,1:T(8,128)(2,1)}) %all-gather.27.cloned.1.call-update) | async-done | bytes 3538960 | tf_op jit(solution)/shard_map/all_gather | solution.py:663
  (228 shorter events, 149.5 us)
Async XLA Ops:
  7.2 182.3 %copy-start = (bf16[1024,1536]{1,0:T(8,128)(2,1)S(1)}, bf16[1024,1536]{1,0:T(8,128)(2,1)}, u32[]{:S(2)}) copy-start(bf16[1024,1536]{1,0:T(8,128)(2,1)} %param.23) | copy-start | bytes 9437188
  7.2 5.8 copy-start.43
  7.2 5.8 copy-start.44
  7.2 68.8 %all-gather.15.cloned.1.call-start = ((), (), s32[]{:S(2)}) async-start(), calls=%async_computation.10 | async-start | bytes 1474560 | tf_op jit(solution)/shard_map/all_gather | solution.py:663
  13.0 89.3 %all-gather.13.cloned.1.call-start = ((), (), s32[]{:S(2)}) async-start(), calls=%async_computation.9 | async-start | bytes 7077888 | tf_op jit(solution)/shard_map/all_gather | solution.py:663
  31.0 136.0 %all-gather.17.cloned.1.call-start = ((), (), s32[]{:S(2)}) async-start(), calls=%async_computation.11 | async-start | bytes 5308416 | tf_op jit(solution)/shard_map/all_gather | solution.py:663
  56.5 151.8 %all-gather.21.cloned.1.call-start = ((), (), s32[]{:S(2)}) async-start(), calls=%async_computation.13 | async-start | bytes 3932160 | tf_op jit(solution)/shard_map/all_gather | solution.py:663
  128.9 4.2 copy-start.21
  133.1 4.9 copy-start.13
  133.9 3.2 copy-start.25
  134.7 3.3 copy-start.19
  138.0 21.0 %copy-start.7 = (bf16[2048,256]{1,0:T(8,128)(2,1)}, bf16[2048,256]{1,0:T(8,128)(2,1)S(1)}, u32[]{:S(2)}) copy-start(bf16[2048,256]{1,0:T(8,128)(2,1)S(1)} %fusion.19.q_ref) | copy-start | bytes 3145732
  162.2 19.6 %all-to-all-start = ((bf16[8,256,256]{1,2,0:T(8,128)(2,1)}), bf16[8,256,256]{1,2,0:T(8,128)(2,1)}, u32[]{:S(2)}, u32[]{:S(2)}) async-start(bf16[8,256,256]{1,2,0:T(8,128)(2,1)} %copy.169), calls=%async_computation | async-start | bytes 2097152 | tf_op jit(solution)/shard_map/all_to_all | solution.py:724
  166.5 88.2 %all-gather.19.cloned.1.call-start = ((), (), s32[]{:S(2)}) async-start(), calls=%async_computation.12 | async-start | bytes 7077888 | tf_op jit(solution)/shard_map/all_gather | solution.py:663
  189.4 104.3 %all-gather.23.cloned.1.call-start = ((), (), s32[]{:S(2)}) async-start(), calls=%async_computation.14 | async-start | bytes 1966080 | tf_op jit(solution)/shard_map/all_gather | solution.py:663
  190.2 149.6 %all-gather.33.cloned.1.call-start = ((), (), s32[]{:S(2)}) async-start(), calls=%async_computation.23 | async-start | bytes 7077888 | tf_op jit(solution)/shard_map/all_gather | solution.py:663
  191.0 234.2 %reduce-scatter.13.cloned.1.call-start = ((), (), s32[]{:S(2)}) async-start(), calls=%async_computation.16 | async-start | bytes 7077888 | tf_op jit(solution)/shard_map/reduce_scatter | solution.py:749
  208.3 55.2 %copy-start.46 = (bf16[1536,1024]{0,1:T(8,128)(2,1)S(1)}, bf16[1536,1024]{0,1:T(8,128)(2,1)}, u32[]{:S(2)}) copy-start(bf16[1536,1024]{0,1:T(8,128)(2,1)} %all-gather.21.cloned.1.call-done) | copy-start | bytes 9437188
  254.7 8.9 copy-start.45
  352.9 3.4 copy-start.49
  363.3 128.5 %all-gather.25.cloned.1.call-start = ((), (), s32[]{:S(2)}) async-start(), calls=%async_computation.18 | async-start | bytes 7077888 | tf_op jit(solution)/shard_map/all_gather | solution.py:663
  366.2 198.2 %reduce-scatter.17.cloned.1.call-start = ((), (), s32[]{:S(2)}) async-start(), calls=%async_computation.21 | async-start | bytes 1966080 | tf_op jit(solution)/shard_map/reduce_scatter | solution.py:782
  375.0 7.9 copy-start.50
  375.0 216.6 %reduce-scatter.21.cloned.1.call-start = ((), (), s32[]{:S(2)}) async-start(), calls=%async_computation.25 | async-start | bytes 3932160
  392.1 33.1 %copy-start.16 = (f32[256,1536]{1,0:T(8,128)S(1)}, f32[256,1536]{1,0:T(8,128)}, u32[]{:S(2)}) copy-start(f32[256,1536]{1,0:T(8,128)} %copy-done.15) | copy-start | bytes 4718596
  392.1 34.9 %copy-start.27 = (bf16[1,256,1536]{2,1,0:T(8,128)(2,1)S(1)}, bf16[1,256,1536]{2,1,0:T(8,128)(2,1)}, u32[]{:S(2)}) copy-start(bf16[1,256,1536]{2,1,0:T(8,128)(2,1)} %param.14) | copy-start | bytes 2359300
  428.4 6.1 copy-start.31
  430.8 24.4 %all-to-all-start.2 = ((bf16[256,8,192]{0,2,1:T(8,128)(2,1)}), bf16[256,8,192]{0,2,1:T(8,128)(2,1)S(1)}, u32[]{:S(2)}, u32[]{:S(2)}) async-start(bf16[256,8,192]{0,2,1:T(8,128)(2,1)} %bitcast.35), calls=%async_computation.5 | async-start | bytes 1572864 | tf_op jit(solution)/shard_map/all_to_all | solution.py:765
  455.2 42.7 %all-to-all-start.1 = ((bf16[256,8,256]{2,0,1:T(8,128)(2,1)}), bf16[256,8,256]{2,0,1:T(8,128)(2,1)S(1)}, u32[]{:S(2)}, u32[]{:S(2)}) async-start(bf16[256,8,256]{2,0,1:T(8,128)(2,1)} %bitcast.152), calls=%async_computation.3 | async-start | bytes 2097152 | tf_op jit(solution)/shard_map/all_to_all | solution.py:763
  458.8 177.1 %reduce-scatter.19.cloned.1.call-start = ((), (), s32[]{:S(2)}) async-start(), calls=%async_computation.24 | async-start | bytes 2457600
  491.8 7.0 copy-start.8
  547.4 3.9 copy-start.30
  547.4 4.7 copy-start.26
  554.2 6.6 copy-start.33
  564.3 29.7 %copy-start.32 = (bf16[1536,4,2,64]{0,3,2,1:T(8,128)(2,1)S(1)}, bf16[1536,4,2,64]{0,3,2,1:T(8,128)(2,1)}, u32[]{:S(2)}) copy-start(bf16[1536,4,2,64]{0,3,2,1:T(8,128)(2,1)} %pad.8) | copy-start | bytes 4718596
  564.3 29.7 %copy-start.34 = (bf16[2048,256]{1,0:T(8,128)(2,1)S(1)}, bf16[2048,256]{1,0:T(8,128)(2,1)}, u32[]{:S(2)}) copy-start(bf16[2048,256]{1,0:T(8,128)(2,1)} %copy-done.33) | copy-start | bytes 3145732
  564.3 29.7 %copy-start.37 = (bf16[2048,128]{1,0:T(8,128)(2,1)S(1)}, bf16[2048,128]{1,0:T(8,128)(2,1)}, u32[]{:S(2)}) copy-start(bf16[2048,128]{1,0:T(8,128)(2,1)} %convert.41) | copy-start | bytes 1572868
  564.3 104.8 %all-gather.31.cloned.1.call-start = ((), (), s32[]{:S(2)}) async-start(), calls=%async_computation.22 | async-start | bytes 3538944 | tf_op jit(solution)/shard_map/all_gather | solution.py:663
  565.0 152.9 %all-gather.29.cloned.1.call-start = ((), (), s32[]{:S(2)}) async-start(), calls=%async_computation.20 | async-start | bytes 7077888 | tf_op jit(solution)/shard_map/all_gather | solution.py:663
  593.9 189.1 %reduce-scatter.15.cloned.1.call-start = ((), (), s32[]{:S(2)}) async-start(), calls=%async_computation.17 | async-start | bytes 7077888 | tf_op jit(solution)/shard_map/reduce_scatter | solution.py:771
  600.3 248.3 %reduce-scatter.11.cloned.1.call-start = ((), (), s32[]{:S(2)}) async-start(), calls=%async_computation.15 | async-start | bytes 7077888 | tf_op jit(solution)/shard_map/reduce_scatter | solution.py:737
  608.7 276.7 %all-gather.27.cloned.1.call-start = ((), (), s32[]{:S(2)}) async-start(), calls=%async_computation.19 | async-start | bytes 3981312 | tf_op jit(solution)/shard_map/all_gather | solution.py:663
  749.4 33.6 %copy-start.18 = (bf16[1,256,1536]{2,1,0:T(8,128)(2,1)S(1)}, bf16[1,256,1536]{2,1,0:T(8,128)(2,1)}, u32[]{:S(2)}) copy-start(bf16[1,256,1536]{2,1,0:T(8,128)(2,1)} %param.12) | copy-start | bytes 2359300
  749.4 33.6 %copy-start.40 = (f32[1536]{0:T(1024)S(1)}, f32[1536]{0:T(1024)}, u32[]{:S(2)}) copy-start(f32[1536]{0:T(1024)} %copy-done.39) | copy-start | bytes 18436
  749.4 33.6 %copy-start.42 = (f32[256]{0:T(256)S(1)}, f32[256]{0:T(256)}, u32[]{:S(2)}) copy-start(f32[256]{0:T(256)} %copy-done.41) | copy-start | bytes 3076
  749.4 99.2 %copy-start.28 = (bf16[1,256,1536]{2,1,0:T(8,128)(2,1)S(1)}, bf16[1,256,1536]{2,1,0:T(8,128)(2,1)}, u32[]{:S(2)}) copy-start(bf16[1,256,1536]{2,1,0:T(8,128)(2,1)} %param.14) | copy-start | bytes 2359300
  756.7 92.0 %copy-start.17 = (f32[256,1536]{1,0:T(8,128)S(1)}, f32[256,1536]{1,0:T(8,128)}, u32[]{:S(2)}) copy-start(f32[256,1536]{1,0:T(8,128)} %copy-done.15) | copy-start | bytes 4718596
  907.2 3.2 copy-start.1
  (23 other events, 33.9 us)
Sparse Core Ops, SparseCore 0:
  13.1 42.0 all-gather.14
  57.7 44.5 all-gather.12
  104.2 38.7 all-gather.16
  145.0 63.2 all-gather.20
  210.6 44.0 all-gather.18
  256.7 37.0 all-gather.22
  295.6 44.2 all-gather.32
  363.4 61.7 reduce-scatter.12
  427.1 64.6 all-gather.24
  493.9 35.4 reduce-scatter.16
  532.3 59.2 reduce-scatter.20
  594.3 41.5 reduce-scatter.18
  637.8 31.2 all-gather.30
  671.4 46.5 all-gather.28
  721.2 61.7 reduce-scatter.14
  786.2 62.3 reduce-scatter.10
  850.9 34.4 all-gather.26

commit v2 on v0

--- a/solution.py
+++ b/solution.py
@@ -1,8 +1,11 @@
+import functools
 import math
 
 import jax
 import jax.numpy as jnp
 from jax import lax
+from jax.experimental import pallas as pl
+from jax.experimental.pallas import tpu as pltpu
 from jax.sharding import PartitionSpec as P
 
 QUERY_HEADS = 16
@@ -362,9 +365,1384 @@
     )
 
 
+LANES = 128
+HALF = HEAD_SIZE // 2
+GROUP = QUERY_HEADS // KEY_VALUE_HEADS
+score_scale = HEAD_SIZE ** (-0.5)
+
+
+def contract(left, right, left_dim, right_dim):
+    return lax.dot_general(
+        left, right, (((left_dim,), (right_dim,)), ((), ())), preferred_element_type=jnp.float32
+    )
+
+
+def in_vmem(count):
+    return [pl.BlockSpec(memory_space=pltpu.VMEM)] * count
+
+
+def padding(heads):
+    column = jnp.arange(heads * HEAD_SIZE, dtype=jnp.int32)
+    half_at, rest = column // HALF, column % HALF
+    target = half_at * (LANES // 2) + rest
+    lanes = jnp.arange(heads * LANES, dtype=jnp.int32)
+    return (target[:, None] == lanes[None, :]).astype(jnp.bfloat16)
+
+
+def turn(part, cosine, sine):
+    return part * cosine + pltpu.roll(part, LANES // 2, 1) * sine
+
+
+def tables(inner_ref, outer_ref, index, per_tile):
+    inner_cos, inner_sin = inner_ref[0], inner_ref[1]
+    sign = jnp.where(
+        lax.broadcasted_iota(jnp.int32, inner_cos.shape, 1) < LANES // 2, -1.0, 1.0
+    )
+    cosines, sines = [], []
+    for part in range(per_tile):
+        at = pl.ds(index * per_tile + part, 1)
+        outer_cos, outer_sin = outer_ref[0, at, :], outer_ref[1, at, :]
+        cosines.append(inner_cos * outer_cos - inner_sin * outer_sin)
+        sines.append(sign * (inner_sin * outer_cos + inner_cos * outer_sin))
+    return jnp.concatenate(cosines, axis=0), jnp.concatenate(sines, axis=0)
+
+
+def forward_kernel(
+    slot_ref,
+    xa_ref,
+    xb_ref,
+    gain_ref,
+    w_ref,
+    pad_ref,
+    inner_ref,
+    outer_ref,
+    gained_ref,
+    qkv_ref,
+    o_ref,
+    lse_ref,
+    wp,
+    qs,
+    vt,
+    s_ref,
+):
+    index = pl.program_id(0)
+    block = xa_ref.shape[0]
+    tile = 2 * block
+    width = GROUP * tile
+    heads = GROUP + 2
+
+    @pl.when(index == 0)
+    def _():
+        wp[...] = contract(w_ref[...], pad_ref[...], 1, 0).astype(jnp.bfloat16)
+
+    x = jnp.concatenate([xa_ref[...], xb_ref[...]], axis=0).astype(jnp.float32)
+    normed = x * lax.rsqrt(jnp.mean(x * x, axis=-1, keepdims=True) + norm_epsilon)
+    gained = (normed * gain_ref[...]).astype(jnp.bfloat16)
+    gained_ref[...] = gained
+    raw = contract(gained, wp[...], 1, 0)
+    cosine, sine = tables(inner_ref, outer_ref, index, 2)
+    here = pl.ds(pl.multiple_of(index * tile, tile), tile)
+    for head in range(heads):
+        lanes = slice(head * LANES, (head + 1) * LANES)
+        part = raw[:, lanes]
+        if head <= GROUP:
+            part = turn(part, cosine, sine)
+        part = part.astype(jnp.bfloat16)
+        qkv_ref[here, lanes] = part
+        if head < GROUP:
+            qs[head * tile : (head + 1) * tile, :] = part
+        if head == heads - 1:
+            vt[:, here] = part.T
+    queries = qs[...]
+    key_at = lax.broadcasted_iota(jnp.int32, (tile, width), 0)
+    query_at = lax.rem(lax.broadcasted_iota(jnp.int32, (tile, width), 1), tile)
+    diagonal = key_at <= query_at
+
+    def scores_of(step):
+        at = pl.ds(pl.multiple_of(step * tile, tile), tile)
+        keys = qkv_ref[at, GROUP * LANES : (GROUP + 1) * LANES]
+        return contract(keys, queries, 1, 1) * score_scale
+
+    last = jnp.where(diagonal, scores_of(index), score_with_mask)
+    s_ref[here, :] = last
+    peak = jnp.max(last, axis=0, keepdims=True)
+
+    def first_pass(step, peak):
+        scores = scores_of(step)
+        s_ref[pl.ds(pl.multiple_of(step * tile, tile), tile), :] = scores
+        return jnp.maximum(peak, jnp.max(scores, axis=0, keepdims=True))
+
+    peak = lax.fori_loop(0, index, first_pass, peak)
+
+    def second_pass(step, state):
+        total, out = state
+        at = pl.ds(pl.multiple_of(step * tile, tile), tile)
+        probs = jnp.exp(s_ref[at, :] - peak)
+        total = total + jnp.sum(probs, axis=0, keepdims=True)
+        out = out + contract(vt[:, at], probs.astype(jnp.bfloat16), 1, 0)
+        return (total, out)
+
+    total, out = lax.fori_loop(
+        0,
+        index + 1,
+        second_pass,
+        (jnp.zeros((1, width), jnp.float32), jnp.zeros((LANES, width), jnp.float32)),
+    )
+    lse_ref[pl.ds(index, 1), :] = peak + jnp.log(total)
+    out = (out * (1.0 / total)).T.astype(jnp.bfloat16)
+    out = jnp.concatenate([out[head * tile : (head + 1) * tile, :] for head in range(GROUP)], axis=1)
+    out = contract(out, pad_ref[: GROUP * HEAD_SIZE, : GROUP * LANES], 1, 1).astype(jnp.bfloat16)
+    for part in range(2):
+        target = pl.ds(pl.multiple_of(slot_ref[index * 2 + part] * block, block), block)
+        o_ref[target, :] = out[part * block : (part + 1) * block, :]
+
+
+def attend(slots, x, gain, w, pad, inner, outer):
+    rows, model = x.shape
+    block = rows // slots.shape[0]
+    tile = 2 * block
+    width = GROUP * tile
+    columns = pad.shape[1]
+    whole = lambda *shape: pl.BlockSpec(shape, lambda i, s: (0,) * len(shape))
+    return pl.pallas_call(
+        forward_kernel,
+        grid_spec=pltpu.PrefetchScalarGridSpec(
+            num_scalar_prefetch=1,
+            grid=(rows // tile,),
+            in_specs=[
+                pl.BlockSpec((block, model), lambda i, s: (s[2 * i], 0)),
+                pl.BlockSpec((block, model), lambda i, s: (s[2 * i + 1], 0)),
+                whole(1, model),
+                whole(*w.shape),
+                whole(*pad.shape),
+                whole(*inner.shape),
+                whole(*outer.shape),
+            ],
+            out_specs=(
+                pl.BlockSpec((tile, model), lambda i, s: (i, 0)),
+                whole(rows, columns),
+                whole(rows, GROUP * HEAD_SIZE),
+                whole(rows // tile, width),
+            ),
+            scratch_shapes=[
+                pltpu.VMEM((model, columns), jnp.bfloat16),
+                pltpu.VMEM((width, LANES), jnp.bfloat16),
+                pltpu.VMEM((LANES, rows), jnp.bfloat16),
+                pltpu.VMEM((rows, width), jnp.float32),
+            ],
+        ),
+        out_shape=(
+            jax.ShapeDtypeStruct((rows, model), jnp.bfloat16),
+            jax.ShapeDtypeStruct((rows, columns), jnp.bfloat16),
+            jax.ShapeDtypeStruct((rows, GROUP * HEAD_SIZE), jnp.bfloat16),
+            jax.ShapeDtypeStruct((rows // tile, width), jnp.float32),
+        ),
+        compiler_params=pltpu.CompilerParams(vmem_limit_bytes=44 << 20),
+        cost_estimate=pl.CostEstimate(
+            flops=4 * GROUP * rows * rows * LANES // 2 + 2 * rows * model * columns,
+            bytes_accessed=4 * rows * model,
+            transcendentals=GROUP * rows * rows // 2,
+        ),
+        name="attend",
+    )(slots, x, x, gain, w, pad, inner, outer)
+
+
+def backward_kernel(
+    slot_ref,
+    ga_ref,
+    gb_ref,
+    gained_ref,
+    qkv_ref,
+    o_ref,
+    lse_ref,
+    w_ref,
+    wo_ref,
+    pad_ref,
+    inner_ref,
+    outer_ref,
+    dx_ref,
+    dw_ref,
+    dwo_ref,
+    wp,
+    qs,
+    gs,
+    kt,
+    dk,
+    dv,
+    dw,
+    dwo,
+):
+    step_at = pl.program_id(0)
+    tiles = pl.num_programs(0)
+    index = tiles - 1 - step_at
+    block = ga_ref.shape[0]
+    tile = 2 * block
+    width = GROUP * tile
+    rows = qkv_ref.shape[0]
+    first_key, first_value = GROUP * LANES, (GROUP + 1) * LANES
+
+    @pl.when(step_at == 0)
+    def _():
+        wp[...] = contract(w_ref[...], pad_ref[...], 1, 0).astype(jnp.bfloat16)
+        kt[...] = qkv_ref[:, first_key:first_value].T
+        dk[...] = jnp.zeros_like(dk)
+        dv[...] = jnp.zeros_like(dv)
+        dw[...] = jnp.zeros_like(dw)
+        dwo[...] = jnp.zeros_like(dwo)
+
+    here = pl.ds(pl.multiple_of(index * tile, tile), tile)
+    sources = [
+        pl.ds(pl.multiple_of(slot_ref[index * 2 + part] * block, block), block) for part in (0, 1)
+    ]
+    grad_attn = jnp.concatenate([ga_ref[...], gb_ref[...]], axis=0)
+    o = jnp.concatenate([o_ref[source, :] for source in sources], axis=0)
+    dwo[...] += contract(o, grad_attn, 0, 0)
+    grads = contract(grad_attn, wo_ref[...], 1, 1).astype(jnp.bfloat16)
+    products = (grads.astype(jnp.float32) * o.astype(jnp.float32)).T
+    grads = contract(grads, pad_ref[: GROUP * HEAD_SIZE, : GROUP * LANES], 1, 0).astype(jnp.bfloat16)
+    deltas = []
+    for head in range(GROUP):
+        lanes = slice(head * LANES, (head + 1) * LANES)
+        at = slice(head * tile, (head + 1) * tile)
+        qs[at, :] = qkv_ref[here, lanes]
+        gs[at, :] = grads[:, lanes]
+        features = slice(head * HEAD_SIZE, (head + 1) * HEAD_SIZE)
+        deltas.append(jnp.sum(products[features, :], axis=0, keepdims=True))
+    delta = jnp.concatenate(deltas, axis=1)
+    lse = lse_ref[pl.ds(index, 1), :]
+    queries, grads = qs[...], gs[...]
+    key_at = lax.broadcasted_iota(jnp.int32, (tile, width), 0)
+    query_at = lax.rem(lax.broadcasted_iota(jnp.int32, (tile, width), 1), tile)
+    diagonal = key_at <= query_at
+
+    def piece(step, masked):
+        at = pl.ds(pl.multiple_of(step * tile, tile), tile)
+        scores = contract(qkv_ref[at, first_key:first_value], queries, 1, 1) * score_scale
+        probs = jnp.exp(scores - lse)
+        if masked:
+            probs = jnp.where(diagonal, probs, 0.0)
+        probs = probs.astype(jnp.bfloat16)
+        dv[at, :] += contract(probs, grads, 1, 0)
+        grad_probs = contract(qkv_ref[at, first_value:], grads, 1, 1)
+        grad_scores = (probs.astype(jnp.float32) * (grad_probs - delta) * score_scale).astype(
+            jnp.bfloat16
+        )
+        dk[at, :] += contract(grad_scores, queries, 1, 0)
+        return contract(kt[:, at], grad_scores, 1, 0)
+
+    dq = piece(index, True)
+    dq = lax.fori_loop(0, index, lambda step, total: total + piece(step, False), dq)
+    dq = dq.T
+    cosine, sine = tables(inner_ref, outer_ref, index, 2)
+    parts = [turn(dq[head * tile : (head + 1) * tile, :], cosine, -sine) for head in range(GROUP)]
+    parts.append(turn(dk[here, :], cosine, -sine))
+    parts.append(dv[here, :])
+    dqkv = jnp.concatenate([part.astype(jnp.bfloat16) for part in parts], axis=1)
+    dw[...] += contract(dqkv, gained_ref[...], 0, 0)
+    dx = contract(dqkv, wp[...], 1, 1).astype(jnp.bfloat16)
+    for part in (0, 1):
+        dx_ref[sources[part], :] = dx[part * block : (part + 1) * block, :]
+
+    @pl.when(step_at == tiles - 1)
+    def _():
+        packed = contract(pad_ref[...], dw[...].astype(jnp.bfloat16), 1, 0)
+        dw_ref[...] = packed.astype(jnp.bfloat16).T
+        pieces, _, across = dwo_ref.shape
+        for piece in range(pieces):
+            rows_at = slice(piece * HALF, (piece + 1) * HALF)
+            for number in range(dwo.shape[1] // across):
+                columns = slice(number * across, (number + 1) * across)
+                dwo_ref[piece, number * HALF : (number + 1) * HALF, :] = dwo[
+                    rows_at, columns
+                ].astype(jnp.bfloat16)
+
+
+def attend_back(slots, grad_attn, gained, qkv, o, lse, w, wo, pad, inner, outer):
+    rows, model = gained.shape
+    block = rows // slots.shape[0]
+    tile = 2 * block
+    width = GROUP * tile
+    tiles = rows // tile
+    columns = pad.shape[1]
+    across = w.shape[1]
+    wo_pieces = (2 * GROUP, HALF * model // across, across)
+    whole = lambda *shape: pl.BlockSpec(shape, lambda i, s: (0,) * len(shape))
+    return pl.pallas_call(
+        backward_kernel,
+        grid_spec=pltpu.PrefetchScalarGridSpec(
+            num_scalar_prefetch=1,
+            grid=(tiles,),
+            in_specs=[
+                pl.BlockSpec((block, model), lambda i, s: (s[2 * (tiles - 1 - i)], 0)),
+                pl.BlockSpec((block, model), lambda i, s: (s[2 * (tiles - 1 - i) + 1], 0)),
+                pl.BlockSpec((tile, model), lambda i, s: (tiles - 1 - i, 0)),
+                whole(*qkv.shape),
+                whole(*o.shape),
+                whole(*lse.shape),
+                whole(*w.shape),
+                whole(*wo.shape),
+                whole(*pad.shape),
+                whole(*inner.shape),
+                whole(*outer.shape),
+            ],
+            out_specs=(whole(rows, model), whole(*w.shape), whole(*wo_pieces)),
+            scratch_shapes=[
+                pltpu.VMEM((model, columns), jnp.bfloat16),
+                pltpu.VMEM((width, LANES), jnp.bfloat16),
+                pltpu.VMEM((width, LANES), jnp.bfloat16),
+                pltpu.VMEM((LANES, rows), jnp.bfloat16),
+                pltpu.VMEM((rows, LANES), jnp.float32),
+                pltpu.VMEM((rows, LANES), jnp.float32),
+                pltpu.VMEM((columns, model), jnp.float32),
+                pltpu.VMEM(wo.shape, jnp.float32),
+            ],
+        ),
+        out_shape=(
+            jax.ShapeDtypeStruct((rows, model), jnp.bfloat16),
+            jax.ShapeDtypeStruct(w.shape, jnp.bfloat16),
+            jax.ShapeDtypeStruct(wo_pieces, jnp.bfloat16),
+        ),
+        compiler_params=pltpu.CompilerParams(vmem_limit_bytes=56 << 20),
+        cost_estimate=pl.CostEstimate(
+            flops=10 * GROUP * rows * rows * LANES // 2 + 8 * rows * model * columns,
+            bytes_accessed=8 * rows * model,
+            transcendentals=GROUP * rows * rows // 2,
+        ),
+        name="attend_back",
+    )(slots, grad_attn, grad_attn, gained, qkv, o, lse, w, wo, pad, inner, outer)
+MESH_IDS = pl.DeviceIdType.MESH
+ACROSS = (1, 2, 4, 6)
+
+
+def start_barrier(me, line_index=None, line=1):
+    barrier = pltpu.get_barrier_semaphore()
+    peers = [{"ctx": me ^ bit} for bit in range(1, 8)]
+    peers += [{"fsdp": lax.rem(line_index + step, line)} for step in range(1, line)]
+    for peer in peers:
+        pl.semaphore_signal(barrier, inc=1, device_id=peer, device_id_type=MESH_IDS)
+    pl.semaphore_wait(barrier, len(peers))
+
+
+class Copies:
+    def __init__(self, send_sems, recv_sems, base=0):
+        self.send_sems, self.recv_sems, self.next, self.sent = send_sems, recv_sems, base, []
+
+    def number(self):
+        self.next += 1
+        return self.next - 1
+
+    def make(self, number, source, target, peer, landing=None):
+        return pltpu.make_async_remote_copy(
+            src_ref=source,
+            dst_ref=target,
+            send_sem=self.send_sems.at[number],
+            recv_sem=self.recv_sems.at[number if landing is None else landing],
+            device_id=peer,
+            device_id_type=MESH_IDS,
+        )
+
+    def send(self, number, source, target, peer):
+        copy = self.make(number, source, target, peer)
+        copy.start()
+        self.sent.append(copy)
+
+    def arrived(self, number, target):
+        self.make(number, target, target, {"ctx": 0}).wait_recv()
+
+    def finish(self):
+        for copy in self.sent:
+            copy.wait_send()
+
+
+GATHER_COPIES = 13
+
+
+class PlaneGather:
+    def __init__(self, copies, me, own_half, part):
+        self.copies, self.me, self.own_half, self.part = copies, me, own_half, part
+        self.first = copies.next
+        copies.next += GATHER_COPIES
+
+    def peer(self, bit):
+        return {"ctx": self.me ^ bit}
+
+    def begin(self):
+        me, part, own, first = self.me, self.part, self.own_half, self.first
+        send = self.copies.send
+        send(first + 0, own(1), part(me, 1), self.peer(2))
+        send(first + 1, own(0), part(me, 0), self.peer(4))
+        send(first + 2, own(0), part(me, 0), self.peer(2))
+        send(first + 3, own(1), part(me, 1), self.peer(4))
+        send(first + 4, own(0), part(me, 0), self.peer(1))
+        send(first + 5, own(1), part(me, 1), self.peer(1))
+
+    def hear(self, number, slot, half, onward=None):
+        place = self.part(slot, half)
+        self.copies.arrived(self.first + number, place)
+        if onward is not None:
+            self.copies.send(self.first + onward[0], place, place, self.peer(onward[1]))
+
+    def share(self, number, slot, half):
+        place = self.part(slot, half)
+        self.copies.send(self.first + number, place, place, self.peer(1))
+
+    def first_hop(self):
+        me = self.me
+        self.hear(0, me ^ 2, 1, (6, 4))
+        self.share(8, me ^ 2, 1)
+        self.hear(1, me ^ 4, 0, (7, 2))
+        self.share(9, me ^ 4, 0)
+
+    def second_hop(self):
+        me = self.me
+        self.hear(2, me ^ 2, 0)
+        self.share(10, me ^ 2, 0)
+        self.hear(3, me ^ 4, 1)
+        self.share(11, me ^ 4, 1)
+
+    def third_hop(self):
+        me = self.me
+        self.hear(6, me ^ 6, 1)
+        self.hear(7, me ^ 6, 0)
+        self.share(12, me ^ 6, slice(None))
+
+    def last(self):
+        me, arrived, part = self.me, self.copies.arrived, self.part
+        arrived(self.first + 4, part(me ^ 1, 0))
+        arrived(self.first + 5, part(me ^ 1, 1))
+        arrived(self.first + 8, part(me ^ 3, 1))
+        arrived(self.first + 9, part(me ^ 5, 0))
+        arrived(self.first + 10, part(me ^ 3, 0))
+        arrived(self.first + 11, part(me ^ 5, 1))
+        arrived(self.first + 12, part(me ^ 7, slice(None)))
+
+
+def run_gathers(gathers):
+    for gather in gathers:
+        gather.begin()
+    for gather in gathers:
+        gather.first_hop()
+    for gather in gathers:
+        gather.second_hop()
+    for gather in gathers:
+        gather.third_hop()
+    for gather in gathers:
+        gather.last()
+
+
+def row_half(ref, rows):
+    half = rows // 2
+
+    def own(side):
+        return ref.at[pl.ds(side * half, half), :]
+
+    return own
+
+
+def row_part(ref, rows):
+    half = rows // 2
+
+    def part(slot, side):
+        if isinstance(side, slice):
+            return ref.at[pl.ds(pl.multiple_of(slot * rows, rows), rows), :]
+        return ref.at[pl.ds(pl.multiple_of(slot * rows + side * half, half), half), :]
+
+    return part
+
+
+class LineGather:
+    def __init__(self, copies, index, line, place):
+        self.copies, self.index, self.line, self.place = copies, index, line, place
+        self.first = copies.next
+        copies.next += 2 * (line - 1)
+
+    def move(self, step, upward, act):
+        index, line = self.index, self.line
+        if upward:
+            slot, there = index - step, index + 1
+            leaves = (slot >= 0) & (there < line)
+        else:
+            slot, there = index + step, index - 1
+            leaves = (slot < line) & (there >= 0)
+        number = self.first + step + (0 if upward else line - 1)
+
+        @pl.when(leaves)
+        def _():
+            place = self.place(jnp.clip(slot, 0, line - 1))
+            act(self.copies.make(number, place, place, {"fsdp": jnp.clip(there, 0, line - 1)}))
+
+    def hear(self, step, upward):
+        index, line = self.index, self.line
+        slot = index - 1 - step if upward else index + 1 + step
+        comes = (slot >= 0) & (slot < line)
+        number = self.first + step + (0 if upward else line - 1)
+
+        @pl.when(comes)
+        def _():
+            place = self.place(jnp.clip(slot, 0, line - 1))
+            self.copies.make(number, place, place, {"fsdp": 0}).wait_recv()
+
+    def begin(self):
+        for upward in (True, False):
+            self.move(0, upward, lambda copy: copy.start())
+
+    def hop(self, step):
+        for upward in (True, False):
+            self.hear(step - 1, upward)
+            if step < self.line - 1:
+                self.move(step, upward, lambda copy: copy.start())
+
+    def finish(self):
+        for step in range(self.line - 1):
+            for upward in (True, False):
+                self.move(step, upward, lambda copy: copy.wait_send())
+
+
+def anywhere(count):
+    return [pl.BlockSpec(memory_space=pl.ANY)] * count
+
+
+def local_copies(pairs, sems):
+    copies = [
+        pltpu.make_async_copy(source, target, sems.at[number])
+        for number, (source, target) in enumerate(pairs)
+    ]
+    for copy in copies:
+        copy.start()
+    return copies
+
+
+def remote_params(number):
+    return pltpu.CompilerParams(
+        collective_id=number, has_side_effects=True, vmem_limit_bytes=48 << 20
+    )
+
+
+def first_kernel(line, x_ref, qkv_ref, wo_ref, gain_ref, xo_ref, qkvo_ref, woo_ref, gaino_ref, send, recv, here):
+    me, index = lax.axis_index("ctx"), lax.axis_index("fsdp")
+    rows = x_ref.shape[0]
+    start_barrier(me, index, line)
+    part = row_part(xo_ref, rows)
+    local = local_copies(
+        [
+            (qkv_ref, qkvo_ref.at[index]),
+            (wo_ref, woo_ref.at[index]),
+            (gain_ref, gaino_ref.at[index]),
+            (x_ref, part(me, slice(None))),
+        ],
+        here,
+    )
+    copies = Copies(send, recv)
+    gather = PlaneGather(copies, me, row_half(x_ref, rows), part)
+    lines = [
+        LineGather(copies, index, line, lambda slot, ref=ref: ref.at[slot])
+        for ref in (qkvo_ref, gaino_ref, woo_ref)
+    ]
+    gather.begin()
+    for copy in local[:3]:
+        copy.wait()
+    for each in lines:
+        each.begin()
+    gather.first_hop()
+    for step in range(1, line):
+        for each in lines:
+            each.hop(step)
+        if step == 1:
+            gather.second_hop()
+    gather.third_hop()
+    gather.last()
+    for each in lines:
+        each.finish()
+    copies.finish()
+    local[3].wait()
+
+
+def first_exchange(line, x, qkv, wo, gains):
+    plane = lax.axis_size("ctx")
+    count = GATHER_COPIES + 6 * (line - 1)
+    return pl.pallas_call(
+        functools.partial(first_kernel, line),
+        out_shape=(
+            jax.ShapeDtypeStruct((plane * x.shape[0], x.shape[1]), x.dtype),
+            *(jax.ShapeDtypeStruct((line, *a.shape), a.dtype) for a in (qkv, wo, gains)),
+        ),
+        in_specs=anywhere(4),
+        out_specs=tuple(anywhere(4)),
+        scratch_shapes=[
+            pltpu.SemaphoreType.DMA((count,)),
+            pltpu.SemaphoreType.DMA((count,)),
+            pltpu.SemaphoreType.DMA((4,)),
+        ],
+        compiler_params=remote_params(1),
+        name="first_exchange",
+    )(x, qkv, wo, gains)
+
+
+def second_kernel(line, o_ref, wo_ref, dy_ref, att_ref, woo_ref, dyo_ref, send, recv, here):
+    me = lax.axis_index("ctx")
+    rows = dy_ref.shape[0]
+    start_barrier(me)
+    copies = Copies(send, recv)
+
+    def columns(slot):
+        return att_ref.at[slot]
+
+    def block(slot):
+        return o_ref.at[pl.ds(pl.multiple_of(slot * rows, rows), rows), :]
+
+    numbers = {}
+    for bit in (6, 7, 4, 5, 2, 3, 1):
+        numbers[bit] = copies.number()
+        copies.send(numbers[bit], block(me ^ bit), columns(me), {"ctx": me ^ bit})
+    local = local_copies(
+        [
+            (block(me), columns(me)),
+            (wo_ref, woo_ref.at[:, me]),
+            (dy_ref, row_part(dyo_ref, rows)(me, slice(None))),
+        ],
+        here,
+    )
+    middle = line // 2
+
+    def wo_half(side):
+        return wo_ref.at[pl.ds(side * middle, middle)]
+
+    def wo_part(slot, side):
+        if isinstance(side, slice):
+            return woo_ref.at[:, slot]
+        return woo_ref.at[pl.ds(side * middle, middle), slot]
+
+    run_gathers(
+        [
+            PlaneGather(copies, me, wo_half, wo_part),
+            PlaneGather(copies, me, row_half(dy_ref, rows), row_part(dyo_ref, rows)),
+        ]
+    )
+    for bit, number in numbers.items():
+        copies.arrived(number, columns(me ^ bit))
+    for copy in local:
+        copy.wait()
+    copies.finish()
+
+
+def second_exchange(o, wo, dy):
+    plane = lax.axis_size("ctx")
+    rows = dy.shape[0]
+    line, part, model = wo.shape
+    count = 2 * GATHER_COPIES + 7
+    return pl.pallas_call(
+        functools.partial(second_kernel, line),
+        out_shape=(
+            jax.ShapeDtypeStruct((plane, rows, o.shape[1]), o.dtype),
+            jax.ShapeDtypeStruct((line, plane, part, model), wo.dtype),
+            jax.ShapeDtypeStruct((plane * rows, model), dy.dtype),
+        ),
+        in_specs=anywhere(3),
+        out_specs=tuple(anywhere(3)),
+        scratch_shapes=[
+            pltpu.SemaphoreType.DMA((count,)),
+            pltpu.SemaphoreType.DMA((count,)),
+            pltpu.SemaphoreType.DMA((3,)),
+        ],
+        compiler_params=remote_params(2),
+        name="second_exchange",
+    )(o, wo, dy)
+
+
+def gather_kernel(x_ref, xo_ref, send, recv, here):
+    me = lax.axis_index("ctx")
+    rows = x_ref.shape[0]
+    start_barrier(me)
+    part = row_part(xo_ref, rows)
+    local = local_copies([(x_ref, part(me, slice(None)))], here)
+    copies = Copies(send, recv)
+    run_gathers([PlaneGather(copies, me, row_half(x_ref, rows), part)])
+    copies.finish()
+    local[0].wait()
+
+
+def plane_gather(x, number):
+    plane = lax.axis_size("ctx")
+    return pl.pallas_call(
+        gather_kernel,
+        out_shape=jax.ShapeDtypeStruct((plane * x.shape[0], x.shape[1]), x.dtype),
+        in_specs=anywhere(1),
+        out_specs=anywhere(1)[0],
+        scratch_shapes=[
+            pltpu.SemaphoreType.DMA((GATHER_COPIES,)),
+            pltpu.SemaphoreType.DMA((GATHER_COPIES,)),
+            pltpu.SemaphoreType.DMA((1,)),
+        ],
+        compiler_params=remote_params(number),
+        name=f"plane_gather_{number}",
+    )(x)
+
+
+REDUCE_COPIES = 10
+
+
+class PlaneReduce:
+    def __init__(self, copies, me, block, heard, held, landed):
+        self.copies, self.me, self.block = copies, me, block
+        self.heard, self.held, self.landed = heard, held, landed
+        self.first = copies.next
+        copies.next += REDUCE_COPIES
+        self.half = heard.shape[1] // 2
+
+    def side(self, ref, slot, half):
+        return ref.at[slot, pl.ds(half * self.half, self.half), :]
+
+    def share(self, order):
+        partner = self.me ^ 1
+        bit = (6, 2, 4, 0)[order]
+        self.copies.send(
+            self.first + order, self.block(partner ^ bit), self.heard.at[order], {"ctx": partner}
+        )
+
+    def combine(self, order, rows, extra=None):
+        bit = (6, 2, 4)[order]
+        total = self.block(self.me ^ bit)[rows, :].astype(jnp.float32) + self.heard[
+            order, rows, :
+        ].astype(jnp.float32)
+        if extra is not None:
+            total = total + extra
+        self.held[order, rows, :] = total.astype(self.held.dtype)
+
+    def first_sends(self):
+        me, copies, first, half = self.me, self.copies, self.first, self.half
+        upper, lower = pl.ds(0, half), pl.ds(half, half)
+        x, y = {"ctx": me ^ 2}, {"ctx": me ^ 4}
+        held, landed, side = self.held, self.landed, self.side
+        arrived = copies.arrived
+        arrived(first + 0, self.heard.at[0])
+        self.combine(0, pl.ds(0, 2 * half))
+        copies.send(first + 4, side(held, 0, 0), side(landed, 0, 0), x)
+        copies.send(first + 5, side(held, 0, 1), side(landed, 0, 1), y)
+        arrived(first + 1, self.heard.at[1])
+        self.combine(1, upper)
+        copies.send(first + 6, side(held, 1, 0), side(landed, 1, 0), x)
+        arrived(first + 2, self.heard.at[2])
+        self.combine(2, lower)
+        copies.send(first + 7, side(held, 2, 1), side(landed, 2, 1), y)
+
+    def second_sends(self):
+        me, copies, first, half = self.me, self.copies, self.first, self.half
+        upper, lower = pl.ds(0, half), pl.ds(half, half)
+        x, y = {"ctx": me ^ 2}, {"ctx": me ^ 4}
+        held, landed, side = self.held, self.landed, self.side
+        arrived = copies.arrived
+        arrived(first + 5, side(landed, 0, 1))
+        self.combine(1, lower, landed[0, lower, :].astype(jnp.float32))
+        copies.send(first + 8, side(held, 1, 1), side(landed, 1, 1), x)
+        arrived(first + 4, side(landed, 0, 0))
+        self.combine(2, upper, landed[0, upper, :].astype(jnp.float32))
+        copies.send(first + 9, side(held, 2, 0), side(landed, 2, 0), y)
+        arrived(first + 3, self.heard.at[3])
+
+    def sum_half(self, which):
+        first, half = self.first, self.half
+        rows = pl.ds(which * half, half)
+        self.copies.arrived(first + (6, 8)[which], self.side(self.landed, 1, which))
+        self.copies.arrived(first + (9, 7)[which], self.side(self.landed, 2, which))
+        return (
+            self.block(self.me)[rows, :].astype(jnp.float32)
+            + self.heard[3, rows, :].astype(jnp.float32)
+            + self.landed[1, rows, :].astype(jnp.float32)
+            + self.landed[2, rows, :].astype(jnp.float32)
+        )
+def feed_kernel(
+    line,
+    g_ref,
+    dy_ref,
+    w_ref,
+    sum_ref,
+    out_ref,
+    dw_ref,
+    down_ref,
+    all_g,
+    hid,
+    hid_t,
+    gate_t,
+    up_t,
+    part,
+    heard,
+    held,
+    landed,
+    stage,
+    send,
+    recv,
+    here,
+):
+    me = lax.axis_index("ctx")
+    rows = g_ref.shape[0]
+    width, model = down_ref.shape
+    blocks = model // width
+    unit = width // line
+    start_barrier(me)
+    copies = Copies(send, recv)
+    gather = PlaneGather(copies, me, row_half(g_ref, rows), row_part(all_g, rows))
+    gather.begin()
+
+    def at(slot):
+        return pl.ds(pl.multiple_of(slot * rows, rows), rows)
+
+    all_g[at(me), :] = g_ref[...]
+    gate_ref, up_ref = w_ref.at[:, :width], w_ref.at[:, width : 2 * width]
+    for z in range(line):
+        for number in range(blocks):
+            source = pl.ds((z * blocks + number) * unit, unit)
+            down_ref[pl.ds(z * unit, unit), number * width : (number + 1) * width] = w_ref[
+                source, 2 * width :
+            ]
+
+    def block(slot):
+        return part.at[at(slot), :]
+
+    reduce = PlaneReduce(copies, me, block, heard, held, landed)
+
+    def chunk(order):
+        place = at(me ^ order)
+        g = all_g[place, :]
+        dy = dy_ref[place, :]
+        gate_values = contract(g, gate_ref[...], 1, 0)
+        up_values = contract(g, up_ref[...], 1, 0)
+        sigmoid_gate = 1.0 / (1.0 + jnp.exp(-gate_values))
+        activated = gate_values * sigmoid_gate
+        hidden_act = (activated * up_values).astype(jnp.bfloat16)
+        hid[place, :] = hidden_act
+        hid_t[:, place] = hidden_act.T
+        grad_hidden = contract(dy, down_ref[...], 1, 1)
+        grad_gate = (
+            grad_hidden * up_values * sigmoid_gate * (1.0 + gate_values * (1.0 - sigmoid_gate))
+        ).astype(jnp.bfloat16)
+        grad_up = (grad_hidden * activated).astype(jnp.bfloat16)
+        gate_t[:, place] = grad_gate.T
+        up_t[:, place] = grad_up.T
+        part[place, :] = (
+            contract(grad_gate, gate_ref[...], 1, 1) + contract(grad_up, up_ref[...], 1, 1)
+        ).astype(jnp.bfloat16)
+
+    def step(order, carry):
+        for number, slot, sides, when in (
+            (4, 1, 0, 1),
+            (5, 1, 1, 1),
+            (8, 3, 1, 3),
+            (10, 3, 0, 3),
+            (9, 5, 0, 5),
+            (11, 5, 1, 5),
+            (12, 7, slice(None), 7),
+        ):
+
+            @pl.when(order == when)
+            def _(number=number, slot=slot, sides=sides):
+                copies.arrived(gather.first + number, gather.part(me ^ slot, sides))
+
+        chunk(order)
+        return carry
+
+    lax.fori_loop(0, 2, step, 0)
+    gather.first_hop()
+    gather.second_hop()
+    reduce.share(3)
+    lax.fori_loop(2, 6, step, 0)
+    gather.third_hop()
+    reduce.share(1)
+    reduce.share(2)
+    lax.fori_loop(6, 8, step, 0)
+    reduce.share(0)
+
+    chunks = dy_ref.shape[0] // rows
+
+    def give(number, carry):
+        slot = lax.rem(number, 2)
+        copy = pltpu.make_async_copy(stage.at[slot], out_ref.at[at(number), :], here.at[slot])
+
+        @pl.when(number >= 2)
+        def _():
+            copy.wait()
+
+        stage[slot] = contract(hid[at(number), :], down_ref[...], 1, 0).astype(jnp.bfloat16)
+        copy.start()
+        return carry
+
+    def weights(number, carry):
+        columns = pl.ds(pl.multiple_of(number * width, width), width)
+        total = contract(hid_t[...], dy_ref[:, columns], 1, 0).astype(jnp.bfloat16)
+        for z in range(line):
+            target = pl.ds(pl.multiple_of((z * blocks + number) * unit, unit), unit)
+            dw_ref[target, 2 * width :] = total[z * unit : (z + 1) * unit, :]
+        for side, left in enumerate((gate_t, up_t)):
+            total = contract(left[...], all_g[:, columns], 1, 0).astype(jnp.bfloat16)
+            dw_ref[columns, side * width : (side + 1) * width] = total.T
+        return carry
+
+    lax.fori_loop(0, 2, give, 0)
+    reduce.first_sends()
+    lax.fori_loop(2, chunks, give, 0)
+    reduce.second_sends()
+    lax.fori_loop(0, blocks, weights, 0)
+    half = rows // 2
+    for which in (1, 0):
+        sum_ref[pl.ds(which * half, half), :] = reduce.sum_half(which)
+    for slot in (0, 1):
+        pltpu.make_async_copy(stage.at[slot], out_ref.at[at(slot), :], here.at[slot]).wait()
+    copies.finish()
+
+
+def feed(g, dy, w):
+    plane, line = lax.axis_size("ctx"), lax.axis_size("fsdp")
+    rows, model = g.shape
+    tokens = plane * rows
+    width = w.shape[1] // 3
+    count = GATHER_COPIES + REDUCE_COPIES
+    half_type = jnp.bfloat16
+    return pl.pallas_call(
+        functools.partial(feed_kernel, line),
+        out_shape=(
+            jax.ShapeDtypeStruct((rows, model), jnp.float32),
+            jax.ShapeDtypeStruct((tokens, model), half_type),
+            jax.ShapeDtypeStruct(w.shape, half_type),
+        ),
+        in_specs=in_vmem(3),
+        out_specs=(*in_vmem(1), *anywhere(1), *in_vmem(1)),
+        scratch_shapes=[
+            pltpu.VMEM((width, model), half_type),
+            pltpu.VMEM((tokens, model), half_type),
+            pltpu.VMEM((tokens, width), half_type),
+            pltpu.VMEM((width, tokens), half_type),
+            pltpu.VMEM((width, tokens), half_type),
+            pltpu.VMEM((width, tokens), half_type),
+            pltpu.VMEM((tokens, model), half_type),
+            pltpu.VMEM((4, rows, model), half_type),
+            pltpu.VMEM((3, rows, model), half_type),
+            pltpu.VMEM((3, rows, model), half_type),
+            pltpu.VMEM((2, rows, model), half_type),
+            pltpu.SemaphoreType.DMA((count,)),
+            pltpu.SemaphoreType.DMA((count,)),
+            pltpu.SemaphoreType.DMA((2,)),
+        ],
+        compiler_params=pltpu.CompilerParams(
+            collective_id=3, has_side_effects=True, vmem_limit_bytes=60 << 20
+        ),
+        name="feed",
+    )(g, dy, w)
+
+
+def gradients_kernel(line, shapes, *refs):
+    count = len(shapes)
+    pieces, terms_ref = refs[:count], refs[count]
+    wholes, total_ref = refs[count + 1 : 2 * count + 1], refs[2 * count + 1]
+    heard, plane_sum, across, send, recv, here = refs[2 * count + 2 :]
+    me, index = lax.axis_index("ctx"), lax.axis_index("fsdp")
+    start_barrier(me, index, line)
+    copies = Copies(send, recv)
+    gathers, pairs = [], []
+    for piece, whole in zip(pieces, wholes):
+        rows = piece.shape[0]
+        part = row_part(whole, rows)
+        gathers.append(PlaneGather(copies, me, row_half(piece, rows), part))
+        pairs.append((piece, part(me, slice(None))))
+    first = copies.next
+    copies.next += 7 + line - 1
+    for bit in range(1, 8):
+        copies.send(first + bit - 1, terms_ref, heard.at[bit], {"ctx": me ^ bit})
+    for gather in gathers:
+        gather.begin()
+    local = local_copies(pairs, here)
+    total = terms_ref[...]
+    for bit in range(1, 8):
+        copies.arrived(first + bit - 1, heard.at[bit])
+        total = total + heard[bit]
+    plane_sum[...] = total
+    for step in range(1, line):
+        peer = {"fsdp": lax.rem(index + step, line)}
+        copies.send(first + 6 + step, plane_sum, across.at[step], peer)
+    for gather in gathers:
+        gather.first_hop()
+    for gather in gathers:
+        gather.second_hop()
+    for step in range(1, line):
+        copies.arrived(first + 6 + step, across.at[step])
+        total = total + across[step]
+    total_ref[...] = total
+    for gather in gathers:
+        gather.third_hop()
+    for gather in gathers:
+        gather.last()
+    for copy in local:
+        copy.wait()
+    copies.finish()
+
+
+def gather_gradients(pieces, terms, number):
+    plane, line = lax.axis_size("ctx"), lax.axis_size("fsdp")
+    count = len(pieces)
+    copies = GATHER_COPIES * count + 7 + line - 1
+    shapes = tuple(piece.shape for piece in pieces)
+    return pl.pallas_call(
+        functools.partial(gradients_kernel, line, shapes),
+        out_shape=(
+            *(
+                jax.ShapeDtypeStruct((plane * piece.shape[0], piece.shape[1]), piece.dtype)
+                for piece in pieces
+            ),
+            jax.ShapeDtypeStruct(terms.shape, terms.dtype),
+        ),
+        in_specs=anywhere(count) + in_vmem(1),
+        out_specs=(*anywhere(count), *in_vmem(1)),
+        scratch_shapes=[
+            pltpu.VMEM((plane, *terms.shape), terms.dtype),
+            pltpu.VMEM(terms.shape, terms.dtype),
+            pltpu.VMEM((line, *terms.shape), terms.dtype),
+            pltpu.SemaphoreType.DMA((copies,)),
+            pltpu.SemaphoreType.DMA((copies,)),
+            pltpu.SemaphoreType.DMA((count,)),
+        ],
+        compiler_params=remote_params(number),
+        name=f"gather_gradients_{number}",
+    )(*pieces, terms)
+
+
+def spread_kernel(gate_in, up_in, down_in, gate_ref, up_ref, down_ref):
+    plane, shard, unit = gate_in.shape
+    for source, target in ((gate_in, gate_ref), (up_in, up_ref)):
+        for slot in range(plane):
+            target[:, slot * unit : (slot + 1) * unit] = source[slot].astype(jnp.float32)
+    step = pl.program_id(0)
+    width = down_in.shape[2]
+    blocks = shard // unit
+    for slot in range(down_in.shape[0]):
+        for number in range(blocks):
+            down_ref[slot * unit : (slot + 1) * unit, number * width : (number + 1) * width] = (
+                down_in[slot, number * unit : (number + 1) * unit, :].astype(jnp.float32)
+            )
+
+
+def spread_feed(pieces, shard, line, unit):
+    plane = lax.axis_size("ctx")
+    width = line * unit
+    model = line * shard
+    pieces = pieces.reshape(plane, shard, 3 * width)
+    each = plane // line
+    return pl.pallas_call(
+        spread_kernel,
+        grid=(line,),
+        in_specs=[
+            pl.BlockSpec((plane, shard, unit), lambda z: (0, 0, z)),
+            pl.BlockSpec((plane, shard, unit), lambda z: (0, 0, line + z)),
+            pl.BlockSpec((each, shard, width), lambda z: (z, 0, 2)),
+        ],
+        out_specs=(
+            pl.BlockSpec((shard, plane * unit), lambda z: (0, z)),
+            pl.BlockSpec((shard, plane * unit), lambda z: (0, z)),
+            pl.BlockSpec((each * unit, model), lambda z: (z, 0)),
+        ),
+        out_shape=(
+            jax.ShapeDtypeStruct((shard, plane * width), jnp.float32),
+            jax.ShapeDtypeStruct((shard, plane * width), jnp.float32),
+            jax.ShapeDtypeStruct((plane * unit, model), jnp.float32),
+        ),
+        compiler_params=pltpu.CompilerParams(vmem_limit_bytes=40 << 20),
+        name="spread_feed",
+    )(pieces, pieces, pieces)
+
+
+def spread_attention_kernel(in_ref, q_ref, k_ref, v_ref, wo_ref):
+    plane, _, across = in_ref.shape
+    shard = q_ref.shape[0]
+    key_width = k_ref.shape[1] // plane
+    query_width = q_ref.shape[1] // plane
+    first = 0
+    for target, width in ((q_ref, query_width), (k_ref, key_width), (v_ref, key_width)):
+        target[...] = jnp.concatenate(
+            [
+                in_ref[slot, :shard, first : first + width].astype(jnp.float32)
+                for slot in range(plane)
+            ],
+            axis=1,
+        )
+        first += width
+    for slot in range(plane):
+        for number in range(wo_ref.shape[1] // across):
+            source = slice(shard + number * HALF, shard + (number + 1) * HALF)
+            wo_ref[slot * HALF : (slot + 1) * HALF, number * across : (number + 1) * across] = (
+                in_ref[slot, source, :].astype(jnp.float32)
+            )
+
+
+def spread_attention(pieces, shard, model, query_width, key_width):
+    plane = lax.axis_size("ctx")
+    pieces = pieces.reshape(plane, -1, pieces.shape[1])
+    f32 = jnp.float32
+    return pl.pallas_call(
+        spread_attention_kernel,
+        in_specs=in_vmem(1),
+        out_specs=tuple(in_vmem(4)),
+        out_shape=(
+            jax.ShapeDtypeStruct((shard, plane * query_width), f32),
+            jax.ShapeDtypeStruct((shard, plane * key_width), f32),
+            jax.ShapeDtypeStruct((shard, plane * key_width), f32),
+            jax.ShapeDtypeStruct((plane * HALF, model), f32),
+        ),
+        compiler_params=pltpu.CompilerParams(vmem_limit_bytes=40 << 20),
+        name="spread_attention",
+    )(pieces)
+
+
+def last_sums_kernel(
+    dx_ref, out_ref, dqkv_ref, wo_ref, dx_sum, out_sum, grads_ref, heard, held, landed, send, recv, here
+):
+    me = lax.axis_index("ctx")
+    rows = dx_sum.shape[0]
+    start_barrier(me)
+    copies = Copies(send, recv)
+
+    def at(slot):
+        return pl.ds(pl.multiple_of(slot * rows, rows), rows)
+
+    pieces, wo_rows = wo_ref.shape[:2]
+    line, grad_rows = grads_ref.shape[:2]
+    shard = grad_rows - wo_rows
+    to_first = pieces * lax.rem(me, 2)
+    line_slot = lax.div(me, 2)
+    wo_first = copies.next
+    copies.next += pieces
+
+    def wo_place(slot):
+        return grads_ref.at[slot, pl.ds(shard, wo_rows), :]
+
+    def wo_copy(piece):
+        return copies.make(
+            wo_first + piece,
+            wo_ref.at[piece],
+            wo_place(line_slot),
+            {"ctx": to_first + piece},
+            wo_first + line_slot,
+        )
+
+    for piece in range(pieces):
+
+        @pl.when(to_first + piece != me)
+        def _(piece=piece):
+            wo_copy(piece).start()
+
+        @pl.when(to_first + piece == me)
+        def _(piece=piece):
+            wo_place(line_slot)[...] = wo_ref[piece]
+
+    reduces = []
+    for number, ref in enumerate((dx_ref, out_ref)):
+        reduces.append(
+            PlaneReduce(
+                copies,
+                me,
+                lambda slot, ref=ref: ref.at[at(slot), :],
+                heard.at[number],
+                held.at[number],
+                landed.at[number],
+            )
+        )
+    for reduce in reduces:
+        for order in range(4):
+            reduce.share(order)
+    for slot in range(line):
+        grads_ref[slot, :shard, :] = dqkv_ref[slot * shard : (slot + 1) * shard, :]
+    for reduce in reduces:
+        reduce.first_sends()
+    for reduce in reduces:
+        reduce.second_sends()
+    half = rows // 2
+    for which in (1, 0):
+        for reduce, target in zip(reduces, (dx_sum, out_sum)):
+            target[pl.ds(which * half, half), :] = reduce.sum_half(which)
+    for slot in range(line):
+
+        @pl.when(2 * slot + lax.div(me, pieces) != me)
+        def _(slot=slot):
+            copies.make(
+                wo_first, wo_ref.at[0], wo_place(slot), {"ctx": 0}, wo_first + slot
+            ).wait_recv()
+
+    for piece in range(pieces):
+
+        @pl.when(to_first + piece != me)
+        def _(piece=piece):
+            wo_copy(piece).wait_send()
+
+    copies.finish()
+
+
+def last_sums(dx, out, dqkv, wo, line):
+    plane = lax.axis_size("ctx")
+    rows, model = dx.shape[0] // plane, dx.shape[1]
+    count = 2 * REDUCE_COPIES + wo.shape[0]
+    across = dqkv.shape[1]
+    return pl.pallas_call(
+        last_sums_kernel,
+        out_shape=(
+            jax.ShapeDtypeStruct((rows, model), jnp.float32),
+            jax.ShapeDtypeStruct((rows, model), jnp.float32),
+            jax.ShapeDtypeStruct((line, dqkv.shape[0] // line + wo.shape[1], across), dqkv.dtype),
+        ),
+        in_specs=in_vmem(4),
+        out_specs=tuple(in_vmem(3)),
+        scratch_shapes=[
+            pltpu.VMEM((2, 4, rows, model), dx.dtype),
+            pltpu.VMEM((2, 3, rows, model), dx.dtype),
+            pltpu.VMEM((2, 3, rows, model), dx.dtype),
+            pltpu.SemaphoreType.DMA((count,)),
+            pltpu.SemaphoreType.DMA((count,)),
+            pltpu.SemaphoreType.DMA((1,)),
+        ],
+        compiler_params=remote_params(7),
+        name="last_sums",
+    )(dx, out, dqkv, wo)
+def head_local(
+    block_input,
+    block_table,
+    output_grad,
+    attention_gain,
+    query_weight,
+    key_weight,
+    value_projection,
+    output_weight,
+    feedforward_gain,
+    gate_weight,
+    up_weight,
+    down_weight,
+):
+    me = lax.axis_index("ctx")
+    plane = lax.axis_size("ctx")
+    line = lax.axis_size("fsdp")
+    rows, model = block_input.shape[1:]
+    shard = model // line
+    hidden = gate_weight.shape[1]
+    unit = hidden // (line * plane)
+    table_row = block_table[0]
+    slot_count = table_row.shape[0]
+    block = rows * plane // slot_count
+    places = jnp.arange(slot_count, dtype=jnp.int32)
+    slots = jnp.sum(jnp.where(table_row[None, :] == places[:, None], places[None, :], 0), axis=1)
+
+    def mine(array, width):
+        return lax.dynamic_slice_in_dim(array, me * width, width, 1)
+
+    query_width = query_weight.shape[1] // plane
+    key_width = key_weight.shape[1] // plane
+    qkv_mine = jnp.concatenate(
+        [
+            mine(query_weight, query_width),
+            mine(key_weight, key_width),
+            mine(value_projection, key_width),
+        ],
+        axis=1,
+    )
+    wo_mine = lax.dynamic_slice_in_dim(output_weight, me * HALF, HALF, 0)
+    gains_mine = jnp.stack([attention_gain, feedforward_gain])
+    x_all, qkv_w, wo_line, gains = first_exchange(
+        line, block_input[0], qkv_mine, wo_mine, gains_mine
+    )
+
+    feed_width = line * unit
+    blocks = [
+        lax.dynamic_slice_in_dim(array, (z * plane + me) * unit, unit, 1)
+        for array in (gate_weight, up_weight)
+        for z in range(line)
+    ]
+    down_mine = lax.dynamic_slice_in_dim(down_weight, me * unit, unit, 0)
+    down_mine = jnp.concatenate(
+        [down_mine[:, at : at + feed_width] for at in range(0, model, feed_width)], axis=0
+    )
+    feed_mine = jnp.concatenate([*blocks, down_mine], axis=1)
+    feed_mine, x_all = lax.optimization_barrier((feed_mine, x_all))
+    feed_w = lax.all_gather(feed_mine, "fsdp", axis=0, tiled=True)
+
+    steps_index = jnp.arange(HALF, dtype=jnp.float32)
+    inverse = jnp.exp(steps_index * jnp.float32(-2.0 * math.log(rotary_base) / HEAD_SIZE))
+
+    def table_of(positions):
+        angles = positions.astype(jnp.float32)[:, None] * inverse[None, :]
+        both = jnp.stack([jnp.cos(angles), jnp.sin(angles)])
+        both = jnp.pad(both, ((0, 0), (0, 0), (0, LANES // 2 - HALF)))
+        return jnp.concatenate([both, both], axis=2)
+
+    inner = table_of(jnp.arange(block, dtype=jnp.int32))
+    outer = table_of(places * block)
+    pad = padding(GROUP + 2)
+
+    gains = jnp.transpose(gains, (1, 0, 2)).reshape(2, model).astype(jnp.float32)
+    qkv_w = qkv_w.reshape(model, -1)
+    gained_one, qkv, o, lse = attend(slots, x_all, gains[:1], qkv_w, pad, inner, outer)
+
+    attended, wo_full, grad_all = second_exchange(o, wo_line, output_grad[0])
+    attended = jnp.transpose(attended, (1, 0, 2)).reshape(rows, -1)
+    wo_full = wo_full.reshape(-1, model)
+    inputs = block_input[0].astype(jnp.float32)
+    residual = inputs + product(attended, wo_full)
+    scale_two = norm_scale(residual)
+    normed_two = residual * scale_two
+    grad_normed_two, out_parts, feed_grads = feed(
+        (normed_two * gains[1]).astype(jnp.bfloat16), grad_all, feed_w
+    )
+    feed_grads = lax.psum_scatter(feed_grads, "fsdp", scatter_dimension=0, tiled=True)
+    feedforward_term = jnp.sum(grad_normed_two * normed_two, axis=0)
+    grad_scaled_two = grad_normed_two * gains[1]
+    grad_residual = output_grad[0].astype(jnp.float32) + scale_two * (
+        grad_scaled_two
+        - normed_two * jnp.mean(grad_scaled_two * normed_two, axis=-1, keepdims=True)
+    )
+    grad_attn = plane_gather(grad_residual.astype(jnp.bfloat16), 6)
+    own = GROUP * HEAD_SIZE
+    wo_mine = lax.dynamic_slice_in_dim(wo_full, me * own, own, 0)
+    dx, qkv_term, wo_term = attend_back(
+        slots, grad_attn, gained_one, qkv, o, lse, qkv_w, wo_mine, pad, inner, outer
+    )
+    grad_normed_one, out_sum, attention_grads = last_sums(dx, out_parts, qkv_term, wo_term, line)
+    attention_grads = lax.psum_scatter(
+        attention_grads.reshape(-1, attention_grads.shape[2]),
+        "fsdp",
+        scatter_dimension=0,
+        tiled=True,
+    )
+    layer_output = (residual + out_sum).astype(jnp.bfloat16)
+    scale_one = norm_scale(inputs)
+    normed_one = inputs * scale_one
+    attention_term = jnp.sum(grad_normed_one * normed_one, axis=0)
+    grad_scaled_one = grad_normed_one * gains[0]
+    input_grad = grad_residual + scale_one * (
+        grad_scaled_one
+        - normed_one * jnp.mean(grad_scaled_one * normed_one, axis=-1, keepdims=True)
+    )
+    feed_pieces, gain_terms = gather_gradients(
+        [feed_grads], jnp.stack([attention_term, feedforward_term]), 8
+    )
+    gate_grad, up_grad, down_grad = spread_feed(feed_pieces, shard, line, unit)
+    attention_pieces = plane_gather(attention_grads, 9)
+    query_grad, key_grad, value_grad, out_grad = spread_attention(
+        attention_pieces, shard, model, query_width, key_width
+    )
+    gain_terms = lax.dynamic_slice_in_dim(gain_terms, lax.axis_index("fsdp") * shard, shard, 1)
+    return (
+        layer_output[None],
+        input_grad[None],
+        gain_terms[0],
+        query_grad,
+        key_grad,
+        value_grad,
+        out_grad,
+        gain_terms[1],
+        gate_grad,
+        up_grad,
+        down_grad,
+    )
+
+
 def solution(mesh):
+    plane, line = mesh.shape["ctx"], mesh.shape["fsdp"]
+    fits = plane == KEY_VALUE_HEADS == 8 and plane * line * HALF == QUERY_HEADS * HEAD_SIZE
+    plan = head_local if fits else local
     return jax.shard_map(
-        local,
+        plan,
         mesh=mesh,
         in_specs=(
             P("fsdp", "ctx", None),

time: 2370 us -> 588 us (0.25)
  waiting for transfers between devices: 1970 us -> 94.2 us
  Pallas kernels: 0 us -> 431 us
  matrix products: 211 us -> 4.07 us
  blocking collectives: 50.5 us -> 0 us
  other arithmetic: 50 us -> 9 us
  local copies, waits for them, and re-layouts: 66.7 us -> 34.3 us
    reduce_scatter x9 -> x2, waiting for transfers between devices: 970 us -> 93.7 us  [the longest x1 62.3 us: head_local(): lax.psum_scatter(feed_grads, 'fsdp', scatter_dimension=0, tiled=True)]
    all_gather x9 -> x1, waiting for transfers between devices: 857 us -> 0.01 us  [head_local(): feed_w = lax.all_gather(feed_mine, 'fsdp', axis=0, tiled=True)]
    pallas_call x0 -> x11, Pallas kernels: none -> 431 us  [the longest x1 72.8 us: feed(): pl.pallas_call(functools.partial(feed_kernel, line), out_shape=(jax.Shape...]
    dot_general x28 -> x0, matrix products: 170 us -> none  [the longest x7 38.6 us: back_product(): lax.dot_general(matrix, operand, (((1,), (1,)), ((), ())), preferred_elem...]
    psum x1 -> x0, waiting for transfers between devices: 137 us -> none  [local(): lax.psum(shares[1].astype(jnp.bfloat16), 'ctx').astype(jnp.float32)]
    dot_general x7 -> x1, matrix products: 40.9 us -> 4.07 us  [product(): return jnp.dot(matrix, operand, preferred_element_type=jnp.float32)]
    all_gather x2 -> x0, blocking collectives: 26.2 us -> none  [the longest x1 13.6 us: local(): lax.all_gather(attention_gain, 'fsdp', axis=0, tiled=True)]
  transfers between devices with their start and end apart: 19 -> 3, of which waited for: 19 -> 2; matrix products, arithmetic and copies ran while one was open for 7% -> 3% of each run, Pallas kernels for 0% -> 20%
where the time goes in v2:
time: 588 us; the launch traced here: 587 us
  Pallas kernels  431 us (73%)
  waiting for transfers between devices  94.2 us (16%)
  local copies, waits for them, and re-layouts  34.3 us (6%)
  between operations  14.2 us (2%)
  other arithmetic  9 us (2%)
    pallas_call x1, Pallas kernels, feed(): pl.pallas_call(functools.partial(feed_kernel, line), out_shape=(jax.Shape...  72.8 us
    pallas_call x1, Pallas kernels, last_sums(): pl.pallas_call(last_sums_kernel, out_shape=(jax.ShapeDtypeStruct((rows, m...  67.1 us
    reduce_scatter x1, waiting for transfers between devices, head_local(): lax.psum_scatter(feed_grads, 'fsdp', scatter_dimension=0, tiled=True)  62.3 us
    pallas_call x1, Pallas kernels, second_exchange(): pl.pallas_call(functools.partial(second_kernel, line), out_shape=(jax.Sha...  62.2 us
    pallas_call x2, Pallas kernels, plane_gather(): pl.pallas_call(gather_kernel, out_shape=jax.ShapeDtypeStruct((plane * x.s...  51.7 us
    pallas_call x1, Pallas kernels, attend_back(): pl.pallas_call(backward_kernel, grid_spec=pltpu.PrefetchScalarGridSpec(nu...  50.6 us
    pallas_call x1, Pallas kernels, gather_gradients(): pl.pallas_call(functools.partial(gradients_kernel, line, shapes), out_sha...  47.1 us
    pallas_call x1, Pallas kernels, first_exchange(): pl.pallas_call(functools.partial(first_kernel, line), out_shape=(jax.Shap...  38.3 us
  transfers between devices with their start and end apart: 3, of which 2 were waited for; matrix products, arithmetic and copies ran while one was open for 3% of the time, Pallas kernels for 20%

profile of v2, /device:TPU:0, one launch (start us, length us, event | category | flops | bytes accessed | tf_op | source)
XLA Modules:
  0.0 586.7 jit_solution(291126550373249)
XLA Ops:
  7.3 0.8 stack.28
  8.0 0.7 stack.29
  8.7 0.9 dynamic-slice_dynamic-update-slice_fusion.7
  9.6 0.9 dynamic-slice_dynamic-update-slice_fusion.6
  10.5 0.9 dynamic-slice_dynamic-update-slice_fusion.5
  11.5 0.9 dynamic-slice_dynamic-update-slice_fusion.4
  12.4 0.9 dynamic-slice_dynamic-update-slice_fusion.3
  13.3 0.9 dynamic-slice_dynamic-update-slice_fusion.2
  14.2 0.9 dynamic-slice_dynamic-update-slice_fusion.1
  15.2 0.9 dynamic-slice_dynamic-update-slice_fusion
  16.2 1.2 constant_dynamic-slice_fusion.5
  17.3 1.2 constant_dynamic-slice_fusion.3
  18.7 1.1 constant_dynamic-slice_fusion
  19.8 38.3 %first_exchange.1 = (bf16[2048,1536]{1,0:T(8,128)(2,1)}, bf16[4,384,384]{2,1,0:T(8,128)(2,1)S(1)}, bf16[4,48,1536]{2,1,0:T(8,128)(2,1)S(1)}, bf16[4,2,384]{2,1,0:T(2,128)(2,1)S(1)}) custom-call(bf16[256,1536]{1,0:T(8,128)(2,1)S(1)} %bitcast.32, bf16[384,384]{1,0:T(8,128)(2,1)S(1)} %pad_maximum_fusion.qkv_ref, ...), custom_call_target="tpu_custom_call" | custom-call | tf_op jit(solution)/shard_map/first_exchange/pallas_call | solution.py:963
  58.1 0.8 copy-done.12
  58.9 1.0 copy-done.18
  61.0 1.4 copy-done.19
  62.4 30.0 %attend.1 = (bf16[2048,1536]{1,0:T(8,128)(2,1)}, bf16[2048,512]{1,0:T(8,128)(2,1)S(1)}, bf16[2048,192]{1,0:T(8,128)(2,1)S(1)}, f32[8,512]{1,0:T(8,128)S(1)}) custom-call(s32[16]{0:T(128)S(1)} %select_reduce_fusion.slot_ref, bf16[2048,1536]{1,0:T(8,128)(2,1)} %get-tuple-element.43.xa_ref.xb_ref, bf16[2048,1536]{1,0:T(8,128)(2,1)} %get-tuple-element.43.xa_ref.xb_ref, ...), custom_call_target="tpu_custom_call" | custom-call | flops 5368709120 | bytes 12582912 | tf_op jit(solution)/shard_map/attend/pallas_call | solution.py:507
  92.5 1.3 copy-done.21
  93.8 0.6 copy-done.22
  94.4 62.2 %second_exchange.1 = (bf16[8,256,192]{2,1,0:T(8,128)(2,1)S(1)}, bf16[4,8,48,1536]{3,2,1,0:T(8,128)(2,1)}, bf16[2048,1536]{1,0:T(8,128)(2,1)}) custom-call(bf16[2048,192]{1,0:T(8,128)(2,1)S(1)} %get-tuple-element.46.o_ref, bf16[4,48,1536]{2,1,0:T(8,128)(2,1)S(1)} %copy-done.13, bf16[256,1536]{1,0:T(8,128)(2,1)S(1)} %bitcast.34), custom_call_target="tpu_custom_call" | custom-call | tf_op jit(solution)/shard_map/second_exchange/pallas_call | solution.py:1033
  156.6 1.0 copy-done.10
  157.6 2.2 copy.27
  159.8 4.1 multiply_reduce_fusion.2
  163.9 2.4 constant_dynamic-slice_fusion.1.wo_ref
  166.2 1.1 multiply_convert_fusion.g_ref
  167.3 72.8 %feed.1 = (f32[256,1536]{1,0:T(8,128)}, bf16[2048,1536]{1,0:T(8,128)(2,1)}, bf16[1536,1536]{1,0:T(8,128)(2,1)}) custom-call(bf16[256,1536]{1,0:T(8,128)(2,1)} %multiply_convert_fusion.g_ref, bf16[2048,1536]{1,0:T(8,128)(2,1)} %get-tuple-element.50.dy_ref, bf16[1536,1536]{1,0:T(8,128)(2,1)} %all-gather.2.cloned.1.call-done.w_ref), custom_call_target="tpu_custom_call" | custom-call | tf_op jit(solution)/shard_map/feed/pallas_call | solution.py:1299
  240.2 2.0 multiply_reduce_fusion
  242.2 0.5 fusion.22.x_ref
  242.7 31.7 %plane_gather_6.1.ga_ref.gb_ref = bf16[2048,1536]{1,0:T(8,128)(2,1)} custom-call(bf16[256,1536]{1,0:T(8,128)(2,1)S(1)} %fusion.22.x_ref), custom_call_target="tpu_custom_call" | custom-call | tf_op jit(solution)/shard_map/plane_gather_6/pallas_call | solution.py:1066
  274.4 50.6 %attend_back.1 = (bf16[2048,1536]{1,0:T(8,128)(2,1)}, bf16[1536,384]{1,0:T(8,128)(2,1)}, bf16[4,192,384]{2,1,0:T(8,128)(2,1)}) custom-call(s32[16]{0:T(128)} %copy-done.20, bf16[2048,1536]{1,0:T(8,128)(2,1)} %plane_gather_6.1.ga_ref.gb_ref, bf16[2048,1536]{1,0:T(8,128)(2,1)} %plane_gather_6.1.ga_ref.gb_ref, bf16[2048,1536]{1,0:T(8,128)(2,1)} %get-tuple-element.53.gained_ref, ...), custom_call_target="tpu_custom_call" | custom-call | flops 18253611008 | bytes 25165824 | tf_op jit(solution)/shard_map/attend_back/pallas_call | solution.py:670
  325.0 1.3 copy-done.7
  326.2 1.1 copy-done.11
  327.3 67.1 %last_sums.1 = (f32[256,1536]{1,0:T(8,128)S(1)}, f32[256,1536]{1,0:T(8,128)S(1)}, bf16[4,576,384]{2,1,0:T(8,128)(2,1)}) custom-call(bf16[2048,1536]{1,0:T(8,128)(2,1)} %get-tuple-element.56.dx_ref, bf16[2048,1536]{1,0:T(8,128)(2,1)} %get-tuple-element.57.out_ref, bf16[1536,384]{1,0:T(8,128)(2,1)S(1)} %copy-done.7, bf16[4,192,384]{2,1,0:T(8,128)(2,1)S(1)} %copy-done.11), custom_call_target="tpu_custom_call" | custom-call | tf_op jit(solution)/shard_map/last_sums/pallas_call | solution.py:1580
  394.4 1.1 copy-done.5
  396.6 0.5 fusion.8
  397.2 0.6 copy-done.6
  398.2 3.7 fusion.7
  401.9 31.4 %reduce-scatter.5.cloned.1.call-done.x_ref = bf16[576,384]{1,0:T(8,128)(2,1)} async-done(((bf16[2304,384]{1,0:T(8,128)(2,1)}), bf16[576,384]{1,0:T(8,128)(2,1)}) %reduce-scatter.5.cloned.1.call-update) | async-done | bytes 442384 | tf_op jit(solution)/shard_map/reduce_scatter | solution.py:1701
  433.4 1.0 copy-done.14
  434.4 20.0 %plane_gather_9.1 = bf16[4608,384]{1,0:T(8,128)(2,1)S(1)} custom-call(bf16[576,384]{1,0:T(8,128)(2,1)S(1)} %copy-done.14), custom_call_target="tpu_custom_call" | custom-call | tf_op jit(solution)/shard_map/plane_gather_9/pallas_call | solution.py:1066
  454.4 3.2 spread_attention.1
  457.7 62.3 %reduce-scatter.3.cloned.1.call-done.refs_0_ = bf16[384,1536]{1,0:T(8,128)(2,1)} async-done(((bf16[1536,1536]{1,0:T(8,128)(2,1)}), bf16[384,1536]{1,0:T(8,128)(2,1)}) %reduce-scatter.3.cloned.1.call-update) | async-done | bytes 1179664 | tf_op jit(solution)/shard_map/reduce_scatter | solution.py:1687
  520.0 1.3 copy-done.8
  521.2 47.1 %gather_gradients_8.1 = (bf16[3072,1536]{1,0:T(8,128)(2,1)}, f32[2,1536]{1,0:T(2,128)S(1)}) custom-call(bf16[384,1536]{1,0:T(8,128)(2,1)S(1)} %copy-done.8, f32[2,1536]{1,0:T(2,128)S(1)} %pad_maximum_fusion.4.refs_1_), custom_call_target="tpu_custom_call" | custom-call | tf_op jit(solution)/shard_map/gather_gradients_8/pallas_call | solution.py:1382
  568.3 3.7 copy-done.2
  572.0 7.5 %spread_feed.1 = (f32[384,4096]{1,0:T(8,128)}, f32[384,4096]{1,0:T(8,128)}, f32[1024,1536]{1,0:T(8,128)}) custom-call(bf16[8,384,1536]{2,1,0:T(8,128)(2,1)S(1)} %bitcast.29, bf16[8,384,1536]{2,1,0:T(8,128)(2,1)S(1)} %bitcast.30, bf16[8,384,1536]{2,1,0:T(8,128)(2,1)S(1)} %bitcast.31), custom_call_target="tpu_custom_call" | custom-call | tf_op jit(solution)/shard_map/spread_feed/pallas_call | solution.py:1427
  579.5 0.7 dynamic-slice_reduce_fusion
  (80 shorter events, 2.8 us)
Async XLA Ops:
  7.2 8.9 %copy-start = (bf16[384,1536]{1,0:T(8,128)(2,1)S(1)}, bf16[384,1536]{1,0:T(8,128)(2,1)}, u32[]{:S(2)}) copy-start(bf16[384,1536]{1,0:T(8,128)(2,1)} %param.19) | copy-start | bytes 3538948
  7.2 160.1 %all-gather.2.cloned.1.call-start = ((), (), s32[]{:S(2)}) async-start(), calls=%async_computation.2 | async-start | bytes 5898240 | tf_op jit(solution)/shard_map/all_gather | solution.py:1658
  16.2 3.6 copy-start.3
  19.8 40.1 %copy-start.26 = (bf16[384,1536]{1,0:T(8,128)(2,1)}, bf16[384,1536]{1,0:T(8,128)(2,1)S(1)}, u32[]{:S(2)}) copy-start(bf16[384,1536]{1,0:T(8,128)(2,1)S(1)} %maximum_dynamic-update-slice_fusion) | copy-start | bytes 3538948
  19.8 40.6 %copy-start.27 = (s32[1,16]{1,0:T(1,128)S(1)}, s32[1,16]{1,0:T(1,128)}, u32[]{:S(2)}) copy-start(s32[1,16]{1,0:T(1,128)} %param.13) | copy-start | bytes 196
  58.1 0.8 copy-start.12
  58.9 1.0 copy-start.18
  59.9 373.4 %reduce-scatter.5.cloned.1.call-start = ((), (), s32[]{:S(2)}) async-start(), calls=%async_computation.4 | async-start | bytes 2211840 | tf_op jit(solution)/shard_map/reduce_scatter | solution.py:1701
  60.5 31.9 %copy-start.20 = (s32[16]{0:T(128)}, s32[16]{0:T(128)S(1)}, u32[]{:S(2)}) copy-start(s32[16]{0:T(128)S(1)} %select_reduce_fusion.slot_ref) | copy-start | bytes 196
  60.8 31.7 %copy-start.17 = (f32[2,16,128]{2,1,0:T(8,128)}, f32[2,16,128]{2,1,0:T(8,128)S(1)}, u32[]{:S(2)}) copy-start(f32[2,16,128]{2,1,0:T(8,128)S(1)} %pad_maximum_fusion.3.outer_ref) | copy-start | bytes 49156
  60.9 31.6 %copy-start.16 = (f32[2,128,128]{2,1,0:T(8,128)}, f32[2,128,128]{2,1,0:T(8,128)S(1)}, u32[]{:S(2)}) copy-start(f32[2,128,128]{2,1,0:T(8,128)S(1)} %pad_maximum_fusion.1.inner_ref) | copy-start | bytes 393220
  61.0 31.5 %copy-start.15 = (bf16[384,512]{1,0:T(8,128)(2,1)}, bf16[384,512]{1,0:T(8,128)(2,1)S(1)}, u32[]{:S(2)}) copy-start(bf16[384,512]{1,0:T(8,128)(2,1)S(1)} %fusion.11.pad_ref) | copy-start | bytes 1179652
  61.0 1.4 copy-start.19
  62.4 32.0 %copy-start.4 = (bf16[1,256,1536]{2,1,0:T(8,128)(2,1)S(1)}, bf16[1,256,1536]{2,1,0:T(8,128)(2,1)}, u32[]{:S(2)}) copy-start(bf16[1,256,1536]{2,1,0:T(8,128)(2,1)} %param.14) | copy-start | bytes 2359300
  62.4 32.0 %copy-start.13 = (bf16[4,48,1536]{2,1,0:T(8,128)(2,1)S(1)}, bf16[4,48,1536]{2,1,0:T(8,128)(2,1)}, u32[]{:S(2)}) copy-start(bf16[4,48,1536]{2,1,0:T(8,128)(2,1)} %copy-done.12) | copy-start | bytes 1769476
  92.5 1.3 copy-start.21
  93.8 0.6 copy-start.22
  94.4 65.4 %copy-start.9 = (bf16[2048,192]{1,0:T(8,128)(2,1)}, bf16[2048,192]{1,0:T(8,128)(2,1)S(1)}, u32[]{:S(2)}) copy-start(bf16[2048,192]{1,0:T(8,128)(2,1)S(1)} %get-tuple-element.46.o_ref) | copy-start | bytes 2359300
  156.6 1.0 copy-start.10
  163.8 78.3 %copy-start.23 = (f32[256,1536]{1,0:T(8,128)}, f32[256,1536]{1,0:T(8,128)S(1)}, u32[]{:S(2)}) copy-start(f32[256,1536]{1,0:T(8,128)S(1)} %get-tuple-element.92) | copy-start | bytes 4718596
  240.2 2.0 copy-start.25
  324.9 1.3 copy-start.7
  326.2 1.1 copy-start.11
  394.4 1.1 copy-start.5
  395.6 124.4 %reduce-scatter.3.cloned.1.call-start = ((), (), s32[]{:S(2)}) async-start(), calls=%async_computation.3 | async-start | bytes 5898240 | tf_op jit(solution)/shard_map/reduce_scatter | solution.py:1687
  396.4 1.4 copy-start.6
  396.4 1.9 copy-start.24
  433.4 1.0 copy-start.14
  520.0 1.3 copy-start.8
  568.3 3.7 copy-start.2
  572.0 8.2 %copy-start.1 = (bf16[384,1536]{1,0:T(8,128)(2,1)S(1)}, bf16[384,1536]{1,0:T(8,128)(2,1)}, u32[]{:S(2)}) copy-start(bf16[384,1536]{1,0:T(8,128)(2,1)} %param.19) | copy-start | bytes 3538948
Sparse Core Ops, SparseCore 0:
  60.1 88.4 all-gather.1
  395.7 37.5 reduce-scatter.4
  435.7 84.2 reduce-scatter.2

commit v3 on v2

--- a/solution.py
+++ b/solution.py
@@ -7,6 +7,7 @@
 from jax.experimental import pallas as pl
 from jax.experimental.pallas import tpu as pltpu
 from jax.sharding import PartitionSpec as P
+
 
 QUERY_HEADS = 16
 KEY_VALUE_HEADS = 8
@@ -369,6 +370,7 @@
 HALF = HEAD_SIZE // 2
 GROUP = QUERY_HEADS // KEY_VALUE_HEADS
 score_scale = HEAD_SIZE ** (-0.5)
+binary_scale = score_scale * math.log2(math.e)
 
 
 def contract(left, right, left_dim, right_dim):
@@ -461,34 +463,43 @@
     def scores_of(step):
         at = pl.ds(pl.multiple_of(step * tile, tile), tile)
         keys = qkv_ref[at, GROUP * LANES : (GROUP + 1) * LANES]
-        return contract(keys, queries, 1, 1) * score_scale
+        return contract(keys, queries, 1, 1) * binary_scale
 
     last = jnp.where(diagonal, scores_of(index), score_with_mask)
     s_ref[here, :] = last
     peak = jnp.max(last, axis=0, keepdims=True)
 
-    def first_pass(step, peak):
-        scores = scores_of(step)
-        s_ref[pl.ds(pl.multiple_of(step * tile, tile), tile), :] = scores
-        return jnp.maximum(peak, jnp.max(scores, axis=0, keepdims=True))
-
-    peak = lax.fori_loop(0, index, first_pass, peak)
-
-    def second_pass(step, state):
+    def in_pairs(one, state):
+        state = lax.fori_loop(
+            0, lax.div(index, 2), lambda pair, state: one((2 * pair, 2 * pair + 1), state), state
+        )
+        return lax.fori_loop(0, lax.rem(index, 2), lambda _, state: one((index - 1,), state), state)
+
+    def first_pass(steps, peak):
+        found = [scores_of(step) for step in steps]
+        for step, scores in zip(steps, found):
+            s_ref[pl.ds(pl.multiple_of(step * tile, tile), tile), :] = scores
+            peak = jnp.maximum(peak, jnp.max(scores, axis=0, keepdims=True))
+        return peak
+
+    peak = in_pairs(first_pass, peak)
+
+    def second_pass(steps, state):
         total, out = state
-        at = pl.ds(pl.multiple_of(step * tile, tile), tile)
-        probs = jnp.exp(s_ref[at, :] - peak)
-        total = total + jnp.sum(probs, axis=0, keepdims=True)
-        out = out + contract(vt[:, at], probs.astype(jnp.bfloat16), 1, 0)
+        for step in steps:
+            at = pl.ds(pl.multiple_of(step * tile, tile), tile)
+            probs = jnp.exp2(s_ref[at, :] - peak)
+            total = total + jnp.sum(probs, axis=0, keepdims=True)
+            out = out + contract(vt[:, at], probs.astype(jnp.bfloat16), 1, 0)
         return (total, out)
 
-    total, out = lax.fori_loop(
-        0,
-        index + 1,
+    total, out = in_pairs(
         second_pass,
-        (jnp.zeros((1, width), jnp.float32), jnp.zeros((LANES, width), jnp.float32)),
-    )
-    lse_ref[pl.ds(index, 1), :] = peak + jnp.log(total)
+        second_pass(
+            (index,), (jnp.zeros((1, width), jnp.float32), jnp.zeros((LANES, width), jnp.float32))
+        ),
+    )
+    lse_ref[pl.ds(index, 1), :] = peak + jnp.log2(total)
     out = (out * (1.0 / total)).T.astype(jnp.bfloat16)
     out = jnp.concatenate([out[head * tile : (head + 1) * tile, :] for head in range(GROUP)], axis=1)
     out = contract(out, pad_ref[: GROUP * HEAD_SIZE, : GROUP * LANES], 1, 1).astype(jnp.bfloat16)
@@ -549,20 +560,18 @@
 
 def backward_kernel(
     slot_ref,
-    ga_ref,
-    gb_ref,
     gained_ref,
     qkv_ref,
     o_ref,
+    do_ref,
     lse_ref,
     w_ref,
-    wo_ref,
+    dwo_ref,
     pad_ref,
     inner_ref,
     outer_ref,
     dx_ref,
-    dw_ref,
-    dwo_ref,
+    grads_ref,
     wp,
     qs,
     gs,
@@ -570,15 +579,13 @@
     dk,
     dv,
     dw,
-    dwo,
 ):
     step_at = pl.program_id(0)
     tiles = pl.num_programs(0)
     index = tiles - 1 - step_at
-    block = ga_ref.shape[0]
-    tile = 2 * block
+    tile = gained_ref.shape[0]
+    block = tile // 2
     width = GROUP * tile
-    rows = qkv_ref.shape[0]
     first_key, first_value = GROUP * LANES, (GROUP + 1) * LANES
 
     @pl.when(step_at == 0)
@@ -588,16 +595,13 @@
         dk[...] = jnp.zeros_like(dk)
         dv[...] = jnp.zeros_like(dv)
         dw[...] = jnp.zeros_like(dw)
-        dwo[...] = jnp.zeros_like(dwo)
 
     here = pl.ds(pl.multiple_of(index * tile, tile), tile)
     sources = [
         pl.ds(pl.multiple_of(slot_ref[index * 2 + part] * block, block), block) for part in (0, 1)
     ]
-    grad_attn = jnp.concatenate([ga_ref[...], gb_ref[...]], axis=0)
     o = jnp.concatenate([o_ref[source, :] for source in sources], axis=0)
-    dwo[...] += contract(o, grad_attn, 0, 0)
-    grads = contract(grad_attn, wo_ref[...], 1, 1).astype(jnp.bfloat16)
+    grads = jnp.concatenate([do_ref[source, :] for source in sources], axis=0)
     products = (grads.astype(jnp.float32) * o.astype(jnp.float32)).T
     grads = contract(grads, pad_ref[: GROUP * HEAD_SIZE, : GROUP * LANES], 1, 0).astype(jnp.bfloat16)
     deltas = []
@@ -610,32 +614,36 @@
         deltas.append(jnp.sum(products[features, :], axis=0, keepdims=True))
     delta = jnp.concatenate(deltas, axis=1)
     lse = lse_ref[pl.ds(index, 1), :]
-    queries, grads = qs[...], gs[...]
     key_at = lax.broadcasted_iota(jnp.int32, (tile, width), 0)
     query_at = lax.rem(lax.broadcasted_iota(jnp.int32, (tile, width), 1), tile)
     diagonal = key_at <= query_at
 
-    def piece(step, masked):
-        at = pl.ds(pl.multiple_of(step * tile, tile), tile)
-        scores = contract(qkv_ref[at, first_key:first_value], queries, 1, 1) * score_scale
-        probs = jnp.exp(scores - lse)
-        if masked:
-            probs = jnp.where(diagonal, probs, 0.0)
-        probs = probs.astype(jnp.bfloat16)
-        dv[at, :] += contract(probs, grads, 1, 0)
-        grad_probs = contract(qkv_ref[at, first_value:], grads, 1, 1)
-        grad_scores = (probs.astype(jnp.float32) * (grad_probs - delta) * score_scale).astype(
-            jnp.bfloat16
-        )
-        dk[at, :] += contract(grad_scores, queries, 1, 0)
-        return contract(kt[:, at], grad_scores, 1, 0)
-
-    dq = piece(index, True)
-    dq = lax.fori_loop(0, index, lambda step, total: total + piece(step, False), dq)
-    dq = dq.T
+    def pieces(steps, masked=False):
+        queries, grads = qs[...], gs[...]
+        places = [pl.ds(pl.multiple_of(step * tile, tile), tile) for step in steps]
+        scores = [contract(qkv_ref[at, first_key:first_value], queries, 1, 1) for at in places]
+        grad_probs = [contract(qkv_ref[at, first_value:], grads, 1, 1) for at in places]
+        total = None
+        for at, score, grad_prob in zip(places, scores, grad_probs):
+            probs = jnp.exp2(score * binary_scale - lse)
+            if masked:
+                probs = jnp.where(diagonal, probs, 0.0)
+            dv[at, :] += contract(probs.astype(jnp.bfloat16), grads, 1, 0)
+            grad_scores = (probs * (grad_prob - delta)).astype(jnp.bfloat16)
+            dk[at, :] += contract(grad_scores, queries, 1, 0)
+            part = contract(kt[:, at], grad_scores, 1, 0)
+            total = part if total is None else total + part
+        return total
+
+    dq = pieces((index,), True)
+    dq = lax.fori_loop(
+        0, lax.div(index, 2), lambda pair, total: total + pieces((2 * pair, 2 * pair + 1)), dq
+    )
+    dq = lax.fori_loop(0, lax.rem(index, 2), lambda _, total: total + pieces((index - 1,)), dq)
+    dq = dq.T * score_scale
     cosine, sine = tables(inner_ref, outer_ref, index, 2)
     parts = [turn(dq[head * tile : (head + 1) * tile, :], cosine, -sine) for head in range(GROUP)]
-    parts.append(turn(dk[here, :], cosine, -sine))
+    parts.append(turn(dk[here, :] * score_scale, cosine, -sine))
     parts.append(dv[here, :])
     dqkv = jnp.concatenate([part.astype(jnp.bfloat16) for part in parts], axis=1)
     dw[...] += contract(dqkv, gained_ref[...], 0, 0)
@@ -646,26 +654,23 @@
     @pl.when(step_at == tiles - 1)
     def _():
         packed = contract(pad_ref[...], dw[...].astype(jnp.bfloat16), 1, 0)
-        dw_ref[...] = packed.astype(jnp.bfloat16).T
-        pieces, _, across = dwo_ref.shape
-        for piece in range(pieces):
-            rows_at = slice(piece * HALF, (piece + 1) * HALF)
-            for number in range(dwo.shape[1] // across):
-                columns = slice(number * across, (number + 1) * across)
-                dwo_ref[piece, number * HALF : (number + 1) * HALF, :] = dwo[
-                    rows_at, columns
-                ].astype(jnp.bfloat16)
-
-
-def attend_back(slots, grad_attn, gained, qkv, o, lse, w, wo, pad, inner, outer):
+        packed = packed.astype(jnp.bfloat16).T
+        line, _ = dwo_ref.shape[:2]
+        shard = packed.shape[0] // line
+        for slot in range(line):
+            grads_ref[slot, :shard, :] = packed[slot * shard : (slot + 1) * shard, :]
+            grads_ref[slot, shard:, :] = dwo_ref[slot]
+
+
+def attend_back(slots, gained, qkv, o, do, lse, w, dwo, pad, inner, outer):
     rows, model = gained.shape
     block = rows // slots.shape[0]
     tile = 2 * block
     width = GROUP * tile
     tiles = rows // tile
     columns = pad.shape[1]
-    across = w.shape[1]
-    wo_pieces = (2 * GROUP, HALF * model // across, across)
+    line, dealt, across = dwo.shape
+    grads = (line, model // line + dealt, across)
     whole = lambda *shape: pl.BlockSpec(shape, lambda i, s: (0,) * len(shape))
     return pl.pallas_call(
         backward_kernel,
@@ -673,19 +678,18 @@
             num_scalar_prefetch=1,
             grid=(tiles,),
             in_specs=[
-                pl.BlockSpec((block, model), lambda i, s: (s[2 * (tiles - 1 - i)], 0)),
-                pl.BlockSpec((block, model), lambda i, s: (s[2 * (tiles - 1 - i) + 1], 0)),
                 pl.BlockSpec((tile, model), lambda i, s: (tiles - 1 - i, 0)),
                 whole(*qkv.shape),
                 whole(*o.shape),
+                whole(*do.shape),
                 whole(*lse.shape),
                 whole(*w.shape),
-                whole(*wo.shape),
+                whole(*dwo.shape),
                 whole(*pad.shape),
                 whole(*inner.shape),
                 whole(*outer.shape),
             ],
-            out_specs=(whole(rows, model), whole(*w.shape), whole(*wo_pieces)),
+            out_specs=(whole(rows, model), whole(*grads)),
             scratch_shapes=[
                 pltpu.VMEM((model, columns), jnp.bfloat16),
                 pltpu.VMEM((width, LANES), jnp.bfloat16),
@@ -694,24 +698,23 @@
                 pltpu.VMEM((rows, LANES), jnp.float32),
                 pltpu.VMEM((rows, LANES), jnp.float32),
                 pltpu.VMEM((columns, model), jnp.float32),
-                pltpu.VMEM(wo.shape, jnp.float32),
             ],
         ),
         out_shape=(
             jax.ShapeDtypeStruct((rows, model), jnp.bfloat16),
-            jax.ShapeDtypeStruct(w.shape, jnp.bfloat16),
-            jax.ShapeDtypeStruct(wo_pieces, jnp.bfloat16),
+            jax.ShapeDtypeStruct(grads, jnp.bfloat16),
         ),
-        compiler_params=pltpu.CompilerParams(vmem_limit_bytes=56 << 20),
+        compiler_params=pltpu.CompilerParams(vmem_limit_bytes=44 << 20),
         cost_estimate=pl.CostEstimate(
-            flops=10 * GROUP * rows * rows * LANES // 2 + 8 * rows * model * columns,
+            flops=10 * GROUP * rows * rows * LANES // 2 + 4 * rows * model * columns,
             bytes_accessed=8 * rows * model,
             transcendentals=GROUP * rows * rows // 2,
         ),
         name="attend_back",
-    )(slots, grad_attn, grad_attn, gained, qkv, o, lse, w, wo, pad, inner, outer)
+    )(slots, gained, qkv, o, do, lse, w, dwo, pad, inner, outer)
+
+
 MESH_IDS = pl.DeviceIdType.MESH
-ACROSS = (1, 2, 4, 6)
 
 
 def start_barrier(me, line_index=None, line=1):
@@ -851,8 +854,9 @@
 
 
 class LineGather:
-    def __init__(self, copies, index, line, place):
-        self.copies, self.index, self.line, self.place = copies, index, line, place
+    def __init__(self, copies, index, line, own, place):
+        self.copies, self.index, self.line = copies, index, line
+        self.own, self.place = own, place
         self.first = copies.next
         copies.next += 2 * (line - 1)
 
@@ -869,7 +873,8 @@
         @pl.when(leaves)
         def _():
             place = self.place(jnp.clip(slot, 0, line - 1))
-            act(self.copies.make(number, place, place, {"fsdp": jnp.clip(there, 0, line - 1)}))
+            source = self.own if step == 0 else place
+            act(self.copies.make(number, source, place, {"fsdp": jnp.clip(there, 0, line - 1)}))
 
     def hear(self, step, upward):
         index, line = self.index, self.line
@@ -912,141 +917,239 @@
     return copies
 
 
-def remote_params(number):
+def remote_params(number, mebibytes=48):
     return pltpu.CompilerParams(
-        collective_id=number, has_side_effects=True, vmem_limit_bytes=48 << 20
-    )
-
-
-def first_kernel(line, x_ref, qkv_ref, wo_ref, gain_ref, xo_ref, qkvo_ref, woo_ref, gaino_ref, send, recv, here):
+        collective_id=number, has_side_effects=True, vmem_limit_bytes=mebibytes << 20
+    )
+
+
+def first_kernel(
+    line,
+    x_ref,
+    qkv_ref,
+    wo_ref,
+    gain_ref,
+    gate_ref,
+    up_ref,
+    down_ref,
+    xo_ref,
+    qkvo_ref,
+    woo_ref,
+    gaino_ref,
+    feedo_ref,
+    feed,
+    send,
+    recv,
+    here,
+):
     me, index = lax.axis_index("ctx"), lax.axis_index("fsdp")
+    plane = lax.axis_size("ctx")
     rows = x_ref.shape[0]
-    start_barrier(me, index, line)
     part = row_part(xo_ref, rows)
+    wo_rows = woo_ref.shape[1]
+    wo_own = wo_ref.at[pl.ds(pl.multiple_of(me * wo_rows, wo_rows), wo_rows), :]
     local = local_copies(
         [
             (qkv_ref, qkvo_ref.at[index]),
-            (wo_ref, woo_ref.at[index]),
+            (wo_own, woo_ref.at[index]),
             (gain_ref, gaino_ref.at[index]),
             (x_ref, part(me, slice(None))),
         ],
         here,
     )
+    start_barrier(me, index, line)
     copies = Copies(send, recv)
     gather = PlaneGather(copies, me, row_half(x_ref, rows), part)
     lines = [
-        LineGather(copies, index, line, lambda slot, ref=ref: ref.at[slot])
-        for ref in (qkvo_ref, gaino_ref, woo_ref)
+        LineGather(copies, index, line, own, lambda slot, ref=ref: ref.at[slot])
+        for own, ref in ((qkv_ref, qkvo_ref), (gain_ref, gaino_ref), (wo_own, woo_ref))
     ]
     gather.begin()
-    for copy in local[:3]:
-        copy.wait()
     for each in lines:
         each.begin()
+    width = feed.shape[1] // 3
+    unit = width // line
+    pairs = []
+    for side, ref in enumerate((gate_ref, up_ref)):
+        for z in range(line):
+            source = pl.ds(pl.multiple_of((z * plane + me) * unit, unit), unit)
+            target = pl.ds(side * width + z * unit, unit)
+            pairs.append((ref.at[:, source], feed.at[:, target]))
+    for number in range(feed.shape[0] // unit):
+        pairs.append(
+            (
+                down_ref.at[
+                    pl.ds(pl.multiple_of(me * unit, unit), unit), pl.ds(number * width, width)
+                ],
+                feed.at[pl.ds(number * unit, unit), pl.ds(2 * width, width)],
+            )
+        )
+    packed = local_copies(pairs, here.at[pl.ds(4, len(pairs))])
     gather.first_hop()
     for step in range(1, line):
         for each in lines:
             each.hop(step)
         if step == 1:
             gather.second_hop()
+            for copy in packed:
+                copy.wait()
+            packed = local_copies([(feed, feedo_ref)], here.at[pl.ds(4 + len(pairs), 1)])
     gather.third_hop()
     gather.last()
     for each in lines:
         each.finish()
     copies.finish()
-    local[3].wait()
-
-
-def first_exchange(line, x, qkv, wo, gains):
+    for copy in local:
+        copy.wait()
+    packed[0].wait()
+
+
+def first_exchange(line, x, qkv, wo, gains, gate, up, down):
     plane = lax.axis_size("ctx")
     count = GATHER_COPIES + 6 * (line - 1)
+    model = x.shape[1]
+    shard = model // line
+    width = gate.shape[1] // plane
+    own_rows = wo.shape[0] // plane
+    feed = (shard, 3 * width)
+    packing = 2 * line + shard * line // width + 1
     return pl.pallas_call(
         functools.partial(first_kernel, line),
         out_shape=(
-            jax.ShapeDtypeStruct((plane * x.shape[0], x.shape[1]), x.dtype),
-            *(jax.ShapeDtypeStruct((line, *a.shape), a.dtype) for a in (qkv, wo, gains)),
+            jax.ShapeDtypeStruct((plane * x.shape[0], model), x.dtype),
+            jax.ShapeDtypeStruct((line, *qkv.shape), qkv.dtype),
+            jax.ShapeDtypeStruct((line, own_rows, model), wo.dtype),
+            jax.ShapeDtypeStruct((line, *gains.shape), gains.dtype),
+            jax.ShapeDtypeStruct(feed, gate.dtype),
         ),
-        in_specs=anywhere(4),
-        out_specs=tuple(anywhere(4)),
+        in_specs=anywhere(7),
+        out_specs=tuple(anywhere(5)),
         scratch_shapes=[
+            pltpu.VMEM(feed, gate.dtype),
+            pltpu.SemaphoreType.DMA((count,)),
+            pltpu.SemaphoreType.DMA((count,)),
+            pltpu.SemaphoreType.DMA((4 + packing,)),
+        ],
+        compiler_params=remote_params(1),
+        name="first_exchange",
+    )(x, qkv, wo, gains, gate, up, down)
+
+
+def second_kernel(
+    line,
+    o_ref,
+    wo_ref,
+    dy_ref,
+    x_ref,
+    gain_ref,
+    dyo_ref,
+    own_ref,
+    residual_ref,
+    normed_ref,
+    scale_ref,
+    gained_ref,
+    att,
+    wo,
+    send,
+    recv,
+    here,
+):
+    me = lax.axis_index("ctx")
+    rows = dy_ref.shape[0]
+    local = local_copies(
+        [
+            (o_ref.at[pl.ds(pl.multiple_of(me * rows, rows), rows), :], att.at[me]),
+            (wo_ref, wo.at[:, me]),
+            (dy_ref, row_part(dyo_ref, rows)(me, slice(None))),
+        ],
+        here.at[pl.ds(0, 3)],
+    )
+    start_barrier(me)
+    copies = Copies(send, recv)
+
+    def block(slot):
+        return o_ref.at[pl.ds(pl.multiple_of(slot * rows, rows), rows), :]
+
+    numbers = {}
+    for bit in (6, 7, 4, 5, 2, 3, 1):
+        numbers[bit] = copies.number()
+        copies.send(numbers[bit], block(me ^ bit), att.at[me], {"ctx": me ^ bit})
+    middle = line // 2
+
+    def wo_half(side):
+        return wo_ref.at[pl.ds(side * middle, middle)]
+
+    def wo_part(slot, side):
+        if isinstance(side, slice):
+            return wo.at[:, slot]
+        return wo.at[pl.ds(side * middle, middle), slot]
+
+    wo_gather = PlaneGather(copies, me, wo_half, wo_part)
+    dy_gather = PlaneGather(copies, me, row_half(dy_ref, rows), row_part(dyo_ref, rows))
+    wo_gather.begin()
+    wo_gather.first_hop()
+    wo_gather.second_hop()
+    dy_gather.begin()
+    wo_gather.third_hop()
+    wo_gather.last()
+    for bit, number in numbers.items():
+        copies.arrived(number, att.at[me ^ bit])
+    local[0].wait()
+    local[1].wait()
+    per_head = 2 * GROUP
+    own = wo.at[lax.div(me, 2), pl.ds(per_head * lax.rem(me, 2), per_head)]
+    keep = local_copies([(own, own_ref)], here.at[pl.ds(3, 1)])
+    plane = att.shape[0]
+    total = x_ref[...].astype(jnp.float32)
+    for slot in range(plane):
+        first = per_head * (slot % 2)
+        weight = jnp.concatenate(
+            [wo[slot // 2, first + piece] for piece in range(per_head)], axis=0
+        )
+        total = total + contract(att[slot], weight, 1, 0)
+    residual_ref[...] = total
+    scale = lax.rsqrt(jnp.mean(total * total, axis=-1, keepdims=True) + norm_epsilon)
+    normed = total * scale
+    scale_ref[...] = scale
+    normed_ref[...] = normed
+    gained_ref[...] = (normed * gain_ref[...]).astype(jnp.bfloat16)
+    dy_gather.first_hop()
+    dy_gather.second_hop()
+    dy_gather.third_hop()
+    dy_gather.last()
+    local[2].wait()
+    keep[0].wait()
+    copies.finish()
+
+
+def second_exchange(o, wo, dy, x, gain):
+    plane = lax.axis_size("ctx")
+    rows = dy.shape[0]
+    line, part, model = wo.shape
+    count = 2 * GATHER_COPIES + 7
+    f32 = jnp.float32
+    return pl.pallas_call(
+        functools.partial(second_kernel, line),
+        out_shape=(
+            jax.ShapeDtypeStruct((plane * rows, model), dy.dtype),
+            jax.ShapeDtypeStruct((2 * GROUP, part, model), wo.dtype),
+            jax.ShapeDtypeStruct((rows, model), f32),
+            jax.ShapeDtypeStruct((rows, model), f32),
+            jax.ShapeDtypeStruct((rows, 1), f32),
+            jax.ShapeDtypeStruct((rows, model), dy.dtype),
+        ),
+        in_specs=anywhere(3) + in_vmem(2),
+        out_specs=(*anywhere(2), *in_vmem(4)),
+        scratch_shapes=[
+            pltpu.VMEM((plane, rows, o.shape[1]), o.dtype),
+            pltpu.VMEM((line, plane, part, model), wo.dtype),
             pltpu.SemaphoreType.DMA((count,)),
             pltpu.SemaphoreType.DMA((count,)),
             pltpu.SemaphoreType.DMA((4,)),
         ],
-        compiler_params=remote_params(1),
-        name="first_exchange",
-    )(x, qkv, wo, gains)
-
-
-def second_kernel(line, o_ref, wo_ref, dy_ref, att_ref, woo_ref, dyo_ref, send, recv, here):
-    me = lax.axis_index("ctx")
-    rows = dy_ref.shape[0]
-    start_barrier(me)
-    copies = Copies(send, recv)
-
-    def columns(slot):
-        return att_ref.at[slot]
-
-    def block(slot):
-        return o_ref.at[pl.ds(pl.multiple_of(slot * rows, rows), rows), :]
-
-    numbers = {}
-    for bit in (6, 7, 4, 5, 2, 3, 1):
-        numbers[bit] = copies.number()
-        copies.send(numbers[bit], block(me ^ bit), columns(me), {"ctx": me ^ bit})
-    local = local_copies(
-        [
-            (block(me), columns(me)),
-            (wo_ref, woo_ref.at[:, me]),
-            (dy_ref, row_part(dyo_ref, rows)(me, slice(None))),
-        ],
-        here,
-    )
-    middle = line // 2
-
-    def wo_half(side):
-        return wo_ref.at[pl.ds(side * middle, middle)]
-
-    def wo_part(slot, side):
-        if isinstance(side, slice):
-            return woo_ref.at[:, slot]
-        return woo_ref.at[pl.ds(side * middle, middle), slot]
-
-    run_gathers(
-        [
-            PlaneGather(copies, me, wo_half, wo_part),
-            PlaneGather(copies, me, row_half(dy_ref, rows), row_part(dyo_ref, rows)),
-        ]
-    )
-    for bit, number in numbers.items():
-        copies.arrived(number, columns(me ^ bit))
-    for copy in local:
-        copy.wait()
-    copies.finish()
-
-
-def second_exchange(o, wo, dy):
-    plane = lax.axis_size("ctx")
-    rows = dy.shape[0]
-    line, part, model = wo.shape
-    count = 2 * GATHER_COPIES + 7
-    return pl.pallas_call(
-        functools.partial(second_kernel, line),
-        out_shape=(
-            jax.ShapeDtypeStruct((plane, rows, o.shape[1]), o.dtype),
-            jax.ShapeDtypeStruct((line, plane, part, model), wo.dtype),
-            jax.ShapeDtypeStruct((plane * rows, model), dy.dtype),
-        ),
-        in_specs=anywhere(3),
-        out_specs=tuple(anywhere(3)),
-        scratch_shapes=[
-            pltpu.SemaphoreType.DMA((count,)),
-            pltpu.SemaphoreType.DMA((count,)),
-            pltpu.SemaphoreType.DMA((3,)),
-        ],
         compiler_params=remote_params(2),
         name="second_exchange",
-    )(o, wo, dy)
+    )(o, wo, dy, x, gain)
 
 
 def gather_kernel(x_ref, xo_ref, send, recv, here):
@@ -1074,8 +1177,158 @@
             pltpu.SemaphoreType.DMA((1,)),
         ],
         compiler_params=remote_params(number),
-        name=f"plane_gather_{number}",
     )(x)
+
+
+def deal_rows(copies, me, pieces, wo_ref, place, recv_first):
+    to_first = pieces * lax.rem(me, 2)
+    line_slot = lax.div(me, 2)
+
+    def copy(piece):
+        return copies.make(
+            recv_first + piece,
+            wo_ref.at[piece],
+            place(line_slot),
+            {"ctx": to_first + piece},
+            recv_first + line_slot,
+        )
+
+    for piece in range(pieces):
+
+        @pl.when(to_first + piece != me)
+        def _(piece=piece):
+            copy(piece).start()
+
+        @pl.when(to_first + piece == me)
+        def _(piece=piece):
+            place(line_slot)[...] = wo_ref[piece]
+
+    def finish(line):
+        for slot in range(line):
+
+            @pl.when(2 * slot + lax.div(me, pieces) != me)
+            def _(slot=slot):
+                copies.make(
+                    recv_first, wo_ref.at[0], place(slot), {"ctx": 0}, recv_first + slot
+                ).wait_recv()
+
+        for piece in range(pieces):
+
+            @pl.when(to_first + piece != me)
+            def _(piece=piece):
+                copy(piece).wait_send()
+
+    return finish
+
+
+def third_kernel(
+    sum_ref,
+    normed_ref,
+    scale_ref,
+    gain_ref,
+    dy_ref,
+    o_ref,
+    wo_ref,
+    residual_ref,
+    term_ref,
+    do_ref,
+    dwo_ref,
+    own,
+    all_grads,
+    dwo,
+    pieces_ref,
+    send,
+    recv,
+):
+    me = lax.axis_index("ctx")
+    rows = dy_ref.shape[0]
+    start_barrier(me)
+    copies = Copies(send, recv)
+    part = row_part(all_grads, rows)
+    gather = PlaneGather(copies, me, row_half(own, rows), part)
+    grad_normed, normed = sum_ref[...], normed_ref[...]
+    products = grad_normed * normed
+    scaled = grad_normed * gain_ref[...]
+    mean = jnp.mean(scaled * normed, axis=-1, keepdims=True)
+    residual = dy_ref[...].astype(jnp.float32) + scale_ref[...] * (scaled - normed * mean)
+    own[...] = residual.astype(jnp.bfloat16)
+    gather.begin()
+    residual_ref[...] = residual
+    term_ref[...] = jnp.sum(products, axis=0, keepdims=True)
+    part(me, slice(None))[...] = own[...]
+    dwo[...] = jnp.zeros_like(dwo)
+
+    def step(order, carry):
+        for number, slot, sides, when in (
+            (4, 1, 0, 1),
+            (5, 1, 1, 1),
+            (8, 3, 1, 3),
+            (10, 3, 0, 3),
+            (9, 5, 0, 5),
+            (11, 5, 1, 5),
+            (12, 7, slice(None), 7),
+        ):
+
+            @pl.when(order == when)
+            def _(number=number, slot=slot, sides=sides):
+                copies.arrived(gather.first + number, gather.part(me ^ slot, sides))
+
+        place = pl.ds(pl.multiple_of((me ^ order) * rows, rows), rows)
+        grads = all_grads[place, :]
+        do_ref[place, :] = contract(grads, wo_ref[...], 1, 1).astype(jnp.bfloat16)
+        share = contract(o_ref[place, :], grads, 0, 0)
+        dwo[...] += share
+        return carry
+
+    lax.fori_loop(0, 2, step, 0)
+    gather.first_hop()
+    gather.second_hop()
+    lax.fori_loop(2, 6, step, 0)
+    gather.third_hop()
+    lax.fori_loop(6, 8, step, 0)
+    line, _, across = dwo_ref.shape
+    count = pieces_ref.shape[0]
+    for piece in range(count):
+        rows_at = slice(piece * HALF, (piece + 1) * HALF)
+        for number in range(dwo.shape[1] // across):
+            columns = slice(number * across, (number + 1) * across)
+            pieces_ref[piece, number * HALF : (number + 1) * HALF, :] = dwo[
+                rows_at, columns
+            ].astype(jnp.bfloat16)
+    first = copies.next
+    finish = deal_rows(copies, me, count, pieces_ref, lambda slot: dwo_ref.at[slot], first)
+    finish(line)
+    copies.finish()
+
+
+def third_exchange(line, grad_normed, normed, scale, gain, dy, o, wo, across):
+    plane = lax.axis_size("ctx")
+    rows, model = dy.shape
+    pieces = 2 * GROUP
+    dealt = (HALF * model // across, across)
+    half_type, f32 = jnp.bfloat16, jnp.float32
+    count = GATHER_COPIES + pieces
+    return pl.pallas_call(
+        third_kernel,
+        out_shape=(
+            jax.ShapeDtypeStruct((rows, model), f32),
+            jax.ShapeDtypeStruct((1, model), f32),
+            jax.ShapeDtypeStruct(o.shape, half_type),
+            jax.ShapeDtypeStruct((line, *dealt), half_type),
+        ),
+        in_specs=in_vmem(7),
+        out_specs=tuple(in_vmem(4)),
+        scratch_shapes=[
+            pltpu.VMEM((rows, model), half_type),
+            pltpu.VMEM((plane * rows, model), half_type),
+            pltpu.VMEM(wo.shape, f32),
+            pltpu.VMEM((pieces, *dealt), half_type),
+            pltpu.SemaphoreType.DMA((count,)),
+            pltpu.SemaphoreType.DMA((count,)),
+        ],
+        compiler_params=remote_params(6),
+        name="third_exchange",
+    )(grad_normed, normed, scale, gain, dy, o, wo)
 
 
 REDUCE_COPIES = 10
@@ -1088,6 +1341,7 @@
         self.first = copies.next
         copies.next += REDUCE_COPIES
         self.half = heard.shape[1] // 2
+        self.x, self.y = {"ctx": me ^ 2}, {"ctx": me ^ 4}
 
     def side(self, ref, slot, half):
         return ref.at[slot, pl.ds(half * self.half, self.half), :]
@@ -1108,35 +1362,52 @@
             total = total + extra
         self.held[order, rows, :] = total.astype(self.held.dtype)
 
+    def onward(self, number):
+        order, half, peer = {
+            4: (0, 0, self.x),
+            5: (0, 1, self.y),
+            6: (1, 0, self.x),
+            7: (2, 1, self.y),
+            8: (1, 1, self.x),
+            9: (2, 0, self.y),
+        }[number]
+        held, landed = self.side(self.held, order, half), self.side(self.landed, order, half)
+        return self.copies.make(self.first + number, held, landed, peer)
+
+    def finish(self):
+        for number in range(4, REDUCE_COPIES):
+            self.onward(number).wait_send()
+
+    def diagonal_sends(self):
+        first, half = self.first, self.half
+        self.copies.arrived(first + 0, self.heard.at[0])
+        self.combine(0, pl.ds(0, 2 * half))
+        self.onward(4).start()
+        self.onward(5).start()
+
+    def neighbour_sends(self):
+        first, half = self.first, self.half
+        self.copies.arrived(first + 1, self.heard.at[1])
+        self.combine(1, pl.ds(0, half))
+        self.onward(6).start()
+        self.copies.arrived(first + 2, self.heard.at[2])
+        self.combine(2, pl.ds(half, half))
+        self.onward(7).start()
+
     def first_sends(self):
-        me, copies, first, half = self.me, self.copies, self.first, self.half
+        self.diagonal_sends()
+        self.neighbour_sends()
+
+    def second_sends(self):
+        first, half = self.first, self.half
         upper, lower = pl.ds(0, half), pl.ds(half, half)
-        x, y = {"ctx": me ^ 2}, {"ctx": me ^ 4}
-        held, landed, side = self.held, self.landed, self.side
-        arrived = copies.arrived
-        arrived(first + 0, self.heard.at[0])
-        self.combine(0, pl.ds(0, 2 * half))
-        copies.send(first + 4, side(held, 0, 0), side(landed, 0, 0), x)
-        copies.send(first + 5, side(held, 0, 1), side(landed, 0, 1), y)
-        arrived(first + 1, self.heard.at[1])
-        self.combine(1, upper)
-        copies.send(first + 6, side(held, 1, 0), side(landed, 1, 0), x)
-        arrived(first + 2, self.heard.at[2])
-        self.combine(2, lower)
-        copies.send(first + 7, side(held, 2, 1), side(landed, 2, 1), y)
-
-    def second_sends(self):
-        me, copies, first, half = self.me, self.copies, self.first, self.half
-        upper, lower = pl.ds(0, half), pl.ds(half, half)
-        x, y = {"ctx": me ^ 2}, {"ctx": me ^ 4}
-        held, landed, side = self.held, self.landed, self.side
-        arrived = copies.arrived
+        landed, side, arrived = self.landed, self.side, self.copies.arrived
         arrived(first + 5, side(landed, 0, 1))
         self.combine(1, lower, landed[0, lower, :].astype(jnp.float32))
-        copies.send(first + 8, side(held, 1, 1), side(landed, 1, 1), x)
+        self.onward(8).start()
         arrived(first + 4, side(landed, 0, 0))
         self.combine(2, upper, landed[0, upper, :].astype(jnp.float32))
-        copies.send(first + 9, side(held, 2, 0), side(landed, 2, 0), y)
+        self.onward(9).start()
         arrived(first + 3, self.heard.at[3])
 
     def sum_half(self, which):
@@ -1150,6 +1421,8 @@
             + self.landed[1, rows, :].astype(jnp.float32)
             + self.landed[2, rows, :].astype(jnp.float32)
         )
+
+
 def feed_kernel(
     line,
     g_ref,
@@ -1168,10 +1441,10 @@
     heard,
     held,
     landed,
-    stage,
+    out_mine,
+    out_heard,
     send,
     recv,
-    here,
 ):
     me = lax.axis_index("ctx")
     rows = g_ref.shape[0]
@@ -1245,24 +1518,36 @@
     gather.second_hop()
     reduce.share(3)
     lax.fori_loop(2, 6, step, 0)
-    gather.third_hop()
     reduce.share(1)
     reduce.share(2)
+    gather.third_hop()
+    reduce.neighbour_sends()
     lax.fori_loop(6, 8, step, 0)
     reduce.share(0)
 
-    chunks = dy_ref.shape[0] // rows
+    out_first = copies.next
+    copies.next += 4
+
+    def bit_of(number):
+        return jnp.where(number == 0, 6, jnp.where(number == 3, 0, 2 * number))
+
+    def out_copy(number):
+        return copies.make(out_first + number, out_mine.at[number], out_heard.at[number], partner)
+
+    def out_of(slot):
+        return contract(hid[at(slot), :], down_ref[...], 1, 0)
+
+    partner = {"ctx": me ^ 1}
 
     def give(number, carry):
-        slot = lax.rem(number, 2)
-        copy = pltpu.make_async_copy(stage.at[slot], out_ref.at[at(number), :], here.at[slot])
-
-        @pl.when(number >= 2)
-        def _():
-            copy.wait()
-
-        stage[slot] = contract(hid[at(number), :], down_ref[...], 1, 0).astype(jnp.bfloat16)
-        copy.start()
+        out_mine[number] = out_of(me ^ 1 ^ bit_of(number)).astype(jnp.bfloat16)
+        out_copy(number).start()
+        return carry
+
+    def keep(number, carry):
+        total = out_of(me ^ bit_of(number))
+        out_copy(number).wait_recv()
+        out_ref[number] = (total + out_heard[number].astype(jnp.float32)).astype(jnp.bfloat16)
         return carry
 
     def weights(number, carry):
@@ -1276,16 +1561,18 @@
             dw_ref[columns, side * width : (side + 1) * width] = total.T
         return carry
 
-    lax.fori_loop(0, 2, give, 0)
-    reduce.first_sends()
-    lax.fori_loop(2, chunks, give, 0)
+    lax.fori_loop(0, 1, give, 0)
+    reduce.diagonal_sends()
+    lax.fori_loop(1, 4, give, 0)
     reduce.second_sends()
+    lax.fori_loop(0, 4, keep, 0)
     lax.fori_loop(0, blocks, weights, 0)
     half = rows // 2
     for which in (1, 0):
         sum_ref[pl.ds(which * half, half), :] = reduce.sum_half(which)
-    for slot in (0, 1):
-        pltpu.make_async_copy(stage.at[slot], out_ref.at[at(slot), :], here.at[slot]).wait()
+    for number in range(4):
+        out_copy(number).wait_send()
+    reduce.finish()
     copies.finish()
 
 
@@ -1294,17 +1581,17 @@
     rows, model = g.shape
     tokens = plane * rows
     width = w.shape[1] // 3
-    count = GATHER_COPIES + REDUCE_COPIES
+    count = GATHER_COPIES + REDUCE_COPIES + 4
     half_type = jnp.bfloat16
     return pl.pallas_call(
         functools.partial(feed_kernel, line),
         out_shape=(
             jax.ShapeDtypeStruct((rows, model), jnp.float32),
-            jax.ShapeDtypeStruct((tokens, model), half_type),
+            jax.ShapeDtypeStruct((4, rows, model), half_type),
             jax.ShapeDtypeStruct(w.shape, half_type),
         ),
         in_specs=in_vmem(3),
-        out_specs=(*in_vmem(1), *anywhere(1), *in_vmem(1)),
+        out_specs=tuple(in_vmem(3)),
         scratch_shapes=[
             pltpu.VMEM((width, model), half_type),
             pltpu.VMEM((tokens, model), half_type),
@@ -1316,10 +1603,10 @@
             pltpu.VMEM((4, rows, model), half_type),
             pltpu.VMEM((3, rows, model), half_type),
             pltpu.VMEM((3, rows, model), half_type),
-            pltpu.VMEM((2, rows, model), half_type),
+            pltpu.VMEM((4, rows, model), half_type),
+            pltpu.VMEM((4, rows, model), half_type),
             pltpu.SemaphoreType.DMA((count,)),
             pltpu.SemaphoreType.DMA((count,)),
-            pltpu.SemaphoreType.DMA((2,)),
         ],
         compiler_params=pltpu.CompilerParams(
             collective_id=3, has_side_effects=True, vmem_limit_bytes=60 << 20
@@ -1328,79 +1615,115 @@
     )(g, dy, w)
 
 
-def gradients_kernel(line, shapes, *refs):
-    count = len(shapes)
-    pieces, terms_ref = refs[:count], refs[count]
-    wholes, total_ref = refs[count + 1 : 2 * count + 1], refs[2 * count + 1]
-    heard, plane_sum, across, send, recv, here = refs[2 * count + 2 :]
+def last_kernel(
+    line,
+    dx_ref,
+    residual_ref,
+    x_ref,
+    gain_ref,
+    term_ref,
+    piece_ref,
+    input_ref,
+    whole_ref,
+    total_ref,
+    heard,
+    held,
+    landed,
+    terms,
+    terms_heard,
+    plane_sum,
+    across,
+    send,
+    recv,
+    here,
+):
     me, index = lax.axis_index("ctx"), lax.axis_index("fsdp")
     start_barrier(me, index, line)
     copies = Copies(send, recv)
-    gathers, pairs = [], []
-    for piece, whole in zip(pieces, wholes):
-        rows = piece.shape[0]
-        part = row_part(whole, rows)
-        gathers.append(PlaneGather(copies, me, row_half(piece, rows), part))
-        pairs.append((piece, part(me, slice(None))))
+    rows = residual_ref.shape[0]
+
+    def block(slot):
+        return dx_ref.at[pl.ds(pl.multiple_of(slot * rows, rows), rows), :]
+
+    reduce = PlaneReduce(copies, me, block, heard, held, landed)
+    piece_rows = piece_ref.shape[0]
+    part = row_part(whole_ref, piece_rows)
+    gather = PlaneGather(copies, me, row_half(piece_ref, piece_rows), part)
+    for order in range(4):
+        reduce.share(order)
+    local = local_copies([(piece_ref, part(me, slice(None)))], here)
+    reduce.first_sends()
+    gather.begin()
+    reduce.second_sends()
+    gather.first_hop()
+    gather.second_hop()
+    half = rows // 2
+    gain = gain_ref[...]
+    total = jnp.zeros_like(gain)
+    for which in (1, 0):
+        at = pl.ds(which * half, half)
+        grad = reduce.sum_half(which)
+        x = x_ref[at, :].astype(jnp.float32)
+        scale = lax.rsqrt(jnp.mean(x * x, axis=-1, keepdims=True) + norm_epsilon)
+        normed = x * scale
+        total = total + jnp.sum(grad * normed, axis=0, keepdims=True)
+        scaled = grad * gain
+        mean = jnp.mean(scaled * normed, axis=-1, keepdims=True)
+        input_ref[0, at, :] = residual_ref[at, :] + scale * (scaled - normed * mean)
+    terms[0:1, :] = total
+    terms[1:2, :] = term_ref[...]
     first = copies.next
     copies.next += 7 + line - 1
     for bit in range(1, 8):
-        copies.send(first + bit - 1, terms_ref, heard.at[bit], {"ctx": me ^ bit})
-    for gather in gathers:
-        gather.begin()
-    local = local_copies(pairs, here)
-    total = terms_ref[...]
+        copies.send(first + bit - 1, terms, terms_heard.at[bit], {"ctx": me ^ bit})
+    gather.third_hop()
+    total = terms[...]
     for bit in range(1, 8):
-        copies.arrived(first + bit - 1, heard.at[bit])
-        total = total + heard[bit]
+        copies.arrived(first + bit - 1, terms_heard.at[bit])
+        total = total + terms_heard[bit]
     plane_sum[...] = total
     for step in range(1, line):
         peer = {"fsdp": lax.rem(index + step, line)}
         copies.send(first + 6 + step, plane_sum, across.at[step], peer)
-    for gather in gathers:
-        gather.first_hop()
-    for gather in gathers:
-        gather.second_hop()
     for step in range(1, line):
         copies.arrived(first + 6 + step, across.at[step])
         total = total + across[step]
     total_ref[...] = total
-    for gather in gathers:
-        gather.third_hop()
-    for gather in gathers:
-        gather.last()
-    for copy in local:
-        copy.wait()
+    gather.last()
+    local[0].wait()
+    reduce.finish()
     copies.finish()
 
 
-def gather_gradients(pieces, terms, number):
-    plane, line = lax.axis_size("ctx"), lax.axis_size("fsdp")
-    count = len(pieces)
-    copies = GATHER_COPIES * count + 7 + line - 1
-    shapes = tuple(piece.shape for piece in pieces)
+def last_exchange(line, dx, residual, x, gain, term, piece):
+    plane = lax.axis_size("ctx")
+    rows, model = x.shape
+    f32 = jnp.float32
+    copies = GATHER_COPIES + REDUCE_COPIES + 7 + line - 1
     return pl.pallas_call(
-        functools.partial(gradients_kernel, line, shapes),
+        functools.partial(last_kernel, line),
         out_shape=(
-            *(
-                jax.ShapeDtypeStruct((plane * piece.shape[0], piece.shape[1]), piece.dtype)
-                for piece in pieces
-            ),
-            jax.ShapeDtypeStruct(terms.shape, terms.dtype),
+            jax.ShapeDtypeStruct((1, rows, model), f32),
+            jax.ShapeDtypeStruct((plane * piece.shape[0], piece.shape[1]), piece.dtype),
+            jax.ShapeDtypeStruct((2, model), f32),
         ),
-        in_specs=anywhere(count) + in_vmem(1),
-        out_specs=(*anywhere(count), *in_vmem(1)),
+        in_specs=in_vmem(5) + anywhere(1),
+        out_specs=(*in_vmem(1), *anywhere(1), *in_vmem(1)),
         scratch_shapes=[
-            pltpu.VMEM((plane, *terms.shape), terms.dtype),
-            pltpu.VMEM(terms.shape, terms.dtype),
-            pltpu.VMEM((line, *terms.shape), terms.dtype),
+            pltpu.VMEM((4, rows, model), dx.dtype),
+            pltpu.VMEM((3, rows, model), dx.dtype),
+            pltpu.VMEM((3, rows, model), dx.dtype),
+            pltpu.VMEM((2, model), f32),
+            pltpu.VMEM((plane, 2, model), f32),
+            pltpu.VMEM((2, model), f32),
+            pltpu.VMEM((line, 2, model), f32),
             pltpu.SemaphoreType.DMA((copies,)),
             pltpu.SemaphoreType.DMA((copies,)),
-            pltpu.SemaphoreType.DMA((count,)),
+            pltpu.SemaphoreType.DMA((1,)),
         ],
-        compiler_params=remote_params(number),
-        name=f"gather_gradients_{number}",
-    )(*pieces, terms)
+        compiler_params=remote_params(7),
+        name="last_exchange",
+    )(dx, residual, x, gain, term, piece)
 
 
 def spread_kernel(gate_in, up_in, down_in, gate_ref, up_ref, down_ref):
@@ -1408,7 +1731,6 @@
     for source, target in ((gate_in, gate_ref), (up_in, up_ref)):
         for slot in range(plane):
             target[:, slot * unit : (slot + 1) * unit] = source[slot].astype(jnp.float32)
-    step = pl.program_id(0)
     width = down_in.shape[2]
     blocks = shard // unit
     for slot in range(down_in.shape[0]):
@@ -1442,7 +1764,7 @@
             jax.ShapeDtypeStruct((shard, plane * width), jnp.float32),
             jax.ShapeDtypeStruct((plane * unit, model), jnp.float32),
         ),
-        compiler_params=pltpu.CompilerParams(vmem_limit_bytes=40 << 20),
+        compiler_params=pltpu.CompilerParams(vmem_limit_bytes=62 << 20),
         name="spread_feed",
     )(pieces, pieces, pieces)
 
@@ -1489,114 +1811,6 @@
     )(pieces)
 
 
-def last_sums_kernel(
-    dx_ref, out_ref, dqkv_ref, wo_ref, dx_sum, out_sum, grads_ref, heard, held, landed, send, recv, here
-):
-    me = lax.axis_index("ctx")
-    rows = dx_sum.shape[0]
-    start_barrier(me)
-    copies = Copies(send, recv)
-
-    def at(slot):
-        return pl.ds(pl.multiple_of(slot * rows, rows), rows)
-
-    pieces, wo_rows = wo_ref.shape[:2]
-    line, grad_rows = grads_ref.shape[:2]
-    shard = grad_rows - wo_rows
-    to_first = pieces * lax.rem(me, 2)
-    line_slot = lax.div(me, 2)
-    wo_first = copies.next
-    copies.next += pieces
-
-    def wo_place(slot):
-        return grads_ref.at[slot, pl.ds(shard, wo_rows), :]
-
-    def wo_copy(piece):
-        return copies.make(
-            wo_first + piece,
-            wo_ref.at[piece],
-            wo_place(line_slot),
-            {"ctx": to_first + piece},
-            wo_first + line_slot,
-        )
-
-    for piece in range(pieces):
-
-        @pl.when(to_first + piece != me)
-        def _(piece=piece):
-            wo_copy(piece).start()
-
-        @pl.when(to_first + piece == me)
-        def _(piece=piece):
-            wo_place(line_slot)[...] = wo_ref[piece]
-
-    reduces = []
-    for number, ref in enumerate((dx_ref, out_ref)):
-        reduces.append(
-            PlaneReduce(
-                copies,
-                me,
-                lambda slot, ref=ref: ref.at[at(slot), :],
-                heard.at[number],
-                held.at[number],
-                landed.at[number],
-            )
-        )
-    for reduce in reduces:
-        for order in range(4):
-            reduce.share(order)
-    for slot in range(line):
-        grads_ref[slot, :shard, :] = dqkv_ref[slot * shard : (slot + 1) * shard, :]
-    for reduce in reduces:
-        reduce.first_sends()
-    for reduce in reduces:
-        reduce.second_sends()
-    half = rows // 2
-    for which in (1, 0):
-        for reduce, target in zip(reduces, (dx_sum, out_sum)):
-            target[pl.ds(which * half, half), :] = reduce.sum_half(which)
-    for slot in range(line):
-
-        @pl.when(2 * slot + lax.div(me, pieces) != me)
-        def _(slot=slot):
-            copies.make(
-                wo_first, wo_ref.at[0], wo_place(slot), {"ctx": 0}, wo_first + slot
-            ).wait_recv()
-
-    for piece in range(pieces):
-
-        @pl.when(to_first + piece != me)
-        def _(piece=piece):
-            wo_copy(piece).wait_send()
-
-    copies.finish()
-
-
-def last_sums(dx, out, dqkv, wo, line):
-    plane = lax.axis_size("ctx")
-    rows, model = dx.shape[0] // plane, dx.shape[1]
-    count = 2 * REDUCE_COPIES + wo.shape[0]
-    across = dqkv.shape[1]
-    return pl.pallas_call(
-        last_sums_kernel,
-        out_shape=(
-            jax.ShapeDtypeStruct((rows, model), jnp.float32),
-            jax.ShapeDtypeStruct((rows, model), jnp.float32),
-            jax.ShapeDtypeStruct((line, dqkv.shape[0] // line + wo.shape[1], across), dqkv.dtype),
-        ),
-        in_specs=in_vmem(4),
-        out_specs=tuple(in_vmem(3)),
-        scratch_shapes=[
-            pltpu.VMEM((2, 4, rows, model), dx.dtype),
-            pltpu.VMEM((2, 3, rows, model), dx.dtype),
-            pltpu.VMEM((2, 3, rows, model), dx.dtype),
-            pltpu.SemaphoreType.DMA((count,)),
-            pltpu.SemaphoreType.DMA((count,)),
-            pltpu.SemaphoreType.DMA((1,)),
-        ],
-        compiler_params=remote_params(7),
-        name="last_sums",
-    )(dx, out, dqkv, wo)
 def head_local(
     block_input,
     block_table,
@@ -1637,24 +1851,17 @@
         ],
         axis=1,
     )
-    wo_mine = lax.dynamic_slice_in_dim(output_weight, me * HALF, HALF, 0)
     gains_mine = jnp.stack([attention_gain, feedforward_gain])
-    x_all, qkv_w, wo_line, gains = first_exchange(
-        line, block_input[0], qkv_mine, wo_mine, gains_mine
-    )
-
-    feed_width = line * unit
-    blocks = [
-        lax.dynamic_slice_in_dim(array, (z * plane + me) * unit, unit, 1)
-        for array in (gate_weight, up_weight)
-        for z in range(line)
-    ]
-    down_mine = lax.dynamic_slice_in_dim(down_weight, me * unit, unit, 0)
-    down_mine = jnp.concatenate(
-        [down_mine[:, at : at + feed_width] for at in range(0, model, feed_width)], axis=0
-    )
-    feed_mine = jnp.concatenate([*blocks, down_mine], axis=1)
-    feed_mine, x_all = lax.optimization_barrier((feed_mine, x_all))
+    x_all, qkv_w, wo_line, gains, feed_mine = first_exchange(
+        line,
+        block_input[0],
+        qkv_mine,
+        output_weight,
+        gains_mine,
+        gate_weight,
+        up_weight,
+        down_weight,
+    )
     feed_w = lax.all_gather(feed_mine, "fsdp", axis=0, tiled=True)
 
     steps_index = jnp.arange(HALF, dtype=jnp.float32)
@@ -1674,30 +1881,33 @@
     qkv_w = qkv_w.reshape(model, -1)
     gained_one, qkv, o, lse = attend(slots, x_all, gains[:1], qkv_w, pad, inner, outer)
 
-    attended, wo_full, grad_all = second_exchange(o, wo_line, output_grad[0])
-    attended = jnp.transpose(attended, (1, 0, 2)).reshape(rows, -1)
-    wo_full = wo_full.reshape(-1, model)
-    inputs = block_input[0].astype(jnp.float32)
-    residual = inputs + product(attended, wo_full)
-    scale_two = norm_scale(residual)
-    normed_two = residual * scale_two
-    grad_normed_two, out_parts, feed_grads = feed(
-        (normed_two * gains[1]).astype(jnp.bfloat16), grad_all, feed_w
-    )
+    grad_all, wo_mine, residual, normed_two, scale_two, gained_two = second_exchange(
+        o, wo_line, output_grad[0], block_input[0], gains[1:]
+    )
+    wo_mine = wo_mine.reshape(-1, model)
+    grad_normed_two, out_parts, feed_grads = feed(gained_two, grad_all, feed_w)
     feed_grads = lax.psum_scatter(feed_grads, "fsdp", scatter_dimension=0, tiled=True)
-    feedforward_term = jnp.sum(grad_normed_two * normed_two, axis=0)
-    grad_scaled_two = grad_normed_two * gains[1]
-    grad_residual = output_grad[0].astype(jnp.float32) + scale_two * (
-        grad_scaled_two
-        - normed_two * jnp.mean(grad_scaled_two * normed_two, axis=-1, keepdims=True)
-    )
-    grad_attn = plane_gather(grad_residual.astype(jnp.bfloat16), 6)
-    own = GROUP * HEAD_SIZE
-    wo_mine = lax.dynamic_slice_in_dim(wo_full, me * own, own, 0)
-    dx, qkv_term, wo_term = attend_back(
-        slots, grad_attn, gained_one, qkv, o, lse, qkv_w, wo_mine, pad, inner, outer
-    )
-    grad_normed_one, out_sum, attention_grads = last_sums(dx, out_parts, qkv_term, wo_term, line)
+    grad_residual, feedforward_term, grad_o, wo_term = third_exchange(
+        line,
+        grad_normed_two,
+        normed_two,
+        scale_two,
+        gains[1:],
+        output_grad[0],
+        o,
+        wo_mine,
+        qkv_w.shape[1],
+    )
+    out_parts, grad_o = lax.optimization_barrier((out_parts, grad_o))
+    out_sum = out_parts[3].astype(jnp.float32)
+    for part, bit in enumerate((6, 2, 4)):
+        pairs = [(device, device ^ bit) for device in range(plane)]
+        heard = lax.ppermute(out_parts[part], "ctx", pairs)
+        out_sum = out_sum + heard.astype(jnp.float32)
+    dx, attention_grads = attend_back(
+        slots, gained_one, qkv, o, grad_o, lse, qkv_w, wo_term, pad, inner, outer
+    )
+    attention_grads, feed_grads = lax.optimization_barrier((attention_grads, feed_grads))
     attention_grads = lax.psum_scatter(
         attention_grads.reshape(-1, attention_grads.shape[2]),
         "fsdp",
@@ -1705,16 +1915,9 @@
         tiled=True,
     )
     layer_output = (residual + out_sum).astype(jnp.bfloat16)
-    scale_one = norm_scale(inputs)
-    normed_one = inputs * scale_one
-    attention_term = jnp.sum(grad_normed_one * normed_one, axis=0)
-    grad_scaled_one = grad_normed_one * gains[0]
-    input_grad = grad_residual + scale_one * (
-        grad_scaled_one
-        - normed_one * jnp.mean(grad_scaled_one * normed_one, axis=-1, keepdims=True)
-    )
-    feed_pieces, gain_terms = gather_gradients(
-        [feed_grads], jnp.stack([attention_term, feedforward_term]), 8
+    dx, layer_output = lax.optimization_barrier((dx, layer_output))
+    input_grad, feed_pieces, gain_terms = last_exchange(
+        line, dx, grad_residual, block_input[0], gains[:1], feedforward_term, feed_grads
     )
     gate_grad, up_grad, down_grad = spread_feed(feed_pieces, shard, line, unit)
     attention_pieces = plane_gather(attention_grads, 9)
@@ -1724,7 +1927,7 @@
     gain_terms = lax.dynamic_slice_in_dim(gain_terms, lax.axis_index("fsdp") * shard, shard, 1)
     return (
         layer_output[None],
-        input_grad[None],
+        input_grad,
         gain_terms[0],
         query_grad,
         key_grad,
@@ -1740,7 +1943,12 @@
 def solution(mesh):
     plane, line = mesh.shape["ctx"], mesh.shape["fsdp"]
     fits = plane == KEY_VALUE_HEADS == 8 and plane * line * HALF == QUERY_HEADS * HEAD_SIZE
-    plan = head_local if fits else local
+    if fits:
+        return placed(mesh, head_local)
+    return placed(mesh, local)
+
+
+def placed(mesh, plan):
     return jax.shard_map(
         plan,
         mesh=mesh,

time: 588 us -> 474 us (0.81)
  waiting for transfers between devices: 94.2 us -> 40.1 us
  Pallas kernels: 431 us -> 392 us
  local copies, waits for them, and re-layouts: 34.3 us -> 19.9 us
    reduce_scatter x1, waiting for transfers between devices: 62.3 us -> 6.23 us  [head_local(): lax.psum_scatter(feed_grads, 'fsdp', scatter_dimension=0, tiled=True)]
    ppermute x0 -> x3, waiting for transfers between devices: none -> 33.9 us  [head_local(): heard = lax.ppermute(out_parts[part], 'ctx', pairs)]
    pallas_call x2 -> x1, Pallas kernels: 51.7 us -> 19.4 us  [plane_gather(): pl.pallas_call(gather_kernel, out_shape=jax.ShapeDtypeStruct((plane * x.s...]
    reduce_scatter x1, waiting for transfers between devices: 31.4 us -> 0.01 us  [head_local(): lax.psum_scatter(attention_grads.reshape(-1, attention_grads.shape[2]), '...]
    pallas_call x1, Pallas kernels: 50.6 us -> 34.7 us  [attend_back(): pl.pallas_call(backward_kernel, grid_spec=pltpu.PrefetchScalarGridSpec(nu...]
    unnamed x64 -> x49, local copies, waits for them, and re-layouts: 24 us -> 13.3 us
    pallas_call x2, Pallas kernels: 114 us -> 121 us  [the longest x1 79.3 us: last_exchange(): pl.pallas_call(functools.partial(last_kernel, line), out_shape=(jax.Shape...]
  transfers between devices with their start and end apart: 3 -> 6, of which waited for: 2 -> 3; matrix products, arithmetic and copies ran while one was open for 3% -> 2% of each run, Pallas kernels for 20% -> 54%
where the time goes in v3:
time: 474 us
  Pallas kernels  392 us (83%)
  waiting for transfers between devices  40.1 us (8%)
  local copies, waits for them, and re-layouts  19.9 us (4%)
  between operations  14.1 us (3%)
    pallas_call x1, Pallas kernels, last_exchange(): pl.pallas_call(functools.partial(last_kernel, line), out_shape=(jax.Shape...  79.3 us
    pallas_call x1, Pallas kernels, feed(): pl.pallas_call(functools.partial(feed_kernel, line), out_shape=(jax.Shape...  74.4 us
    pallas_call x1, Pallas kernels, second_exchange(): pl.pallas_call(functools.partial(second_kernel, line), out_shape=(jax.Sha...  64.2 us
    pallas_call x1, Pallas kernels, third_exchange(): pl.pallas_call(third_kernel, out_shape=(jax.ShapeDtypeStruct((rows, model...  41.3 us
    pallas_call x1, Pallas kernels, first_exchange(): pl.pallas_call(functools.partial(first_kernel, line), out_shape=(jax.Shap...  38.3 us
    pallas_call x1, Pallas kernels, attend_back(): pl.pallas_call(backward_kernel, grid_spec=pltpu.PrefetchScalarGridSpec(nu...  34.7 us
    ppermute x3, waiting for transfers between devices, head_local(): heard = lax.ppermute(out_parts[part], 'ctx', pairs)  33.9 us
    pallas_call x1, Pallas kernels, attend(): pl.pallas_call(forward_kernel, grid_spec=pltpu.PrefetchScalarGridSpec(num...  26 us
  transfers between devices with their start and end apart: 6, of which 3 were waited for; matrix products, arithmetic and copies ran while one was open for 2% of the time, Pallas kernels for 54%

profile of v3, /device:TPU:0, one launch (start us, length us, event | category | flops | bytes accessed | tf_op | source)
XLA Modules:
  0.0 473.7 jit_solution(16521387386550236154)
XLA Ops:
  7.2 0.0 all-gather.2.cloned.1.call-start
  7.3 0.8 stack.19
  8.1 0.7 stack.20
  8.8 0.1 constant_dynamic-slice_fusion.2
  8.9 1.2 constant_dynamic-slice_fusion
  10.1 0.2 pad_maximum_fusion.qkv_ref
  10.2 1.3 copy-done.9
  11.5 38.3 %first_exchange.1 = (bf16[2048,1536]{1,0:T(8,128)(2,1)}, bf16[4,384,384]{2,1,0:T(8,128)(2,1)S(1)}, bf16[4,48,1536]{2,1,0:T(8,128)(2,1)S(1)}, bf16[4,2,384]{2,1,0:T(2,128)(2,1)S(1)}, bf16[384,1536]{1,0:T(8,128)(2,1)}) custom-call(bf16[256,1536]{1,0:T(8,128)(2,1)S(1)} %bitcast.23, bf16[384,384]{1,0:T(8,128)(2,1)S(1)} %pad_maximum_fusion.qkv_ref, ...), custom_call_target="tpu_custom_call" | custom-call | tf_op jit(solution)/shard_map/first_exchange/pallas_call | solution.py:1016
  49.8 0.8 copy-done.12
  50.6 1.0 copy-done.17
  51.6 0.0 reduce-scatter.3.cloned.1.call-start
  51.7 0.2 multiply_cosine_fusion
  51.9 0.1 copy.24
  52.1 0.2 copy-done.23
  52.3 0.1 select_reduce_fusion.slot_ref
  52.4 0.1 multiply_cosine_fusion.1
  52.5 0.1 pad_maximum_fusion.3.outer_ref
  52.6 0.1 pad_maximum_fusion.1.inner_ref
  52.7 0.1 fusion.4.pad_ref
  52.9 1.4 copy-done.18
  54.3 26.0 %attend.1 = (bf16[2048,1536]{1,0:T(8,128)(2,1)}, bf16[2048,512]{1,0:T(8,128)(2,1)S(1)}, bf16[2048,192]{1,0:T(8,128)(2,1)S(1)}, f32[8,512]{1,0:T(8,128)S(1)}) custom-call(s32[16]{0:T(128)S(1)} %select_reduce_fusion.slot_ref, bf16[2048,1536]{1,0:T(8,128)(2,1)} %get-tuple-element.51.xa_ref.xb_ref, bf16[2048,1536]{1,0:T(8,128)(2,1)} %get-tuple-element.51.xa_ref.xb_ref, ...), custom_call_target="tpu_custom_call" | custom-call | flops 5368709120 | bytes 12582912 | tf_op jit(solution)/shard_map/attend/pallas_call | solution.py:518
  80.3 1.3 copy-done.20
  81.6 64.2 %second_exchange.1 = (bf16[2048,1536]{1,0:T(8,128)(2,1)}, bf16[4,48,1536]{2,1,0:T(8,128)(2,1)S(1)}, f32[256,1536]{1,0:T(8,128)}, f32[256,1536]{1,0:T(8,128)}, f3...) custom-call(bf16[2048,192]{1,0:T(8,128)(2,1)S(1)} %get-tuple-element.56.o_ref, bf16[4,48,1536]{2,1,0:T(8,128)(2,1)S(1)} %copy-done.13, ...), custom_call_target="tpu_custom_call" | custom-call | tf_op jit(solution)/shard_map/second_exchange/pallas_call | solution.py:1131
  145.8 0.9 copy-done.11
  146.7 74.4 %feed.1 = (f32[256,1536]{1,0:T(8,128)}, bf16[4,256,1536]{2,1,0:T(8,128)(2,1)}, bf16[1536,1536]{1,0:T(8,128)(2,1)}) custom-call(bf16[256,1536]{1,0:T(8,128)(2,1)} %copy-done.11, bf16[2048,1536]{1,0:T(8,128)(2,1)} %get-tuple-element.59.dy_ref, bf16[1536,1536]{1,0:T(8,128)(2,1)} %all-gather.2.cloned.1.call-done.w_ref), custom_call_target="tpu_custom_call" | custom-call | tf_op jit(solution)/shard_map/feed/pallas_call | solution.py:1586
  221.1 0.0 reduce-scatter.3.cloned.1.call-update
  221.2 0.0 reduce-scatter.5.cloned.1.call-start
  221.2 41.3 %third_exchange.1 = (f32[256,1536]{1,0:T(8,128)S(1)}, f32[1,1536]{1,0:T(1,128)S(1)}, bf16[2048,192]{1,0:T(8,128)(2,1)S(1)}, bf16[4,192,384]{2,1,0:T(8,128)(2,1)S(1)}) custom-call(f32[256,1536]{1,0:T(8,128)} %get-tuple-element.62.sum_ref, f32[256,1536]{1,0:T(8,128)} %get-tuple-element.63.normed_ref, f32[256,1]{1,0:T(8,128)S(1)} %get-tuple-element.64.scale_ref, ...), custom_call_target="tpu_custom_call" | custom-call | tf_op jit(solution)/shard_map/third_exchange/pallas_call | solution.py:1311
  262.6 1.1 copy-done.7
  263.7 34.7 %attend_back.1 = (bf16[2048,1536]{1,0:T(8,128)(2,1)}, bf16[4,576,384]{2,1,0:T(8,128)(2,1)S(1)}) custom-call(s32[16]{0:T(128)S(1)} %select_reduce_fusion.slot_ref, bf16[2048,1536]{1,0:T(8,128)(2,1)} %get-tuple-element.54.gained_ref, bf16[2048,512]{1,0:T(8,128)(2,1)S(1)} %copy-done.21, bf16[2048,192]{1,0:T(8,128)(2,1)S(1)} %get-tuple-element.56.o_ref, ...), custom_call_target="tpu_custom_call" | custom-call | flops 11811160064 | bytes 25165824 | tf_op jit(solution)/shard_map/attend_back/pallas_call | solution.py:675
  298.4 1.2 copy-done.4
  299.7 6.2 %reduce-scatter.3.cloned.1.call-done.piece_ref = bf16[384,1536]{1,0:T(8,128)(2,1)} async-done(((bf16[1536,1536]{1,0:T(8,128)(2,1)}), bf16[384,1536]{1,0:T(8,128)(2,1)}) %reduce-scatter.3.cloned.1.call-update) | async-done | bytes 1179664 | tf_op jit(solution)/shard_map/reduce_scatter | solution.py:1889
  305.9 3.1 slice_bitcast_fusion.2
  309.0 2.4 collective-permute-start
  311.4 0.6 collective-permute-start.1
  311.9 0.5 collective-permute-start.2
  312.5 18.2 %collective-permute-done = bf16[256,1536]{1,0:T(8,128)(2,1)} collective-permute-done((bf16[256,1536]{1,0:T(8,128)(2,1)}, bf16[256,1536]{1,0:T(8,128)(2,1)}, u32[]{:S(2)}, u32[]{:S(2)}) %collective-permute-start) | collective-permute-done | bytes 786464 | tf_op jit(solution)/shard_map/ppermute | solution.py:1905
  330.6 15.7 %collective-permute-done.1 = bf16[256,1536]{1,0:T(8,128)(2,1)} collective-permute-done((bf16[256,1536]{1,0:T(8,128)(2,1)}, bf16[256,1536]{1,0:T(8,128)(2,1)}, u32[]{:S(2)}, u32[]{:S(2)}) %collective-permute-start.1) | collective-permute-done | bytes 786464 | tf_op jit(solution)/shard_map/ppermute | solution.py:1905
  346.3 3.4 fusion.3
  349.7 79.3 %last_exchange.1 = (f32[1,256,1536]{2,1,0:T(8,128)S(1)}, bf16[3072,1536]{1,0:T(8,128)(2,1)}, f32[2,1536]{1,0:T(2,128)S(1)}) custom-call(bf16[2048,1536]{1,0:T(8,128)(2,1)} %get-tuple-element.74.dx_ref, f32[256,1536]{1,0:T(8,128)S(1)} %copy-done.8, bf16[256,1536]{1,0:T(8,128)(2,1)S(1)} %bitcast.25, f32[1,1536]{1,0:T(1,128)S(1)} %bitcast.33, ...), custom_call_target="tpu_custom_call" | custom-call | tf_op jit(solution)/shard_map/last_exchange/pallas_call | solution.py:1703
  429.0 1.1 copy-done.5
  430.2 10.8 %spread_feed.1 = (f32[384,4096]{1,0:T(8,128)}, f32[384,4096]{1,0:T(8,128)}, f32[1024,1536]{1,0:T(8,128)}) custom-call(bf16[8,384,1536]{2,1,0:T(8,128)(2,1)} %bitcast.36, bf16[8,384,1536]{2,1,0:T(8,128)(2,1)} %bitcast.37, bf16[8,384,1536]{2,1,0:T(8,128)(2,1)} %bitcast.38), custom_call_target="tpu_custom_call" | custom-call | tf_op jit(solution)/shard_map/spread_feed/pallas_call | solution.py:1749
  441.0 0.7 dynamic-slice_reduce_fusion
  441.7 1.0 copy-done.14
  442.7 19.4 %shard_map.203 = bf16[4608,384]{1,0:T(8,128)(2,1)S(1)} custom-call(bf16[576,384]{1,0:T(8,128)(2,1)S(1)} %copy-done.14), custom_call_target="tpu_custom_call" | custom-call | tf_op jit(solution)/shard_map/pallas_call | solution.py:1169
  462.0 3.2 spread_attention.1
  465.3 1.1 copy.26
  466.4 0.7 copy-done.1
  (51 shorter events, 0.2 us)
Async XLA Ops:
  7.2 1.6 copy-start
  7.2 3.0 copy-start.2
  7.2 139.5 %all-gather.2.cloned.1.call-start = ((), (), s32[]{:S(2)}) async-start(), calls=%async_computation.2 | async-start | bytes 5898240 | tf_op jit(solution)/shard_map/all_gather | solution.py:1865
  10.2 1.3 copy-start.9
  49.8 0.8 copy-start.12
  50.6 1.0 copy-start.17
  51.6 0.7 copy-start.23
  51.6 254.2 %reduce-scatter.3.cloned.1.call-start = ((), (), s32[]{:S(2)}) async-start(), calls=%async_computation.3 | async-start | bytes 5898240 | tf_op jit(solution)/shard_map/reduce_scatter | solution.py:1889
  52.9 27.4 %copy-start.15 = (bf16[384,512]{1,0:T(8,128)(2,1)}, bf16[384,512]{1,0:T(8,128)(2,1)S(1)}, u32[]{:S(2)}) copy-start(bf16[384,512]{1,0:T(8,128)(2,1)S(1)} %fusion.4.pad_ref) | copy-start | bytes 1179652
  52.9 1.4 copy-start.18
  54.3 27.3 %copy-start.3 = (bf16[1,256,1536]{2,1,0:T(8,128)(2,1)S(1)}, bf16[1,256,1536]{2,1,0:T(8,128)(2,1)}, u32[]{:S(2)}) copy-start(bf16[1,256,1536]{2,1,0:T(8,128)(2,1)} %param.14) | copy-start | bytes 2359300
  54.3 27.3 %copy-start.13 = (bf16[4,48,1536]{2,1,0:T(8,128)(2,1)S(1)}, bf16[4,48,1536]{2,1,0:T(8,128)(2,1)}, u32[]{:S(2)}) copy-start(bf16[4,48,1536]{2,1,0:T(8,128)(2,1)} %copy-done.12) | copy-start | bytes 1769476
  80.3 1.3 copy-start.20
  145.8 0.9 copy-start.11
  221.2 220.5 %reduce-scatter.5.cloned.1.call-start = ((), (), s32[]{:S(2)}) async-start(), calls=%async_computation.4 | async-start | bytes 2211840 | tf_op jit(solution)/shard_map/reduce_scatter | solution.py:1911
  221.2 42.5 %copy-start.16 = (bf16[384,512]{1,0:T(8,128)(2,1)S(1)}, bf16[384,512]{1,0:T(8,128)(2,1)}, u32[]{:S(2)}) copy-start(bf16[384,512]{1,0:T(8,128)(2,1)} %copy-done.15) | copy-start | bytes 1179652
  221.2 42.5 %copy-start.19 = (bf16[4,384,384]{2,1,0:T(8,128)(2,1)S(1)}, bf16[4,384,384]{2,1,0:T(8,128)(2,1)}, u32[]{:S(2)}) copy-start(bf16[4,384,384]{2,1,0:T(8,128)(2,1)} %copy-done.17) | copy-start | bytes 3538948
  221.2 42.5 %copy-start.21 = (bf16[2048,512]{1,0:T(8,128)(2,1)S(1)}, bf16[2048,512]{1,0:T(8,128)(2,1)}, u32[]{:S(2)}) copy-start(bf16[2048,512]{1,0:T(8,128)(2,1)} %copy-done.20) | copy-start | bytes 6291460
  262.6 1.1 copy-start.7
  298.4 1.2 copy-start.4
  305.9 40.4 %copy-start.22 = (f32[256,1536]{1,0:T(8,128)S(1)}, f32[256,1536]{1,0:T(8,128)}, u32[]{:S(2)}) copy-start(f32[256,1536]{1,0:T(8,128)} %get-tuple-element.71) | copy-start | bytes 4718596
  309.0 21.7 %collective-permute-start = (bf16[256,1536]{1,0:T(8,128)(2,1)}, bf16[256,1536]{1,0:T(8,128)(2,1)}, u32[]{:S(2)}, u32[]{:S(2)}) collective-permute-start(bf16[256,1536]{1,0:T(8,128)(2,1)} %get-tuple-element.93), channel_id=1, source_target_pairs={{0,24},{4,28},{8,16},{12,20},{16,8},{20,12},{24,0},{28,4},{1,25},{... | collective-permute-start | bytes 2359304 | tf_op jit(solution)/shard_map/ppermute | solution.py:1905
  311.4 35.0 %collective-permute-start.1 = (bf16[256,1536]{1,0:T(8,128)(2,1)}, bf16[256,1536]{1,0:T(8,128)(2,1)}, u32[]{:S(2)}, u32[]{:S(2)}) collective-permute-start(bf16[256,1536]{1,0:T(8,128)(2,1)} %get-tuple-element.95), channel_id=1, source_target_pairs={{0,8},{4,12},{8,0},{12,4},{16,24},{20,28},{24,16},{28,20},{1,9},{5... | collective-permute-start | bytes 2359304 | tf_op jit(solution)/shard_map/ppermute | solution.py:1905
  311.9 34.4 %collective-permute-start.2 = (bf16[256,1536]{1,0:T(8,128)(2,1)S(1)}, bf16[256,1536]{1,0:T(8,128)(2,1)}, u32[]{:S(2)}, u32[]{:S(2)}) collective-permute-start(bf16[256,1536]{1,0:T(8,128)(2,1)S(1)} %get-tuple-element.94), channel_id=1, source_target_pairs={{0,16},{4,20},{8,24},{12,28},{16,0},{20,4},{24,8},{28,12},{1,17},{... | collective-permute-start | bytes 2359304 | tf_op jit(solution)/shard_map/ppermute | solution.py:1905
  346.3 3.4 copy-start.8
  346.3 3.4 copy-start.10
  429.0 1.1 copy-start.5
  441.7 1.0 copy-start.14
  462.0 3.3 copy-start.6
  465.3 1.8 copy-start.1
Sparse Core Ops, SparseCore 0:
  51.8 88.6 all-gather.1
  221.3 84.5 reduce-scatter.2
  308.8 38.9 reduce-scatter.4

commit v4 on v3

--- a/solution.py
+++ b/solution.py
@@ -418,9 +418,9 @@
     pad_ref,
     inner_ref,
     outer_ref,
-    gained_ref,
     qkv_ref,
     o_ref,
+    ot_ref,
     lse_ref,
     wp,
     qs,
@@ -440,7 +440,6 @@
     x = jnp.concatenate([xa_ref[...], xb_ref[...]], axis=0).astype(jnp.float32)
     normed = x * lax.rsqrt(jnp.mean(x * x, axis=-1, keepdims=True) + norm_epsilon)
     gained = (normed * gain_ref[...]).astype(jnp.bfloat16)
-    gained_ref[...] = gained
     raw = contract(gained, wp[...], 1, 0)
     cosine, sine = tables(inner_ref, outer_ref, index, 2)
     here = pl.ds(pl.multiple_of(index * tile, tile), tile)
@@ -505,7 +504,9 @@
     out = contract(out, pad_ref[: GROUP * HEAD_SIZE, : GROUP * LANES], 1, 1).astype(jnp.bfloat16)
     for part in range(2):
         target = pl.ds(pl.multiple_of(slot_ref[index * 2 + part] * block, block), block)
-        o_ref[target, :] = out[part * block : (part + 1) * block, :]
+        rows_at = slice(part * block, (part + 1) * block)
+        o_ref[target, :] = out[rows_at, :]
+        ot_ref[:, target] = out[rows_at, :].T
 
 
 def attend(slots, x, gain, w, pad, inner, outer):
@@ -530,23 +531,24 @@
                 whole(*outer.shape),
             ],
             out_specs=(
-                pl.BlockSpec((tile, model), lambda i, s: (i, 0)),
                 whole(rows, columns),
                 whole(rows, GROUP * HEAD_SIZE),
+                whole(GROUP * HEAD_SIZE, rows),
                 whole(rows // tile, width),
+                whole(model, columns),
             ),
             scratch_shapes=[
-                pltpu.VMEM((model, columns), jnp.bfloat16),
                 pltpu.VMEM((width, LANES), jnp.bfloat16),
                 pltpu.VMEM((LANES, rows), jnp.bfloat16),
                 pltpu.VMEM((rows, width), jnp.float32),
             ],
         ),
         out_shape=(
-            jax.ShapeDtypeStruct((rows, model), jnp.bfloat16),
             jax.ShapeDtypeStruct((rows, columns), jnp.bfloat16),
             jax.ShapeDtypeStruct((rows, GROUP * HEAD_SIZE), jnp.bfloat16),
+            jax.ShapeDtypeStruct((GROUP * HEAD_SIZE, rows), jnp.bfloat16),
             jax.ShapeDtypeStruct((rows // tile, width), jnp.float32),
+            jax.ShapeDtypeStruct((model, columns), jnp.bfloat16),
         ),
         compiler_params=pltpu.CompilerParams(vmem_limit_bytes=44 << 20),
         cost_estimate=pl.CostEstimate(
@@ -560,41 +562,33 @@
 
 def backward_kernel(
     slot_ref,
-    gained_ref,
     qkv_ref,
     o_ref,
     do_ref,
     lse_ref,
-    w_ref,
-    dwo_ref,
     pad_ref,
     inner_ref,
     outer_ref,
-    dx_ref,
-    grads_ref,
-    wp,
+    dqkv_ref,
     qs,
     gs,
     kt,
     dk,
     dv,
-    dw,
 ):
     step_at = pl.program_id(0)
     tiles = pl.num_programs(0)
     index = tiles - 1 - step_at
-    tile = gained_ref.shape[0]
-    block = tile // 2
+    block = qkv_ref.shape[0] // slot_ref.shape[0]
+    tile = 2 * block
     width = GROUP * tile
     first_key, first_value = GROUP * LANES, (GROUP + 1) * LANES
 
     @pl.when(step_at == 0)
     def _():
-        wp[...] = contract(w_ref[...], pad_ref[...], 1, 0).astype(jnp.bfloat16)
         kt[...] = qkv_ref[:, first_key:first_value].T
         dk[...] = jnp.zeros_like(dk)
         dv[...] = jnp.zeros_like(dv)
-        dw[...] = jnp.zeros_like(dw)
 
     here = pl.ds(pl.multiple_of(index * tile, tile), tile)
     sources = [
@@ -646,72 +640,42 @@
     parts.append(turn(dk[here, :] * score_scale, cosine, -sine))
     parts.append(dv[here, :])
     dqkv = jnp.concatenate([part.astype(jnp.bfloat16) for part in parts], axis=1)
-    dw[...] += contract(dqkv, gained_ref[...], 0, 0)
-    dx = contract(dqkv, wp[...], 1, 1).astype(jnp.bfloat16)
     for part in (0, 1):
-        dx_ref[sources[part], :] = dx[part * block : (part + 1) * block, :]
-
-    @pl.when(step_at == tiles - 1)
-    def _():
-        packed = contract(pad_ref[...], dw[...].astype(jnp.bfloat16), 1, 0)
-        packed = packed.astype(jnp.bfloat16).T
-        line, _ = dwo_ref.shape[:2]
-        shard = packed.shape[0] // line
-        for slot in range(line):
-            grads_ref[slot, :shard, :] = packed[slot * shard : (slot + 1) * shard, :]
-            grads_ref[slot, shard:, :] = dwo_ref[slot]
-
-
-def attend_back(slots, gained, qkv, o, do, lse, w, dwo, pad, inner, outer):
-    rows, model = gained.shape
+        dqkv_ref[sources[part], :] = dqkv[part * block : (part + 1) * block, :]
+
+
+def attend_back(slots, qkv, o, do, lse, pad, inner, outer):
+    rows, columns = qkv.shape
     block = rows // slots.shape[0]
     tile = 2 * block
     width = GROUP * tile
     tiles = rows // tile
-    columns = pad.shape[1]
-    line, dealt, across = dwo.shape
-    grads = (line, model // line + dealt, across)
+    operands = (qkv, o, do, lse, pad, inner, outer)
     whole = lambda *shape: pl.BlockSpec(shape, lambda i, s: (0,) * len(shape))
     return pl.pallas_call(
         backward_kernel,
         grid_spec=pltpu.PrefetchScalarGridSpec(
             num_scalar_prefetch=1,
             grid=(tiles,),
-            in_specs=[
-                pl.BlockSpec((tile, model), lambda i, s: (tiles - 1 - i, 0)),
-                whole(*qkv.shape),
-                whole(*o.shape),
-                whole(*do.shape),
-                whole(*lse.shape),
-                whole(*w.shape),
-                whole(*dwo.shape),
-                whole(*pad.shape),
-                whole(*inner.shape),
-                whole(*outer.shape),
-            ],
-            out_specs=(whole(rows, model), whole(*grads)),
+            in_specs=[whole(*operand.shape) for operand in operands],
+            out_specs=whole(rows, columns),
             scratch_shapes=[
-                pltpu.VMEM((model, columns), jnp.bfloat16),
                 pltpu.VMEM((width, LANES), jnp.bfloat16),
                 pltpu.VMEM((width, LANES), jnp.bfloat16),
                 pltpu.VMEM((LANES, rows), jnp.bfloat16),
                 pltpu.VMEM((rows, LANES), jnp.float32),
                 pltpu.VMEM((rows, LANES), jnp.float32),
-                pltpu.VMEM((columns, model), jnp.float32),
             ],
         ),
-        out_shape=(
-            jax.ShapeDtypeStruct((rows, model), jnp.bfloat16),
-            jax.ShapeDtypeStruct(grads, jnp.bfloat16),
-        ),
-        compiler_params=pltpu.CompilerParams(vmem_limit_bytes=44 << 20),
+        out_shape=jax.ShapeDtypeStruct((rows, columns), jnp.bfloat16),
+        compiler_params=pltpu.CompilerParams(vmem_limit_bytes=40 << 20),
         cost_estimate=pl.CostEstimate(
-            flops=10 * GROUP * rows * rows * LANES // 2 + 4 * rows * model * columns,
-            bytes_accessed=8 * rows * model,
+            flops=10 * GROUP * rows * rows * LANES // 2,
+            bytes_accessed=8 * rows * columns,
             transcendentals=GROUP * rows * rows // 2,
         ),
         name="attend_back",
-    )(slots, gained, qkv, o, do, lse, w, dwo, pad, inner, outer)
+    )(slots, *operands)
 
 
 MESH_IDS = pl.DeviceIdType.MESH
@@ -1035,15 +999,55 @@
     )(x, qkv, wo, gains, gate, up, down)
 
 
+def deal_rows(copies, me, pieces, wo_ref, place, recv_first):
+    to_first = pieces * lax.rem(me, 2)
+    line_slot = lax.div(me, 2)
+
+    def copy(piece):
+        return copies.make(
+            recv_first + piece,
+            wo_ref.at[piece],
+            place(line_slot),
+            {"ctx": to_first + piece},
+            recv_first + line_slot,
+        )
+
+    for piece in range(pieces):
+
+        @pl.when(to_first + piece != me)
+        def _(piece=piece):
+            copy(piece).start()
+
+        @pl.when(to_first + piece == me)
+        def _(piece=piece):
+            place(line_slot)[...] = wo_ref[piece]
+
+    def finish(line):
+        for slot in range(line):
+
+            @pl.when(2 * slot + lax.div(me, pieces) != me)
+            def _(slot=slot):
+                copies.make(
+                    recv_first, wo_ref.at[0], place(slot), {"ctx": 0}, recv_first + slot
+                ).wait_recv()
+
+        for piece in range(pieces):
+
+            @pl.when(to_first + piece != me)
+            def _(piece=piece):
+                copy(piece).wait_send()
+
+    return finish
+
+
 def second_kernel(
-    line,
     o_ref,
     wo_ref,
-    dy_ref,
+    ot_ref,
     x_ref,
     gain_ref,
-    dyo_ref,
     own_ref,
+    dealt_ref,
     residual_ref,
     normed_ref,
     scale_ref,
@@ -1055,14 +1059,13 @@
     here,
 ):
     me = lax.axis_index("ctx")
-    rows = dy_ref.shape[0]
+    rows = x_ref.shape[0]
     local = local_copies(
         [
             (o_ref.at[pl.ds(pl.multiple_of(me * rows, rows), rows), :], att.at[me]),
             (wo_ref, wo.at[:, me]),
-            (dy_ref, row_part(dyo_ref, rows)(me, slice(None))),
         ],
-        here.at[pl.ds(0, 3)],
+        here.at[pl.ds(0, 2)],
     )
     start_barrier(me)
     copies = Copies(send, recv)
@@ -1074,6 +1077,7 @@
     for bit in (6, 7, 4, 5, 2, 3, 1):
         numbers[bit] = copies.number()
         copies.send(numbers[bit], block(me ^ bit), att.at[me], {"ctx": me ^ bit})
+    line = wo_ref.shape[0]
     middle = line // 2
 
     def wo_half(side):
@@ -1085,20 +1089,22 @@
         return wo.at[pl.ds(side * middle, middle), slot]
 
     wo_gather = PlaneGather(copies, me, wo_half, wo_part)
-    dy_gather = PlaneGather(copies, me, row_half(dy_ref, rows), row_part(dyo_ref, rows))
     wo_gather.begin()
     wo_gather.first_hop()
     wo_gather.second_hop()
-    dy_gather.begin()
+    pieces = ot_ref.shape[0]
+    first = copies.next
+    copies.next += pieces
+    finish = deal_rows(copies, me, pieces, ot_ref, lambda slot: dealt_ref.at[slot], first)
     wo_gather.third_hop()
     wo_gather.last()
     for bit, number in numbers.items():
         copies.arrived(number, att.at[me ^ bit])
-    local[0].wait()
-    local[1].wait()
+    for copy in local:
+        copy.wait()
     per_head = 2 * GROUP
     own = wo.at[lax.div(me, 2), pl.ds(per_head * lax.rem(me, 2), per_head)]
-    keep = local_copies([(own, own_ref)], here.at[pl.ds(3, 1)])
+    keep = local_copies([(own, own_ref)], here.at[pl.ds(2, 1)])
     plane = att.shape[0]
     total = x_ref[...].astype(jnp.float32)
     for slot in range(plane):
@@ -1113,43 +1119,41 @@
     scale_ref[...] = scale
     normed_ref[...] = normed
     gained_ref[...] = (normed * gain_ref[...]).astype(jnp.bfloat16)
-    dy_gather.first_hop()
-    dy_gather.second_hop()
-    dy_gather.third_hop()
-    dy_gather.last()
-    local[2].wait()
+    finish(line)
     keep[0].wait()
     copies.finish()
 
 
-def second_exchange(o, wo, dy, x, gain):
+def second_exchange(o, wo, ot, x, gain):
     plane = lax.axis_size("ctx")
-    rows = dy.shape[0]
+    rows = x.shape[0]
     line, part, model = wo.shape
-    count = 2 * GATHER_COPIES + 7
+    pieces = 2 * GROUP
+    ot = ot.reshape(pieces, -1, ot.shape[1])
+    count = GATHER_COPIES + 7 + pieces
     f32 = jnp.float32
     return pl.pallas_call(
-        functools.partial(second_kernel, line),
+        second_kernel,
         out_shape=(
-            jax.ShapeDtypeStruct((plane * rows, model), dy.dtype),
-            jax.ShapeDtypeStruct((2 * GROUP, part, model), wo.dtype),
+            jax.ShapeDtypeStruct((pieces, part, model), wo.dtype),
+            jax.ShapeDtypeStruct((line, *ot.shape[1:]), ot.dtype),
             jax.ShapeDtypeStruct((rows, model), f32),
             jax.ShapeDtypeStruct((rows, model), f32),
             jax.ShapeDtypeStruct((rows, 1), f32),
-            jax.ShapeDtypeStruct((rows, model), dy.dtype),
+            jax.ShapeDtypeStruct((rows, model), x.dtype),
         ),
-        in_specs=anywhere(3) + in_vmem(2),
-        out_specs=(*anywhere(2), *in_vmem(4)),
+        in_specs=anywhere(2) + in_vmem(3),
+        out_specs=(*anywhere(1), *in_vmem(5)),
         scratch_shapes=[
             pltpu.VMEM((plane, rows, o.shape[1]), o.dtype),
             pltpu.VMEM((line, plane, part, model), wo.dtype),
             pltpu.SemaphoreType.DMA((count,)),
             pltpu.SemaphoreType.DMA((count,)),
-            pltpu.SemaphoreType.DMA((4,)),
+            pltpu.SemaphoreType.DMA((3,)),
         ],
         compiler_params=remote_params(2),
         name="second_exchange",
-    )(o, wo, dy, x, gain)
+    )(o, wo, ot, x, gain)
 
 
 def gather_kernel(x_ref, xo_ref, send, recv, here):
@@ -1180,54 +1184,13 @@
     )(x)
 
 
-def deal_rows(copies, me, pieces, wo_ref, place, recv_first):
-    to_first = pieces * lax.rem(me, 2)
-    line_slot = lax.div(me, 2)
-
-    def copy(piece):
-        return copies.make(
-            recv_first + piece,
-            wo_ref.at[piece],
-            place(line_slot),
-            {"ctx": to_first + piece},
-            recv_first + line_slot,
-        )
-
-    for piece in range(pieces):
-
-        @pl.when(to_first + piece != me)
-        def _(piece=piece):
-            copy(piece).start()
-
-        @pl.when(to_first + piece == me)
-        def _(piece=piece):
-            place(line_slot)[...] = wo_ref[piece]
-
-    def finish(line):
-        for slot in range(line):
-
-            @pl.when(2 * slot + lax.div(me, pieces) != me)
-            def _(slot=slot):
-                copies.make(
-                    recv_first, wo_ref.at[0], place(slot), {"ctx": 0}, recv_first + slot
-                ).wait_recv()
-
-        for piece in range(pieces):
-
-            @pl.when(to_first + piece != me)
-            def _(piece=piece):
-                copy(piece).wait_send()
-
-    return finish
-
-
 def third_kernel(
     sum_ref,
     normed_ref,
     scale_ref,
     gain_ref,
     dy_ref,
-    o_ref,
+    ot_ref,
     wo_ref,
     residual_ref,
     term_ref,
@@ -1236,7 +1199,6 @@
     own,
     all_grads,
     dwo,
-    pieces_ref,
     send,
     recv,
 ):
@@ -1276,8 +1238,7 @@
         place = pl.ds(pl.multiple_of((me ^ order) * rows, rows), rows)
         grads = all_grads[place, :]
         do_ref[place, :] = contract(grads, wo_ref[...], 1, 1).astype(jnp.bfloat16)
-        share = contract(o_ref[place, :], grads, 0, 0)
-        dwo[...] += share
+        dwo[...] += contract(ot_ref[:, place], grads, 1, 0)
         return carry
 
     lax.fori_loop(0, 2, step, 0)
@@ -1287,48 +1248,40 @@
     gather.third_hop()
     lax.fori_loop(6, 8, step, 0)
     line, _, across = dwo_ref.shape
-    count = pieces_ref.shape[0]
-    for piece in range(count):
-        rows_at = slice(piece * HALF, (piece + 1) * HALF)
+    for slot in range(line):
+        rows_at = slice(slot * HALF, (slot + 1) * HALF)
         for number in range(dwo.shape[1] // across):
             columns = slice(number * across, (number + 1) * across)
-            pieces_ref[piece, number * HALF : (number + 1) * HALF, :] = dwo[
-                rows_at, columns
-            ].astype(jnp.bfloat16)
-    first = copies.next
-    finish = deal_rows(copies, me, count, pieces_ref, lambda slot: dwo_ref.at[slot], first)
-    finish(line)
+            dwo_ref[slot, number * HALF : (number + 1) * HALF, :] = dwo[rows_at, columns].astype(
+                jnp.bfloat16
+            )
     copies.finish()
 
 
-def third_exchange(line, grad_normed, normed, scale, gain, dy, o, wo, across):
+def third_exchange(line, grad_normed, normed, scale, gain, dy, ot, wo, across):
     plane = lax.axis_size("ctx")
     rows, model = dy.shape
-    pieces = 2 * GROUP
-    dealt = (HALF * model // across, across)
     half_type, f32 = jnp.bfloat16, jnp.float32
-    count = GATHER_COPIES + pieces
     return pl.pallas_call(
         third_kernel,
         out_shape=(
             jax.ShapeDtypeStruct((rows, model), f32),
             jax.ShapeDtypeStruct((1, model), f32),
-            jax.ShapeDtypeStruct(o.shape, half_type),
-            jax.ShapeDtypeStruct((line, *dealt), half_type),
+            jax.ShapeDtypeStruct((plane * rows, wo.shape[0]), half_type),
+            jax.ShapeDtypeStruct((line, HALF * model // across, across), half_type),
         ),
         in_specs=in_vmem(7),
         out_specs=tuple(in_vmem(4)),
         scratch_shapes=[
             pltpu.VMEM((rows, model), half_type),
             pltpu.VMEM((plane * rows, model), half_type),
-            pltpu.VMEM(wo.shape, f32),
-            pltpu.VMEM((pieces, *dealt), half_type),
-            pltpu.SemaphoreType.DMA((count,)),
-            pltpu.SemaphoreType.DMA((count,)),
+            pltpu.VMEM((line * HALF, model), f32),
+            pltpu.SemaphoreType.DMA((GATHER_COPIES,)),
+            pltpu.SemaphoreType.DMA((GATHER_COPIES,)),
         ],
         compiler_params=remote_params(6),
         name="third_exchange",
-    )(grad_normed, normed, scale, gain, dy, o, wo)
+    )(grad_normed, normed, scale, gain, dy, ot, wo)
 
 
 REDUCE_COPIES = 10
@@ -1426,12 +1379,21 @@
 def feed_kernel(
     line,
     g_ref,
-    dy_ref,
+    dy0_hbm,
+    dy2_hbm,
+    dy4_hbm,
+    dy6_hbm,
+    w_hbm,
+    sum_ref,
+    out6_hbm,
+    out2_hbm,
+    out4_hbm,
+    out0_hbm,
+    dw_hbm,
     w_ref,
-    sum_ref,
-    out_ref,
     dw_ref,
     down_ref,
+    dy_ref,
     all_g,
     hid,
     hid_t,
@@ -1445,21 +1407,35 @@
     out_heard,
     send,
     recv,
+    here,
 ):
     me = lax.axis_index("ctx")
     rows = g_ref.shape[0]
     width, model = down_ref.shape
     blocks = model // width
     unit = width // line
+
+    def at(slot):
+        return pl.ds(pl.multiple_of(slot * rows, rows), rows)
+
+    heard_grads = (dy0_hbm, dy2_hbm, dy4_hbm, dy6_hbm)
+    local = local_copies(
+        [(w_hbm, w_ref)]
+        + [(ref, dy_ref.at[at(me ^ (2 * number)), :]) for number, ref in enumerate(heard_grads)],
+        here.at[pl.ds(0, 5)],
+    )
     start_barrier(me)
     copies = Copies(send, recv)
     gather = PlaneGather(copies, me, row_half(g_ref, rows), row_part(all_g, rows))
     gather.begin()
-
-    def at(slot):
-        return pl.ds(pl.multiple_of(slot * rows, rows), rows)
-
+    dy_first = copies.next
+    copies.next += 4
+    for number, ref in enumerate(heard_grads):
+        place = dy_ref.at[at(me ^ (2 * number)), :]
+        copies.send(dy_first + number, ref, place, {"ctx": me ^ 1})
     all_g[at(me), :] = g_ref[...]
+    for copy in local:
+        copy.wait()
     gate_ref, up_ref = w_ref.at[:, :width], w_ref.at[:, width : 2 * width]
     for z in range(line):
         for number in range(blocks):
@@ -1496,6 +1472,13 @@
         ).astype(jnp.bfloat16)
 
     def step(order, carry):
+        for number in range(4):
+
+            @pl.when(order == 2 * number + 1)
+            def _(number=number):
+                place = dy_ref.at[at(me ^ (2 * number + 1)), :]
+                copies.arrived(dy_first + number, place)
+
         for number, slot, sides, when in (
             (4, 1, 0, 1),
             (5, 1, 1, 1),
@@ -1547,7 +1530,7 @@
     def keep(number, carry):
         total = out_of(me ^ bit_of(number))
         out_copy(number).wait_recv()
-        out_ref[number] = (total + out_heard[number].astype(jnp.float32)).astype(jnp.bfloat16)
+        out_heard[number] = (total + out_heard[number].astype(jnp.float32)).astype(jnp.bfloat16)
         return carry
 
     def weights(number, carry):
@@ -1566,34 +1549,47 @@
     lax.fori_loop(1, 4, give, 0)
     reduce.second_sends()
     lax.fori_loop(0, 4, keep, 0)
+    outputs = local_copies(
+        [
+            (out_heard.at[number], ref)
+            for number, ref in enumerate((out6_hbm, out2_hbm, out4_hbm, out0_hbm))
+        ],
+        here.at[pl.ds(0, 4)],
+    )
     lax.fori_loop(0, blocks, weights, 0)
+    outputs += local_copies([(dw_ref, dw_hbm)], here.at[pl.ds(4, 1)])
     half = rows // 2
     for which in (1, 0):
         sum_ref[pl.ds(which * half, half), :] = reduce.sum_half(which)
     for number in range(4):
         out_copy(number).wait_send()
+    for copy in outputs:
+        copy.wait()
     reduce.finish()
     copies.finish()
 
 
-def feed(g, dy, w):
+def feed(g, grads, w):
     plane, line = lax.axis_size("ctx"), lax.axis_size("fsdp")
     rows, model = g.shape
     tokens = plane * rows
     width = w.shape[1] // 3
-    count = GATHER_COPIES + REDUCE_COPIES + 4
+    count = GATHER_COPIES + REDUCE_COPIES + 8
     half_type = jnp.bfloat16
     return pl.pallas_call(
         functools.partial(feed_kernel, line),
         out_shape=(
             jax.ShapeDtypeStruct((rows, model), jnp.float32),
-            jax.ShapeDtypeStruct((4, rows, model), half_type),
+            *[jax.ShapeDtypeStruct((rows, model), half_type)] * 4,
             jax.ShapeDtypeStruct(w.shape, half_type),
         ),
-        in_specs=in_vmem(3),
-        out_specs=tuple(in_vmem(3)),
+        in_specs=in_vmem(1) + anywhere(5),
+        out_specs=(*in_vmem(1), *anywhere(5)),
         scratch_shapes=[
+            pltpu.VMEM(w.shape, half_type),
+            pltpu.VMEM(w.shape, half_type),
             pltpu.VMEM((width, model), half_type),
+            pltpu.VMEM((tokens, model), half_type),
             pltpu.VMEM((tokens, model), half_type),
             pltpu.VMEM((tokens, width), half_type),
             pltpu.VMEM((width, tokens), half_type),
@@ -1607,28 +1603,147 @@
             pltpu.VMEM((4, rows, model), half_type),
             pltpu.SemaphoreType.DMA((count,)),
             pltpu.SemaphoreType.DMA((count,)),
+            pltpu.SemaphoreType.DMA((5,)),
         ],
         compiler_params=pltpu.CompilerParams(
             collective_id=3, has_side_effects=True, vmem_limit_bytes=60 << 20
         ),
         name="feed",
-    )(g, dy, w)
-
-
-def last_kernel(
-    line,
-    dx_ref,
-    residual_ref,
+    )(g, *grads, w)
+
+
+def input_kernel(
+    dqkv_ref,
+    wp_ref,
+    x_hbm,
     x_ref,
     gain_ref,
+    residual_ref,
+    dwo_ref,
+    pad_ref,
+    input_ref,
+    grads_ref,
     term_ref,
-    piece_ref,
-    input_ref,
-    whole_ref,
-    total_ref,
+    all_x,
+    part,
+    dw,
     heard,
     held,
     landed,
+    send,
+    recv,
+    here,
+):
+    me = lax.axis_index("ctx")
+    rows = residual_ref.shape[0]
+    fetch = local_copies([(x_hbm, all_x)], here)
+    start_barrier(me)
+    copies = Copies(send, recv)
+
+    def at(slot):
+        return pl.ds(pl.multiple_of(slot * rows, rows), rows)
+
+    def compute(slot):
+        place = at(slot)
+        part[place, :] = contract(dqkv_ref[place, :], wp_ref[...], 1, 1).astype(jnp.bfloat16)
+
+    reduce = PlaneReduce(copies, me, lambda slot: part.at[at(slot), :], heard, held, landed)
+    compute(me ^ 7)
+    reduce.share(0)
+    compute(me ^ 6)
+    compute(me ^ 3)
+    reduce.share(1)
+    reduce.diagonal_sends()
+    compute(me ^ 2)
+    compute(me ^ 5)
+    reduce.share(2)
+    compute(me ^ 4)
+    reduce.neighbour_sends()
+    compute(me ^ 1)
+    reduce.share(3)
+    compute(me)
+    gain = gain_ref[...]
+    dw[...] = jnp.zeros_like(dw)
+    fetch[0].wait()
+
+    def weights(slot, carry):
+        place = at(slot)
+        x = all_x[place, :].astype(jnp.float32)
+        normed = x * lax.rsqrt(jnp.mean(x * x, axis=-1, keepdims=True) + norm_epsilon)
+        gained = (normed * gain).astype(jnp.bfloat16)
+        dw[...] += contract(dqkv_ref[place, :], gained, 0, 0)
+        return carry
+
+    plane = part.shape[0] // rows
+    lax.fori_loop(0, plane // 2, weights, 0)
+    reduce.second_sends()
+    lax.fori_loop(plane // 2, plane, weights, 0)
+    packed = contract(pad_ref[...], dw[...].astype(jnp.bfloat16), 1, 0)
+    packed = packed.astype(jnp.bfloat16).T
+    line = dwo_ref.shape[0]
+    shard = packed.shape[0] // line
+    for slot in range(line):
+        grads_ref[slot, :shard, :] = packed[slot * shard : (slot + 1) * shard, :]
+        grads_ref[slot, shard:, :] = dwo_ref[slot]
+    half = rows // 2
+    total = jnp.zeros_like(gain)
+    for which in (1, 0):
+        here_rows = pl.ds(which * half, half)
+        grad = reduce.sum_half(which)
+        x = x_ref[here_rows, :].astype(jnp.float32)
+        scale = lax.rsqrt(jnp.mean(x * x, axis=-1, keepdims=True) + norm_epsilon)
+        normed = x * scale
+        total = total + jnp.sum(grad * normed, axis=0, keepdims=True)
+        scaled = grad * gain
+        mean = jnp.mean(scaled * normed, axis=-1, keepdims=True)
+        input_ref[0, here_rows, :] = residual_ref[here_rows, :] + scale * (scaled - normed * mean)
+    term_ref[...] = total
+    reduce.finish()
+    copies.finish()
+
+
+def input_exchange(dqkv, wp, all_x, x, gain, residual, dwo, pad):
+    rows, model = x.shape
+    line, dealt, across = dwo.shape
+    f32 = jnp.float32
+    return pl.pallas_call(
+        input_kernel,
+        out_shape=(
+            jax.ShapeDtypeStruct((1, rows, model), f32),
+            jax.ShapeDtypeStruct((line, model // line + dealt, across), dwo.dtype),
+            jax.ShapeDtypeStruct((1, model), f32),
+        ),
+        in_specs=in_vmem(2) + anywhere(1) + in_vmem(5),
+        out_specs=tuple(in_vmem(3)),
+        scratch_shapes=[
+            pltpu.VMEM(all_x.shape, all_x.dtype),
+            pltpu.VMEM(all_x.shape, all_x.dtype),
+            pltpu.VMEM((dqkv.shape[1], model), f32),
+            pltpu.VMEM((4, rows, model), x.dtype),
+            pltpu.VMEM((3, rows, model), x.dtype),
+            pltpu.VMEM((3, rows, model), x.dtype),
+            pltpu.SemaphoreType.DMA((REDUCE_COPIES,)),
+            pltpu.SemaphoreType.DMA((REDUCE_COPIES,)),
+            pltpu.SemaphoreType.DMA((1,)),
+        ],
+        compiler_params=remote_params(7),
+        name="input_exchange",
+    )(dqkv, wp, all_x, x, gain, residual, dwo, pad)
+
+
+def pieces_kernel(
+    line,
+    piece_ref,
+    term_one_ref,
+    term_two_ref,
+    residual_ref,
+    out0_ref,
+    out2_ref,
+    out4_ref,
+    out6_ref,
+    whole_ref,
+    total_ref,
+    output_ref,
     terms,
     terms_heard,
     plane_sum,
@@ -1640,43 +1755,23 @@
     me, index = lax.axis_index("ctx"), lax.axis_index("fsdp")
     start_barrier(me, index, line)
     copies = Copies(send, recv)
-    rows = residual_ref.shape[0]
-
-    def block(slot):
-        return dx_ref.at[pl.ds(pl.multiple_of(slot * rows, rows), rows), :]
-
-    reduce = PlaneReduce(copies, me, block, heard, held, landed)
-    piece_rows = piece_ref.shape[0]
-    part = row_part(whole_ref, piece_rows)
-    gather = PlaneGather(copies, me, row_half(piece_ref, piece_rows), part)
-    for order in range(4):
-        reduce.share(order)
+    rows = piece_ref.shape[0]
+    part = row_part(whole_ref, rows)
+    gather = PlaneGather(copies, me, row_half(piece_ref, rows), part)
+    first = copies.next
+    copies.next += 7 + line - 1
+    terms[0:1, :] = term_one_ref[...]
+    terms[1:2, :] = term_two_ref[...]
+    gather.begin()
     local = local_copies([(piece_ref, part(me, slice(None)))], here)
-    reduce.first_sends()
-    gather.begin()
-    reduce.second_sends()
+    for bit in range(1, 8):
+        copies.send(first + bit - 1, terms, terms_heard.at[bit], {"ctx": me ^ bit})
+    total = residual_ref[...]
+    for ref in (out0_ref, out2_ref, out4_ref, out6_ref):
+        total = total + ref[...].astype(jnp.float32)
+    output_ref[0] = total.astype(output_ref.dtype)
     gather.first_hop()
     gather.second_hop()
-    half = rows // 2
-    gain = gain_ref[...]
-    total = jnp.zeros_like(gain)
-    for which in (1, 0):
-        at = pl.ds(which * half, half)
-        grad = reduce.sum_half(which)
-        x = x_ref[at, :].astype(jnp.float32)
-        scale = lax.rsqrt(jnp.mean(x * x, axis=-1, keepdims=True) + norm_epsilon)
-        normed = x * scale
-        total = total + jnp.sum(grad * normed, axis=0, keepdims=True)
-        scaled = grad * gain
-        mean = jnp.mean(scaled * normed, axis=-1, keepdims=True)
-        input_ref[0, at, :] = residual_ref[at, :] + scale * (scaled - normed * mean)
-    terms[0:1, :] = total
-    terms[1:2, :] = term_ref[...]
-    first = copies.next
-    copies.next += 7 + line - 1
-    for bit in range(1, 8):
-        copies.send(first + bit - 1, terms, terms_heard.at[bit], {"ctx": me ^ bit})
-    gather.third_hop()
     total = terms[...]
     for bit in range(1, 8):
         copies.arrived(first + bit - 1, terms_heard.at[bit])
@@ -1685,34 +1780,31 @@
     for step in range(1, line):
         peer = {"fsdp": lax.rem(index + step, line)}
         copies.send(first + 6 + step, plane_sum, across.at[step], peer)
+    gather.third_hop()
     for step in range(1, line):
         copies.arrived(first + 6 + step, across.at[step])
         total = total + across[step]
     total_ref[...] = total
     gather.last()
     local[0].wait()
-    reduce.finish()
     copies.finish()
 
 
-def last_exchange(line, dx, residual, x, gain, term, piece):
+def pieces_exchange(line, piece, term_one, term_two, residual, outs):
     plane = lax.axis_size("ctx")
-    rows, model = x.shape
+    rows, model = residual.shape
     f32 = jnp.float32
-    copies = GATHER_COPIES + REDUCE_COPIES + 7 + line - 1
+    copies = GATHER_COPIES + 7 + line - 1
     return pl.pallas_call(
-        functools.partial(last_kernel, line),
+        functools.partial(pieces_kernel, line),
         out_shape=(
-            jax.ShapeDtypeStruct((1, rows, model), f32),
             jax.ShapeDtypeStruct((plane * piece.shape[0], piece.shape[1]), piece.dtype),
             jax.ShapeDtypeStruct((2, model), f32),
+            jax.ShapeDtypeStruct((1, rows, model), jnp.bfloat16),
         ),
-        in_specs=in_vmem(5) + anywhere(1),
-        out_specs=(*in_vmem(1), *anywhere(1), *in_vmem(1)),
+        in_specs=anywhere(1) + in_vmem(7),
+        out_specs=(*anywhere(1), *in_vmem(2)),
         scratch_shapes=[
-            pltpu.VMEM((4, rows, model), dx.dtype),
-            pltpu.VMEM((3, rows, model), dx.dtype),
-            pltpu.VMEM((3, rows, model), dx.dtype),
             pltpu.VMEM((2, model), f32),
             pltpu.VMEM((plane, 2, model), f32),
             pltpu.VMEM((2, model), f32),
@@ -1721,9 +1813,9 @@
             pltpu.SemaphoreType.DMA((copies,)),
             pltpu.SemaphoreType.DMA((1,)),
         ],
-        compiler_params=remote_params(7),
-        name="last_exchange",
-    )(dx, residual, x, gain, term, piece)
+        compiler_params=remote_params(8),
+        name="pieces_exchange",
+    )(piece, term_one, term_two, residual, *outs)
 
 
 def spread_kernel(gate_in, up_in, down_in, gate_ref, up_ref, down_ref):
@@ -1879,13 +1971,18 @@
 
     gains = jnp.transpose(gains, (1, 0, 2)).reshape(2, model).astype(jnp.float32)
     qkv_w = qkv_w.reshape(model, -1)
-    gained_one, qkv, o, lse = attend(slots, x_all, gains[:1], qkv_w, pad, inner, outer)
-
-    grad_all, wo_mine, residual, normed_two, scale_two, gained_two = second_exchange(
-        o, wo_line, output_grad[0], block_input[0], gains[1:]
-    )
-    wo_mine = wo_mine.reshape(-1, model)
-    grad_normed_two, out_parts, feed_grads = feed(gained_two, grad_all, feed_w)
+    grad_rows, x_all = lax.optimization_barrier((output_grad[0], x_all))
+    grad_parts = [grad_rows]
+    for bit in (2, 4, 6):
+        pairs = [(device, device ^ bit) for device in range(plane)]
+        grad_parts.append(lax.ppermute(grad_rows, "ctx", pairs))
+    qkv, o, o_columns, lse, qkv_pad = attend(
+        slots, x_all, gains[:1], qkv_w, pad, inner, outer
+    )
+    wo_mine, columns_mine, residual, normed_two, scale_two, gained_two = second_exchange(
+        o, wo_line, o_columns, block_input[0], gains[1:]
+    )
+    grad_normed_two, *out_parts, feed_grads = feed(gained_two, grad_parts, feed_w)
     feed_grads = lax.psum_scatter(feed_grads, "fsdp", scatter_dimension=0, tiled=True)
     grad_residual, feedforward_term, grad_o, wo_term = third_exchange(
         line,
@@ -1894,18 +1991,18 @@
         scale_two,
         gains[1:],
         output_grad[0],
-        o,
-        wo_mine,
+        columns_mine.reshape(-1, columns_mine.shape[2]),
+        wo_mine.reshape(-1, model),
         qkv_w.shape[1],
     )
-    out_parts, grad_o = lax.optimization_barrier((out_parts, grad_o))
-    out_sum = out_parts[3].astype(jnp.float32)
+    *out_parts, grad_o = lax.optimization_barrier((*out_parts, grad_o))
+    outs = [out_parts[3]]
     for part, bit in enumerate((6, 2, 4)):
         pairs = [(device, device ^ bit) for device in range(plane)]
-        heard = lax.ppermute(out_parts[part], "ctx", pairs)
-        out_sum = out_sum + heard.astype(jnp.float32)
-    dx, attention_grads = attend_back(
-        slots, gained_one, qkv, o, grad_o, lse, qkv_w, wo_term, pad, inner, outer
+        outs.append(lax.ppermute(out_parts[part], "ctx", pairs))
+    grads = attend_back(slots, qkv, o, grad_o, lse, pad, inner, outer)
+    input_grad, attention_grads, attention_term = input_exchange(
+        grads, qkv_pad, x_all, block_input[0], gains[:1], grad_residual, wo_term, pad
     )
     attention_grads, feed_grads = lax.optimization_barrier((attention_grads, feed_grads))
     attention_grads = lax.psum_scatter(
@@ -1914,10 +2011,8 @@
         scatter_dimension=0,
         tiled=True,
     )
-    layer_output = (residual + out_sum).astype(jnp.bfloat16)
-    dx, layer_output = lax.optimization_barrier((dx, layer_output))
-    input_grad, feed_pieces, gain_terms = last_exchange(
-        line, dx, grad_residual, block_input[0], gains[:1], feedforward_term, feed_grads
+    feed_pieces, gain_terms, layer_output = pieces_exchange(
+        line, feed_grads, attention_term, feedforward_term, residual, outs
     )
     gate_grad, up_grad, down_grad = spread_feed(feed_pieces, shard, line, unit)
     attention_pieces = plane_gather(attention_grads, 9)
@@ -1926,7 +2021,7 @@
     )
     gain_terms = lax.dynamic_slice_in_dim(gain_terms, lax.axis_index("fsdp") * shard, shard, 1)
     return (
-        layer_output[None],
+        layer_output,
         input_grad,
         gain_terms[0],
         query_grad,

time: 474 us -> 444 us (0.937)
  Pallas kernels: 392 us -> 351 us
  local copies, waits for them, and re-layouts: 19.9 us -> 26.1 us
    pallas_call x2 -> x3, Pallas kernels: 144 us -> 128 us  [the longest x1 46.8 us: pieces_exchange(): pl.pallas_call(functools.partial(pieces_kernel, line), out_shape=(jax.Sha...]
    pallas_call x1, Pallas kernels: 34.7 us -> 20.2 us  [attend_back(): pl.pallas_call(backward_kernel, grid_spec=pltpu.PrefetchScalarGridSpec(nu...]
    all_gather x1, waiting for transfers between devices: 0.01 us -> 8.98 us  [head_local(): feed_w = lax.all_gather(feed_mine, 'fsdp', axis=0, tiled=True)]
    unnamed x49 -> x90, local copies, waits for them, and re-layouts: 13.3 us -> 21.8 us
    pallas_call x1, Pallas kernels: 41.3 us -> 33.9 us  [third_exchange(): pl.pallas_call(third_kernel, out_shape=(jax.ShapeDtypeStruct((rows, model...]
    reduce_scatter x1, waiting for transfers between devices: 6.23 us -> 0.01 us  [head_local(): lax.psum_scatter(feed_grads, 'fsdp', scatter_dimension=0, tiled=True)]
    ppermute x3 -> x6, waiting for transfers between devices: 33.9 us -> 33.7 us  [the longest x3 33.7 us: head_local(): outs.append(lax.ppermute(out_parts[part], 'ctx', pairs))]
  transfers between devices with their start and end apart: 6 -> 9, of which waited for: 3 -> 4; matrix products, arithmetic and copies ran while one was open for 2% -> 1% of each run, Pallas kernels for 54% -> 49%
where the time goes in v4:
time: 444 us; the launch traced here: 443 us
  Pallas kernels  351 us (79%)
  waiting for transfers between devices  42.8 us (10%)
  local copies, waits for them, and re-layouts  26.1 us (6%)
  between operations  14.3 us (3%)
  starting transfers between devices  7.45 us (2%)
    pallas_call x1, Pallas kernels, feed(): pl.pallas_call(functools.partial(feed_kernel, line), out_shape=(jax.Shape...  71.4 us
    pallas_call x1, Pallas kernels, pieces_exchange(): pl.pallas_call(functools.partial(pieces_kernel, line), out_shape=(jax.Sha...  46.8 us
    pallas_call x1, Pallas kernels, second_exchange(): pl.pallas_call(second_kernel, out_shape=(jax.ShapeDtypeStruct((pieces, pa...  43.6 us
    pallas_call x1, Pallas kernels, first_exchange(): pl.pallas_call(functools.partial(first_kernel, line), out_shape=(jax.Shap...  38.3 us
    pallas_call x1, Pallas kernels, input_exchange(): pl.pallas_call(input_kernel, out_shape=(jax.ShapeDtypeStruct((1, rows, mo...  37.8 us
    pallas_call x1, Pallas kernels, third_exchange(): pl.pallas_call(third_kernel, out_shape=(jax.ShapeDtypeStruct((rows, model...  33.9 us
    ppermute x3, waiting for transfers between devices, head_local(): outs.append(lax.ppermute(out_parts[part], 'ctx', pairs))  33.7 us
    pallas_call x1, Pallas kernels, attend(): pl.pallas_call(forward_kernel, grid_spec=pltpu.PrefetchScalarGridSpec(num...  25.5 us
  transfers between devices with their start and end apart: 9, of which 4 were waited for; matrix products, arithmetic and copies ran while one was open for 1% of the time, Pallas kernels for 49%

profile of v4, /device:TPU:0, one launch (start us, length us, event | category | flops | bytes accessed | tf_op | source)
XLA Modules:
  0.0 443.0 jit_solution(7246841783338260670)
XLA Ops:
  7.3 0.8 stack.19
  8.1 0.7 stack.20
  8.9 1.2 constant_dynamic-slice_fusion
  10.2 1.3 copy-done.9
  11.5 38.3 %first_exchange.1 = (bf16[2048,1536]{1,0:T(8,128)(2,1)}, bf16[4,384,384]{2,1,0:T(8,128)(2,1)S(1)}, bf16[4,48,1536]{2,1,0:T(8,128)(2,1)S(1)}, bf16[4,2,384]{2,1,0:T(2,128)(2,1)S(1)}, bf16[384,1536]{1,0:T(8,128)(2,1)}) custom-call(bf16[256,1536]{1,0:T(8,128)(2,1)S(1)} %bitcast.15, bf16[384,384]{1,0:T(8,128)(2,1)S(1)} %pad_maximum_fusion.qkv_ref, ...), custom_call_target="tpu_custom_call" | custom-call | tf_op jit(solution)/shard_map/first_exchange/pallas_call | solution.py:980
  49.8 0.8 copy-done.19
  50.6 1.0 copy-done.35
  51.7 1.4 collective-permute-start
  53.1 1.2 collective-permute-start.1
  54.3 1.0 collective-permute-start.2
  56.3 1.4 copy-done.36
  57.6 25.5 %attend.1 = (bf16[2048,512]{1,0:T(8,128)(2,1)S(1)}, bf16[2048,192]{1,0:T(8,128)(2,1)S(1)}, bf16[192,2048]{1,0:T(8,128)(2,1)S(1)}, f32[8,512]{1,0:T(8,128)S(1)}, bf16[1536,512]{1,0:T(8,128)(2,1)S(1)}) custom-call(s32[16]{0:T(128)S(1)} %select_reduce_fusion.slot_ref, bf16[2048,1536]{1,0:T(8,128)(2,1)} %get-tuple-element.60.xa_ref.xb_ref.x_hbm, ...), custom_call_target="tpu_custom_call" | custom-call | flops 5368709120 | bytes 12582912 | tf_op jit(solution)/shard_map/attend/pallas_call | solution.py:519
  83.2 1.3 copy-done.39
  84.5 43.6 %second_exchange.1 = (bf16[4,48,1536]{2,1,0:T(8,128)(2,1)S(1)}, bf16[4,48,2048]{2,1,0:T(8,128)(2,1)S(1)}, f32[256,1536]{1,0:T(8,128)}, f32[256,1536]{1,0:T(8,128...) custom-call(bf16[2048,192]{1,0:T(8,128)(2,1)S(1)} %get-tuple-element.64.o_ref, ...), custom_call_target="tpu_custom_call" | custom-call | tf_op jit(solution)/shard_map/second_exchange/pallas_call | solution.py:1135
  128.1 0.9 copy-done.14
  129.0 0.9 copy-done.17
  129.9 0.8 copy-done.21
  130.7 0.7 copy-done.24
  131.4 9.0 %all-gather.2.cloned.1.call-done.w_hbm = bf16[1536,1536]{1,0:T(8,128)(2,1)} async-done(((bf16[384,1536]{1,0:T(8,128)(2,1)}), bf16[1536,1536]{1,0:T(8,128)(2,1)}) %all-gather.2.cloned.1.call-update) | async-done | bytes 4718608 | tf_op jit(solution)/shard_map/all_gather | solution.py:1957
  140.3 71.4 %feed.1 = (f32[256,1536]{1,0:T(8,128)}, bf16[256,1536]{1,0:T(8,128)(2,1)}, bf16[256,1536]{1,0:T(8,128)(2,1)}, bf16[256,1536]{1,0:T(8,128)(2,1)}, bf16[256,1536]{1,0:T(8,128)(2,1)}, /*index=5*/bf16[1536,1536]{1,0:T(8,128)(2,1)}) custom-call(bf16[256,1536]{1,0:T(8,128)(2,1)} %copy-done.14, bf16[256,1536]{1,0:T(8,128)(2,1)} %bitcast.18, ...), custom_call_target="tpu_custom_call" | custom-call | tf_op jit(solution)/shard_map/feed/pallas_call | solution.py:1579
  211.8 0.3 reduce-scatter.5.cloned.1.call-start
  212.0 0.8 copy-done.4
  212.9 1.1 copy-done.18
  214.0 1.1 copy-done.22
  215.1 1.0 copy-done.25
  216.1 33.9 %third_exchange.1 = (f32[256,1536]{1,0:T(8,128)S(1)}, f32[1,1536]{1,0:T(1,128)S(1)}, bf16[2048,192]{1,0:T(8,128)(2,1)S(1)}, bf16[4,192,384]{2,1,0:T(8,128)(2,1)S(1)}) custom-call(f32[256,1536]{1,0:T(8,128)} %get-tuple-element.74.sum_ref, f32[256,1536]{1,0:T(8,128)} %get-tuple-element.75.normed_ref, f32[256,1]{1,0:T(8,128)S(1)} %copy-done.25, ...), custom_call_target="tpu_custom_call" | custom-call | tf_op jit(solution)/shard_map/third_exchange/pallas_call | solution.py:1265
  250.1 20.2 %attend_back.1.dqkv_ref = bf16[2048,512]{1,0:T(8,128)(2,1)S(1)} custom-call(s32[16]{0:T(128)S(1)} %copy-done.38, bf16[2048,512]{1,0:T(8,128)(2,1)S(1)} %copy-done.40, bf16[2048,192]{1,0:T(8,128)(2,1)S(1)} %copy-done.12, bf16[2048,192]{1,0:T(8,128)(2,1)S(1)} %get-tuple-element.80.do_ref, f32[8,512]{1,0:T(8,128)S(1)} %copy-done.42, ...), custom_call_target="tpu_custom_call" | custom-call | flops 5368709120 | bytes 8388608 | tf_op jit(solution)/shard_map/attend_back/pallas_call | solution.py:655
  270.3 1.3 copy-done.5
  271.6 37.8 %input_exchange.1 = (f32[1,256,1536]{2,1,0:T(8,128)S(1)}, bf16[4,576,384]{2,1,0:T(8,128)(2,1)}, f32[1,1536]{1,0:T(1,128)S(1)}) custom-call(bf16[2048,512]{1,0:T(8,128)(2,1)} %copy-done.5, bf16[1536,512]{1,0:T(8,128)(2,1)S(1)} %get-tuple-element.82.wp_ref, bf16[2048,1536]{1,0:T(8,128)(2,1)} %get-tuple-element.60.xa_ref.xb_ref.x_hbm, ...), custom_call_target="tpu_custom_call" | custom-call | tf_op jit(solution)/shard_map/input_exchange/pallas_call | solution.py:1709
  309.4 1.1 copy-done.6
  310.5 0.6 copy-done.32
  311.2 1.5 collective-permute-start.3
  312.7 0.6 collective-permute-start.4
  313.3 1.5 collective-permute-start.5
  314.7 18.1 %collective-permute-done.3.out2_ref = bf16[256,1536]{1,0:T(8,128)(2,1)S(1)} collective-permute-done((bf16[256,1536]{1,0:T(8,128)(2,1)}, bf16[256,1536]{1,0:T(8,128)(2,1)S(1)}, u32[]{:S(2)}, u32[]{:S(2)}) %collective-permute-start.3) | collective-permute-done | bytes 786464 | tf_op jit(solution)/shard_map/ppermute | solution.py:2002
  332.8 14.8 %collective-permute-done.4.out4_ref = bf16[256,1536]{1,0:T(8,128)(2,1)S(1)} collective-permute-done((bf16[256,1536]{1,0:T(8,128)(2,1)}, bf16[256,1536]{1,0:T(8,128)(2,1)S(1)}, u32[]{:S(2)}, u32[]{:S(2)}) %collective-permute-start.4) | collective-permute-done | bytes 786464 | tf_op jit(solution)/shard_map/ppermute | solution.py:2002
  347.6 0.9 collective-permute-done.5.out6_ref
  348.5 1.1 copy-done.13
  349.6 46.8 %pieces_exchange.1 = (bf16[3072,1536]{1,0:T(8,128)(2,1)}, f32[2,1536]{1,0:T(2,128)S(1)}, bf16[1,256,1536]{2,1,0:T(8,128)(2,1)S(1)}) custom-call(bf16[384,1536]{1,0:T(8,128)(2,1)S(1)} %copy-done.10, f32[1,1536]{1,0:T(1,128)S(1)} %copy-done.33, f32[1,1536]{1,0:T(1,128)S(1)} %copy-done.31, f32[256,1536]{1,0:T(8,128)} %get-tuple-element.90.residual_ref, ...), custom_call_target="tpu_custom_call" | custom-call | tf_op jit(solution)/shard_map/pieces_exchange/pallas_call | solution.py:1798
  396.4 0.9 copy-done.15
  397.3 0.6 copy-done.34
  397.9 10.8 %spread_feed.1 = (f32[384,4096]{1,0:T(8,128)}, f32[384,4096]{1,0:T(8,128)}, f32[1024,1536]{1,0:T(8,128)}) custom-call(bf16[8,384,1536]{2,1,0:T(8,128)(2,1)} %bitcast.31, bf16[8,384,1536]{2,1,0:T(8,128)(2,1)} %bitcast.32, bf16[8,384,1536]{2,1,0:T(8,128)(2,1)} %bitcast.33), custom_call_target="tpu_custom_call" | custom-call | tf_op jit(solution)/shard_map/spread_feed/pallas_call | solution.py:1841
  408.7 1.4 dynamic-slice_reduce_fusion
  410.1 1.0 copy-done.23
  411.1 20.0 %shard_map.203 = bf16[4608,384]{1,0:T(8,128)(2,1)S(1)} custom-call(bf16[576,384]{1,0:T(8,128)(2,1)S(1)} %copy-done.23), custom_call_target="tpu_custom_call" | custom-call | tf_op jit(solution)/shard_map/pallas_call | solution.py:1173
  431.1 3.2 spread_attention.1
  434.4 0.9 copy.27
  435.3 1.1 copy.28
  (97 shorter events, 1.5 us)
Async XLA Ops:
  7.2 1.6 copy-start
  7.2 3.0 copy-start.2
  7.2 133.1 %all-gather.2.cloned.1.call-start = ((), (), s32[]{:S(2)}) async-start(), calls=%async_computation.2 | async-start | bytes 5898240 | tf_op jit(solution)/shard_map/all_gather | solution.py:1957
  10.2 1.3 copy-start.9
  11.5 40.2 %copy-start.3 = (bf16[1,256,1536]{2,1,0:T(8,128)(2,1)S(1)}, bf16[1,256,1536]{2,1,0:T(8,128)(2,1)}, u32[]{:S(2)}) copy-start(bf16[1,256,1536]{2,1,0:T(8,128)(2,1)} %param.14) | copy-start | bytes 2359300
  50.6 1.0 copy-start.35
  51.6 4.0 copy-start.43
  51.6 259.5 %reduce-scatter.3.cloned.1.call-start = ((), (), s32[]{:S(2)}) async-start(), calls=%async_computation.3 | async-start | bytes 5898240 | tf_op jit(solution)/shard_map/reduce_scatter | solution.py:1986
  51.7 79.6 %collective-permute-start = (bf16[256,1536]{1,0:T(8,128)(2,1)S(1)}, bf16[256,1536]{1,0:T(8,128)(2,1)}, u32[]{:S(2)}, u32[]{:S(2)}) collective-permute-start(bf16[256,1536]{1,0:T(8,128)(2,1)S(1)} %bitcast.19), channel_id=1, source_target_pairs={{0,8},{4,12},{8,0},{12,4},{16,24},{20,28},{24,16},{28,20},{1,9},{5... | collective-permute-start | bytes 2359304 | tf_op jit(solution)/shard_map/ppermute | solution.py:1978
  53.1 78.3 %collective-permute-start.1 = (bf16[256,1536]{1,0:T(8,128)(2,1)S(1)}, bf16[256,1536]{1,0:T(8,128)(2,1)}, u32[]{:S(2)}, u32[]{:S(2)}) collective-permute-start(bf16[256,1536]{1,0:T(8,128)(2,1)S(1)} %bitcast.20), channel_id=1, source_target_pairs={{0,16},{4,20},{8,24},{12,28},{16,0},{20,4},{24,8},{28,12},{1,17},{... | collective-permute-start | bytes 2359304 | tf_op jit(solution)/shard_map/ppermute | solution.py:1978
  54.3 77.1 %collective-permute-start.2 = (bf16[256,1536]{1,0:T(8,128)(2,1)S(1)}, bf16[256,1536]{1,0:T(8,128)(2,1)}, u32[]{:S(2)}, u32[]{:S(2)}) collective-permute-start(bf16[256,1536]{1,0:T(8,128)(2,1)S(1)} %bitcast.21), channel_id=1, source_target_pairs={{0,24},{4,28},{8,16},{12,20},{16,8},{20,12},{24,0},{28,4},{1,25},{... | collective-permute-start | bytes 2359304 | tf_op jit(solution)/shard_map/ppermute | solution.py:1978
  55.7 27.4 %copy-start.37 = (s32[16]{0:T(128)}, s32[16]{0:T(128)S(1)}, u32[]{:S(2)}) copy-start(s32[16]{0:T(128)S(1)} %select_reduce_fusion.slot_ref) | copy-start | bytes 196
  55.9 27.2 %copy-start.28 = (f32[2,16,128]{2,1,0:T(8,128)}, f32[2,16,128]{2,1,0:T(8,128)S(1)}, u32[]{:S(2)}) copy-start(f32[2,16,128]{2,1,0:T(8,128)S(1)} %pad_maximum_fusion.3.outer_ref) | copy-start | bytes 49156
  56.1 27.1 %copy-start.26 = (f32[2,128,128]{2,1,0:T(8,128)}, f32[2,128,128]{2,1,0:T(8,128)S(1)}, u32[]{:S(2)}) copy-start(f32[2,128,128]{2,1,0:T(8,128)S(1)} %pad_maximum_fusion.1.inner_ref) | copy-start | bytes 393220
  56.3 1.4 copy-start.36
  57.6 26.9 %copy-start.20 = (bf16[4,48,1536]{2,1,0:T(8,128)(2,1)S(1)}, bf16[4,48,1536]{2,1,0:T(8,128)(2,1)}, u32[]{:S(2)}) copy-start(bf16[4,48,1536]{2,1,0:T(8,128)(2,1)} %copy-done.19) | copy-start | bytes 1769476
  83.2 1.3 copy-start.39
  84.5 46.8 %copy-start.11 = (bf16[2048,192]{1,0:T(8,128)(2,1)}, bf16[2048,192]{1,0:T(8,128)(2,1)S(1)}, u32[]{:S(2)}) copy-start(bf16[2048,192]{1,0:T(8,128)(2,1)S(1)} %get-tuple-element.64.o_ref) | copy-start | bytes 2359300
  84.5 46.9 %copy-start.41 = (f32[8,512]{1,0:T(8,128)}, f32[8,512]{1,0:T(8,128)S(1)}, u32[]{:S(2)}) copy-start(f32[8,512]{1,0:T(8,128)S(1)} %get-tuple-element.81.lse_ref) | copy-start | bytes 49156
  128.1 0.9 copy-start.14
  129.0 0.9 copy-start.17
  211.7 1.1 copy-start.4
  211.8 198.4 %reduce-scatter.5.cloned.1.call-start = ((), (), s32[]{:S(2)}) async-start(), calls=%async_computation.4 | async-start | bytes 2211840 | tf_op jit(solution)/shard_map/reduce_scatter | solution.py:2008
  212.9 1.1 copy-start.18
  214.0 1.1 copy-start.22
  215.1 1.0 copy-start.25
  216.0 34.0 %copy-start.12 = (bf16[2048,192]{1,0:T(8,128)(2,1)S(1)}, bf16[2048,192]{1,0:T(8,128)(2,1)}, u32[]{:S(2)}) copy-start(bf16[2048,192]{1,0:T(8,128)(2,1)} %copy-done.11) | copy-start | bytes 2359300
  216.0 34.0 %copy-start.27 = (f32[2,128,128]{2,1,0:T(8,128)S(1)}, f32[2,128,128]{2,1,0:T(8,128)}, u32[]{:S(2)}) copy-start(f32[2,128,128]{2,1,0:T(8,128)} %copy-done.26) | copy-start | bytes 393220
  216.0 34.0 %copy-start.29 = (f32[2,16,128]{2,1,0:T(8,128)S(1)}, f32[2,16,128]{2,1,0:T(8,128)}, u32[]{:S(2)}) copy-start(f32[2,16,128]{2,1,0:T(8,128)} %copy-done.28) | copy-start | bytes 49156
  216.0 34.0 %copy-start.38 = (s32[16]{0:T(128)S(1)}, s32[16]{0:T(128)}, u32[]{:S(2)}) copy-start(s32[16]{0:T(128)} %copy-done.37) | copy-start | bytes 196
  216.0 34.0 %copy-start.40 = (bf16[2048,512]{1,0:T(8,128)(2,1)S(1)}, bf16[2048,512]{1,0:T(8,128)(2,1)}, u32[]{:S(2)}) copy-start(bf16[2048,512]{1,0:T(8,128)(2,1)} %copy-done.39) | copy-start | bytes 6291460
  216.0 34.0 %copy-start.42 = (f32[8,512]{1,0:T(8,128)S(1)}, f32[8,512]{1,0:T(8,128)}, u32[]{:S(2)}) copy-start(f32[8,512]{1,0:T(8,128)} %copy-done.41) | copy-start | bytes 49156
  250.0 20.3 %copy-start.8 = (f32[256,1536]{1,0:T(8,128)}, f32[256,1536]{1,0:T(8,128)S(1)}, u32[]{:S(2)}) copy-start(f32[256,1536]{1,0:T(8,128)S(1)} %get-tuple-element.83.residual_ref) | copy-start | bytes 4718596
  250.0 20.3 %copy-start.30 = (f32[1,1536]{1,0:T(1,128)}, f32[1,1536]{1,0:T(1,128)S(1)}, u32[]{:S(2)}) copy-start(f32[1,1536]{1,0:T(1,128)S(1)} %get-tuple-element.89.term_two_ref) | copy-start | bytes 18436
  270.3 1.3 copy-start.5
  309.4 1.1 copy-start.6
  311.1 37.3 %copy-start.31 = (f32[1,1536]{1,0:T(1,128)S(1)}, f32[1,1536]{1,0:T(1,128)}, u32[]{:S(2)}) copy-start(f32[1,1536]{1,0:T(1,128)} %copy-done.30) | copy-start | bytes 18436
  311.1 37.3 %copy-start.10 = (bf16[384,1536]{1,0:T(8,128)(2,1)S(1)}, bf16[384,1536]{1,0:T(8,128)(2,1)}, u32[]{:S(2)}) copy-start(bf16[384,1536]{1,0:T(8,128)(2,1)} %reduce-scatter.3.cloned.1.call-done.piece_ref) | copy-start | bytes 3538948
  311.1 37.3 %copy-start.33 = (f32[1,1536]{1,0:T(1,128)S(1)}, f32[1,1536]{1,0:T(1,128)}, u32[]{:S(2)}) copy-start(f32[1,1536]{1,0:T(1,128)} %copy-done.32) | copy-start | bytes 18436
  311.2 21.6 %collective-permute-start.3 = (bf16[256,1536]{1,0:T(8,128)(2,1)}, bf16[256,1536]{1,0:T(8,128)(2,1)S(1)}, u32[]{:S(2)}, u32[]{:S(2)}) collective-permute-start(bf16[256,1536]{1,0:T(8,128)(2,1)} %get-tuple-element.92), channel_id=1, source_target_pairs={{0,24},{4,28},{8,16},{12,20},{16,8},{20,12},{24,0},{28,4},{1,25},{... | collective-permute-start | bytes 2359304 | tf_op jit(solution)/shard_map/ppermute | solution.py:2002
  312.7 34.9 %collective-permute-start.4 = (bf16[256,1536]{1,0:T(8,128)(2,1)}, bf16[256,1536]{1,0:T(8,128)(2,1)S(1)}, u32[]{:S(2)}, u32[]{:S(2)}) collective-permute-start(bf16[256,1536]{1,0:T(8,128)(2,1)} %get-tuple-element.93), channel_id=1, source_target_pairs={{0,8},{4,12},{8,0},{12,4},{16,24},{20,28},{24,16},{28,20},{1,9},{5... | collective-permute-start | bytes 2359304 | tf_op jit(solution)/shard_map/ppermute | solution.py:2002
  313.3 35.2 %collective-permute-start.5 = (bf16[256,1536]{1,0:T(8,128)(2,1)}, bf16[256,1536]{1,0:T(8,128)(2,1)S(1)}, u32[]{:S(2)}, u32[]{:S(2)}) collective-permute-start(bf16[256,1536]{1,0:T(8,128)(2,1)} %get-tuple-element.94), channel_id=1, source_target_pairs={{0,16},{4,20},{8,24},{12,28},{16,0},{20,4},{24,8},{28,12},{1,17},{... | collective-permute-start | bytes 2359304 | tf_op jit(solution)/shard_map/ppermute | solution.py:2002
  348.5 1.1 copy-start.13
  396.4 0.9 copy-start.15
  410.1 1.0 copy-start.23
  431.1 3.3 copy-start.16
  431.1 4.1 copy-start.7
  434.4 2.0 copy-start.1
  (5 other events, 3.5 us)
Sparse Core Ops, SparseCore 0:
  51.8 88.5 all-gather.1
  211.9 82.7 reduce-scatter.2
  311.3 36.1 reduce-scatter.4

commit v5 on v4

--- a/solution.py
+++ b/solution.py
@@ -418,14 +418,17 @@
     pad_ref,
     inner_ref,
     outer_ref,
-    qkv_ref,
+    qkv_hbm,
     o_ref,
     ot_ref,
     lse_ref,
+    wp_hbm,
+    qkv_ref,
     wp,
     qs,
     vt,
     s_ref,
+    here,
 ):
     index = pl.program_id(0)
     block = xa_ref.shape[0]
@@ -436,24 +439,31 @@
     @pl.when(index == 0)
     def _():
         wp[...] = contract(w_ref[...], pad_ref[...], 1, 0).astype(jnp.bfloat16)
+        pltpu.make_async_copy(wp, wp_hbm, here.at[1]).start()
 
     x = jnp.concatenate([xa_ref[...], xb_ref[...]], axis=0).astype(jnp.float32)
     normed = x * lax.rsqrt(jnp.mean(x * x, axis=-1, keepdims=True) + norm_epsilon)
     gained = (normed * gain_ref[...]).astype(jnp.bfloat16)
     raw = contract(gained, wp[...], 1, 0)
     cosine, sine = tables(inner_ref, outer_ref, index, 2)
-    here = pl.ds(pl.multiple_of(index * tile, tile), tile)
+    here_rows = pl.ds(pl.multiple_of(index * tile, tile), tile)
     for head in range(heads):
         lanes = slice(head * LANES, (head + 1) * LANES)
         part = raw[:, lanes]
         if head <= GROUP:
             part = turn(part, cosine, sine)
         part = part.astype(jnp.bfloat16)
-        qkv_ref[here, lanes] = part
+        qkv_ref[here_rows, lanes] = part
         if head < GROUP:
             qs[head * tile : (head + 1) * tile, :] = part
         if head == heads - 1:
-            vt[:, here] = part.T
+            vt[:, here_rows] = part.T
+
+    def save(number):
+        place = pl.ds(pl.multiple_of(number * tile, tile), tile)
+        return pltpu.make_async_copy(qkv_ref.at[place, :], qkv_hbm.at[place, :], here.at[0])
+
+    save(index).start()
     queries = qs[...]
     key_at = lax.broadcasted_iota(jnp.int32, (tile, width), 0)
     query_at = lax.rem(lax.broadcasted_iota(jnp.int32, (tile, width), 1), tile)
@@ -465,7 +475,7 @@
         return contract(keys, queries, 1, 1) * binary_scale
 
     last = jnp.where(diagonal, scores_of(index), score_with_mask)
-    s_ref[here, :] = last
+    s_ref[here_rows, :] = last
     peak = jnp.max(last, axis=0, keepdims=True)
 
     def in_pairs(one, state):
@@ -507,6 +517,12 @@
         rows_at = slice(part * block, (part + 1) * block)
         o_ref[target, :] = out[rows_at, :]
         ot_ref[:, target] = out[rows_at, :].T
+
+    save(index).wait()
+
+    @pl.when(index == pl.num_programs(0) - 1)
+    def _():
+        pltpu.make_async_copy(wp, wp_hbm, here.at[1]).wait()
 
 
 def attend(slots, x, gain, w, pad, inner, outer):
@@ -531,16 +547,19 @@
                 whole(*outer.shape),
             ],
             out_specs=(
-                whole(rows, columns),
+                pl.BlockSpec(memory_space=pl.ANY),
                 whole(rows, GROUP * HEAD_SIZE),
                 whole(GROUP * HEAD_SIZE, rows),
                 whole(rows // tile, width),
-                whole(model, columns),
+                pl.BlockSpec(memory_space=pl.ANY),
             ),
             scratch_shapes=[
+                pltpu.VMEM((rows, columns), jnp.bfloat16),
+                pltpu.VMEM((model, columns), jnp.bfloat16),
                 pltpu.VMEM((width, LANES), jnp.bfloat16),
                 pltpu.VMEM((LANES, rows), jnp.bfloat16),
                 pltpu.VMEM((rows, width), jnp.float32),
+                pltpu.SemaphoreType.DMA((2,)),
             ],
         ),
         out_shape=(
@@ -550,7 +569,7 @@
             jax.ShapeDtypeStruct((rows // tile, width), jnp.float32),
             jax.ShapeDtypeStruct((model, columns), jnp.bfloat16),
         ),
-        compiler_params=pltpu.CompilerParams(vmem_limit_bytes=44 << 20),
+        compiler_params=pltpu.CompilerParams(vmem_limit_bytes=62 << 20),
         cost_estimate=pl.CostEstimate(
             flops=4 * GROUP * rows * rows * LANES // 2 + 2 * rows * model * columns,
             bytes_accessed=4 * rows * model,
@@ -721,7 +740,7 @@
             copy.wait_send()
 
 
-GATHER_COPIES = 13
+GATHER_COPIES = 14
 
 
 class PlaneGather:
@@ -730,71 +749,71 @@
         self.first = copies.next
         copies.next += GATHER_COPIES
 
-    def peer(self, bit):
-        return {"ctx": self.me ^ bit}
+    def copy(self, number):
+        bit, half, receiver = (
+            (0, 1, 2),
+            (0, 0, 4),
+            (0, 0, 2),
+            (0, 1, 4),
+            (0, 0, 1),
+            (0, 1, 1),
+            (2, 1, 4),
+            (4, 0, 2),
+            (2, 1, 1),
+            (4, 0, 1),
+            (2, 0, 1),
+            (4, 1, 1),
+            (6, 1, 1),
+            (6, 0, 1),
+        )[number]
+        place = self.part(self.me ^ bit, half)
+        source = self.own_half(half) if bit == 0 else place
+        return self.copies.make(self.first + number, source, place, {"ctx": self.me ^ receiver})
+
+    def send(self, *numbers):
+        for number in numbers:
+            self.copy(number).start()
+
+    def hear(self, number, bit, half):
+        self.copies.arrived(self.first + number, self.part(self.me ^ bit, half))
 
     def begin(self):
-        me, part, own, first = self.me, self.part, self.own_half, self.first
-        send = self.copies.send
-        send(first + 0, own(1), part(me, 1), self.peer(2))
-        send(first + 1, own(0), part(me, 0), self.peer(4))
-        send(first + 2, own(0), part(me, 0), self.peer(2))
-        send(first + 3, own(1), part(me, 1), self.peer(4))
-        send(first + 4, own(0), part(me, 0), self.peer(1))
-        send(first + 5, own(1), part(me, 1), self.peer(1))
-
-    def hear(self, number, slot, half, onward=None):
-        place = self.part(slot, half)
-        self.copies.arrived(self.first + number, place)
-        if onward is not None:
-            self.copies.send(self.first + onward[0], place, place, self.peer(onward[1]))
-
-    def share(self, number, slot, half):
-        place = self.part(slot, half)
-        self.copies.send(self.first + number, place, place, self.peer(1))
+        self.send(0, 1, 2, 3, 4, 5)
 
     def first_hop(self):
-        me = self.me
-        self.hear(0, me ^ 2, 1, (6, 4))
-        self.share(8, me ^ 2, 1)
-        self.hear(1, me ^ 4, 0, (7, 2))
-        self.share(9, me ^ 4, 0)
+        self.hear(0, 2, 1)
+        self.send(6, 8)
+        self.hear(1, 4, 0)
+        self.send(7, 9)
 
     def second_hop(self):
-        me = self.me
-        self.hear(2, me ^ 2, 0)
-        self.share(10, me ^ 2, 0)
-        self.hear(3, me ^ 4, 1)
-        self.share(11, me ^ 4, 1)
+        self.hear(2, 2, 0)
+        self.send(10)
+        self.hear(3, 4, 1)
+        self.send(11)
 
     def third_hop(self):
-        me = self.me
-        self.hear(6, me ^ 6, 1)
-        self.hear(7, me ^ 6, 0)
-        self.share(12, me ^ 6, slice(None))
+        self.hear(6, 6, 1)
+        self.send(12)
+        self.hear(7, 6, 0)
+        self.send(13)
+
+    def shared(self, bit):
+        for number, half in {1: (4, 0), 3: (8, 1), 5: (9, 0), 7: (12, 1)}[bit], {
+            1: (5, 1),
+            3: (10, 0),
+            5: (11, 1),
+            7: (13, 0),
+        }[bit]:
+            self.hear(number, bit, half)
 
     def last(self):
-        me, arrived, part = self.me, self.copies.arrived, self.part
-        arrived(self.first + 4, part(me ^ 1, 0))
-        arrived(self.first + 5, part(me ^ 1, 1))
-        arrived(self.first + 8, part(me ^ 3, 1))
-        arrived(self.first + 9, part(me ^ 5, 0))
-        arrived(self.first + 10, part(me ^ 3, 0))
-        arrived(self.first + 11, part(me ^ 5, 1))
-        arrived(self.first + 12, part(me ^ 7, slice(None)))
-
-
-def run_gathers(gathers):
-    for gather in gathers:
-        gather.begin()
-    for gather in gathers:
-        gather.first_hop()
-    for gather in gathers:
-        gather.second_hop()
-    for gather in gathers:
-        gather.third_hop()
-    for gather in gathers:
-        gather.last()
+        for bit in (1, 3, 5, 7):
+            self.shared(bit)
+
+    def finish(self):
+        for number in range(GATHER_COPIES):
+            self.copy(number).wait_send()
 
 
 def row_half(ref, rows):
@@ -867,6 +886,10 @@
                 self.move(step, upward, lambda copy: copy.wait_send())
 
 
+def in_hbm(count):
+    return [pl.BlockSpec(memory_space=pltpu.HBM)] * count
+
+
 def anywhere(count):
     return [pl.BlockSpec(memory_space=pl.ANY)] * count
 
@@ -881,7 +904,7 @@
     return copies
 
 
-def remote_params(number, mebibytes=48):
+def remote_params(number, mebibytes=62):
     return pltpu.CompilerParams(
         collective_id=number, has_side_effects=True, vmem_limit_bytes=mebibytes << 20
     )
@@ -902,6 +925,7 @@
     gaino_ref,
     feedo_ref,
     feed,
+    own,
     send,
     recv,
     here,
@@ -917,18 +941,20 @@
             (qkv_ref, qkvo_ref.at[index]),
             (wo_own, woo_ref.at[index]),
             (gain_ref, gaino_ref.at[index]),
-            (x_ref, part(me, slice(None))),
+            (x_ref, own),
         ],
-        here,
+        here.at[pl.ds(0, 4)],
     )
     start_barrier(me, index, line)
     copies = Copies(send, recv)
-    gather = PlaneGather(copies, me, row_half(x_ref, rows), part)
+    gather = PlaneGather(copies, me, row_half(own, rows), part)
     lines = [
         LineGather(copies, index, line, own, lambda slot, ref=ref: ref.at[slot])
         for own, ref in ((qkv_ref, qkvo_ref), (gain_ref, gaino_ref), (wo_own, woo_ref))
     ]
+    local.pop().wait()
     gather.begin()
+    local += local_copies([(own, part(me, slice(None)))], here.at[pl.ds(3, 1)])
     for each in lines:
         each.begin()
     width = feed.shape[1] // 3
@@ -960,9 +986,9 @@
             packed = local_copies([(feed, feedo_ref)], here.at[pl.ds(4 + len(pairs), 1)])
     gather.third_hop()
     gather.last()
+    gather.finish()
     for each in lines:
         each.finish()
-    copies.finish()
     for copy in local:
         copy.wait()
     packed[0].wait()
@@ -986,10 +1012,11 @@
             jax.ShapeDtypeStruct((line, *gains.shape), gains.dtype),
             jax.ShapeDtypeStruct(feed, gate.dtype),
         ),
-        in_specs=anywhere(7),
+        in_specs=in_hbm(1) + anywhere(1) + in_hbm(1) + anywhere(1) + in_hbm(3),
         out_specs=tuple(anywhere(5)),
         scratch_shapes=[
             pltpu.VMEM(feed, gate.dtype),
+            pltpu.VMEM(x.shape, x.dtype),
             pltpu.SemaphoreType.DMA((count,)),
             pltpu.SemaphoreType.DMA((count,)),
             pltpu.SemaphoreType.DMA((4 + packing,)),
@@ -999,7 +1026,7 @@
     )(x, qkv, wo, gains, gate, up, down)
 
 
-def deal_rows(copies, me, pieces, wo_ref, place, recv_first):
+def deal_rows(copies, me, pieces, wo_ref, place, recv_first, here):
     to_first = pieces * lax.rem(me, 2)
     line_slot = lax.div(me, 2)
 
@@ -1020,7 +1047,7 @@
 
         @pl.when(to_first + piece == me)
         def _(piece=piece):
-            place(line_slot)[...] = wo_ref[piece]
+            pltpu.make_async_copy(wo_ref.at[piece], place(line_slot), here).start()
 
     def finish(line):
         for slot in range(line):
@@ -1037,20 +1064,86 @@
             def _(piece=piece):
                 copy(piece).wait_send()
 
+            @pl.when(to_first + piece == me)
+            def _(piece=piece):
+                pltpu.make_async_copy(wo_ref.at[piece], place(line_slot), here).wait()
+
     return finish
+
+
+class NearShares:
+    def __init__(self, copies, me, refs, place):
+        self.copies, self.me, self.refs, self.place = copies, me, refs, place
+        self.first = copies.next
+        copies.next += 7
+
+    def copy(self, number):
+        me, (own, near_x, near_y) = self.me, self.refs
+        half = own.shape[0] // 2
+        partner = {"ctx": me ^ 1}
+        source, target, peer = (
+            lambda: (near_y.at[pl.ds(0, half)], self.place(me ^ 4, 0), {"ctx": me ^ 2}),
+            lambda: (near_x.at[pl.ds(half, half)], self.place(me ^ 2, 1), {"ctx": me ^ 4}),
+            lambda: (own, self.place(me, None), partner),
+            lambda: (near_x, self.place(me ^ 2, None), partner),
+            lambda: (near_y, self.place(me ^ 4, None), partner),
+            lambda: (self.place(me ^ 6, 0), self.place(me ^ 6, 0), partner),
+            lambda: (self.place(me ^ 6, 1), self.place(me ^ 6, 1), partner),
+        )[number]()
+        return self.copies.make(self.first + number, source, target, peer)
+
+    def begin(self):
+        for number in range(5):
+            self.copy(number).start()
+
+    def diagonal(self):
+        for side in (0, 1):
+            self.copies.arrived(self.first + side, self.place(self.me ^ 6, side))
+            self.copy(5 + side).start()
+
+    def shared(self, bit):
+        if bit == 7:
+            for side in (0, 1):
+                self.copies.arrived(self.first + 5 + side, self.place(self.me ^ 7, side))
+        else:
+            self.copies.arrived(self.first + 2 + bit // 2, self.place(self.me ^ bit, None))
+
+    def finish(self):
+        for number in range(7):
+            self.copy(number).wait_send()
+
+
+def block_place(ref, rows):
+    half = rows // 2
+
+    def place(slot, side):
+        if side is None:
+            return ref.at[pl.ds(pl.multiple_of(slot * rows, rows), rows), :]
+        return ref.at[pl.ds(pl.multiple_of(slot * rows + side * half, half), half), :]
+
+    return place
 
 
 def second_kernel(
     o_ref,
-    wo_ref,
-    ot_ref,
+    wo0_hbm,
+    wo2_hbm,
+    wo4_hbm,
+    dy2_hbm,
+    dy4_hbm,
+    x_hbm,
+    gain_ref,
+    own_hbm,
+    dy6_hbm,
+    residual_hbm,
+    normed_hbm,
+    scale_ref,
+    gained_hbm,
+    near_x_hbm,
+    near_y_hbm,
     x_ref,
-    gain_ref,
-    own_ref,
-    dealt_ref,
     residual_ref,
     normed_ref,
-    scale_ref,
     gained_ref,
     att,
     wo,
@@ -1060,12 +1153,20 @@
 ):
     me = lax.axis_index("ctx")
     rows = x_ref.shape[0]
+    half = rows // 2
+    middle = wo.shape[0] // 2
+
+    def wo_place(slot, side):
+        return wo.at[:, slot] if side is None else wo.at[pl.ds(side * middle, middle), slot]
+
+    own_wo = (wo0_hbm, wo2_hbm, wo4_hbm)
     local = local_copies(
         [
             (o_ref.at[pl.ds(pl.multiple_of(me * rows, rows), rows), :], att.at[me]),
-            (wo_ref, wo.at[:, me]),
-        ],
-        here.at[pl.ds(0, 2)],
+            (x_hbm, x_ref),
+        ]
+        + [(ref, wo_place(me ^ (2 * number), None)) for number, ref in enumerate(own_wo)],
+        here.at[pl.ds(0, 5)],
     )
     start_barrier(me)
     copies = Copies(send, recv)
@@ -1077,94 +1178,113 @@
     for bit in (6, 7, 4, 5, 2, 3, 1):
         numbers[bit] = copies.number()
         copies.send(numbers[bit], block(me ^ bit), att.at[me], {"ctx": me ^ bit})
-    line = wo_ref.shape[0]
-    middle = line // 2
-
-    def wo_half(side):
-        return wo_ref.at[pl.ds(side * middle, middle)]
-
-    def wo_part(slot, side):
-        if isinstance(side, slice):
-            return wo.at[:, slot]
-        return wo.at[pl.ds(side * middle, middle), slot]
-
-    wo_gather = PlaneGather(copies, me, wo_half, wo_part)
-    wo_gather.begin()
-    wo_gather.first_hop()
-    wo_gather.second_hop()
-    pieces = ot_ref.shape[0]
-    first = copies.next
-    copies.next += pieces
-    finish = deal_rows(copies, me, pieces, ot_ref, lambda slot: dealt_ref.at[slot], first)
-    wo_gather.third_hop()
-    wo_gather.last()
+    shares = NearShares(copies, me, own_wo, wo_place)
+    shares.begin()
+    dy_first = copies.next
+    copies.next += 2
+    upper, lower = pl.ds(0, half), pl.ds(half, half)
+    copies.send(dy_first, dy4_hbm.at[upper, :], dy6_hbm.at[upper, :], {"ctx": me ^ 2})
+    copies.send(dy_first + 1, dy2_hbm.at[lower, :], dy6_hbm.at[lower, :], {"ctx": me ^ 4})
+    shares.diagonal()
+    for bit in (1, 3, 5, 7):
+        shares.shared(bit)
     for bit, number in numbers.items():
         copies.arrived(number, att.at[me ^ bit])
     for copy in local:
         copy.wait()
     per_head = 2 * GROUP
     own = wo.at[lax.div(me, 2), pl.ds(per_head * lax.rem(me, 2), per_head)]
-    keep = local_copies([(own, own_ref)], here.at[pl.ds(2, 1)])
+    keep = local_copies([(own, own_hbm)], here.at[pl.ds(5, 1)])
     plane = att.shape[0]
-    total = x_ref[...].astype(jnp.float32)
-    for slot in range(plane):
-        first = per_head * (slot % 2)
-        weight = jnp.concatenate(
-            [wo[slot // 2, first + piece] for piece in range(per_head)], axis=0
-        )
-        total = total + contract(att[slot], weight, 1, 0)
-    residual_ref[...] = total
-    scale = lax.rsqrt(jnp.mean(total * total, axis=-1, keepdims=True) + norm_epsilon)
-    normed = total * scale
-    scale_ref[...] = scale
-    normed_ref[...] = normed
-    gained_ref[...] = (normed * gain_ref[...]).astype(jnp.bfloat16)
-    finish(line)
-    keep[0].wait()
+    near = copies.next
+    for side in (0, 1):
+        at = pl.ds(side * half, half)
+        total = x_ref[at, :].astype(jnp.float32)
+        for slot in range(plane):
+            first = per_head * (slot % 2)
+            weight = jnp.concatenate(
+                [wo[slot // 2, first + piece] for piece in range(per_head)], axis=0
+            )
+            total = total + contract(att[slot, at, :], weight, 1, 0)
+        residual_ref[at, :] = total
+        scale = lax.rsqrt(jnp.mean(total * total, axis=-1, keepdims=True) + norm_epsilon)
+        normed = total * scale
+        scale_ref[at, :] = scale
+        normed_ref[at, :] = normed
+        gained_ref[at, :] = (normed * gain_ref[...]).astype(jnp.bfloat16)
+        for number, target, bit in ((0, near_x_hbm, 2), (1, near_y_hbm, 4)):
+            copies.send(
+                near + 2 * side + number,
+                gained_ref.at[at, :],
+                target.at[at, :],
+                {"ctx": me ^ bit},
+            )
+    keep += local_copies(
+        [(residual_ref, residual_hbm), (normed_ref, normed_hbm), (gained_ref, gained_hbm)],
+        here.at[pl.ds(6, 3)],
+    )
+    for copy in keep:
+        copy.wait()
+    shares.finish()
+    copies.arrived(dy_first, dy6_hbm.at[upper, :])
+    copies.arrived(dy_first + 1, dy6_hbm.at[lower, :])
+    for side in (0, 1):
+        at = pl.ds(side * half, half)
+        copies.arrived(near + 2 * side, near_x_hbm.at[at, :])
+        copies.arrived(near + 2 * side + 1, near_y_hbm.at[at, :])
     copies.finish()
 
 
-def second_exchange(o, wo, ot, x, gain):
+def second_exchange(o, own_wo, grads, x, gain):
     plane = lax.axis_size("ctx")
     rows = x.shape[0]
-    line, part, model = wo.shape
-    pieces = 2 * GROUP
-    ot = ot.reshape(pieces, -1, ot.shape[1])
-    count = GATHER_COPIES + 7 + pieces
+    line, part, model = own_wo[0].shape
+    count = 7 + 7 + 2 + 4
     f32 = jnp.float32
     return pl.pallas_call(
         second_kernel,
         out_shape=(
-            jax.ShapeDtypeStruct((pieces, part, model), wo.dtype),
-            jax.ShapeDtypeStruct((line, *ot.shape[1:]), ot.dtype),
+            jax.ShapeDtypeStruct((2 * GROUP, part, model), own_wo[0].dtype),
+            jax.ShapeDtypeStruct((rows, model), x.dtype),
             jax.ShapeDtypeStruct((rows, model), f32),
             jax.ShapeDtypeStruct((rows, model), f32),
             jax.ShapeDtypeStruct((rows, 1), f32),
-            jax.ShapeDtypeStruct((rows, model), x.dtype),
+            *[jax.ShapeDtypeStruct((rows, model), x.dtype)] * 3,
         ),
-        in_specs=anywhere(2) + in_vmem(3),
-        out_specs=(*anywhere(1), *in_vmem(5)),
+        in_specs=in_hbm(7) + in_vmem(1),
+        out_specs=(*anywhere(4), *in_vmem(1), *anywhere(3)),
         scratch_shapes=[
+            pltpu.VMEM(x.shape, x.dtype),
+            pltpu.VMEM(x.shape, f32),
+            pltpu.VMEM(x.shape, f32),
+            pltpu.VMEM(x.shape, x.dtype),
             pltpu.VMEM((plane, rows, o.shape[1]), o.dtype),
-            pltpu.VMEM((line, plane, part, model), wo.dtype),
+            pltpu.VMEM((line, plane, part, model), x.dtype),
             pltpu.SemaphoreType.DMA((count,)),
             pltpu.SemaphoreType.DMA((count,)),
-            pltpu.SemaphoreType.DMA((3,)),
+            pltpu.SemaphoreType.DMA((9,)),
         ],
         compiler_params=remote_params(2),
         name="second_exchange",
-    )(o, wo, ot, x, gain)
-
-
-def gather_kernel(x_ref, xo_ref, send, recv, here):
+    )(o, *own_wo, *grads, x, gain)
+
+
+def gather_kernel(x_ref, xo_ref, own, send, recv, here):
     me = lax.axis_index("ctx")
     rows = x_ref.shape[0]
+    fetch = local_copies([(x_ref, own)], here)
     start_barrier(me)
+    fetch[0].wait()
     part = row_part(xo_ref, rows)
-    local = local_copies([(x_ref, part(me, slice(None)))], here)
     copies = Copies(send, recv)
-    run_gathers([PlaneGather(copies, me, row_half(x_ref, rows), part)])
-    copies.finish()
+    gather = PlaneGather(copies, me, row_half(own, rows), part)
+    gather.begin()
+    local = local_copies([(own, part(me, slice(None)))], here)
+    gather.first_hop()
+    gather.second_hop()
+    gather.third_hop()
+    gather.last()
+    gather.finish()
     local[0].wait()
 
 
@@ -1173,80 +1293,56 @@
     return pl.pallas_call(
         gather_kernel,
         out_shape=jax.ShapeDtypeStruct((plane * x.shape[0], x.shape[1]), x.dtype),
-        in_specs=anywhere(1),
+        in_specs=in_hbm(1),
         out_specs=anywhere(1)[0],
         scratch_shapes=[
+            pltpu.VMEM(x.shape, x.dtype),
             pltpu.SemaphoreType.DMA((GATHER_COPIES,)),
             pltpu.SemaphoreType.DMA((GATHER_COPIES,)),
             pltpu.SemaphoreType.DMA((1,)),
         ],
-        compiler_params=remote_params(number),
+        compiler_params=remote_params(number, 24),
     )(x)
 
 
 def third_kernel(
-    sum_ref,
-    normed_ref,
-    scale_ref,
-    gain_ref,
-    dy_ref,
-    ot_ref,
-    wo_ref,
-    residual_ref,
-    term_ref,
-    do_ref,
-    dwo_ref,
-    own,
-    all_grads,
-    dwo,
-    send,
-    recv,
+    g0_hbm, g2_hbm, g4_hbm, ot_hbm, wo_hbm, do_ref, dwo_ref, ot_ref, wo_ref, all_grads, dwo, send, recv, here
 ):
     me = lax.axis_index("ctx")
-    rows = dy_ref.shape[0]
+    rows = g0_hbm.shape[0]
+    place = block_place(all_grads, rows)
+    own_rows = (g0_hbm, g2_hbm, g4_hbm)
+    fetch = local_copies(
+        [(ref, place(me ^ (2 * number), None)) for number, ref in enumerate(own_rows)]
+        + [(ot_hbm, ot_ref), (wo_hbm, wo_ref)],
+        here,
+    )
     start_barrier(me)
     copies = Copies(send, recv)
-    part = row_part(all_grads, rows)
-    gather = PlaneGather(copies, me, row_half(own, rows), part)
-    grad_normed, normed = sum_ref[...], normed_ref[...]
-    products = grad_normed * normed
-    scaled = grad_normed * gain_ref[...]
-    mean = jnp.mean(scaled * normed, axis=-1, keepdims=True)
-    residual = dy_ref[...].astype(jnp.float32) + scale_ref[...] * (scaled - normed * mean)
-    own[...] = residual.astype(jnp.bfloat16)
-    gather.begin()
-    residual_ref[...] = residual
-    term_ref[...] = jnp.sum(products, axis=0, keepdims=True)
-    part(me, slice(None))[...] = own[...]
+    shares = NearShares(copies, me, own_rows, place)
+    shares.begin()
     dwo[...] = jnp.zeros_like(dwo)
+    for copy in fetch:
+        copy.wait()
 
     def step(order, carry):
-        for number, slot, sides, when in (
-            (4, 1, 0, 1),
-            (5, 1, 1, 1),
-            (8, 3, 1, 3),
-            (10, 3, 0, 3),
-            (9, 5, 0, 5),
-            (11, 5, 1, 5),
-            (12, 7, slice(None), 7),
-        ):
-
-            @pl.when(order == when)
-            def _(number=number, slot=slot, sides=sides):
-                copies.arrived(gather.first + number, gather.part(me ^ slot, sides))
-
-        place = pl.ds(pl.multiple_of((me ^ order) * rows, rows), rows)
-        grads = all_grads[place, :]
-        do_ref[place, :] = contract(grads, wo_ref[...], 1, 1).astype(jnp.bfloat16)
-        dwo[...] += contract(ot_ref[:, place], grads, 1, 0)
+        @pl.when(order == 5)
+        def _():
+            shares.diagonal()
+
+        for bit in (1, 3, 5, 7):
+
+            @pl.when(order == bit)
+            def _(bit=bit):
+                shares.shared(bit)
+
+        here_rows = pl.ds(pl.multiple_of((me ^ order) * rows, rows), rows)
+        grads = all_grads[here_rows, :]
+        do_ref[here_rows, :] = contract(grads, wo_ref[...], 1, 1).astype(jnp.bfloat16)
+        dwo[...] += contract(ot_ref[:, here_rows], grads, 1, 0)
         return carry
 
-    lax.fori_loop(0, 2, step, 0)
-    gather.first_hop()
-    gather.second_hop()
-    lax.fori_loop(2, 6, step, 0)
-    gather.third_hop()
-    lax.fori_loop(6, 8, step, 0)
+    lax.fori_loop(0, 8, step, 0)
     line, _, across = dwo_ref.shape
     for slot in range(line):
         rows_at = slice(slot * HALF, (slot + 1) * HALF)
@@ -1255,33 +1351,33 @@
             dwo_ref[slot, number * HALF : (number + 1) * HALF, :] = dwo[rows_at, columns].astype(
                 jnp.bfloat16
             )
-    copies.finish()
-
-
-def third_exchange(line, grad_normed, normed, scale, gain, dy, ot, wo, across):
+    shares.finish()
+
+
+def third_exchange(line, own_rows, ot, wo, across):
     plane = lax.axis_size("ctx")
-    rows, model = dy.shape
+    rows, model = own_rows[0].shape
     half_type, f32 = jnp.bfloat16, jnp.float32
     return pl.pallas_call(
         third_kernel,
         out_shape=(
-            jax.ShapeDtypeStruct((rows, model), f32),
-            jax.ShapeDtypeStruct((1, model), f32),
             jax.ShapeDtypeStruct((plane * rows, wo.shape[0]), half_type),
             jax.ShapeDtypeStruct((line, HALF * model // across, across), half_type),
         ),
-        in_specs=in_vmem(7),
-        out_specs=tuple(in_vmem(4)),
+        in_specs=anywhere(5),
+        out_specs=tuple(in_vmem(2)),
         scratch_shapes=[
-            pltpu.VMEM((rows, model), half_type),
+            pltpu.VMEM(ot.shape, ot.dtype),
+            pltpu.VMEM(wo.shape, wo.dtype),
             pltpu.VMEM((plane * rows, model), half_type),
             pltpu.VMEM((line * HALF, model), f32),
-            pltpu.SemaphoreType.DMA((GATHER_COPIES,)),
-            pltpu.SemaphoreType.DMA((GATHER_COPIES,)),
+            pltpu.SemaphoreType.DMA((7,)),
+            pltpu.SemaphoreType.DMA((7,)),
+            pltpu.SemaphoreType.DMA((5,)),
         ],
         compiler_params=remote_params(6),
         name="third_exchange",
-    )(grad_normed, normed, scale, gain, dy, ot, wo)
+    )(*own_rows, ot, wo)
 
 
 REDUCE_COPIES = 10
@@ -1300,10 +1396,13 @@
         return ref.at[slot, pl.ds(half * self.half, self.half), :]
 
     def share(self, order):
+        self.shared(order).start()
+
+    def shared(self, order):
         partner = self.me ^ 1
-        bit = (6, 2, 4, 0)[order]
-        self.copies.send(
-            self.first + order, self.block(partner ^ bit), self.heard.at[order], {"ctx": partner}
+        source = self.block(partner ^ (6, 2, 4, 0)[order])
+        return self.copies.make(
+            self.first + order, source, self.heard.at[order], {"ctx": partner}
         )
 
     def combine(self, order, rows, extra=None):
@@ -1328,6 +1427,8 @@
         return self.copies.make(self.first + number, held, landed, peer)
 
     def finish(self):
+        for order in range(4):
+            self.shared(order).wait_send()
         for number in range(4, REDUCE_COPIES):
             self.onward(number).wait_send()
 
@@ -1338,18 +1439,15 @@
         self.onward(4).start()
         self.onward(5).start()
 
+    def neighbour_send(self, order):
+        first, half = self.first, self.half
+        self.copies.arrived(first + order, self.heard.at[order])
+        self.combine(order, pl.ds((order - 1) * half, half))
+        self.onward(5 + order).start()
+
     def neighbour_sends(self):
-        first, half = self.first, self.half
-        self.copies.arrived(first + 1, self.heard.at[1])
-        self.combine(1, pl.ds(0, half))
-        self.onward(6).start()
-        self.copies.arrived(first + 2, self.heard.at[2])
-        self.combine(2, pl.ds(half, half))
-        self.onward(7).start()
-
-    def first_sends(self):
-        self.diagonal_sends()
-        self.neighbour_sends()
+        self.neighbour_send(1)
+        self.neighbour_send(2)
 
     def second_sends(self):
         first, half = self.first, self.half
@@ -1361,7 +1459,9 @@
         arrived(first + 4, side(landed, 0, 0))
         self.combine(2, upper, landed[0, upper, :].astype(jnp.float32))
         self.onward(9).start()
-        arrived(first + 3, self.heard.at[3])
+
+    def own_share(self):
+        self.copies.arrived(self.first + 3, self.heard.at[3])
 
     def sum_half(self, which):
         first, half = self.first, self.half
@@ -1378,18 +1478,30 @@
 
 def feed_kernel(
     line,
-    g_ref,
+    g0_hbm,
+    g2_hbm,
+    g4_hbm,
     dy0_hbm,
     dy2_hbm,
     dy4_hbm,
     dy6_hbm,
     w_hbm,
-    sum_ref,
+    ot_hbm,
+    normed_hbm,
+    scale_ref,
+    gain_ref,
+    residual_ref,
+    term_ref,
+    own_ref,
+    near_x_ref,
+    near_y_ref,
+    dealt_hbm,
     out6_hbm,
     out2_hbm,
     out4_hbm,
     out0_hbm,
     dw_hbm,
+    normed_ref,
     w_ref,
     dw_ref,
     down_ref,
@@ -1410,32 +1522,47 @@
     here,
 ):
     me = lax.axis_index("ctx")
-    rows = g_ref.shape[0]
+    rows = residual_ref.shape[0]
+    half = rows // 2
     width, model = down_ref.shape
     blocks = model // width
     unit = width // line
+    partner = {"ctx": me ^ 1}
 
     def at(slot):
         return pl.ds(pl.multiple_of(slot * rows, rows), rows)
 
-    heard_grads = (dy0_hbm, dy2_hbm, dy4_hbm, dy6_hbm)
+    own_grads = (dy0_hbm, dy2_hbm, dy4_hbm, dy6_hbm)
+    own_rows = (g0_hbm, g2_hbm, g4_hbm)
+    place = block_place(all_g, rows)
+    dy_place = block_place(dy_ref, rows)
     local = local_copies(
         [(w_hbm, w_ref)]
-        + [(ref, dy_ref.at[at(me ^ (2 * number)), :]) for number, ref in enumerate(heard_grads)],
-        here.at[pl.ds(0, 5)],
+        + [(ref, place(me ^ (2 * number), None)) for number, ref in enumerate(own_rows)]
+        + [(ref, dy_place(me ^ (2 * number), None)) for number, ref in enumerate(own_grads)]
+        + [(normed_hbm, normed_ref)],
+        here.at[pl.ds(0, 9)],
     )
     start_barrier(me)
     copies = Copies(send, recv)
-    gather = PlaneGather(copies, me, row_half(g_ref, rows), row_part(all_g, rows))
-    gather.begin()
+    shares = NearShares(copies, me, own_rows, place)
+    shares.begin()
     dy_first = copies.next
     copies.next += 4
-    for number, ref in enumerate(heard_grads):
-        place = dy_ref.at[at(me ^ (2 * number)), :]
-        copies.send(dy_first + number, ref, place, {"ctx": me ^ 1})
-    all_g[at(me), :] = g_ref[...]
-    for copy in local:
-        copy.wait()
+    for number, ref in enumerate(own_grads):
+        copies.send(dy_first + number, ref, dy_place(me ^ (2 * number), None), partner)
+    deal_first = copies.next
+    copies.next += ot_hbm.shape[0]
+    dealt = deal_rows(
+        copies,
+        me,
+        ot_hbm.shape[0],
+        ot_hbm,
+        lambda slot: dealt_hbm.at[slot],
+        deal_first,
+        here.at[9],
+    )
+    local[0].wait()
     gate_ref, up_ref = w_ref.at[:, :width], w_ref.at[:, width : 2 * width]
     for z in range(line):
         for number in range(blocks):
@@ -1443,6 +1570,9 @@
             down_ref[pl.ds(z * unit, unit), number * width : (number + 1) * width] = w_ref[
                 source, 2 * width :
             ]
+    for copy in local[1:]:
+        copy.wait()
+    gain = gain_ref[...]
 
     def block(slot):
         return part.at[at(slot), :]
@@ -1471,43 +1601,53 @@
             contract(grad_gate, gate_ref[...], 1, 1) + contract(grad_up, up_ref[...], 1, 1)
         ).astype(jnp.bfloat16)
 
-    def step(order, carry):
-        for number in range(4):
-
-            @pl.when(order == 2 * number + 1)
-            def _(number=number):
-                place = dy_ref.at[at(me ^ (2 * number + 1)), :]
-                copies.arrived(dy_first + number, place)
-
-        for number, slot, sides, when in (
-            (4, 1, 0, 1),
-            (5, 1, 1, 1),
-            (8, 3, 1, 3),
-            (10, 3, 0, 3),
-            (9, 5, 0, 5),
-            (11, 5, 1, 5),
-            (12, 7, slice(None), 7),
-        ):
-
-            @pl.when(order == when)
-            def _(number=number, slot=slot, sides=sides):
-                copies.arrived(gather.first + number, gather.part(me ^ slot, sides))
-
-        chunk(order)
+    def step(number, carry):
+        @pl.when(number == 1)
+        def _():
+            shares.shared(3)
+            copies.arrived(dy_first + 1, dy_place(me ^ 3, None))
+
+        @pl.when(number == 2)
+        def _():
+            reduce.share(1)
+            shares.diagonal()
+
+        @pl.when(number == 3)
+        def _():
+            reduce.neighbour_send(1)
+            shares.shared(7)
+            copies.arrived(dy_first + 3, dy_place(me ^ 7, None))
+
+        @pl.when(number == 4)
+        def _():
+            reduce.share(0)
+            reduce.diagonal_sends()
+
+        @pl.when(number == 5)
+        def _():
+            shares.shared(5)
+            copies.arrived(dy_first + 2, dy_place(me ^ 5, None))
+
+        @pl.when(number == 6)
+        def _():
+            reduce.share(2)
+            reduce.neighbour_send(2)
+
+        @pl.when(number == 7)
+        def _():
+            reduce.second_sends()
+            shares.shared(1)
+            copies.arrived(dy_first, dy_place(me ^ 1, None))
+
+        pair = lax.div(number, 2)
+        chunk(
+            lax.rem(number, 2)
+            + jnp.where(pair == 0, 2, jnp.where(pair == 1, 6, jnp.where(pair == 2, 4, 0)))
+        )
         return carry
 
-    lax.fori_loop(0, 2, step, 0)
-    gather.first_hop()
-    gather.second_hop()
+    lax.fori_loop(0, 8, step, 0)
     reduce.share(3)
-    lax.fori_loop(2, 6, step, 0)
-    reduce.share(1)
-    reduce.share(2)
-    gather.third_hop()
-    reduce.neighbour_sends()
-    lax.fori_loop(6, 8, step, 0)
-    reduce.share(0)
-
     out_first = copies.next
     copies.next += 4
 
@@ -1519,8 +1659,6 @@
 
     def out_of(slot):
         return contract(hid[at(slot), :], down_ref[...], 1, 0)
-
-    partner = {"ctx": me ^ 1}
 
     def give(number, carry):
         out_mine[number] = out_of(me ^ 1 ^ bit_of(number)).astype(jnp.bfloat16)
@@ -1544,10 +1682,29 @@
             dw_ref[columns, side * width : (side + 1) * width] = total.T
         return carry
 
-    lax.fori_loop(0, 1, give, 0)
-    reduce.diagonal_sends()
-    lax.fori_loop(1, 4, give, 0)
-    reduce.second_sends()
+    reduce.own_share()
+    lax.fori_loop(0, 4, give, 0)
+    near = copies.next
+    copies.next += 4
+    total = jnp.zeros_like(gain)
+    for which in (1, 0):
+        rows_at = pl.ds(which * half, half)
+        grad_normed, normed = reduce.sum_half(which), normed_ref[rows_at, :]
+        scaled = grad_normed * gain
+        mean = jnp.mean(scaled * normed, axis=-1, keepdims=True)
+        total = total + jnp.sum(grad_normed * normed, axis=0, keepdims=True)
+        dy = dy_ref[pl.ds(pl.multiple_of(me * rows + which * half, half), half), :]
+        residual = dy.astype(jnp.float32) + scale_ref[rows_at, :] * (scaled - normed * mean)
+        residual_ref[rows_at, :] = residual
+        own_ref[rows_at, :] = residual.astype(jnp.bfloat16)
+        for number, target, bit in ((0, near_x_ref, 2), (1, near_y_ref, 4)):
+            copies.send(
+                near + 2 * which + number,
+                own_ref.at[rows_at, :],
+                target.at[rows_at, :],
+                {"ctx": me ^ bit},
+            )
+    term_ref[...] = total
     lax.fori_loop(0, 4, keep, 0)
     outputs = local_copies(
         [
@@ -1558,34 +1715,43 @@
     )
     lax.fori_loop(0, blocks, weights, 0)
     outputs += local_copies([(dw_ref, dw_hbm)], here.at[pl.ds(4, 1)])
-    half = rows // 2
-    for which in (1, 0):
-        sum_ref[pl.ds(which * half, half), :] = reduce.sum_half(which)
     for number in range(4):
         out_copy(number).wait_send()
     for copy in outputs:
         copy.wait()
+    dealt(dealt_hbm.shape[0])
+    shares.finish()
     reduce.finish()
+    for which in (1, 0):
+        rows_at = pl.ds(which * half, half)
+        copies.arrived(near + 2 * which, near_x_ref.at[rows_at, :])
+        copies.arrived(near + 2 * which + 1, near_y_ref.at[rows_at, :])
     copies.finish()
 
 
-def feed(g, grads, w):
+def feed(own_rows, grads, w, ot, normed, scale, gain):
     plane, line = lax.axis_size("ctx"), lax.axis_size("fsdp")
-    rows, model = g.shape
+    rows, model = own_rows[0].shape
     tokens = plane * rows
     width = w.shape[1] // 3
-    count = GATHER_COPIES + REDUCE_COPIES + 8
+    pieces = 2 * GROUP
+    ot = ot.reshape(pieces, -1, ot.shape[1])
+    count = 7 + 4 + pieces + REDUCE_COPIES + 4 + 4
     half_type = jnp.bfloat16
     return pl.pallas_call(
         functools.partial(feed_kernel, line),
         out_shape=(
             jax.ShapeDtypeStruct((rows, model), jnp.float32),
+            jax.ShapeDtypeStruct((1, model), jnp.float32),
+            *[jax.ShapeDtypeStruct((rows, model), half_type)] * 3,
+            jax.ShapeDtypeStruct((line, *ot.shape[1:]), ot.dtype),
             *[jax.ShapeDtypeStruct((rows, model), half_type)] * 4,
             jax.ShapeDtypeStruct(w.shape, half_type),
         ),
-        in_specs=in_vmem(1) + anywhere(5),
-        out_specs=(*in_vmem(1), *anywhere(5)),
+        in_specs=anywhere(10) + in_vmem(2),
+        out_specs=(*in_vmem(3), *anywhere(8)),
         scratch_shapes=[
+            pltpu.VMEM((rows, model), jnp.float32),
             pltpu.VMEM(w.shape, half_type),
             pltpu.VMEM(w.shape, half_type),
             pltpu.VMEM((width, model), half_type),
@@ -1603,28 +1769,30 @@
             pltpu.VMEM((4, rows, model), half_type),
             pltpu.SemaphoreType.DMA((count,)),
             pltpu.SemaphoreType.DMA((count,)),
-            pltpu.SemaphoreType.DMA((5,)),
+            pltpu.SemaphoreType.DMA((10,)),
         ],
         compiler_params=pltpu.CompilerParams(
-            collective_id=3, has_side_effects=True, vmem_limit_bytes=60 << 20
+            collective_id=3, has_side_effects=True, vmem_limit_bytes=62 << 20
         ),
         name="feed",
-    )(g, *grads, w)
+    )(*own_rows, *grads, w, ot, normed, scale, gain)
 
 
 def input_kernel(
     dqkv_ref,
-    wp_ref,
+    wp_hbm,
     x_hbm,
-    x_ref,
+    residual_hbm,
+    dwo_hbm,
     gain_ref,
-    residual_ref,
-    dwo_ref,
     pad_ref,
     input_ref,
     grads_ref,
     term_ref,
+    wp_ref,
     all_x,
+    residual_ref,
+    dwo_ref,
     part,
     dw,
     heard,
@@ -1636,7 +1804,9 @@
 ):
     me = lax.axis_index("ctx")
     rows = residual_ref.shape[0]
-    fetch = local_copies([(x_hbm, all_x)], here)
+    fetch = local_copies(
+        [(wp_hbm, wp_ref), (x_hbm, all_x), (residual_hbm, residual_ref), (dwo_hbm, dwo_ref)], here
+    )
     start_barrier(me)
     copies = Copies(send, recv)
 
@@ -1648,6 +1818,7 @@
         part[place, :] = contract(dqkv_ref[place, :], wp_ref[...], 1, 1).astype(jnp.bfloat16)
 
     reduce = PlaneReduce(copies, me, lambda slot: part.at[at(slot), :], heard, held, landed)
+    fetch[0].wait()
     compute(me ^ 7)
     reduce.share(0)
     compute(me ^ 6)
@@ -1664,7 +1835,8 @@
     compute(me)
     gain = gain_ref[...]
     dw[...] = jnp.zeros_like(dw)
-    fetch[0].wait()
+    for copy in fetch[1:]:
+        copy.wait()
 
     def weights(slot, carry):
         place = at(slot)
@@ -1677,6 +1849,7 @@
     plane = part.shape[0] // rows
     lax.fori_loop(0, plane // 2, weights, 0)
     reduce.second_sends()
+    reduce.own_share()
     lax.fori_loop(plane // 2, plane, weights, 0)
     packed = contract(pad_ref[...], dw[...].astype(jnp.bfloat16), 1, 0)
     packed = packed.astype(jnp.bfloat16).T
@@ -1690,7 +1863,8 @@
     for which in (1, 0):
         here_rows = pl.ds(which * half, half)
         grad = reduce.sum_half(which)
-        x = x_ref[here_rows, :].astype(jnp.float32)
+        own_rows = pl.ds(pl.multiple_of(me * rows + which * half, half), half)
+        x = all_x[own_rows, :].astype(jnp.float32)
         scale = lax.rsqrt(jnp.mean(x * x, axis=-1, keepdims=True) + norm_epsilon)
         normed = x * scale
         total = total + jnp.sum(grad * normed, axis=0, keepdims=True)
@@ -1702,8 +1876,8 @@
     copies.finish()
 
 
-def input_exchange(dqkv, wp, all_x, x, gain, residual, dwo, pad):
-    rows, model = x.shape
+def input_exchange(dqkv, wp, x, residual, dwo, gain, pad):
+    rows, model = residual.shape
     line, dealt, across = dwo.shape
     f32 = jnp.float32
     return pl.pallas_call(
@@ -1713,37 +1887,43 @@
             jax.ShapeDtypeStruct((line, model // line + dealt, across), dwo.dtype),
             jax.ShapeDtypeStruct((1, model), f32),
         ),
-        in_specs=in_vmem(2) + anywhere(1) + in_vmem(5),
+        in_specs=in_vmem(1) + in_hbm(4) + in_vmem(2),
         out_specs=tuple(in_vmem(3)),
         scratch_shapes=[
-            pltpu.VMEM(all_x.shape, all_x.dtype),
-            pltpu.VMEM(all_x.shape, all_x.dtype),
+            pltpu.VMEM(wp.shape, wp.dtype),
+            pltpu.VMEM(x.shape, x.dtype),
+            pltpu.VMEM(residual.shape, residual.dtype),
+            pltpu.VMEM(dwo.shape, dwo.dtype),
+            pltpu.VMEM(x.shape, x.dtype),
             pltpu.VMEM((dqkv.shape[1], model), f32),
             pltpu.VMEM((4, rows, model), x.dtype),
             pltpu.VMEM((3, rows, model), x.dtype),
             pltpu.VMEM((3, rows, model), x.dtype),
             pltpu.SemaphoreType.DMA((REDUCE_COPIES,)),
             pltpu.SemaphoreType.DMA((REDUCE_COPIES,)),
-            pltpu.SemaphoreType.DMA((1,)),
+            pltpu.SemaphoreType.DMA((4,)),
         ],
         compiler_params=remote_params(7),
         name="input_exchange",
-    )(dqkv, wp, all_x, x, gain, residual, dwo, pad)
+    )(dqkv, wp, x, residual, dwo, gain, pad)
 
 
 def pieces_kernel(
     line,
     piece_ref,
+    residual_hbm,
+    out0_hbm,
+    out2_hbm,
+    out4_hbm,
+    out6_hbm,
     term_one_ref,
     term_two_ref,
-    residual_ref,
-    out0_ref,
-    out2_ref,
-    out4_ref,
-    out6_ref,
     whole_ref,
     total_ref,
     output_ref,
+    own,
+    residual_ref,
+    outs_ref,
     terms,
     terms_heard,
     plane_sum,
@@ -1753,22 +1933,31 @@
     here,
 ):
     me, index = lax.axis_index("ctx"), lax.axis_index("fsdp")
+    outs = (out0_hbm, out2_hbm, out4_hbm, out6_hbm)
+    fetch = local_copies(
+        [(piece_ref, own), (residual_hbm, residual_ref)]
+        + [(ref, outs_ref.at[number]) for number, ref in enumerate(outs)],
+        here.at[pl.ds(0, 6)],
+    )
     start_barrier(me, index, line)
     copies = Copies(send, recv)
     rows = piece_ref.shape[0]
     part = row_part(whole_ref, rows)
-    gather = PlaneGather(copies, me, row_half(piece_ref, rows), part)
+    gather = PlaneGather(copies, me, row_half(own, rows), part)
+    fetch[0].wait()
     first = copies.next
     copies.next += 7 + line - 1
     terms[0:1, :] = term_one_ref[...]
     terms[1:2, :] = term_two_ref[...]
     gather.begin()
-    local = local_copies([(piece_ref, part(me, slice(None)))], here)
+    local = local_copies([(own, part(me, slice(None)))], here.at[pl.ds(6, 1)])
     for bit in range(1, 8):
         copies.send(first + bit - 1, terms, terms_heard.at[bit], {"ctx": me ^ bit})
+    for copy in fetch[1:]:
+        copy.wait()
     total = residual_ref[...]
-    for ref in (out0_ref, out2_ref, out4_ref, out6_ref):
-        total = total + ref[...].astype(jnp.float32)
+    for number in range(4):
+        total = total + outs_ref[number].astype(jnp.float32)
     output_ref[0] = total.astype(output_ref.dtype)
     gather.first_hop()
     gather.second_hop()
@@ -1786,6 +1975,7 @@
         total = total + across[step]
     total_ref[...] = total
     gather.last()
+    gather.finish()
     local[0].wait()
     copies.finish()
 
@@ -1802,20 +1992,23 @@
             jax.ShapeDtypeStruct((2, model), f32),
             jax.ShapeDtypeStruct((1, rows, model), jnp.bfloat16),
         ),
-        in_specs=anywhere(1) + in_vmem(7),
+        in_specs=anywhere(6) + in_vmem(2),
         out_specs=(*anywhere(1), *in_vmem(2)),
         scratch_shapes=[
+            pltpu.VMEM(piece.shape, piece.dtype),
+            pltpu.VMEM((rows, model), f32),
+            pltpu.VMEM((4, rows, model), outs[0].dtype),
             pltpu.VMEM((2, model), f32),
             pltpu.VMEM((plane, 2, model), f32),
             pltpu.VMEM((2, model), f32),
             pltpu.VMEM((line, 2, model), f32),
             pltpu.SemaphoreType.DMA((copies,)),
             pltpu.SemaphoreType.DMA((copies,)),
-            pltpu.SemaphoreType.DMA((1,)),
+            pltpu.SemaphoreType.DMA((7,)),
         ],
-        compiler_params=remote_params(8),
+        compiler_params=remote_params(8, 24),
         name="pieces_exchange",
-    )(piece, term_one, term_two, residual, *outs)
+    )(piece, residual, *outs, term_one, term_two)
 
 
 def spread_kernel(gate_in, up_in, down_in, gate_ref, up_ref, down_ref):
@@ -1856,7 +2049,7 @@
             jax.ShapeDtypeStruct((shard, plane * width), jnp.float32),
             jax.ShapeDtypeStruct((plane * unit, model), jnp.float32),
         ),
-        compiler_params=pltpu.CompilerParams(vmem_limit_bytes=62 << 20),
+        compiler_params=pltpu.CompilerParams(vmem_limit_bytes=36 << 20),
         name="spread_feed",
     )(pieces, pieces, pieces)
 
@@ -1971,26 +2164,32 @@
 
     gains = jnp.transpose(gains, (1, 0, 2)).reshape(2, model).astype(jnp.float32)
     qkv_w = qkv_w.reshape(model, -1)
-    grad_rows, x_all = lax.optimization_barrier((output_grad[0], x_all))
-    grad_parts = [grad_rows]
-    for bit in (2, 4, 6):
+    grad_rows, wo_line, x_all = lax.optimization_barrier((output_grad[0], wo_line, x_all))
+    grad_parts, wo_parts = [grad_rows], [wo_line]
+    for bit in (2, 4):
         pairs = [(device, device ^ bit) for device in range(plane)]
         grad_parts.append(lax.ppermute(grad_rows, "ctx", pairs))
+        wo_parts.append(lax.ppermute(wo_line, "ctx", pairs))
     qkv, o, o_columns, lse, qkv_pad = attend(
         slots, x_all, gains[:1], qkv_w, pad, inner, outer
     )
-    wo_mine, columns_mine, residual, normed_two, scale_two, gained_two = second_exchange(
-        o, wo_line, o_columns, block_input[0], gains[1:]
-    )
-    grad_normed_two, *out_parts, feed_grads = feed(gained_two, grad_parts, feed_w)
-    feed_grads = lax.psum_scatter(feed_grads, "fsdp", scatter_dimension=0, tiled=True)
-    grad_residual, feedforward_term, grad_o, wo_term = third_exchange(
-        line,
-        grad_normed_two,
+    wo_mine, far_grads, residual, normed_two, scale_two, *gained_two = second_exchange(
+        o, wo_parts, grad_parts[1:], block_input[0], gains[1:]
+    )
+    grad_residual, feedforward_term, *rest = feed(
+        gained_two,
+        [*grad_parts, far_grads],
+        feed_w,
+        o_columns,
         normed_two,
         scale_two,
         gains[1:],
-        output_grad[0],
+    )
+    grad_attn, columns_mine, out_parts, feed_grads = rest[:3], rest[3], rest[4:8], rest[8]
+    feed_grads = lax.psum_scatter(feed_grads, "fsdp", scatter_dimension=0, tiled=True)
+    grad_o, wo_term = third_exchange(
+        line,
+        grad_attn,
         columns_mine.reshape(-1, columns_mine.shape[2]),
         wo_mine.reshape(-1, model),
         qkv_w.shape[1],
@@ -2002,7 +2201,7 @@
         outs.append(lax.ppermute(out_parts[part], "ctx", pairs))
     grads = attend_back(slots, qkv, o, grad_o, lse, pad, inner, outer)
     input_grad, attention_grads, attention_term = input_exchange(
-        grads, qkv_pad, x_all, block_input[0], gains[:1], grad_residual, wo_term, pad
+        grads, qkv_pad, x_all, grad_residual, wo_term, gains[:1], pad
     )
     attention_grads, feed_grads = lax.optimization_barrier((attention_grads, feed_grads))
     attention_grads = lax.psum_scatter(

time: 444 us -> 420 us (0.946)
  Pallas kernels: 351 us -> 335 us
  local copies, waits for them, and re-layouts: 26.1 us -> 15.3 us
    pallas_call x2, Pallas kernels: 77.5 us -> 63.8 us  [the longest x1 48.7 us: second_exchange(): pl.pallas_call(second_kernel, out_shape=(jax.ShapeDtypeStruct((2 * GROUP,...]
    unnamed x90 -> x50, local copies, waits for them, and re-layouts: 21.8 us -> 11.2 us
    all_gather x1, waiting for transfers between devices: 8.98 us -> 3.01 us  [head_local(): feed_w = lax.all_gather(feed_mine, 'fsdp', axis=0, tiled=True)]
    reduce_scatter x1, waiting for transfers between devices: 0.01 us -> 5.34 us  [head_local(): lax.psum_scatter(feed_grads, 'fsdp', scatter_dimension=0, tiled=True)]
  transfers between devices with their start and end apart: 9 -> 10, of which waited for: 4 -> 4; matrix products, arithmetic and copies ran while one was open for 1% -> 1% of each run, Pallas kernels for 49% -> 49%
where the time goes in v5:
time: 420 us; the launch traced here: 419 us
  Pallas kernels  335 us (80%)
  waiting for transfers between devices  42.3 us (10%)
  local copies, waits for them, and re-layouts  15.3 us (4%)
  between operations  14.1 us (3%)
  starting transfers between devices  7.79 us (2%)
  other arithmetic  4.72 us (1%)
    pallas_call x1, Pallas kernels, feed(): pl.pallas_call(functools.partial(feed_kernel, line), out_shape=(jax.Shape...  68.8 us
    pallas_call x1, Pallas kernels, second_exchange(): pl.pallas_call(second_kernel, out_shape=(jax.ShapeDtypeStruct((2 * GROUP,...  48.7 us
    pallas_call x1, Pallas kernels, pieces_exchange(): pl.pallas_call(functools.partial(pieces_kernel, line), out_shape=(jax.Sha...  47.4 us
    pallas_call x1, Pallas kernels, first_exchange(): pl.pallas_call(functools.partial(first_kernel, line), out_shape=(jax.Shap...  38.3 us
    pallas_call x1, Pallas kernels, input_exchange(): pl.pallas_call(input_kernel, out_shape=(jax.ShapeDtypeStruct((1, rows, mo...  38 us
    ppermute x3, waiting for transfers between devices, head_local(): outs.append(lax.ppermute(out_parts[part], 'ctx', pairs))  33.8 us
    pallas_call x1, Pallas kernels, attend(): pl.pallas_call(forward_kernel, grid_spec=pltpu.PrefetchScalarGridSpec(num...  27.6 us
    pallas_call x1, Pallas kernels, attend_back(): pl.pallas_call(backward_kernel, grid_spec=pltpu.PrefetchScalarGridSpec(nu...  20.2 us
  transfers between devices with their start and end apart: 10, of which 4 were waited for; matrix products, arithmetic and copies ran while one was open for 1% of the time, Pallas kernels for 49%

profile of v5, /device:TPU:0, one launch (start us, length us, event | category | flops | bytes accessed | tf_op | source)
XLA Modules:
  0.0 419.2 jit_solution(7349334271668297285)
XLA Ops:
  7.2 0.8 stack.19
  8.0 0.7 stack.20
  8.7 0.1 constant_dynamic-slice_fusion.2
  8.8 0.6 pad_maximum_fusion.4.gain_ref
  9.4 1.1 constant_dynamic-slice_fusion
  10.6 0.9 pad_maximum_fusion.qkv_ref
  11.4 38.3 %first_exchange.1 = (bf16[2048,1536]{1,0:T(8,128)(2,1)}, bf16[4,384,384]{2,1,0:T(8,128)(2,1)}, bf16[4,48,1536]{2,1,0:T(8,128)(2,1)}, bf16[4,2,384]{2,1,0:T(2,128)(2,1)}, bf16[384,1536]{1,0:T(8,128)(2,1)}) custom-call(bf16[256,1536]{1,0:T(8,128)(2,1)} %bitcast.18, bf16[384,384]{1,0:T(8,128)(2,1)} %pad_maximum_fusion.qkv_ref, bf16[384,1536]{1,0:T(8,128)(2,1)} %wo_ref.1, ...), custom_call_target="tpu_custom_call" | custom-call | tf_op jit(solution)/shard_map/first_exchange/pallas_call | solution.py:1006
  49.9 1.3 collective-permute-start.2
  51.2 1.3 collective-permute-start.3
  52.4 0.8 collective-permute-start
  53.2 0.8 collective-permute-start.1
  54.0 0.2 multiply_cosine_fusion
  54.2 0.1 copy.24
  54.3 0.1 multiply_cosine_fusion.1
  54.5 0.7 pad_maximum_fusion.3.outer_ref
  55.2 0.8 pad_maximum_fusion.1.inner_ref
  55.9 0.9 fusion.pad_ref
  56.8 0.6 fusion.10
  57.4 0.6 select_reduce_fusion.slot_ref
  58.0 27.6 %attend.1 = (bf16[2048,512]{1,0:T(8,128)(2,1)}, bf16[2048,192]{1,0:T(8,128)(2,1)}, bf16[192,2048]{1,0:T(8,128)(2,1)}, f32[8,512]{1,0:T(8,128)}, bf16[1536,512]{1,0:T(8,128)(2,1)}) custom-call(s32[16]{0:T(128)} %select_reduce_fusion.slot_ref, bf16[2048,1536]{1,0:T(8,128)(2,1)} %get-tuple-element.67.xa_ref.xb_ref.x_hbm, ...), custom_call_target="tpu_custom_call" | custom-call | flops 5368709120 | bytes 12582912 | tf_op jit(solution)/shard_map/attend/pallas_call | solution.py:535
  85.8 0.8 copy-done.19
  86.6 0.3 copy-done.20
  86.9 48.7 %second_exchange.1 = (bf16[4,48,1536]{2,1,0:T(8,128)(2,1)}, bf16[256,1536]{1,0:T(8,128)(2,1)}, f32[256,1536]{1,0:T(8,128)}, f32[256,1536]{1,0:T(8,128)}, f32[256...) custom-call(bf16[2048,192]{1,0:T(8,128)(2,1)} %get-tuple-element.71.o_ref, ...), custom_call_target="tpu_custom_call" | custom-call | tf_op jit(solution)/shard_map/second_exchange/pallas_call | solution.py:1244
  135.6 3.0 all-gather.2.cloned.1.call-done.w_hbm
  138.6 68.8 %feed.1 = (f32[256,1536]{1,0:T(8,128)}, f32[1,1536]{1,0:T(1,128)}, bf16[256,1536]{1,0:T(8,128)(2,1)}, bf16[256,1536]{1,0:T(8,128)(2,1)}, bf16[256,1536]{1,0:T(8,...) custom-call(bf16[256,1536]{1,0:T(8,128)(2,1)} %get-tuple-element.74., ...), custom_call_target="tpu_custom_call" | custom-call | tf_op jit(solution)/shard_map/feed/pallas_call | solution.py:1741
  207.6 15.1 %third_exchange.1 = (bf16[2048,192]{1,0:T(8,128)(2,1)}, bf16[4,192,384]{2,1,0:T(8,128)(2,1)}) custom-call(bf16[256,1536]{1,0:T(8,128)(2,1)} %get-tuple-element.86.g0_hbm, bf16[256,1536]{1,0:T(8,128)(2,1)} %get-tuple-element.87.g2_hbm, bf16[256,1536]{1,0:T(8,128)(2,1)} %get-tuple-element.88.g4_hbm, bf16[192,2048]{1,0:T(8,128)(2,1)} %bitcast.22, ...), custom_call_target="tpu_custom_call" | custom-call | tf_op jit(solution)/shard_map/third_exchange/pallas_call | solution.py:1361
  222.7 1.2 copy-done.15
  223.9 1.6 copy-done.17
  225.5 20.2 %attend_back.1.dqkv_ref = bf16[2048,512]{1,0:T(8,128)(2,1)S(1)} custom-call(s32[16]{0:T(128)S(1)} %copy-done.16, bf16[2048,512]{1,0:T(8,128)(2,1)S(1)} %copy-done.17, bf16[2048,192]{1,0:T(8,128)(2,1)S(1)} %copy-done.6, bf16[2048,192]{1,0:T(8,128)(2,1)S(1)} %copy-done.15, f32[8,512]{1,0:T(8,128)S(1)} %copy-done.18, bf16[384,512]{1,0:T(8,128)(2,1)S(1)} %copy-done.3, ...), custom_call_target="tpu_custom_call" | custom-call | flops 5368709120 | bytes 8388608 | tf_op jit(solution)/shard_map/attend_back/pallas_call | solution.py:674
  245.7 1.3 copy-done.2
  247.0 38.0 %input_exchange.1 = (f32[1,256,1536]{2,1,0:T(8,128)}, bf16[4,576,384]{2,1,0:T(8,128)(2,1)}, f32[1,1536]{1,0:T(1,128)}) custom-call(bf16[2048,512]{1,0:T(8,128)(2,1)} %copy-done.2, bf16[1536,512]{1,0:T(8,128)(2,1)} %get-tuple-element.94.wp_hbm, bf16[2048,1536]{1,0:T(8,128)(2,1)} %get-tuple-element.67.xa_ref.xb_ref.x_hbm, ...), custom_call_target="tpu_custom_call" | custom-call | tf_op jit(solution)/shard_map/input_exchange/pallas_call | solution.py:1883
  285.0 5.3 %reduce-scatter.3.cloned.1.call-done.piece_ref = bf16[384,1536]{1,0:T(8,128)(2,1)} async-done(((bf16[1536,1536]{1,0:T(8,128)(2,1)}), bf16[384,1536]{1,0:T(8,128)(2,1)}) %reduce-scatter.3.cloned.1.call-update) | async-done | bytes 1179664 | tf_op jit(solution)/shard_map/reduce_scatter | solution.py:2189
  290.4 2.4 collective-permute-start.4
  292.8 0.6 collective-permute-start.5
  293.4 0.6 collective-permute-start.6
  293.9 18.1 %collective-permute-done.4.out2_hbm = bf16[256,1536]{1,0:T(8,128)(2,1)S(1)} collective-permute-done((bf16[256,1536]{1,0:T(8,128)(2,1)}, bf16[256,1536]{1,0:T(8,128)(2,1)S(1)}, u32[]{:S(2)}, u32[]{:S(2)}) %collective-permute-start.4) | collective-permute-done | bytes 786464 | tf_op jit(solution)/shard_map/ppermute | solution.py:2201
  312.0 15.8 %collective-permute-done.5.out4_hbm = bf16[256,1536]{1,0:T(8,128)(2,1)} collective-permute-done((bf16[256,1536]{1,0:T(8,128)(2,1)}, bf16[256,1536]{1,0:T(8,128)(2,1)}, u32[]{:S(2)}, u32[]{:S(2)}) %collective-permute-start.5) | collective-permute-done | bytes 786464 | tf_op jit(solution)/shard_map/ppermute | solution.py:2201
  327.8 1.3 copy-done.5
  329.1 0.7 copy-done.14
  329.8 47.4 %pieces_exchange.1 = (bf16[3072,1536]{1,0:T(8,128)(2,1)S(1)}, f32[2,1536]{1,0:T(2,128)S(1)}, bf16[1,256,1536]{2,1,0:T(8,128)(2,1)S(1)}) custom-call(bf16[384,1536]{1,0:T(8,128)(2,1)S(1)} %copy-done.5, f32[256,1536]{1,0:T(8,128)S(1)} %copy-done.4, bf16[256,1536]{1,0:T(8,128)(2,1)S(1)} %copy-done.7, bf16[256,1536]{1,0:T(8,128)(2,1)S(1)} %collective-permute-done.4.out2_hbm, ...), custom_call_target="tpu_custom_call" | custom-call | tf_op jit(solution)/shard_map/pieces_exchange/pallas_call | solution.py:1988
  377.2 0.9 copy-done.8
  378.0 7.5 %spread_feed.1 = (f32[384,4096]{1,0:T(8,128)}, f32[384,4096]{1,0:T(8,128)}, f32[1024,1536]{1,0:T(8,128)}) custom-call(bf16[8,384,1536]{2,1,0:T(8,128)(2,1)S(1)} %bitcast.14, bf16[8,384,1536]{2,1,0:T(8,128)(2,1)S(1)} %bitcast.15, bf16[8,384,1536]{2,1,0:T(8,128)(2,1)S(1)} %bitcast.16), custom_call_target="tpu_custom_call" | custom-call | tf_op jit(solution)/shard_map/spread_feed/pallas_call | solution.py:2034
  385.6 0.7 dynamic-slice_reduce_fusion
  386.3 1.0 copy-done.10
  387.3 20.1 %shard_map.203 = bf16[4608,384]{1,0:T(8,128)(2,1)S(1)} custom-call(bf16[576,384]{1,0:T(8,128)(2,1)S(1)} %copy-done.10), custom_call_target="tpu_custom_call" | custom-call | tf_op jit(solution)/shard_map/pallas_call | solution.py:1293
  407.4 3.2 spread_attention.1
  410.7 0.9 copy.27
  411.6 1.1 copy.28
  (59 shorter events, 0.4 us)
Async XLA Ops:
  7.2 1.5 copy-start
  7.2 131.4 %all-gather.2.cloned.1.call-start = ((), (), s32[]{:S(2)}) async-start(), calls=%async_computation.2 | async-start | bytes 5898240 | tf_op jit(solution)/shard_map/all_gather | solution.py:2150
  49.8 6.1 %copy-start.22 = (bf16[4,2,384]{2,1,0:T(2,128)(2,1)S(1)}, bf16[4,2,384]{2,1,0:T(2,128)(2,1)}, u32[]{:S(2)}) copy-start(bf16[4,2,384]{2,1,0:T(2,128)(2,1)} %get-tuple-element.68) | copy-start | bytes 18436
  49.8 7.6 %copy-start.23 = (s32[1,16]{1,0:T(1,128)S(1)}, s32[1,16]{1,0:T(1,128)}, u32[]{:S(2)}) copy-start(s32[1,16]{1,0:T(1,128)} %param.13) | copy-start | bytes 196
  49.8 240.5 %reduce-scatter.3.cloned.1.call-start = ((), (), s32[]{:S(2)}) async-start(), calls=%async_computation.3 | async-start | bytes 5898240 | tf_op jit(solution)/shard_map/reduce_scatter | solution.py:2189
  49.9 35.8 %collective-permute-start.2 = (bf16[256,1536]{1,0:T(8,128)(2,1)}, bf16[256,1536]{1,0:T(8,128)(2,1)S(1)}, u32[]{:S(2)}, u32[]{:S(2)}) collective-permute-start(bf16[256,1536]{1,0:T(8,128)(2,1)} %bitcast.1.dy0_hbm), channel_id=1, source_target_pairs={{0,8},{4,12},{8,0},{12,4},{16,24},{20,28},{24,16},{28,20},{1,9},{5... | collective-permute-start | bytes 2359304 | tf_op jit(solution)/shard_map/ppermute | solution.py:2171
  51.2 34.6 %collective-permute-start.3 = (bf16[256,1536]{1,0:T(8,128)(2,1)}, bf16[256,1536]{1,0:T(8,128)(2,1)S(1)}, u32[]{:S(2)}, u32[]{:S(2)}) collective-permute-start(bf16[256,1536]{1,0:T(8,128)(2,1)} %bitcast.1.dy0_hbm), channel_id=1, source_target_pairs={{0,16},{4,20},{8,24},{12,28},{16,0},{20,4},{24,8},{28,12},{1,17},{... | collective-permute-start | bytes 2359304 | tf_op jit(solution)/shard_map/ppermute | solution.py:2171
  52.4 33.2 %collective-permute-start = (bf16[4,48,1536]{2,1,0:T(8,128)(2,1)}, bf16[4,48,1536]{2,1,0:T(8,128)(2,1)}, u32[]{:S(2)}, u32[]{:S(2)}) collective-permute-start(bf16[4,48,1536]{2,1,0:T(8,128)(2,1)} %get-tuple-element.72.wo0_hbm), channel_id=1, source_target_pairs={{0,8},{4,12},{8,0},{12,4},{16,24},{20,28},{24,16},{28,20},{1,9},{5... | collective-permute-start | bytes 1769480 | tf_op jit(solution)/shard_map/ppermute | solution.py:2172
  53.2 32.5 %collective-permute-start.1 = (bf16[4,48,1536]{2,1,0:T(8,128)(2,1)}, bf16[4,48,1536]{2,1,0:T(8,128)(2,1)}, u32[]{:S(2)}, u32[]{:S(2)}) collective-permute-start(bf16[4,48,1536]{2,1,0:T(8,128)(2,1)} %get-tuple-element.72.wo0_hbm), channel_id=1, source_target_pairs={{0,16},{4,20},{8,24},{12,28},{16,0},{20,4},{24,8},{28,12},{1,17},{... | collective-permute-start | bytes 1769480 | tf_op jit(solution)/shard_map/ppermute | solution.py:2172
  85.7 0.9 copy-start.19
  85.7 1.1 copy-start.20
  207.4 15.2 %copy-start.3 = (bf16[384,512]{1,0:T(8,128)(2,1)S(1)}, bf16[384,512]{1,0:T(8,128)(2,1)}, u32[]{:S(2)}) copy-start(bf16[384,512]{1,0:T(8,128)(2,1)} %fusion.pad_ref) | copy-start | bytes 1179652
  207.4 15.2 %copy-start.6 = (bf16[2048,192]{1,0:T(8,128)(2,1)S(1)}, bf16[2048,192]{1,0:T(8,128)(2,1)}, u32[]{:S(2)}) copy-start(bf16[2048,192]{1,0:T(8,128)(2,1)} %get-tuple-element.71.o_ref) | copy-start | bytes 2359300
  207.5 15.2 %copy-start.11 = (f32[2,128,128]{2,1,0:T(8,128)S(1)}, f32[2,128,128]{2,1,0:T(8,128)}, u32[]{:S(2)}) copy-start(f32[2,128,128]{2,1,0:T(8,128)} %pad_maximum_fusion.1.inner_ref) | copy-start | bytes 393220
  207.5 15.2 %copy-start.12 = (f32[2,16,128]{2,1,0:T(8,128)S(1)}, f32[2,16,128]{2,1,0:T(8,128)}, u32[]{:S(2)}) copy-start(f32[2,16,128]{2,1,0:T(8,128)} %pad_maximum_fusion.3.outer_ref) | copy-start | bytes 49156
  207.5 15.2 %copy-start.16 = (s32[16]{0:T(128)S(1)}, s32[16]{0:T(128)}, u32[]{:S(2)}) copy-start(s32[16]{0:T(128)} %select_reduce_fusion.slot_ref) | copy-start | bytes 196
  207.5 15.2 %copy-start.18 = (f32[8,512]{1,0:T(8,128)S(1)}, f32[8,512]{1,0:T(8,128)}, u32[]{:S(2)}) copy-start(f32[8,512]{1,0:T(8,128)} %get-tuple-element.93.lse_ref) | copy-start | bytes 49156
  207.5 178.8 %reduce-scatter.5.cloned.1.call-start = ((), (), s32[]{:S(2)}) async-start(), calls=%async_computation.4 | async-start | bytes 2211840 | tf_op jit(solution)/shard_map/reduce_scatter | solution.py:2207
  222.7 1.2 copy-start.15
  223.9 1.6 copy-start.17
  245.7 1.3 copy-start.2
  247.0 80.8 %copy-start.7 = (bf16[256,1536]{1,0:T(8,128)(2,1)S(1)}, bf16[256,1536]{1,0:T(8,128)(2,1)}, u32[]{:S(2)}) copy-start(bf16[256,1536]{1,0:T(8,128)(2,1)} %get-tuple-element.101.out0_hbm) | copy-start | bytes 2359300
  247.0 80.8 %copy-start.13 = (f32[1,1536]{1,0:T(1,128)S(1)}, f32[1,1536]{1,0:T(1,128)}, u32[]{:S(2)}) copy-start(f32[1,1536]{1,0:T(1,128)} %get-tuple-element.106.term_two_ref) | copy-start | bytes 18436
  285.0 42.8 %copy-start.4 = (f32[256,1536]{1,0:T(8,128)S(1)}, f32[256,1536]{1,0:T(8,128)}, u32[]{:S(2)}) copy-start(f32[256,1536]{1,0:T(8,128)} %get-tuple-element.100.residual_hbm) | copy-start | bytes 4718596
  290.4 21.6 %collective-permute-start.4 = (bf16[256,1536]{1,0:T(8,128)(2,1)}, bf16[256,1536]{1,0:T(8,128)(2,1)S(1)}, u32[]{:S(2)}, u32[]{:S(2)}) collective-permute-start(bf16[256,1536]{1,0:T(8,128)(2,1)} %get-tuple-element.102), channel_id=1, source_target_pairs={{0,24},{4,28},{8,16},{12,20},{16,8},{20,12},{24,0},{28,4},{1,25},{... | collective-permute-start | bytes 2359304 | tf_op jit(solution)/shard_map/ppermute | solution.py:2201
  292.8 35.0 %collective-permute-start.5 = (bf16[256,1536]{1,0:T(8,128)(2,1)}, bf16[256,1536]{1,0:T(8,128)(2,1)}, u32[]{:S(2)}, u32[]{:S(2)}) collective-permute-start(bf16[256,1536]{1,0:T(8,128)(2,1)} %get-tuple-element.103), channel_id=1, source_target_pairs={{0,8},{4,12},{8,0},{12,4},{16,24},{20,28},{24,16},{28,20},{1,9},{5... | collective-permute-start | bytes 2359304 | tf_op jit(solution)/shard_map/ppermute | solution.py:2201
  293.4 34.4 %collective-permute-start.6 = (bf16[256,1536]{1,0:T(8,128)(2,1)}, bf16[256,1536]{1,0:T(8,128)(2,1)}, u32[]{:S(2)}, u32[]{:S(2)}) collective-permute-start(bf16[256,1536]{1,0:T(8,128)(2,1)} %get-tuple-element.104), channel_id=1, source_target_pairs={{0,16},{4,20},{8,24},{12,28},{16,0},{20,4},{24,8},{28,12},{1,17},{... | collective-permute-start | bytes 2359304 | tf_op jit(solution)/shard_map/ppermute | solution.py:2201
  327.8 1.3 copy-start.5
  329.1 0.7 copy-start.14
  377.2 0.9 copy-start.8
  386.3 1.0 copy-start.10
  407.4 3.3 copy-start.9
  407.4 4.1 copy-start.21
  410.7 2.0 copy-start.1
Sparse Core Ops, SparseCore 0:
  49.9 88.5 all-gather.1
  207.6 82.7 reduce-scatter.2
  292.7 38.9 reduce-scatter.4

commit v6 on v5

--- a/solution.py
+++ b/solution.py
@@ -700,13 +700,32 @@
 MESH_IDS = pl.DeviceIdType.MESH
 
 
-def start_barrier(me, line_index=None, line=1):
+NEAR = (1, 2, 4)
+ALL = (1, 2, 3, 4, 5, 6, 7)
+
+
+def start_barrier(me, bits, line_steps=(), line_index=None, line=1):
     barrier = pltpu.get_barrier_semaphore()
-    peers = [{"ctx": me ^ bit} for bit in range(1, 8)]
-    peers += [{"fsdp": lax.rem(line_index + step, line)} for step in range(1, line)]
+    peers = [{"ctx": me ^ bit} for bit in bits]
+    peers += [{"fsdp": lax.rem(line_index + step, line)} for step in line_steps]
     for peer in peers:
         pl.semaphore_signal(barrier, inc=1, device_id=peer, device_id_type=MESH_IDS)
     pl.semaphore_wait(barrier, len(peers))
+
+
+def start_line_barrier(me, index, line):
+    barrier = pltpu.get_barrier_semaphore()
+    for bit in NEAR:
+        pl.semaphore_signal(barrier, inc=1, device_id={"ctx": me ^ bit}, device_id_type=MESH_IDS)
+    up, down = index < line - 1, index > 0
+    for there, exists in ((index + 1, up), (index - 1, down)):
+
+        @pl.when(exists)
+        def _(there=there):
+            peer = {"fsdp": jnp.clip(there, 0, line - 1)}
+            pl.semaphore_signal(barrier, inc=1, device_id=peer, device_id_type=MESH_IDS)
+
+    pl.semaphore_wait(barrier, len(NEAR) + up.astype(jnp.int32) + down.astype(jnp.int32))
 
 
 class Copies:
@@ -945,7 +964,7 @@
         ],
         here.at[pl.ds(0, 4)],
     )
-    start_barrier(me, index, line)
+    start_line_barrier(me, index, line)
     copies = Copies(send, recv)
     gather = PlaneGather(copies, me, row_half(own, rows), part)
     lines = [
@@ -1168,7 +1187,7 @@
         + [(ref, wo_place(me ^ (2 * number), None)) for number, ref in enumerate(own_wo)],
         here.at[pl.ds(0, 5)],
     )
-    start_barrier(me)
+    start_barrier(me, ALL)
     copies = Copies(send, recv)
 
     def block(slot):
@@ -1269,40 +1288,40 @@
     )(o, *own_wo, *grads, x, gain)
 
 
-def gather_kernel(x_ref, xo_ref, own, send, recv, here):
+def near_kernel(own_hbm, near_x_hbm, near_y_hbm, whole_ref, send, recv, here):
     me = lax.axis_index("ctx")
-    rows = x_ref.shape[0]
-    fetch = local_copies([(x_ref, own)], here)
-    start_barrier(me)
-    fetch[0].wait()
-    part = row_part(xo_ref, rows)
+    refs = (own_hbm, near_x_hbm, near_y_hbm)
+    place = block_place(whole_ref, own_hbm.shape[0])
+    local = local_copies(
+        [(ref, place(me ^ (2 * number), None)) for number, ref in enumerate(refs)], here
+    )
+    start_barrier(me, NEAR)
     copies = Copies(send, recv)
-    gather = PlaneGather(copies, me, row_half(own, rows), part)
-    gather.begin()
-    local = local_copies([(own, part(me, slice(None)))], here)
-    gather.first_hop()
-    gather.second_hop()
-    gather.third_hop()
-    gather.last()
-    gather.finish()
-    local[0].wait()
-
-
-def plane_gather(x, number):
+    shares = NearShares(copies, me, refs, place)
+    shares.begin()
+    shares.diagonal()
+    for bit in (1, 3, 5, 7):
+        shares.shared(bit)
+    for copy in local:
+        copy.wait()
+    shares.finish()
+
+
+def near_gather(refs, number):
     plane = lax.axis_size("ctx")
+    rows, columns = refs[0].shape
     return pl.pallas_call(
-        gather_kernel,
-        out_shape=jax.ShapeDtypeStruct((plane * x.shape[0], x.shape[1]), x.dtype),
-        in_specs=in_hbm(1),
-        out_specs=anywhere(1)[0],
+        near_kernel,
+        out_shape=jax.ShapeDtypeStruct((plane * rows, columns), refs[0].dtype),
+        in_specs=anywhere(3),
+        out_specs=in_vmem(1)[0],
         scratch_shapes=[
-            pltpu.VMEM(x.shape, x.dtype),
-            pltpu.SemaphoreType.DMA((GATHER_COPIES,)),
-            pltpu.SemaphoreType.DMA((GATHER_COPIES,)),
-            pltpu.SemaphoreType.DMA((1,)),
+            pltpu.SemaphoreType.DMA((7,)),
+            pltpu.SemaphoreType.DMA((7,)),
+            pltpu.SemaphoreType.DMA((3,)),
         ],
         compiler_params=remote_params(number, 24),
-    )(x)
+    )(*refs)
 
 
 def third_kernel(
@@ -1317,7 +1336,7 @@
         + [(ot_hbm, ot_ref), (wo_hbm, wo_ref)],
         here,
     )
-    start_barrier(me)
+    start_barrier(me, NEAR)
     copies = Copies(send, recv)
     shares = NearShares(copies, me, own_rows, place)
     shares.begin()
@@ -1543,7 +1562,7 @@
         + [(normed_hbm, normed_ref)],
         here.at[pl.ds(0, 9)],
     )
-    start_barrier(me)
+    start_barrier(me, ALL)
     copies = Copies(send, recv)
     shares = NearShares(copies, me, own_rows, place)
     shares.begin()
@@ -1807,7 +1826,7 @@
     fetch = local_copies(
         [(wp_hbm, wp_ref), (x_hbm, all_x), (residual_hbm, residual_ref), (dwo_hbm, dwo_ref)], here
     )
-    start_barrier(me)
+    start_barrier(me, NEAR)
     copies = Copies(send, recv)
 
     def at(slot):
@@ -1939,20 +1958,28 @@
         + [(ref, outs_ref.at[number]) for number, ref in enumerate(outs)],
         here.at[pl.ds(0, 6)],
     )
-    start_barrier(me, index, line)
+    start_barrier(me, ALL, range(1, line), index, line)
     copies = Copies(send, recv)
     rows = piece_ref.shape[0]
     part = row_part(whole_ref, rows)
     gather = PlaneGather(copies, me, row_half(own, rows), part)
-    fetch[0].wait()
     first = copies.next
     copies.next += 7 + line - 1
     terms[0:1, :] = term_one_ref[...]
     terms[1:2, :] = term_two_ref[...]
+    for bit in range(1, 8):
+        copies.send(first + bit - 1, terms, terms_heard.at[bit], {"ctx": me ^ bit})
+    fetch[0].wait()
     gather.begin()
     local = local_copies([(own, part(me, slice(None)))], here.at[pl.ds(6, 1)])
+    total = terms[...]
     for bit in range(1, 8):
-        copies.send(first + bit - 1, terms, terms_heard.at[bit], {"ctx": me ^ bit})
+        copies.arrived(first + bit - 1, terms_heard.at[bit])
+        total = total + terms_heard[bit]
+    plane_sum[...] = total
+    for step in range(1, line):
+        peer = {"fsdp": lax.rem(index + step, line)}
+        copies.send(first + 6 + step, plane_sum, across.at[step], peer)
     for copy in fetch[1:]:
         copy.wait()
     total = residual_ref[...]
@@ -1961,19 +1988,12 @@
     output_ref[0] = total.astype(output_ref.dtype)
     gather.first_hop()
     gather.second_hop()
-    total = terms[...]
-    for bit in range(1, 8):
-        copies.arrived(first + bit - 1, terms_heard.at[bit])
-        total = total + terms_heard[bit]
-    plane_sum[...] = total
-    for step in range(1, line):
-        peer = {"fsdp": lax.rem(index + step, line)}
-        copies.send(first + 6 + step, plane_sum, across.at[step], peer)
-    gather.third_hop()
+    total = plane_sum[...]
     for step in range(1, line):
         copies.arrived(first + 6 + step, across.at[step])
         total = total + across[step]
     total_ref[...] = total
+    gather.third_hop()
     gather.last()
     gather.finish()
     local[0].wait()
@@ -2006,7 +2026,7 @@
             pltpu.SemaphoreType.DMA((copies,)),
             pltpu.SemaphoreType.DMA((7,)),
         ],
-        compiler_params=remote_params(8, 24),
+        compiler_params=remote_params(8),
         name="pieces_exchange",
     )(piece, residual, *outs, term_one, term_two)
 
@@ -2049,7 +2069,7 @@
             jax.ShapeDtypeStruct((shard, plane * width), jnp.float32),
             jax.ShapeDtypeStruct((plane * unit, model), jnp.float32),
         ),
-        compiler_params=pltpu.CompilerParams(vmem_limit_bytes=36 << 20),
+        compiler_params=pltpu.CompilerParams(vmem_limit_bytes=62 << 20),
         name="spread_feed",
     )(pieces, pieces, pieces)
 
@@ -2213,8 +2233,13 @@
     feed_pieces, gain_terms, layer_output = pieces_exchange(
         line, feed_grads, attention_term, feedforward_term, residual, outs
     )
+    attention_grads, gain_terms = lax.optimization_barrier((attention_grads, gain_terms))
+    near_grads = []
+    for bit in (2, 4):
+        pairs = [(device, device ^ bit) for device in range(plane)]
+        near_grads.append(lax.ppermute(attention_grads, "ctx", pairs))
     gate_grad, up_grad, down_grad = spread_feed(feed_pieces, shard, line, unit)
-    attention_pieces = plane_gather(attention_grads, 9)
+    attention_pieces = near_gather([attention_grads, *near_grads], 9)
     query_grad, key_grad, value_grad, out_grad = spread_attention(
         attention_pieces, shard, model, query_width, key_width
     )

time: 420 us -> 412 us (0.981)
  Pallas kernels: 335 us -> 326 us
    pallas_call x1, Pallas kernels: 20.1 us -> 9.63 us  [near_gather(): pl.pallas_call(near_kernel, out_shape=jax.ShapeDtypeStruct((plane * rows,...]
    unnamed x50 -> x42, local copies, waits for them, and re-layouts: 11.2 us -> 8.16 us
  transfers between devices with their start and end apart: 10 -> 12, of which waited for: 4 -> 5; matrix products, arithmetic and copies ran while one was open for 1% -> 1% of each run, Pallas kernels for 49% -> 50%
where the time goes in v6:
time: 412 us
  Pallas kernels  326 us (79%)
  waiting for transfers between devices  44.7 us (11%)
  between operations  14.1 us (3%)
  local copies, waits for them, and re-layouts  13 us (3%)
  starting transfers between devices  9.85 us (2%)
  other arithmetic  4.72 us (1%)
    pallas_call x1, Pallas kernels, feed(): pl.pallas_call(functools.partial(feed_kernel, line), out_shape=(jax.Shape...  68.7 us
    pallas_call x1, Pallas kernels, second_exchange(): pl.pallas_call(second_kernel, out_shape=(jax.ShapeDtypeStruct((2 * GROUP,...  48.6 us
    pallas_call x1, Pallas kernels, pieces_exchange(): pl.pallas_call(functools.partial(pieces_kernel, line), out_shape=(jax.Sha...  48.2 us
    pallas_call x1, Pallas kernels, first_exchange(): pl.pallas_call(functools.partial(first_kernel, line), out_shape=(jax.Shap...  37.2 us
    pallas_call x1, Pallas kernels, input_exchange(): pl.pallas_call(input_kernel, out_shape=(jax.ShapeDtypeStruct((1, rows, mo...  37 us
    ppermute x3, waiting for transfers between devices, head_local(): outs.append(lax.ppermute(out_parts[part], 'ctx', pairs))  33.8 us
    pallas_call x1, Pallas kernels, attend(): pl.pallas_call(forward_kernel, grid_spec=pltpu.PrefetchScalarGridSpec(num...  27.7 us
    pallas_call x1, Pallas kernels, attend_back(): pl.pallas_call(backward_kernel, grid_spec=pltpu.PrefetchScalarGridSpec(nu...  20.2 us
  transfers between devices with their start and end apart: 12, of which 5 were waited for; matrix products, arithmetic and copies ran while one was open for 1% of the time, Pallas kernels for 50%

profile of v6, /device:TPU:0, one launch (start us, length us, event | category | flops | bytes accessed | tf_op | source)
XLA Modules:
  0.0 412.0 jit_solution(14931646744194232660)
XLA Ops:
  7.2 0.8 stack.19
  8.0 0.7 stack.20
  8.7 0.1 constant_dynamic-slice_fusion.2
  8.8 0.6 pad_maximum_fusion.4.gain_ref
  9.4 1.1 constant_dynamic-slice_fusion
  10.6 0.9 pad_maximum_fusion.qkv_ref
  11.4 37.2 %first_exchange.1 = (bf16[2048,1536]{1,0:T(8,128)(2,1)}, bf16[4,384,384]{2,1,0:T(8,128)(2,1)}, bf16[4,48,1536]{2,1,0:T(8,128)(2,1)}, bf16[4,2,384]{2,1,0:T(2,128)(2,1)}, bf16[384,1536]{1,0:T(8,128)(2,1)}) custom-call(bf16[256,1536]{1,0:T(8,128)(2,1)} %bitcast.18, bf16[384,384]{1,0:T(8,128)(2,1)} %pad_maximum_fusion.qkv_ref, bf16[384,1536]{1,0:T(8,128)(2,1)} %wo_ref.1, ...), custom_call_target="tpu_custom_call" | custom-call | tf_op jit(solution)/shard_map/first_exchange/pallas_call | solution.py:1025
  48.8 1.4 collective-permute-start.2
  50.2 1.3 collective-permute-start.3
  51.4 0.8 collective-permute-start
  52.2 0.7 collective-permute-start.1
  52.9 0.2 multiply_cosine_fusion
  53.1 0.1 copy.24
  53.2 0.1 multiply_cosine_fusion.1
  53.4 0.7 pad_maximum_fusion.3.outer_ref
  54.1 0.8 pad_maximum_fusion.1.inner_ref
  54.8 0.9 fusion.pad_ref
  55.7 0.6 fusion.10
  56.3 0.6 select_reduce_fusion.slot_ref
  56.9 27.7 %attend.1 = (bf16[2048,512]{1,0:T(8,128)(2,1)}, bf16[2048,192]{1,0:T(8,128)(2,1)}, bf16[192,2048]{1,0:T(8,128)(2,1)}, f32[8,512]{1,0:T(8,128)}, bf16[1536,512]{1,0:T(8,128)(2,1)}) custom-call(s32[16]{0:T(128)} %select_reduce_fusion.slot_ref, bf16[2048,1536]{1,0:T(8,128)(2,1)} %get-tuple-element.69.xa_ref.xb_ref.x_hbm, ...), custom_call_target="tpu_custom_call" | custom-call | flops 5368709120 | bytes 12582912 | tf_op jit(solution)/shard_map/attend/pallas_call | solution.py:535
  84.7 0.8 copy-done.12
  85.5 0.3 copy-done.13
  85.8 48.6 %second_exchange.1 = (bf16[4,48,1536]{2,1,0:T(8,128)(2,1)}, bf16[256,1536]{1,0:T(8,128)(2,1)}, f32[256,1536]{1,0:T(8,128)}, f32[256,1536]{1,0:T(8,128)}, f32[256...) custom-call(bf16[2048,192]{1,0:T(8,128)(2,1)} %get-tuple-element.73.o_ref, ...), custom_call_target="tpu_custom_call" | custom-call | tf_op jit(solution)/shard_map/second_exchange/pallas_call | solution.py:1263
  134.5 3.5 all-gather.2.cloned.1.call-done.w_hbm
  138.0 68.7 %feed.1 = (f32[256,1536]{1,0:T(8,128)}, f32[1,1536]{1,0:T(1,128)}, bf16[256,1536]{1,0:T(8,128)(2,1)}, bf16[256,1536]{1,0:T(8,128)(2,1)}, bf16[256,1536]{1,0:T(8,...) custom-call(bf16[256,1536]{1,0:T(8,128)(2,1)} %get-tuple-element.76., ...), custom_call_target="tpu_custom_call" | custom-call | tf_op jit(solution)/shard_map/feed/pallas_call | solution.py:1760
  206.9 14.1 %third_exchange.1 = (bf16[2048,192]{1,0:T(8,128)(2,1)}, bf16[4,192,384]{2,1,0:T(8,128)(2,1)}) custom-call(bf16[256,1536]{1,0:T(8,128)(2,1)} %get-tuple-element.88.g0_hbm, bf16[256,1536]{1,0:T(8,128)(2,1)} %get-tuple-element.89.g2_hbm, bf16[256,1536]{1,0:T(8,128)(2,1)} %get-tuple-element.90.g4_hbm, bf16[192,2048]{1,0:T(8,128)(2,1)} %bitcast.22, ...), custom_call_target="tpu_custom_call" | custom-call | tf_op jit(solution)/shard_map/third_exchange/pallas_call | solution.py:1380
  221.1 1.2 copy-done.8
  222.3 1.6 copy-done.10
  223.9 20.2 %attend_back.1.dqkv_ref = bf16[2048,512]{1,0:T(8,128)(2,1)S(1)} custom-call(s32[16]{0:T(128)S(1)} %copy-done.9, bf16[2048,512]{1,0:T(8,128)(2,1)S(1)} %copy-done.10, bf16[2048,192]{1,0:T(8,128)(2,1)S(1)} %copy-done.4, bf16[2048,192]{1,0:T(8,128)(2,1)S(1)} %copy-done.8, f32[8,512]{1,0:T(8,128)S(1)} %copy-done.11, bf16[384,512]{1,0:T(8,128)(2,1)S(1)} %copy-done.3, ...), custom_call_target="tpu_custom_call" | custom-call | flops 5368709120 | bytes 8388608 | tf_op jit(solution)/shard_map/attend_back/pallas_call | solution.py:674
  244.0 1.3 copy-done.2
  245.4 37.0 %input_exchange.1 = (f32[1,256,1536]{2,1,0:T(8,128)}, bf16[4,576,384]{2,1,0:T(8,128)(2,1)}, f32[1,1536]{1,0:T(1,128)}) custom-call(bf16[2048,512]{1,0:T(8,128)(2,1)} %copy-done.2, bf16[1536,512]{1,0:T(8,128)(2,1)} %get-tuple-element.96.wp_hbm, bf16[2048,1536]{1,0:T(8,128)(2,1)} %get-tuple-element.69.xa_ref.xb_ref.x_hbm, ...), custom_call_target="tpu_custom_call" | custom-call | tf_op jit(solution)/shard_map/input_exchange/pallas_call | solution.py:1902
  282.4 7.3 %reduce-scatter.3.cloned.1.call-done.piece_ref = bf16[384,1536]{1,0:T(8,128)(2,1)} async-done(((bf16[1536,1536]{1,0:T(8,128)(2,1)}), bf16[384,1536]{1,0:T(8,128)(2,1)}) %reduce-scatter.3.cloned.1.call-update) | async-done | bytes 1179664 | tf_op jit(solution)/shard_map/reduce_scatter | solution.py:2209
  289.7 2.5 collective-permute-start.4
  292.2 0.6 collective-permute-start.5
  292.7 0.5 collective-permute-start.6
  293.3 18.1 %collective-permute-done.4.out2_hbm = bf16[256,1536]{1,0:T(8,128)(2,1)S(1)} collective-permute-done((bf16[256,1536]{1,0:T(8,128)(2,1)}, bf16[256,1536]{1,0:T(8,128)(2,1)S(1)}, u32[]{:S(2)}, u32[]{:S(2)}) %collective-permute-start.4) | collective-permute-done | bytes 786464 | tf_op jit(solution)/shard_map/ppermute | solution.py:2221
  311.4 15.7 %collective-permute-done.5.out4_hbm = bf16[256,1536]{1,0:T(8,128)(2,1)S(1)} collective-permute-done((bf16[256,1536]{1,0:T(8,128)(2,1)}, bf16[256,1536]{1,0:T(8,128)(2,1)S(1)}, u32[]{:S(2)}, u32[]{:S(2)}) %collective-permute-start.5) | collective-permute-done | bytes 786464 | tf_op jit(solution)/shard_map/ppermute | solution.py:2221
  327.0 0.1 collective-permute-done.6.out6_hbm
  327.1 0.8 copy-done.16
  327.9 48.2 %pieces_exchange.1 = (bf16[3072,1536]{1,0:T(8,128)(2,1)}, f32[2,1536]{1,0:T(2,128)}, bf16[1,256,1536]{2,1,0:T(8,128)(2,1)}) custom-call(bf16[384,1536]{1,0:T(8,128)(2,1)} %reduce-scatter.3.cloned.1.call-done.piece_ref, f32[256,1536]{1,0:T(8,128)} %get-tuple-element.102.residual_hbm, bf16[256,1536]{1,0:T(8,128)(2,1)} %get-tuple-element.103.out0_hbm, ...), custom_call_target="tpu_custom_call" | custom-call | tf_op jit(solution)/shard_map/pieces_exchange/pallas_call | solution.py:2008
  376.1 1.5 collective-permute-start.7
  377.7 0.5 collective-permute-start.8
  378.2 10.9 %spread_feed.1 = (f32[384,4096]{1,0:T(8,128)}, f32[384,4096]{1,0:T(8,128)}, f32[1024,1536]{1,0:T(8,128)}) custom-call(bf16[8,384,1536]{2,1,0:T(8,128)(2,1)} %bitcast.15, bf16[8,384,1536]{2,1,0:T(8,128)(2,1)} %bitcast.16, bf16[8,384,1536]{2,1,0:T(8,128)(2,1)} %bitcast.17), custom_call_target="tpu_custom_call" | custom-call | tf_op jit(solution)/shard_map/spread_feed/pallas_call | solution.py:2054
  389.1 1.4 dynamic-slice_reduce_fusion
  390.5 9.6 %shard_map.203 = bf16[4608,384]{1,0:T(8,128)(2,1)S(1)} custom-call(bf16[576,384]{1,0:T(8,128)(2,1)S(1)} %copy-done.5, bf16[576,384]{1,0:T(8,128)(2,1)S(1)} %collective-permute-done.7.near_x_hbm, bf16[576,384]{1,0:T(8,128)(2,1)S(1)} %collective-permute-done.8.near_y_hbm), custom_call_target="tpu_custom_call" | custom-call | tf_op jit(solution)/shard_map/pallas_call | solution.py:1313
  400.2 3.2 spread_attention.1
  403.4 0.9 copy.27
  404.3 1.1 copy.28
  (55 shorter events, 0.4 us)
Async XLA Ops:
  7.2 1.5 copy-start
  7.2 130.8 %all-gather.2.cloned.1.call-start = ((), (), s32[]{:S(2)}) async-start(), calls=%async_computation.2 | async-start | bytes 5898240 | tf_op jit(solution)/shard_map/all_gather | solution.py:2170
  48.7 6.1 %copy-start.18 = (bf16[4,2,384]{2,1,0:T(2,128)(2,1)S(1)}, bf16[4,2,384]{2,1,0:T(2,128)(2,1)}, u32[]{:S(2)}) copy-start(bf16[4,2,384]{2,1,0:T(2,128)(2,1)} %get-tuple-element.70) | copy-start | bytes 18436
  48.7 7.6 %copy-start.19 = (s32[1,16]{1,0:T(1,128)S(1)}, s32[1,16]{1,0:T(1,128)}, u32[]{:S(2)}) copy-start(s32[1,16]{1,0:T(1,128)} %param.13) | copy-start | bytes 196
  48.7 241.0 %reduce-scatter.3.cloned.1.call-start = ((), (), s32[]{:S(2)}) async-start(), calls=%async_computation.3 | async-start | bytes 5898240 | tf_op jit(solution)/shard_map/reduce_scatter | solution.py:2209
  48.8 35.9 %collective-permute-start.2 = (bf16[256,1536]{1,0:T(8,128)(2,1)}, bf16[256,1536]{1,0:T(8,128)(2,1)S(1)}, u32[]{:S(2)}, u32[]{:S(2)}) collective-permute-start(bf16[256,1536]{1,0:T(8,128)(2,1)} %bitcast.1.dy0_hbm), channel_id=1, source_target_pairs={{0,8},{4,12},{8,0},{12,4},{16,24},{20,28},{24,16},{28,20},{1,9},{5... | collective-permute-start | bytes 2359304 | tf_op jit(solution)/shard_map/ppermute | solution.py:2191
  50.2 34.5 %collective-permute-start.3 = (bf16[256,1536]{1,0:T(8,128)(2,1)}, bf16[256,1536]{1,0:T(8,128)(2,1)S(1)}, u32[]{:S(2)}, u32[]{:S(2)}) collective-permute-start(bf16[256,1536]{1,0:T(8,128)(2,1)} %bitcast.1.dy0_hbm), channel_id=1, source_target_pairs={{0,16},{4,20},{8,24},{12,28},{16,0},{20,4},{24,8},{28,12},{1,17},{... | collective-permute-start | bytes 2359304 | tf_op jit(solution)/shard_map/ppermute | solution.py:2191
  51.4 33.2 %collective-permute-start = (bf16[4,48,1536]{2,1,0:T(8,128)(2,1)}, bf16[4,48,1536]{2,1,0:T(8,128)(2,1)}, u32[]{:S(2)}, u32[]{:S(2)}) collective-permute-start(bf16[4,48,1536]{2,1,0:T(8,128)(2,1)} %get-tuple-element.74.wo0_hbm), channel_id=1, source_target_pairs={{0,8},{4,12},{8,0},{12,4},{16,24},{20,28},{24,16},{28,20},{1,9},{5... | collective-permute-start | bytes 1769480 | tf_op jit(solution)/shard_map/ppermute | solution.py:2192
  52.2 32.5 %collective-permute-start.1 = (bf16[4,48,1536]{2,1,0:T(8,128)(2,1)}, bf16[4,48,1536]{2,1,0:T(8,128)(2,1)}, u32[]{:S(2)}, u32[]{:S(2)}) collective-permute-start(bf16[4,48,1536]{2,1,0:T(8,128)(2,1)} %get-tuple-element.74.wo0_hbm), channel_id=1, source_target_pairs={{0,16},{4,20},{8,24},{12,28},{16,0},{20,4},{24,8},{28,12},{1,17},{... | collective-permute-start | bytes 1769480 | tf_op jit(solution)/shard_map/ppermute | solution.py:2192
  84.7 0.9 copy-start.12
  84.7 1.1 copy-start.13
  206.8 14.2 %copy-start.3 = (bf16[384,512]{1,0:T(8,128)(2,1)S(1)}, bf16[384,512]{1,0:T(8,128)(2,1)}, u32[]{:S(2)}) copy-start(bf16[384,512]{1,0:T(8,128)(2,1)} %fusion.pad_ref) | copy-start | bytes 1179652
  206.8 14.2 %copy-start.4 = (bf16[2048,192]{1,0:T(8,128)(2,1)S(1)}, bf16[2048,192]{1,0:T(8,128)(2,1)}, u32[]{:S(2)}) copy-start(bf16[2048,192]{1,0:T(8,128)(2,1)} %get-tuple-element.73.o_ref) | copy-start | bytes 2359300
  206.8 14.2 %copy-start.6 = (f32[2,128,128]{2,1,0:T(8,128)S(1)}, f32[2,128,128]{2,1,0:T(8,128)}, u32[]{:S(2)}) copy-start(f32[2,128,128]{2,1,0:T(8,128)} %pad_maximum_fusion.1.inner_ref) | copy-start | bytes 393220
  206.8 14.2 %copy-start.7 = (f32[2,16,128]{2,1,0:T(8,128)S(1)}, f32[2,16,128]{2,1,0:T(8,128)}, u32[]{:S(2)}) copy-start(f32[2,16,128]{2,1,0:T(8,128)} %pad_maximum_fusion.3.outer_ref) | copy-start | bytes 49156
  206.8 14.2 %copy-start.9 = (s32[16]{0:T(128)S(1)}, s32[16]{0:T(128)}, u32[]{:S(2)}) copy-start(s32[16]{0:T(128)} %select_reduce_fusion.slot_ref) | copy-start | bytes 196
  206.8 14.2 %copy-start.11 = (f32[8,512]{1,0:T(8,128)S(1)}, f32[8,512]{1,0:T(8,128)}, u32[]{:S(2)}) copy-start(f32[8,512]{1,0:T(8,128)} %get-tuple-element.95.lse_ref) | copy-start | bytes 49156
  206.8 169.3 %reduce-scatter.5.cloned.1.call-start = ((), (), s32[]{:S(2)}) async-start(), calls=%async_computation.4 | async-start | bytes 2211840 | tf_op jit(solution)/shard_map/reduce_scatter | solution.py:2227
  221.1 1.2 copy-start.8
  222.3 1.6 copy-start.10
  244.0 1.3 copy-start.2
  289.7 21.6 %collective-permute-start.4 = (bf16[256,1536]{1,0:T(8,128)(2,1)}, bf16[256,1536]{1,0:T(8,128)(2,1)S(1)}, u32[]{:S(2)}, u32[]{:S(2)}) collective-permute-start(bf16[256,1536]{1,0:T(8,128)(2,1)} %get-tuple-element.104), channel_id=1, source_target_pairs={{0,24},{4,28},{8,16},{12,20},{16,8},{20,12},{24,0},{28,4},{1,25},{... | collective-permute-start | bytes 2359304 | tf_op jit(solution)/shard_map/ppermute | solution.py:2221
  292.2 34.9 %collective-permute-start.5 = (bf16[256,1536]{1,0:T(8,128)(2,1)}, bf16[256,1536]{1,0:T(8,128)(2,1)S(1)}, u32[]{:S(2)}, u32[]{:S(2)}) collective-permute-start(bf16[256,1536]{1,0:T(8,128)(2,1)} %get-tuple-element.105), channel_id=1, source_target_pairs={{0,8},{4,12},{8,0},{12,4},{16,24},{20,28},{24,16},{28,20},{1,9},{5... | collective-permute-start | bytes 2359304 | tf_op jit(solution)/shard_map/ppermute | solution.py:2221
  292.7 34.4 %collective-permute-start.6 = (bf16[256,1536]{1,0:T(8,128)(2,1)}, bf16[256,1536]{1,0:T(8,128)(2,1)}, u32[]{:S(2)}, u32[]{:S(2)}) collective-permute-start(bf16[256,1536]{1,0:T(8,128)(2,1)} %get-tuple-element.106), channel_id=1, source_target_pairs={{0,16},{4,20},{8,24},{12,28},{16,0},{20,4},{24,8},{28,12},{1,17},{... | collective-permute-start | bytes 2359304 | tf_op jit(solution)/shard_map/ppermute | solution.py:2221
  311.3 15.7 %copy-start.15 = (bf16[256,1536]{1,0:T(8,128)(2,1)}, bf16[256,1536]{1,0:T(8,128)(2,1)S(1)}, u32[]{:S(2)}) copy-start(bf16[256,1536]{1,0:T(8,128)(2,1)S(1)} %collective-permute-done.4.out2_hbm) | copy-start | bytes 2359300
  327.0 0.9 copy-start.16
  376.1 14.4 %collective-permute-start.7 = (bf16[576,384]{1,0:T(8,128)(2,1)}, bf16[576,384]{1,0:T(8,128)(2,1)S(1)}, u32[]{:S(2)}, u32[]{:S(2)}) collective-permute-start(bf16[576,384]{1,0:T(8,128)(2,1)} %reduce-scatter.5.cloned.1.call-done.own_hbm), channel_id=1, source_target_pairs={{0,8},{4,12},{8,0},{12,4},{16,24},{20,28},{24,16},{28,20},{1,9},{5... | collective-permute-start | bytes 1327112 | tf_op jit(solution)/shard_map/ppermute | solution.py:2240
  377.7 12.8 %collective-permute-start.8 = (bf16[576,384]{1,0:T(8,128)(2,1)}, bf16[576,384]{1,0:T(8,128)(2,1)S(1)}, u32[]{:S(2)}, u32[]{:S(2)}) collective-permute-start(bf16[576,384]{1,0:T(8,128)(2,1)} %reduce-scatter.5.cloned.1.call-done.own_hbm), channel_id=1, source_target_pairs={{0,16},{4,20},{8,24},{12,28},{16,0},{20,4},{24,8},{28,12},{1,17},{... | collective-permute-start | bytes 1327112 | tf_op jit(solution)/shard_map/ppermute | solution.py:2240
  378.2 12.3 %copy-start.5 = (bf16[576,384]{1,0:T(8,128)(2,1)S(1)}, bf16[576,384]{1,0:T(8,128)(2,1)}, u32[]{:S(2)}) copy-start(bf16[576,384]{1,0:T(8,128)(2,1)} %reduce-scatter.5.cloned.1.call-done.own_hbm) | copy-start | bytes 1327108
  400.1 3.3 copy-start.17
  400.2 4.1 %copy-start.14 = (f32[1,256,1536]{2,1,0:T(8,128)S(1)}, f32[1,256,1536]{2,1,0:T(8,128)}, u32[]{:S(2)}) copy-start(f32[1,256,1536]{2,1,0:T(8,128)} %get-tuple-element.145) | copy-start | bytes 4718596
  403.4 2.0 copy-start.1
Sparse Core Ops, SparseCore 0:
  48.8 89.0 all-gather.1
  206.9 82.7 reduce-scatter.2
  292.0 38.9 reduce-scatter.4

commit v7 on v6

--- a/solution.py
+++ b/solution.py
@@ -3,6 +3,7 @@
 
 import jax
 import jax.numpy as jnp
+import numpy as np
 from jax import lax
 from jax.experimental import pallas as pl
 from jax.experimental.pallas import tpu as pltpu
@@ -384,11 +385,18 @@
 
 
 def padding(heads):
-    column = jnp.arange(heads * HEAD_SIZE, dtype=jnp.int32)
-    half_at, rest = column // HALF, column % HALF
-    target = half_at * (LANES // 2) + rest
-    lanes = jnp.arange(heads * LANES, dtype=jnp.int32)
-    return (target[:, None] == lanes[None, :]).astype(jnp.bfloat16)
+    column = np.arange(heads * HEAD_SIZE)
+    target = column // HALF * (LANES // 2) + column % HALF
+    lanes = np.arange(heads * LANES)
+    return jnp.asarray((target[:, None] == lanes[None, :]).astype(np.float32), jnp.bfloat16)
+
+
+def angle_table(positions):
+    inverse = rotary_base ** (-2.0 * np.arange(HALF) / HEAD_SIZE)
+    angles = positions[:, None] * inverse[None, :]
+    both = np.stack([np.cos(angles), np.sin(angles)])
+    both = np.pad(both, ((0, 0), (0, 0), (0, LANES // 2 - HALF)))
+    return jnp.asarray(np.concatenate([both, both], axis=2), jnp.float32)
 
 
 def turn(part, cosine, sine):
@@ -1803,11 +1811,11 @@
     x_hbm,
     residual_hbm,
     dwo_hbm,
+    term_ref,
     gain_ref,
     pad_ref,
     input_ref,
     grads_ref,
-    term_ref,
     wp_ref,
     all_x,
     residual_ref,
@@ -1876,7 +1884,7 @@
     shard = packed.shape[0] // line
     for slot in range(line):
         grads_ref[slot, :shard, :] = packed[slot * shard : (slot + 1) * shard, :]
-        grads_ref[slot, shard:, :] = dwo_ref[slot]
+        grads_ref[slot, shard : shard + dwo_ref.shape[1], :] = dwo_ref[slot]
     half = rows // 2
     total = jnp.zeros_like(gain)
     for which in (1, 0):
@@ -1890,12 +1898,19 @@
         scaled = grad * gain
         mean = jnp.mean(scaled * normed, axis=-1, keepdims=True)
         input_ref[0, here_rows, :] = residual_ref[here_rows, :] + scale * (scaled - normed * mean)
-    term_ref[...] = total
+    blank = jnp.zeros((GAIN_ROWS - 2, grads_ref.shape[2]), jnp.float32)
+    for slot in range(line):
+        columns = slice(slot * shard, (slot + 1) * shard)
+        rows_of = jnp.concatenate([total[:, columns], term_ref[:, columns], blank], axis=0)
+        grads_ref[slot, grads_ref.shape[1] - GAIN_ROWS :, :] = rows_of.astype(grads_ref.dtype)
     reduce.finish()
     copies.finish()
 
 
-def input_exchange(dqkv, wp, x, residual, dwo, gain, pad):
+GAIN_ROWS = 32
+
+
+def input_exchange(dqkv, wp, x, residual, dwo, term, gain, pad):
     rows, model = residual.shape
     line, dealt, across = dwo.shape
     f32 = jnp.float32
@@ -1903,11 +1918,10 @@
         input_kernel,
         out_shape=(
             jax.ShapeDtypeStruct((1, rows, model), f32),
-            jax.ShapeDtypeStruct((line, model // line + dealt, across), dwo.dtype),
-            jax.ShapeDtypeStruct((1, model), f32),
+            jax.ShapeDtypeStruct((line, model // line + dealt + GAIN_ROWS, across), dwo.dtype),
         ),
-        in_specs=in_vmem(1) + in_hbm(4) + in_vmem(2),
-        out_specs=tuple(in_vmem(3)),
+        in_specs=in_vmem(1) + in_hbm(4) + in_vmem(3),
+        out_specs=tuple(in_vmem(2)),
         scratch_shapes=[
             pltpu.VMEM(wp.shape, wp.dtype),
             pltpu.VMEM(x.shape, x.dtype),
@@ -1924,62 +1938,40 @@
         ],
         compiler_params=remote_params(7),
         name="input_exchange",
-    )(dqkv, wp, x, residual, dwo, gain, pad)
+    )(dqkv, wp, x, residual, dwo, term, gain, pad)
 
 
 def pieces_kernel(
-    line,
     piece_ref,
     residual_hbm,
     out0_hbm,
     out2_hbm,
     out4_hbm,
     out6_hbm,
-    term_one_ref,
-    term_two_ref,
     whole_ref,
-    total_ref,
     output_ref,
     own,
     residual_ref,
     outs_ref,
-    terms,
-    terms_heard,
-    plane_sum,
-    across,
     send,
     recv,
     here,
 ):
-    me, index = lax.axis_index("ctx"), lax.axis_index("fsdp")
+    me = lax.axis_index("ctx")
     outs = (out0_hbm, out2_hbm, out4_hbm, out6_hbm)
     fetch = local_copies(
         [(piece_ref, own), (residual_hbm, residual_ref)]
         + [(ref, outs_ref.at[number]) for number, ref in enumerate(outs)],
         here.at[pl.ds(0, 6)],
     )
-    start_barrier(me, ALL, range(1, line), index, line)
+    start_barrier(me, NEAR)
     copies = Copies(send, recv)
     rows = piece_ref.shape[0]
     part = row_part(whole_ref, rows)
     gather = PlaneGather(copies, me, row_half(own, rows), part)
-    first = copies.next
-    copies.next += 7 + line - 1
-    terms[0:1, :] = term_one_ref[...]
-    terms[1:2, :] = term_two_ref[...]
-    for bit in range(1, 8):
-        copies.send(first + bit - 1, terms, terms_heard.at[bit], {"ctx": me ^ bit})
     fetch[0].wait()
     gather.begin()
     local = local_copies([(own, part(me, slice(None)))], here.at[pl.ds(6, 1)])
-    total = terms[...]
-    for bit in range(1, 8):
-        copies.arrived(first + bit - 1, terms_heard.at[bit])
-        total = total + terms_heard[bit]
-    plane_sum[...] = total
-    for step in range(1, line):
-        peer = {"fsdp": lax.rem(index + step, line)}
-        copies.send(first + 6 + step, plane_sum, across.at[step], peer)
     for copy in fetch[1:]:
         copy.wait()
     total = residual_ref[...]
@@ -1988,47 +1980,34 @@
     output_ref[0] = total.astype(output_ref.dtype)
     gather.first_hop()
     gather.second_hop()
-    total = plane_sum[...]
-    for step in range(1, line):
-        copies.arrived(first + 6 + step, across.at[step])
-        total = total + across[step]
-    total_ref[...] = total
     gather.third_hop()
     gather.last()
     gather.finish()
     local[0].wait()
-    copies.finish()
-
-
-def pieces_exchange(line, piece, term_one, term_two, residual, outs):
+
+
+def pieces_exchange(piece, residual, outs):
     plane = lax.axis_size("ctx")
     rows, model = residual.shape
-    f32 = jnp.float32
-    copies = GATHER_COPIES + 7 + line - 1
     return pl.pallas_call(
-        functools.partial(pieces_kernel, line),
+        pieces_kernel,
         out_shape=(
             jax.ShapeDtypeStruct((plane * piece.shape[0], piece.shape[1]), piece.dtype),
-            jax.ShapeDtypeStruct((2, model), f32),
             jax.ShapeDtypeStruct((1, rows, model), jnp.bfloat16),
         ),
-        in_specs=anywhere(6) + in_vmem(2),
-        out_specs=(*anywhere(1), *in_vmem(2)),
+        in_specs=anywhere(6),
+        out_specs=(*anywhere(1), *in_vmem(1)),
         scratch_shapes=[
             pltpu.VMEM(piece.shape, piece.dtype),
-            pltpu.VMEM((rows, model), f32),
+            pltpu.VMEM((rows, model), jnp.float32),
             pltpu.VMEM((4, rows, model), outs[0].dtype),
-            pltpu.VMEM((2, model), f32),
-            pltpu.VMEM((plane, 2, model), f32),
-            pltpu.VMEM((2, model), f32),
-            pltpu.VMEM((line, 2, model), f32),
-            pltpu.SemaphoreType.DMA((copies,)),
-            pltpu.SemaphoreType.DMA((copies,)),
+            pltpu.SemaphoreType.DMA((GATHER_COPIES,)),
+            pltpu.SemaphoreType.DMA((GATHER_COPIES,)),
             pltpu.SemaphoreType.DMA((7,)),
         ],
         compiler_params=remote_params(8),
         name="pieces_exchange",
-    )(piece, residual, *outs, term_one, term_two)
+    )(piece, residual, *outs)
 
 
 def spread_kernel(gate_in, up_in, down_in, gate_ref, up_ref, down_ref):
@@ -2074,7 +2053,7 @@
     )(pieces, pieces, pieces)
 
 
-def spread_attention_kernel(in_ref, q_ref, k_ref, v_ref, wo_ref):
+def spread_attention_kernel(in_ref, q_ref, k_ref, v_ref, wo_ref, gains_ref):
     plane, _, across = in_ref.shape
     shard = q_ref.shape[0]
     key_width = k_ref.shape[1] // plane
@@ -2095,6 +2074,8 @@
             wo_ref[slot * HALF : (slot + 1) * HALF, number * across : (number + 1) * across] = (
                 in_ref[slot, source, :].astype(jnp.float32)
             )
+    terms = [in_ref[slot, in_ref.shape[1] - GAIN_ROWS :, :] for slot in range(plane)]
+    gains_ref[...] = sum(term.astype(jnp.float32) for term in terms)[: gains_ref.shape[0], :]
 
 
 def spread_attention(pieces, shard, model, query_width, key_width):
@@ -2104,12 +2085,13 @@
     return pl.pallas_call(
         spread_attention_kernel,
         in_specs=in_vmem(1),
-        out_specs=tuple(in_vmem(4)),
+        out_specs=tuple(in_vmem(5)),
         out_shape=(
             jax.ShapeDtypeStruct((shard, plane * query_width), f32),
             jax.ShapeDtypeStruct((shard, plane * key_width), f32),
             jax.ShapeDtypeStruct((shard, plane * key_width), f32),
             jax.ShapeDtypeStruct((plane * HALF, model), f32),
+            jax.ShapeDtypeStruct((8, shard), f32),
         ),
         compiler_params=pltpu.CompilerParams(vmem_limit_bytes=40 << 20),
         name="spread_attention",
@@ -2169,17 +2151,8 @@
     )
     feed_w = lax.all_gather(feed_mine, "fsdp", axis=0, tiled=True)
 
-    steps_index = jnp.arange(HALF, dtype=jnp.float32)
-    inverse = jnp.exp(steps_index * jnp.float32(-2.0 * math.log(rotary_base) / HEAD_SIZE))
-
-    def table_of(positions):
-        angles = positions.astype(jnp.float32)[:, None] * inverse[None, :]
-        both = jnp.stack([jnp.cos(angles), jnp.sin(angles)])
-        both = jnp.pad(both, ((0, 0), (0, 0), (0, LANES // 2 - HALF)))
-        return jnp.concatenate([both, both], axis=2)
-
-    inner = table_of(jnp.arange(block, dtype=jnp.int32))
-    outer = table_of(places * block)
+    inner = angle_table(np.arange(block))
+    outer = angle_table(np.arange(slot_count) * block)
     pad = padding(GROUP + 2)
 
     gains = jnp.transpose(gains, (1, 0, 2)).reshape(2, model).astype(jnp.float32)
@@ -2220,8 +2193,8 @@
         pairs = [(device, device ^ bit) for device in range(plane)]
         outs.append(lax.ppermute(out_parts[part], "ctx", pairs))
     grads = attend_back(slots, qkv, o, grad_o, lse, pad, inner, outer)
-    input_grad, attention_grads, attention_term = input_exchange(
-        grads, qkv_pad, x_all, grad_residual, wo_term, gains[:1], pad
+    input_grad, attention_grads = input_exchange(
+        grads, qkv_pad, x_all, grad_residual, wo_term, feedforward_term, gains[:1], pad
     )
     attention_grads, feed_grads = lax.optimization_barrier((attention_grads, feed_grads))
     attention_grads = lax.psum_scatter(
@@ -2230,20 +2203,17 @@
         scatter_dimension=0,
         tiled=True,
     )
-    feed_pieces, gain_terms, layer_output = pieces_exchange(
-        line, feed_grads, attention_term, feedforward_term, residual, outs
-    )
-    attention_grads, gain_terms = lax.optimization_barrier((attention_grads, gain_terms))
+    feed_pieces, layer_output = pieces_exchange(feed_grads, residual, outs)
+    attention_grads, layer_output = lax.optimization_barrier((attention_grads, layer_output))
     near_grads = []
     for bit in (2, 4):
         pairs = [(device, device ^ bit) for device in range(plane)]
         near_grads.append(lax.ppermute(attention_grads, "ctx", pairs))
     gate_grad, up_grad, down_grad = spread_feed(feed_pieces, shard, line, unit)
     attention_pieces = near_gather([attention_grads, *near_grads], 9)
-    query_grad, key_grad, value_grad, out_grad = spread_attention(
+    query_grad, key_grad, value_grad, out_grad, gain_terms = spread_attention(
         attention_pieces, shard, model, query_width, key_width
     )
-    gain_terms = lax.dynamic_slice_in_dim(gain_terms, lax.axis_index("fsdp") * shard, shard, 1)
     return (
         layer_output,
         input_grad,

time: 412 us -> 410 us (level)
  transfers between devices with their start and end apart: 12 -> 12, of which waited for: 5 -> 7; matrix products, arithmetic and copies ran while one was open for 1% -> 0% of each run, Pallas kernels for 50% -> 50%
where the time goes in v7:
time: 410 us; the launch traced here: 409 us
  Pallas kernels  322 us (79%)
  waiting for transfers between devices  48.2 us (12%)
  between operations  14 us (3%)
  local copies, waits for them, and re-layouts  12.1 us (3%)
  starting transfers between devices  9.92 us (2%)
    pallas_call x1, Pallas kernels, feed(): pl.pallas_call(functools.partial(feed_kernel, line), out_shape=(jax.Shape...  68.8 us
    pallas_call x1, Pallas kernels, second_exchange(): pl.pallas_call(second_kernel, out_shape=(jax.ShapeDtypeStruct((2 * GROUP,...  48.7 us
    pallas_call x1, Pallas kernels, pieces_exchange(): pl.pallas_call(pieces_kernel, out_shape=(jax.ShapeDtypeStruct((plane * pi...  44.8 us
    pallas_call x1, Pallas kernels, input_exchange(): pl.pallas_call(input_kernel, out_shape=(jax.ShapeDtypeStruct((1, rows, mo...  37.3 us
    pallas_call x1, Pallas kernels, first_exchange(): pl.pallas_call(functools.partial(first_kernel, line), out_shape=(jax.Shap...  37.2 us
    ppermute x3, waiting for transfers between devices, head_local(): outs.append(lax.ppermute(out_parts[part], 'ctx', pairs))  33.8 us
    pallas_call x1, Pallas kernels, attend(): pl.pallas_call(forward_kernel, grid_spec=pltpu.PrefetchScalarGridSpec(num...  27.7 us
    pallas_call x1, Pallas kernels, attend_back(): pl.pallas_call(backward_kernel, grid_spec=pltpu.PrefetchScalarGridSpec(nu...  20.2 us
  transfers between devices with their start and end apart: 12, of which 7 were waited for; matrix products, arithmetic and copies ran while one was open for 0% of the time, Pallas kernels for 50%

profile of v7, /device:TPU:0, one launch (start us, length us, event | category | flops | bytes accessed | tf_op | source)
XLA Modules:
  0.0 409.4 jit_solution(16636950624334304832)
XLA Ops:
  7.2 0.0 all-gather.2.cloned.1.call-start
  7.2 0.8 stack.10
  8.0 0.7 stack.9
  8.7 0.1 constant_dynamic-slice_fusion.1
  8.8 0.6 pad_maximum_fusion.1.gain_ref
  9.4 1.1 constant_dynamic-slice_fusion
  10.6 0.9 pad_maximum_fusion.qkv_ref
  11.4 37.2 %first_exchange.1 = (bf16[2048,1536]{1,0:T(8,128)(2,1)}, bf16[4,384,384]{2,1,0:T(8,128)(2,1)}, bf16[4,48,1536]{2,1,0:T(8,128)(2,1)}, bf16[4,2,384]{2,1,0:T(2,128)(2,1)}, bf16[384,1536]{1,0:T(8,128)(2,1)}) custom-call(bf16[256,1536]{1,0:T(8,128)(2,1)} %bitcast.18, bf16[384,384]{1,0:T(8,128)(2,1)} %pad_maximum_fusion.qkv_ref, bf16[384,1536]{1,0:T(8,128)(2,1)} %wo_ref.1, ...), custom_call_target="tpu_custom_call" | custom-call | tf_op jit(solution)/shard_map/first_exchange/pallas_call | solution.py:1033
  48.7 0.0 reduce-scatter.3.cloned.1.call-start
  48.7 1.4 collective-permute-start.2
  50.1 1.3 collective-permute-start.3
  51.4 0.8 collective-permute-start
  52.2 0.7 collective-permute-start.1
  52.9 0.7 convert_bitcast_fusion
  53.6 0.6 fusion
  54.2 0.6 select_reduce_fusion.slot_ref
  54.8 27.7 %attend.1 = (bf16[2048,512]{1,0:T(8,128)(2,1)}, bf16[2048,192]{1,0:T(8,128)(2,1)}, bf16[192,2048]{1,0:T(8,128)(2,1)}, f32[8,512]{1,0:T(8,128)}, bf16[1536,512]{1,0:T(8,128)(2,1)}) custom-call(s32[16]{0:T(128)} %select_reduce_fusion.slot_ref, bf16[2048,1536]{1,0:T(8,128)(2,1)} %get-tuple-element.68.xa_ref.xb_ref.x_hbm, ...), custom_call_target="tpu_custom_call" | custom-call | flops 5368709120 | bytes 12582912 | tf_op jit(solution)/shard_map/attend/pallas_call | solution.py:543
  82.6 0.1 collective-permute-done.1.wo4_hbm
  82.7 0.9 copy-done.12
  83.5 0.3 copy-done.13
  83.8 48.7 %second_exchange.1 = (bf16[4,48,1536]{2,1,0:T(8,128)(2,1)}, bf16[256,1536]{1,0:T(8,128)(2,1)}, f32[256,1536]{1,0:T(8,128)}, f32[256,1536]{1,0:T(8,128)}, f32[256...) custom-call(bf16[2048,192]{1,0:T(8,128)(2,1)} %get-tuple-element.72.o_ref, ...), custom_call_target="tpu_custom_call" | custom-call | tf_op jit(solution)/shard_map/second_exchange/pallas_call | solution.py:1271
  132.5 5.5 %all-gather.2.cloned.1.call-done.w_hbm = bf16[1536,1536]{1,0:T(8,128)(2,1)} async-done(((bf16[384,1536]{1,0:T(8,128)(2,1)}), bf16[1536,1536]{1,0:T(8,128)(2,1)}) %all-gather.2.cloned.1.call-update) | async-done | bytes 4718608 | tf_op jit(solution)/shard_map/all_gather | solution.py:2152
  138.0 68.8 %feed.1 = (f32[256,1536]{1,0:T(8,128)}, f32[1,1536]{1,0:T(1,128)}, bf16[256,1536]{1,0:T(8,128)(2,1)}, bf16[256,1536]{1,0:T(8,128)(2,1)}, bf16[256,1536]{1,0:T(8,...) custom-call(bf16[256,1536]{1,0:T(8,128)(2,1)} %get-tuple-element.75., ...), custom_call_target="tpu_custom_call" | custom-call | tf_op jit(solution)/shard_map/feed/pallas_call | solution.py:1768
  206.9 0.0 reduce-scatter.5.cloned.1.call-start
  206.9 13.9 %third_exchange.1 = (bf16[2048,192]{1,0:T(8,128)(2,1)}, bf16[4,192,384]{2,1,0:T(8,128)(2,1)}) custom-call(bf16[256,1536]{1,0:T(8,128)(2,1)} %get-tuple-element.87.g0_hbm, bf16[256,1536]{1,0:T(8,128)(2,1)} %get-tuple-element.88.g2_hbm, bf16[256,1536]{1,0:T(8,128)(2,1)} %get-tuple-element.89.g4_hbm, bf16[192,2048]{1,0:T(8,128)(2,1)} %bitcast.22, ...), custom_call_target="tpu_custom_call" | custom-call | tf_op jit(solution)/shard_map/third_exchange/pallas_call | solution.py:1388
  220.9 1.2 copy-done.6
  222.2 1.6 copy-done.10
  223.7 20.2 %attend_back.1.dqkv_ref = bf16[2048,512]{1,0:T(8,128)(2,1)S(1)} custom-call(s32[16]{0:T(128)S(1)} %copy-done.9, bf16[2048,512]{1,0:T(8,128)(2,1)S(1)} %copy-done.10, bf16[2048,192]{1,0:T(8,128)(2,1)S(1)} %copy-done.3, bf16[2048,192]{1,0:T(8,128)(2,1)S(1)} %copy-done.6, f32[8,512]{1,0:T(8,128)S(1)} %copy-done.11, bf16[384,512]{1,0:T(8,128)(2,1)S(1)} %copy-done.5, ...), custom_call_target="tpu_custom_call" | custom-call | flops 5368709120 | bytes 8388608 | tf_op jit(solution)/shard_map/attend_back/pallas_call | solution.py:682
  243.9 1.3 copy-done.2
  245.2 37.3 %input_exchange.1 = (f32[1,256,1536]{2,1,0:T(8,128)}, bf16[4,608,384]{2,1,0:T(8,128)(2,1)}) custom-call(bf16[2048,512]{1,0:T(8,128)(2,1)} %copy-done.2, bf16[1536,512]{1,0:T(8,128)(2,1)} %get-tuple-element.95.wp_hbm, bf16[2048,1536]{1,0:T(8,128)(2,1)} %get-tuple-element.68.xa_ref.xb_ref.x_hbm, f32[256,1536]{1,0:T(8,128)} %get-tuple-element.96.residual_hbm, ...), custom_call_target="tpu_custom_call" | custom-call | tf_op jit(solution)/shard_map/input_exchange/pallas_call | solution.py:1917
  282.5 7.2 %reduce-scatter.3.cloned.1.call-done.piece_ref = bf16[384,1536]{1,0:T(8,128)(2,1)} async-done(((bf16[1536,1536]{1,0:T(8,128)(2,1)}), bf16[384,1536]{1,0:T(8,128)(2,1)}) %reduce-scatter.3.cloned.1.call-update) | async-done | bytes 1179664 | tf_op jit(solution)/shard_map/reduce_scatter | solution.py:2182
  289.8 2.5 collective-permute-start.4
  292.2 0.6 collective-permute-start.5
  292.8 0.5 collective-permute-start.6
  293.3 18.1 %collective-permute-done.4.out2_hbm = bf16[256,1536]{1,0:T(8,128)(2,1)S(1)} collective-permute-done((bf16[256,1536]{1,0:T(8,128)(2,1)}, bf16[256,1536]{1,0:T(8,128)(2,1)S(1)}, u32[]{:S(2)}, u32[]{:S(2)}) %collective-permute-start.4) | collective-permute-done | bytes 786464 | tf_op jit(solution)/shard_map/ppermute | solution.py:2194
  311.4 15.7 %collective-permute-done.5.out4_hbm = bf16[256,1536]{1,0:T(8,128)(2,1)S(1)} collective-permute-done((bf16[256,1536]{1,0:T(8,128)(2,1)}, bf16[256,1536]{1,0:T(8,128)(2,1)S(1)}, u32[]{:S(2)}, u32[]{:S(2)}) %collective-permute-start.5) | collective-permute-done | bytes 786464 | tf_op jit(solution)/shard_map/ppermute | solution.py:2194
  327.1 0.8 copy-done.17
  328.0 44.8 %pieces_exchange.1 = (bf16[3072,1536]{1,0:T(8,128)(2,1)}, bf16[1,256,1536]{2,1,0:T(8,128)(2,1)}) custom-call(bf16[384,1536]{1,0:T(8,128)(2,1)} %reduce-scatter.3.cloned.1.call-done.piece_ref, f32[256,1536]{1,0:T(8,128)} %get-tuple-element.103.residual_hbm, bf16[256,1536]{1,0:T(8,128)(2,1)} %get-tuple-element.104.out0_hbm, bf16[256,1536]{1,0:T(8,128)(2,1)} %copy-done.16, ...), custom_call_target="tpu_custom_call" | custom-call | tf_op jit(solution)/shard_map/pieces_exchange/pallas_call | solution.py:1992
  372.8 1.5 collective-permute-start.7
  374.4 0.6 collective-permute-start.8
  375.0 10.9 %spread_feed.1 = (f32[384,4096]{1,0:T(8,128)}, f32[384,4096]{1,0:T(8,128)}, f32[1024,1536]{1,0:T(8,128)}) custom-call(bf16[8,384,1536]{2,1,0:T(8,128)(2,1)} %bitcast.15, bf16[8,384,1536]{2,1,0:T(8,128)(2,1)} %bitcast.16, bf16[8,384,1536]{2,1,0:T(8,128)(2,1)} %bitcast.17), custom_call_target="tpu_custom_call" | custom-call | tf_op jit(solution)/shard_map/spread_feed/pallas_call | solution.py:2033
  385.8 0.3 collective-permute-done.7.near_x_hbm
  386.1 1.2 collective-permute-done.8.near_y_hbm
  387.3 9.4 %shard_map.230 = bf16[4864,384]{1,0:T(8,128)(2,1)S(1)} custom-call(bf16[608,384]{1,0:T(8,128)(2,1)S(1)} %copy-done.4, bf16[608,384]{1,0:T(8,128)(2,1)S(1)} %collective-permute-done.7.near_x_hbm, bf16[608,384]{1,0:T(8,128)(2,1)S(1)} %collective-permute-done.8.near_y_hbm), custom_call_target="tpu_custom_call" | custom-call | tf_op jit(solution)/shard_map/pallas_call | solution.py:1321
  396.7 3.6 spread_attention.1
  400.3 0.6 slice_reduce_fusion
  400.9 0.9 copy.28
  401.8 1.1 copy.29
  (40 shorter events, 0.2 us)
Async XLA Ops:
  7.2 1.5 copy-start
  7.2 130.8 %all-gather.2.cloned.1.call-start = ((), (), s32[]{:S(2)}) async-start(), calls=%async_computation.2 | async-start | bytes 5898240 | tf_op jit(solution)/shard_map/all_gather | solution.py:2152
  11.4 42.8 %copy-start.18 = (s32[1,16]{1,0:T(1,128)S(1)}, s32[1,16]{1,0:T(1,128)}, u32[]{:S(2)}) copy-start(s32[1,16]{1,0:T(1,128)} %param.16) | copy-start | bytes 196
  48.7 241.0 %reduce-scatter.3.cloned.1.call-start = ((), (), s32[]{:S(2)}) async-start(), calls=%async_computation.3 | async-start | bytes 5898240 | tf_op jit(solution)/shard_map/reduce_scatter | solution.py:2182
  48.7 33.9 %collective-permute-start.2 = (bf16[256,1536]{1,0:T(8,128)(2,1)}, bf16[256,1536]{1,0:T(8,128)(2,1)S(1)}, u32[]{:S(2)}, u32[]{:S(2)}) collective-permute-start(bf16[256,1536]{1,0:T(8,128)(2,1)} %bitcast.1.dy0_hbm), channel_id=1, source_target_pairs={{0,8},{4,12},{8,0},{12,4},{16,24},{20,28},{24,16},{28,20},{1,9},{5... | collective-permute-start | bytes 2359304 | tf_op jit(solution)/shard_map/ppermute | solution.py:2164
  50.1 32.5 %collective-permute-start.3 = (bf16[256,1536]{1,0:T(8,128)(2,1)}, bf16[256,1536]{1,0:T(8,128)(2,1)S(1)}, u32[]{:S(2)}, u32[]{:S(2)}) collective-permute-start(bf16[256,1536]{1,0:T(8,128)(2,1)} %bitcast.1.dy0_hbm), channel_id=1, source_target_pairs={{0,16},{4,20},{8,24},{12,28},{16,0},{20,4},{24,8},{28,12},{1,17},{... | collective-permute-start | bytes 2359304 | tf_op jit(solution)/shard_map/ppermute | solution.py:2164
  51.4 31.1 %collective-permute-start = (bf16[4,48,1536]{2,1,0:T(8,128)(2,1)}, bf16[4,48,1536]{2,1,0:T(8,128)(2,1)}, u32[]{:S(2)}, u32[]{:S(2)}) collective-permute-start(bf16[4,48,1536]{2,1,0:T(8,128)(2,1)} %get-tuple-element.73.wo0_hbm), channel_id=1, source_target_pairs={{0,8},{4,12},{8,0},{12,4},{16,24},{20,28},{24,16},{28,20},{1,9},{5... | collective-permute-start | bytes 1769480 | tf_op jit(solution)/shard_map/ppermute | solution.py:2165
  52.2 30.5 %collective-permute-start.1 = (bf16[4,48,1536]{2,1,0:T(8,128)(2,1)}, bf16[4,48,1536]{2,1,0:T(8,128)(2,1)}, u32[]{:S(2)}, u32[]{:S(2)}) collective-permute-start(bf16[4,48,1536]{2,1,0:T(8,128)(2,1)} %get-tuple-element.73.wo0_hbm), channel_id=1, source_target_pairs={{0,16},{4,20},{8,24},{12,28},{16,0},{20,4},{24,8},{28,12},{1,17},{... | collective-permute-start | bytes 1769480 | tf_op jit(solution)/shard_map/ppermute | solution.py:2165
  82.7 0.9 copy-start.12
  82.7 1.1 copy-start.13
  206.8 14.1 %copy-start.3 = (bf16[2048,192]{1,0:T(8,128)(2,1)S(1)}, bf16[2048,192]{1,0:T(8,128)(2,1)}, u32[]{:S(2)}) copy-start(bf16[2048,192]{1,0:T(8,128)(2,1)} %get-tuple-element.72.o_ref) | copy-start | bytes 2359300
  206.8 14.1 %copy-start.5 = (bf16[384,512]{1,0:T(8,128)(2,1)S(1)}, bf16[384,512]{1,0:T(8,128)(2,1)}, u32[]{:S(2)}) copy-start(bf16[384,512]{1,0:T(8,128)(2,1)} %constant.24.clone.pad_ref) | copy-start | bytes 1179652
  206.8 14.1 %copy-start.7 = (f32[2,128,128]{2,1,0:T(8,128)S(1)}, f32[2,128,128]{2,1,0:T(8,128)}, u32[]{:S(2)}) copy-start(f32[2,128,128]{2,1,0:T(8,128)} %constant.22.clone.inner_ref) | copy-start | bytes 393220
  206.8 14.1 %copy-start.8 = (f32[2,16,128]{2,1,0:T(8,128)S(1)}, f32[2,16,128]{2,1,0:T(8,128)}, u32[]{:S(2)}) copy-start(f32[2,16,128]{2,1,0:T(8,128)} %constant.23.clone.outer_ref) | copy-start | bytes 49156
  206.8 14.1 %copy-start.9 = (s32[16]{0:T(128)S(1)}, s32[16]{0:T(128)}, u32[]{:S(2)}) copy-start(s32[16]{0:T(128)} %select_reduce_fusion.slot_ref) | copy-start | bytes 196
  206.9 14.1 %copy-start.11 = (f32[8,512]{1,0:T(8,128)S(1)}, f32[8,512]{1,0:T(8,128)}, u32[]{:S(2)}) copy-start(f32[8,512]{1,0:T(8,128)} %get-tuple-element.94.lse_ref) | copy-start | bytes 49156
  206.9 166.0 %reduce-scatter.5.cloned.1.call-start = ((), (), s32[]{:S(2)}) async-start(), calls=%async_computation.4 | async-start | bytes 2334720 | tf_op jit(solution)/shard_map/reduce_scatter | solution.py:2200
  220.9 1.2 copy-start.6
  222.2 1.6 copy-start.10
  243.9 1.3 copy-start.2
  289.8 21.6 %collective-permute-start.4 = (bf16[256,1536]{1,0:T(8,128)(2,1)}, bf16[256,1536]{1,0:T(8,128)(2,1)S(1)}, u32[]{:S(2)}, u32[]{:S(2)}) collective-permute-start(bf16[256,1536]{1,0:T(8,128)(2,1)} %get-tuple-element.105), channel_id=1, source_target_pairs={{0,24},{4,28},{8,16},{12,20},{16,8},{20,12},{24,0},{28,4},{1,25},{... | collective-permute-start | bytes 2359304 | tf_op jit(solution)/shard_map/ppermute | solution.py:2194
  292.2 34.9 %collective-permute-start.5 = (bf16[256,1536]{1,0:T(8,128)(2,1)}, bf16[256,1536]{1,0:T(8,128)(2,1)S(1)}, u32[]{:S(2)}, u32[]{:S(2)}) collective-permute-start(bf16[256,1536]{1,0:T(8,128)(2,1)} %get-tuple-element.106), channel_id=1, source_target_pairs={{0,8},{4,12},{8,0},{12,4},{16,24},{20,28},{24,16},{28,20},{1,9},{5... | collective-permute-start | bytes 2359304 | tf_op jit(solution)/shard_map/ppermute | solution.py:2194
  292.8 34.3 %collective-permute-start.6 = (bf16[256,1536]{1,0:T(8,128)(2,1)}, bf16[256,1536]{1,0:T(8,128)(2,1)}, u32[]{:S(2)}, u32[]{:S(2)}) collective-permute-start(bf16[256,1536]{1,0:T(8,128)(2,1)} %get-tuple-element.107), channel_id=1, source_target_pairs={{0,16},{4,20},{8,24},{12,28},{16,0},{20,4},{24,8},{28,12},{1,17},{... | collective-permute-start | bytes 2359304 | tf_op jit(solution)/shard_map/ppermute | solution.py:2194
  311.4 15.7 %copy-start.16 = (bf16[256,1536]{1,0:T(8,128)(2,1)}, bf16[256,1536]{1,0:T(8,128)(2,1)S(1)}, u32[]{:S(2)}) copy-start(bf16[256,1536]{1,0:T(8,128)(2,1)S(1)} %collective-permute-done.4.out2_hbm) | copy-start | bytes 2359300
  327.1 0.9 copy-start.17
  372.8 13.3 %collective-permute-start.7 = (bf16[608,384]{1,0:T(8,128)(2,1)}, bf16[608,384]{1,0:T(8,128)(2,1)S(1)}, u32[]{:S(2)}, u32[]{:S(2)}) collective-permute-start(bf16[608,384]{1,0:T(8,128)(2,1)} %reduce-scatter.5.cloned.1.call-done.own_hbm), channel_id=1, source_target_pairs={{0,8},{4,12},{8,0},{12,4},{16,24},{20,28},{24,16},{28,20},{1,9},{5... | collective-permute-start | bytes 1400840 | tf_op jit(solution)/shard_map/ppermute | solution.py:2211
  374.4 12.9 %collective-permute-start.8 = (bf16[608,384]{1,0:T(8,128)(2,1)}, bf16[608,384]{1,0:T(8,128)(2,1)S(1)}, u32[]{:S(2)}, u32[]{:S(2)}) collective-permute-start(bf16[608,384]{1,0:T(8,128)(2,1)} %reduce-scatter.5.cloned.1.call-done.own_hbm), channel_id=1, source_target_pairs={{0,16},{4,20},{8,24},{12,28},{16,0},{20,4},{24,8},{28,12},{1,17},{... | collective-permute-start | bytes 1400840 | tf_op jit(solution)/shard_map/ppermute | solution.py:2211
  375.0 12.3 %copy-start.4 = (bf16[608,384]{1,0:T(8,128)(2,1)S(1)}, bf16[608,384]{1,0:T(8,128)(2,1)}, u32[]{:S(2)}) copy-start(bf16[608,384]{1,0:T(8,128)(2,1)} %reduce-scatter.5.cloned.1.call-done.own_hbm) | copy-start | bytes 1400836
  396.7 4.2 %copy-start.15 = (bf16[1,256,1536]{2,1,0:T(8,128)(2,1)S(1)}, bf16[1,256,1536]{2,1,0:T(8,128)(2,1)}, u32[]{:S(2)}) copy-start(bf16[1,256,1536]{2,1,0:T(8,128)(2,1)} %get-tuple-element.138) | copy-start | bytes 2359300
  396.7 5.1 %copy-start.14 = (f32[1,256,1536]{2,1,0:T(8,128)S(1)}, f32[1,256,1536]{2,1,0:T(8,128)}, u32[]{:S(2)}) copy-start(f32[1,256,1536]{2,1,0:T(8,128)} %get-tuple-element.139) | copy-start | bytes 4718596
  400.9 2.0 copy-start.1
Sparse Core Ops, SparseCore 0:
  48.8 89.0 all-gather.1
  206.9 82.7 reduce-scatter.2
  292.0 40.5 reduce-scatter.4
